TPU v7x, 32 devices: a whole 2x2x4 slice. The times are simulated.
32 devices in a mesh: gx: 4 (over y, x), gy: 4 (over z), gz: 2 (over core).
Axes of the slice: x: 2, y: 2, z: 4, core: 2. Of those that a mesh axis runs over, the one named last changes fastest.
Arguments:
- residual: float32 [3, 32, 256, 512], P(None, 'gz', 'gx', 'gy'), may hold values from -32 to 32
- edge_diag: float32 [3, 32, 256, 512], P(None, 'gz', 'gx', 'gy'), may hold values from 6.5 to 9
- node_shift: float32 [32, 256, 512], P('gz', 'gx', 'gy'), may hold values from 0.05 to 3
- coarse_shift: float32 [16, 128, 256], P('gz', 'gx', 'gy'), may hold values from 0.05 to 3
Outputs:
- correction: float32 [3, 32, 256, 512], P(None, 'gz', 'gx', 'gy')
All inputs are finite; a program needn't handle non-finite values.
Results may differ from a plain program's by a relative error of at most 0.000021.
Values sent between devices are 32-bit elements; how exact they have to be, the bound alone decides.
No kernel may reach another device: no remote copies, remote signals or barrier semaphores. Data moves between devices by JAX's collectives and lax.ppermute only.
A program may use at most 128 MiB of HBM per device.

v0:
```python
import jax
import jax.numpy as jnp
from jax import lax
from jax.sharding import PartitionSpec as P


def with_halo(block, sides, width):
    for axis, dim in sides:
        count = lax.axis_size(axis)
        forward = [(i, i + 1) for i in range(count - 1)]
        backward = [(target, source) for source, target in forward]
        low = lax.ppermute(
            lax.slice_in_dim(block, block.shape[dim] - width, None, axis=dim), axis, forward
        )
        high = lax.ppermute(lax.slice_in_dim(block, 0, width, axis=dim), axis, backward)
        block = jnp.concatenate([low, block, high], axis=dim)
    return block


def neighbours(padded):
    total = padded[2:, 1:-1, 1:-1] + padded[:-2, 1:-1, 1:-1]
    total = total + padded[1:-1, 2:, 1:-1] + padded[1:-1, :-2, 1:-1]
    return total + padded[1:-1, 1:-1, 2:] + padded[1:-1, 1:-1, :-2]


def node_faces(field):
    return with_halo(field, (("gx", 1), ("gy", 2), ("gz", 0)), 1)


def coarse_faces(field):
    return with_halo(field, (("gx", 1), ("gy", 2), ("gz", 0)), 1)


def apply_padded(padded, diagonal):
    return diagonal * padded[1:-1, 1:-1, 1:-1] - neighbours(padded)


def local(residual, edge_diag, node_shift, coarse_shift):
    joined = jnp.concatenate((residual, edge_diag), axis=0)
    padded_both = with_halo(joined, (("gx", 2), ("gy", 3), ("gz", 1)), 1)
    padded_diag = padded_both[3:]
    padded = padded_both[:3] / jnp.where(padded_diag > 0.0, padded_diag, 1.0)
    scaled = padded[:, 1:-1, 1:-1, 1:-1]
    edge_near = jnp.stack([neighbours(padded[component]) for component in range(3)])
    smooth_part = 2.0 * scaled - (edge_diag * scaled - edge_near) / edge_diag
    nodal_rhs = (
        padded[0, :-2, 1:-1, 1:-1]
        - scaled[0]
        + (padded[1, 1:-1, :-2, 1:-1] - scaled[1])
        + (padded[2, 1:-1, 1:-1, :-2] - scaled[2])
    )
    node_diag = 6.0 + node_shift
    first_guess = nodal_rhs / node_diag
    node_res = nodal_rhs - apply_padded(node_faces(first_guess), node_diag)
    sx, sy, sz = node_res.shape
    coarse_rhs = node_res.reshape(sx // 2, 2, sy // 2, 2, sz // 2, 2).sum(axis=(1, 3, 5))
    coarse_diag = 6.0 + coarse_shift
    first_dir = coarse_rhs / coarse_diag
    first_image = apply_padded(coarse_faces(first_dir), coarse_diag)
    second_dir = first_image / coarse_diag
    second_image = apply_padded(coarse_faces(second_dir), coarse_diag)
    gone, gtwo, hone, hmix, htwo = lax.psum(
        (
            jnp.sum(first_dir * coarse_rhs),
            jnp.sum(second_dir * coarse_rhs),
            jnp.sum(first_dir * first_image),
            jnp.sum(second_dir * first_image),
            jnp.sum(second_dir * second_image),
        ),
        ("gx", "gy", "gz"),
    )
    coef_two = (gtwo - hmix * gone / hone) / (htwo - hmix * hmix / hone)
    coef_one = (gone - hmix * coef_two) / hone
    coarse_sol = coef_one * first_dir + coef_two * second_dir
    spread = jnp.broadcast_to(
        coarse_sol[:, None, :, None, :, None], (sx // 2, 2, sy // 2, 2, sz // 2, 2)
    ).reshape(sx, sy, sz)
    nodal = first_guess + spread
    final_nodal = nodal + (nodal_rhs - apply_padded(node_faces(nodal), node_diag)) / node_diag
    fpad = node_faces(final_nodal)
    grads = jnp.stack(
        [
            fpad[2:, 1:-1, 1:-1] - final_nodal,
            fpad[1:-1, 2:, 1:-1] - final_nodal,
            fpad[1:-1, 1:-1, 2:] - final_nodal,
        ]
    )
    return smooth_part + grads


def solution(mesh):
    placed = (
        P(None, "gz", "gx", "gy"),
        P(None, "gz", "gx", "gy"),
        P("gz", "gx", "gy"),
        P("gz", "gx", "gy"),
    )
    return jax.shard_map(
        local, mesh=mesh, in_specs=placed, out_specs=P(None, "gz", "gx", "gy"), check_vma=False
    )
```

profile of v0, /device:TPU:0, one launch (start us, length us, event | category | flops | bytes accessed | tf_op | source)
XLA Modules:
  0.0 311.6 jit_solution(5837893788152960340)
XLA Ops:
  2.1 4.9 %collective-permute-start = (f32[6,16,1,128]{3,2,1,0:T(1,128)S(1)}, f32[6,16,1,128]{3,2,1,0:T(1,128)S(1)}, u32[]{:S(2)}, u32[]{:S(2)}) collective-permute-start(f32[6,16,1,128]{3,2,1,0:T(1,128)S(1)} %get-tuple-element.24), channel_id=1, source_target_pairs={{0,8},{8,16},{16,24},{1,9},{9,17},{17,25},{2,10},{10,18},{18,26},{... | collective-permute-start | bytes 147464 | tf_op jit(solution)/shard_map/ppermute | solution.py:12
  8.8 4.3 %collective-permute-done.1 = f32[6,16,1,128]{3,2,1,0:T(1,128)S(1)} collective-permute-done((f32[6,16,1,128]{3,2,1,0:T(1,128)S(1)}, f32[6,16,1,128]{3,2,1,0:T(1,128)S(1)}, u32[]{:S(2)}, u32[]{:S(2)}) %collective-permute-start.1) | collective-permute-done | bytes 49184 | tf_op jit(solution)/shard_map/ppermute | solution.py:15
  13.6 4.0 %fusion.47 = (f32[6,16,66,1]{3,2,1,0:T(8,128)}, f32[6,16,66,1]{3,2,1,0:T(8,128)}) fusion(f32[6,16,66,128]{3,2,1,0:T(8,128)S(1)} %pad_maximum_fusion.1), kind=kLoop, calls=%fused_computation.196 | loop fusion | bytes 101376 | tf_op jit(solution)/shard_map/slice | solution.py:13
  20.2 3.5 %collective-permute-start.2 = (f32[6,16,66,1]{2,1,3,0:T(8,128)S(1)}, f32[6,16,66,1]{2,1,3,0:T(8,128)S(1)}, u32[]{:S(2)}, u32[]{:S(2)}) collective-permute-start(f32[6,16,66,1]{2,1,3,0:T(8,128)S(1)} %copy.5), channel_id=1, source_target_pairs={{0,2},{2,4},{4,6},{1,3},{3,5},{5,7},{8,10},{10,12},{12,14},{9,11},... | collective-permute-start | bytes 76040 | tf_op jit(solution)/shard_map/ppermute | solution.py:12
  42.0 5.0 %pad_maximum_fusion = f32[6,18,66,130]{3,2,1,0:T(8,128)S(1)} fusion(f32[6,1,66,130]{3,2,1,0:T(8,128)S(1)} %collective-permute-done.5, f32[6,16,66,1]{3,2,1,0:T(8,128)S(1)} %copy-done.3, f32[6,16,1,128]{3,2,1,0:T(1,128)S(1)} %collective-permute-done.1, f32[6,16,64,128]{3,2,1,0:T(8,128)S(1)} %constant_dynamic-update-slice_fusion, ...), kind=kLoop, calls=%fused_computation.1 | loop fusion | flops 5559840 | bytes 7413120 | tf_op jit(solution)/shard_map/concatenate | solution.py:16
  48.8 4.3 %collective-permute-start.6 = (f32[16,1,128]{2,1,0:T(1,128)S(1)}, f32[16,1,128]{2,1,0:T(1,128)S(1)}, u32[]{:S(2)}, u32[]{:S(2)}) collective-permute-start(f32[16,1,128]{2,1,0:T(1,128)S(1)} %get-tuple-element.43), channel_id=1, source_target_pairs={{0,8},{8,16},{16,24},{1,9},{9,17},{17,25},{2,10},{10,18},{18,26},{... | collective-permute-start | bytes 24584 | tf_op jit(solution)/shard_map/ppermute | solution.py:12
  54.5 4.2 %collective-permute-done.7 = f32[16,1,128]{2,1,0:T(1,128)S(1)} collective-permute-done((f32[16,1,128]{2,1,0:T(1,128)S(1)}, f32[16,1,128]{2,1,0:T(1,128)S(1)}, u32[]{:S(2)}, u32[]{:S(2)}) %collective-permute-start.7) | collective-permute-done | bytes 8224 | tf_op jit(solution)/shard_map/ppermute | solution.py:15
  64.6 3.9 %collective-permute-done.9 = f32[16,66,1]{1,0,2:T(8,128)S(1)} collective-permute-done((f32[16,66,1]{1,0,2:T(8,128)S(1)}, f32[16,66,1]{1,0,2:T(8,128)S(1)}, u32[]{:S(2)}, u32[]{:S(2)}) %collective-permute-start.9) | collective-permute-done | bytes 4256 | tf_op jit(solution)/shard_map/ppermute | solution.py:15
  75.0 34.9 %reshape.12 = f32[8,2,32,2,64,2]{5,4,3,2,1,0:T(8,128)} reshape(f32[16,64,128]{2,1,0:T(8,128)S(1)} %fusion.21) | data formatting | bytes 1048576 | tf_op jit(solution)/shard_map/reshape | solution.py:56
  109.8 12.2 %reduce_sum.54 = f32[8,32,64]{2,1,0:T(8,128)S(1)} reduce(f32[8,2,32,2,64,2]{5,4,3,2,1,0:T(8,128)} %reshape.12, f32[]{:T(128)} %constant.4.clone.1), dimensions={1,3,5}, to_apply=%region_0.1 | reduce | flops 114688 | bytes 589828 | tf_op jit(solution)/shard_map/reduce_sum | solution.py:56
  126.9 4.2 %collective-permute-done.13 = f32[8,1,64]{2,1,0:T(1,128)S(1)} collective-permute-done((f32[8,1,64]{2,1,0:T(1,128)S(1)}, f32[8,1,64]{2,1,0:T(1,128)S(1)}, u32[]{:S(2)}, u32[]{:S(2)}) %collective-permute-start.13) | collective-permute-done | bytes 2080 | tf_op jit(solution)/shard_map/ppermute | solution.py:15
  131.2 3.5 %collective-permute-start.14 = (f32[8,34,1]{2,1,0:T(8,128)S(1)}, f32[8,34,1]{2,1,0:T(8,128)S(1)}, u32[]{:S(2)}, u32[]{:S(2)}) collective-permute-start(f32[8,34,1]{2,1,0:T(8,128)S(1)} %get-tuple-element.52), channel_id=1, source_target_pairs={{0,2},{2,4},{4,6},{1,3},{3,5},{5,7},{8,10},{10,12},{12,14},{9,11},... | collective-permute-start | bytes 3272 | tf_op jit(solution)/shard_map/ppermute | solution.py:12
  137.5 4.4 %collective-permute-done.15 = f32[8,34,1]{2,1,0:T(8,128)S(1)} collective-permute-done((f32[8,34,1]{2,1,0:T(8,128)S(1)}, f32[8,34,1]{2,1,0:T(8,128)S(1)}, u32[]{:S(2)}, u32[]{:S(2)}) %collective-permute-start.15) | collective-permute-done | bytes 1120 | tf_op jit(solution)/shard_map/ppermute | solution.py:15
  152.3 4.2 %collective-permute-done.19 = f32[8,1,64]{2,1,0:T(1,128)S(1)} collective-permute-done((f32[8,1,64]{2,1,0:T(1,128)S(1)}, f32[8,1,64]{2,1,0:T(1,128)S(1)}, u32[]{:S(2)}, u32[]{:S(2)}) %collective-permute-start.19) | collective-permute-done | bytes 2080 | tf_op jit(solution)/shard_map/ppermute | solution.py:15
  162.1 4.4 %collective-permute-done.21 = f32[8,34,1]{2,1,0:T(8,128)S(1)} collective-permute-done((f32[8,34,1]{2,1,0:T(8,128)S(1)}, f32[8,34,1]{2,1,0:T(8,128)S(1)}, u32[]{:S(2)}, u32[]{:S(2)}) %collective-permute-start.21) | collective-permute-done | bytes 1120 | tf_op jit(solution)/shard_map/ppermute | solution.py:15
  172.7 38.0 %all-reduce = (f32[]{:T(128)}, f32[]{:T(128)}, f32[]{:T(128)}, f32[]{:T(128)}, f32[]{:T(128)}) all-reduce(f32[]{:T(128)} %get-tuple-element.7, f32[]{:T(128)} %get-tuple-element.6, f32[]{:T(128)} %get-tuple-element.8, f32[]{:T(128)} %get-tuple-element.5, f32[]{:T(128)} %fusion.35), channel_id=1, replica_groups=mesh['gx'=4,'gy'=4,'gz'=2] {'gx','gy','gz'}, use_global_device_ids=true, to_apply=%region_6.7 | all-reduce | flops 5 | bytes 40 | tf_op jit(solution)/shard_map/psum | solution.py:62
  217.8 11.4 %broadcast_in_dim.11 = f32[8,2,32,2,64,2]{5,4,3,2,1,0:T(8,128)} broadcast(f32[8,32,64]{2,1,0:T(8,128)S(1)} %multiply_add_fusion), dimensions={0,2,4} | broadcast | bytes 589824 | tf_op jit(solution)/shard_map/broadcast_in_dim | solution.py:75
  229.2 24.0 %reshape.13 = f32[16,64,128]{2,1,0:T(8,128)S(1)} reshape(f32[8,2,32,2,64,2]{5,4,3,2,1,0:T(8,128)} %broadcast_in_dim.11) | data formatting | bytes 1048576 | tf_op jit(solution)/shard_map/reshape | solution.py:77
  253.4 4.2 %collective-permute-start.24 = (f32[16,1,128]{2,1,0:T(1,128)S(1)}, f32[16,1,128]{2,1,0:T(1,128)S(1)}, u32[]{:S(2)}, u32[]{:S(2)}) collective-permute-start(f32[16,1,128]{2,1,0:T(1,128)S(1)} %get-tuple-element.41), channel_id=1, source_target_pairs={{0,8},{8,16},{16,24},{1,9},{9,17},{17,25},{2,10},{10,18},{18,26},{... | collective-permute-start | bytes 24584 | tf_op jit(solution)/shard_map/ppermute | solution.py:12
  258.9 4.2 %collective-permute-done.25 = f32[16,1,128]{2,1,0:T(1,128)S(1)} collective-permute-done((f32[16,1,128]{2,1,0:T(1,128)S(1)}, f32[16,1,128]{2,1,0:T(1,128)S(1)}, u32[]{:S(2)}, u32[]{:S(2)}) %collective-permute-start.25) | collective-permute-done | bytes 8224 | tf_op jit(solution)/shard_map/ppermute | solution.py:15
  263.6 4.0 %collective-permute-start.26 = (f32[16,66,1]{1,0,2:T(8,128)S(1)}, f32[16,66,1]{1,0,2:T(8,128)S(1)}, u32[]{:S(2)}, u32[]{:S(2)}) collective-permute-start(f32[16,66,1]{1,0,2:T(8,128)S(1)} %copy.15), channel_id=1, source_target_pairs={{0,2},{2,4},{4,6},{1,3},{3,5},{5,7},{8,10},{10,12},{12,14},{9,11},... | collective-permute-start | bytes 12680 | tf_op jit(solution)/shard_map/ppermute | solution.py:12
  269.5 3.9 %collective-permute-done.27 = f32[16,66,1]{1,0,2:T(8,128)S(1)} collective-permute-done((f32[16,66,1]{1,0,2:T(8,128)S(1)}, f32[16,66,1]{1,0,2:T(8,128)S(1)}, u32[]{:S(2)}, u32[]{:S(2)}) %collective-permute-start.27) | collective-permute-done | bytes 4256 | tf_op jit(solution)/shard_map/ppermute | solution.py:15
  281.2 4.5 %collective-permute-start.30 = (f32[16,1,128]{2,1,0:T(1,128)S(1)}, f32[16,1,128]{2,1,0:T(1,128)S(1)}, u32[]{:S(2)}, u32[]{:S(2)}) collective-permute-start(f32[16,1,128]{2,1,0:T(1,128)S(1)} %get-tuple-element.39), channel_id=1, source_target_pairs={{0,8},{8,16},{16,24},{1,9},{9,17},{17,25},{2,10},{10,18},{18,26},{... | collective-permute-start | bytes 24584 | tf_op jit(solution)/shard_map/ppermute | solution.py:12
  307.5 4.1 %fusion.3 = f32[3,16,64,128]{3,2,1,0:T(8,128)} fusion(f32[3,16,64,128]{3,2,1,0:T(8,128)S(1)} %copy-done.6, f32[1,16,64,128]{3,2,1,0:T(8,128)S(1)} %copy-done.10, f32[1,16,64,128]{3,2,1,0:T(8,128)S(1)} %copy-done.11, f32[1,16,64,128]{3,2,1,0:T(8,128)S(1)} %fusion.31, f32[1,16,64,128]{3,2,1,0:T(8,128)S(1)} %get-tuple-element.31, ...), kind=kLoop, calls=%fused_computation.7 | loop fusion | flops 3932160 | bytes 7864320 | tf_op jit(solution)/shard_map/add | solution.py:88
  (134 shorter events, 103.8 us)
Async XLA Ops:
  2.1 6.6 %collective-permute-start = (f32[6,16,1,128]{3,2,1,0:T(1,128)S(1)}, f32[6,16,1,128]{3,2,1,0:T(1,128)S(1)}, u32[]{:S(2)}, u32[]{:S(2)}) collective-permute-start(f32[6,16,1,128]{3,2,1,0:T(1,128)S(1)} %get-tuple-element.24), channel_id=1, source_target_pairs={{0,8},{8,16},{16,24},{1,9},{9,17},{17,25},{2,10},{10,18},{18,26},{... | collective-permute-start | bytes 147464 | tf_op jit(solution)/shard_map/ppermute | solution.py:12
  7.0 6.0 %collective-permute-start.1 = (f32[6,16,1,128]{3,2,1,0:T(1,128)S(1)}, f32[6,16,1,128]{3,2,1,0:T(1,128)S(1)}, u32[]{:S(2)}, u32[]{:S(2)}) collective-permute-start(f32[6,16,1,128]{3,2,1,0:T(1,128)S(1)} %get-tuple-element.25), channel_id=1, source_target_pairs={{8,0},{16,8},{24,16},{9,1},{17,9},{25,17},{10,2},{18,10},{26,18},{... | collective-permute-start | bytes 147464 | tf_op jit(solution)/shard_map/ppermute | solution.py:15
  20.2 7.5 %collective-permute-start.2 = (f32[6,16,66,1]{2,1,3,0:T(8,128)S(1)}, f32[6,16,66,1]{2,1,3,0:T(8,128)S(1)}, u32[]{:S(2)}, u32[]{:S(2)}) collective-permute-start(f32[6,16,66,1]{2,1,3,0:T(8,128)S(1)} %copy.5), channel_id=1, source_target_pairs={{0,2},{2,4},{4,6},{1,3},{3,5},{5,7},{8,10},{10,12},{12,14},{9,11},... | collective-permute-start | bytes 76040 | tf_op jit(solution)/shard_map/ppermute | solution.py:12
  26.5 6.0 %collective-permute-start.3 = (f32[6,16,66,1]{2,1,3,0:T(8,128)S(1)}, f32[6,16,66,1]{2,1,3,0:T(8,128)S(1)}, u32[]{:S(2)}, u32[]{:S(2)}) collective-permute-start(f32[6,16,66,1]{2,1,3,0:T(8,128)S(1)} %copy.6), channel_id=1, source_target_pairs={{2,0},{4,2},{6,4},{3,1},{5,3},{7,5},{10,8},{12,10},{14,12},{11,9},... | collective-permute-start | bytes 76040 | tf_op jit(solution)/shard_map/ppermute | solution.py:15
  48.8 5.7 %collective-permute-start.6 = (f32[16,1,128]{2,1,0:T(1,128)S(1)}, f32[16,1,128]{2,1,0:T(1,128)S(1)}, u32[]{:S(2)}, u32[]{:S(2)}) collective-permute-start(f32[16,1,128]{2,1,0:T(1,128)S(1)} %get-tuple-element.43), channel_id=1, source_target_pairs={{0,8},{8,16},{16,24},{1,9},{9,17},{17,25},{2,10},{10,18},{18,26},{... | collective-permute-start | bytes 24584 | tf_op jit(solution)/shard_map/ppermute | solution.py:12
  53.1 5.5 %collective-permute-start.7 = (f32[16,1,128]{2,1,0:T(1,128)S(1)}, f32[16,1,128]{2,1,0:T(1,128)S(1)}, u32[]{:S(2)}, u32[]{:S(2)}) collective-permute-start(f32[16,1,128]{2,1,0:T(1,128)S(1)} %get-tuple-element.44), channel_id=1, source_target_pairs={{8,0},{16,8},{24,16},{9,1},{17,9},{25,17},{10,2},{18,10},{26,18},{... | collective-permute-start | bytes 24584 | tf_op jit(solution)/shard_map/ppermute | solution.py:15
  59.2 5.0 %collective-permute-start.8 = (f32[16,66,1]{1,0,2:T(8,128)S(1)}, f32[16,66,1]{1,0,2:T(8,128)S(1)}, u32[]{:S(2)}, u32[]{:S(2)}) collective-permute-start(f32[16,66,1]{1,0,2:T(8,128)S(1)} %copy.9), channel_id=1, source_target_pairs={{0,2},{2,4},{4,6},{1,3},{3,5},{5,7},{8,10},{10,12},{12,14},{9,11},... | collective-permute-start | bytes 12680 | tf_op jit(solution)/shard_map/ppermute | solution.py:12
  62.9 5.6 %collective-permute-start.9 = (f32[16,66,1]{1,0,2:T(8,128)S(1)}, f32[16,66,1]{1,0,2:T(8,128)S(1)}, u32[]{:S(2)}, u32[]{:S(2)}) collective-permute-start(f32[16,66,1]{1,0,2:T(8,128)S(1)} %copy.10), channel_id=1, source_target_pairs={{2,0},{4,2},{6,4},{3,1},{5,3},{7,5},{10,8},{12,10},{14,12},{11,9},... | collective-permute-start | bytes 12680 | tf_op jit(solution)/shard_map/ppermute | solution.py:15
  122.2 4.7 %collective-permute-start.12 = (f32[8,1,64]{2,1,0:T(1,128)S(1)}, f32[8,1,64]{2,1,0:T(1,128)S(1)}, u32[]{:S(2)}, u32[]{:S(2)}) collective-permute-start(f32[8,1,64]{2,1,0:T(1,128)S(1)} %get-tuple-element.55), channel_id=1, source_target_pairs={{0,8},{8,16},{16,24},{1,9},{9,17},{17,25},{2,10},{10,18},{18,26},{... | collective-permute-start | bytes 6152 | tf_op jit(solution)/shard_map/ppermute | solution.py:12
  125.6 5.5 %collective-permute-start.13 = (f32[8,1,64]{2,1,0:T(1,128)S(1)}, f32[8,1,64]{2,1,0:T(1,128)S(1)}, u32[]{:S(2)}, u32[]{:S(2)}) collective-permute-start(f32[8,1,64]{2,1,0:T(1,128)S(1)} %get-tuple-element.56), channel_id=1, source_target_pairs={{8,0},{16,8},{24,16},{9,1},{17,9},{25,17},{10,2},{18,10},{26,18},{... | collective-permute-start | bytes 6152 | tf_op jit(solution)/shard_map/ppermute | solution.py:15
  131.2 6.3 %collective-permute-start.14 = (f32[8,34,1]{2,1,0:T(8,128)S(1)}, f32[8,34,1]{2,1,0:T(8,128)S(1)}, u32[]{:S(2)}, u32[]{:S(2)}) collective-permute-start(f32[8,34,1]{2,1,0:T(8,128)S(1)} %get-tuple-element.52), channel_id=1, source_target_pairs={{0,2},{2,4},{4,6},{1,3},{3,5},{5,7},{8,10},{10,12},{12,14},{9,11},... | collective-permute-start | bytes 3272 | tf_op jit(solution)/shard_map/ppermute | solution.py:12
  134.7 7.2 %collective-permute-start.15 = (f32[8,34,1]{2,1,0:T(8,128)S(1)}, f32[8,34,1]{2,1,0:T(8,128)S(1)}, u32[]{:S(2)}, u32[]{:S(2)}) collective-permute-start(f32[8,34,1]{2,1,0:T(8,128)S(1)} %get-tuple-element.51), channel_id=1, source_target_pairs={{2,0},{4,2},{6,4},{3,1},{5,3},{7,5},{10,8},{12,10},{14,12},{11,9},... | collective-permute-start | bytes 3272 | tf_op jit(solution)/shard_map/ppermute | solution.py:15
  151.0 5.5 %collective-permute-start.19 = (f32[8,1,64]{2,1,0:T(1,128)S(1)}, f32[8,1,64]{2,1,0:T(1,128)S(1)}, u32[]{:S(2)}, u32[]{:S(2)}) collective-permute-start(f32[8,1,64]{2,1,0:T(1,128)S(1)} %get-tuple-element.54), channel_id=1, source_target_pairs={{8,0},{16,8},{24,16},{9,1},{17,9},{25,17},{10,2},{18,10},{26,18},{... | collective-permute-start | bytes 6152 | tf_op jit(solution)/shard_map/ppermute | solution.py:15
  156.6 5.4 %collective-permute-start.20 = (f32[8,34,1]{2,1,0:T(8,128)S(1)}, f32[8,34,1]{2,1,0:T(8,128)S(1)}, u32[]{:S(2)}, u32[]{:S(2)}) collective-permute-start(f32[8,34,1]{2,1,0:T(8,128)S(1)} %get-tuple-element.50), channel_id=1, source_target_pairs={{0,2},{2,4},{4,6},{1,3},{3,5},{5,7},{8,10},{10,12},{12,14},{9,11},... | collective-permute-start | bytes 3272 | tf_op jit(solution)/shard_map/ppermute | solution.py:12
  159.3 7.2 %collective-permute-start.21 = (f32[8,34,1]{2,1,0:T(8,128)S(1)}, f32[8,34,1]{2,1,0:T(8,128)S(1)}, u32[]{:S(2)}, u32[]{:S(2)}) collective-permute-start(f32[8,34,1]{2,1,0:T(8,128)S(1)} %get-tuple-element.49), channel_id=1, source_target_pairs={{2,0},{4,2},{6,4},{3,1},{5,3},{7,5},{10,8},{12,10},{14,12},{11,9},... | collective-permute-start | bytes 3272 | tf_op jit(solution)/shard_map/ppermute | solution.py:15
  253.4 5.5 %collective-permute-start.24 = (f32[16,1,128]{2,1,0:T(1,128)S(1)}, f32[16,1,128]{2,1,0:T(1,128)S(1)}, u32[]{:S(2)}, u32[]{:S(2)}) collective-permute-start(f32[16,1,128]{2,1,0:T(1,128)S(1)} %get-tuple-element.41), channel_id=1, source_target_pairs={{0,8},{8,16},{16,24},{1,9},{9,17},{17,25},{2,10},{10,18},{18,26},{... | collective-permute-start | bytes 24584 | tf_op jit(solution)/shard_map/ppermute | solution.py:12
  257.5 5.5 %collective-permute-start.25 = (f32[16,1,128]{2,1,0:T(1,128)S(1)}, f32[16,1,128]{2,1,0:T(1,128)S(1)}, u32[]{:S(2)}, u32[]{:S(2)}) collective-permute-start(f32[16,1,128]{2,1,0:T(1,128)S(1)} %get-tuple-element.42), channel_id=1, source_target_pairs={{8,0},{16,8},{24,16},{9,1},{17,9},{25,17},{10,2},{18,10},{26,18},{... | collective-permute-start | bytes 24584 | tf_op jit(solution)/shard_map/ppermute | solution.py:15
  263.6 5.5 %collective-permute-start.26 = (f32[16,66,1]{1,0,2:T(8,128)S(1)}, f32[16,66,1]{1,0,2:T(8,128)S(1)}, u32[]{:S(2)}, u32[]{:S(2)}) collective-permute-start(f32[16,66,1]{1,0,2:T(8,128)S(1)} %copy.15), channel_id=1, source_target_pairs={{0,2},{2,4},{4,6},{1,3},{3,5},{5,7},{8,10},{10,12},{12,14},{9,11},... | collective-permute-start | bytes 12680 | tf_op jit(solution)/shard_map/ppermute | solution.py:12
  267.8 5.6 %collective-permute-start.27 = (f32[16,66,1]{1,0,2:T(8,128)S(1)}, f32[16,66,1]{1,0,2:T(8,128)S(1)}, u32[]{:S(2)}, u32[]{:S(2)}) collective-permute-start(f32[16,66,1]{1,0,2:T(8,128)S(1)} %copy.16), channel_id=1, source_target_pairs={{2,0},{4,2},{6,4},{3,1},{5,3},{7,5},{10,8},{12,10},{14,12},{11,9},... | collective-permute-start | bytes 12680 | tf_op jit(solution)/shard_map/ppermute | solution.py:15
  273.9 4.6 %collective-permute-start.28 = (f32[1,66,130]{2,1,0:T(8,128)S(1)}, f32[1,66,130]{2,1,0:T(8,128)S(1)}, u32[]{:S(2)}, u32[]{:S(2)}) collective-permute-start(f32[1,66,130]{2,1,0:T(8,128)S(1)} %get-tuple-element.26), channel_id=1, source_target_pairs={{1,0},{3,2},{5,4},{7,6},{9,8},{11,10},{13,12},{15,14},{17,16},{19,... | collective-permute-start | bytes 102968 | tf_op jit(solution)/shard_map/ppermute | solution.py:15
  281.2 7.2 %collective-permute-start.30 = (f32[16,1,128]{2,1,0:T(1,128)S(1)}, f32[16,1,128]{2,1,0:T(1,128)S(1)}, u32[]{:S(2)}, u32[]{:S(2)}) collective-permute-start(f32[16,1,128]{2,1,0:T(1,128)S(1)} %get-tuple-element.39), channel_id=1, source_target_pairs={{0,8},{8,16},{16,24},{1,9},{9,17},{17,25},{2,10},{10,18},{18,26},{... | collective-permute-start | bytes 24584 | tf_op jit(solution)/shard_map/ppermute | solution.py:12
  285.7 5.5 %collective-permute-start.31 = (f32[16,1,128]{2,1,0:T(1,128)S(1)}, f32[16,1,128]{2,1,0:T(1,128)S(1)}, u32[]{:S(2)}, u32[]{:S(2)}) collective-permute-start(f32[16,1,128]{2,1,0:T(1,128)S(1)} %get-tuple-element.40), channel_id=1, source_target_pairs={{8,0},{16,8},{24,16},{9,1},{17,9},{25,17},{10,2},{18,10},{26,18},{... | collective-permute-start | bytes 24584 | tf_op jit(solution)/shard_map/ppermute | solution.py:15
  293.8 7.6 %collective-permute-start.32 = (f32[16,66,1]{1,0,2:T(8,128)S(1)}, f32[16,66,1]{1,0,2:T(8,128)S(1)}, u32[]{:S(2)}, u32[]{:S(2)}) collective-permute-start(f32[16,66,1]{1,0,2:T(8,128)S(1)} %copy.21), channel_id=1, source_target_pairs={{0,2},{2,4},{4,6},{1,3},{3,5},{5,7},{8,10},{10,12},{12,14},{9,11},... | collective-permute-start | bytes 12680 | tf_op jit(solution)/shard_map/ppermute | solution.py:12
  297.7 5.6 %collective-permute-start.33 = (f32[16,66,1]{1,0,2:T(8,128)S(1)}, f32[16,66,1]{1,0,2:T(8,128)S(1)}, u32[]{:S(2)}, u32[]{:S(2)}) collective-permute-start(f32[16,66,1]{1,0,2:T(8,128)S(1)} %copy.22), channel_id=1, source_target_pairs={{2,0},{4,2},{6,4},{3,1},{5,3},{7,5},{10,8},{12,10},{14,12},{11,9},... | collective-permute-start | bytes 12680 | tf_op jit(solution)/shard_map/ppermute | solution.py:15
  (24 other events, 152.8 us)
where the time goes:
time: 313 us; the launch traced here: 312 us
  local copies, waits for them, and re-layouts  96.2 us (31%)
  starting transfers between devices  80.9 us (26%)
  waiting for transfers between devices  54.6 us (17%)
  blocking collectives  38 us (12%)
  other arithmetic  34.1 us (11%)
  between operations  7.79 us (2%)
    ppermute x17, starting transfers between devices, with_halo(): lax.ppermute(lax.slice_in_dim(block, block.shape[dim] - width, None, axis...  57.2 us
    ppermute x18, waiting for transfers between devices, with_halo(): lax.ppermute(lax.slice_in_dim(block, 0, width, axis=dim), axis, backward)  47.6 us
    psum x1, blocking collectives, local(): lax.psum((jnp.sum(first_dir * coarse_rhs), jnp.sum(second_dir * coarse_rh...  38 us
    reshape x1, local copies, waits for them, and re-layouts, local(): node_res.reshape(sx // 2, 2, sy // 2, 2, sz // 2, 2).sum(axis=(1, 3, 5))  34.9 us
    reshape x1, local copies, waits for them, and re-layouts, local(): spread = jnp.broadcast_to(coarse_sol[:, None, :, None, :, None], (sx // 2...  24 us
    ppermute x18, starting transfers between devices, with_halo(): lax.ppermute(lax.slice_in_dim(block, 0, width, axis=dim), axis, backward)  23.7 us
    reduce_sum x1, other arithmetic, local(): node_res.reshape(sx // 2, 2, sy // 2, 2, sz // 2, 2).sum(axis=(1, 3, 5))  12.2 us
    broadcast_in_dim x1, local copies, waits for them, and re-layouts, local(): jnp.broadcast_to(coarse_sol[:, None, :, None, :, None], (sx // 2, 2, sy /...  11.4 us
  transfers between devices with their start and end apart: 35, of which 22 were waited for; matrix products, arithmetic and copies ran while one was open for 4% of the time, Pallas kernels for 0%

commit v1 on v0

v1 whole, which is shorter than its diff:
```python
import jax
import jax.numpy as jnp
from jax import lax
from jax.experimental import pallas as pl
from jax.experimental.pallas import tpu as pltpu
from jax.sharding import PartitionSpec as P

F32 = jnp.float32
HIGHEST = lax.Precision.HIGHEST
LANES = 128


def lane_ids(rows):
    return lax.broadcasted_iota(jnp.int32, (rows, LANES), 1)


def row_ids(rows):
    return lax.broadcasted_iota(jnp.int32, (rows, LANES), 0)


def shift_lanes(value, amount):
    return pltpu.roll(value, amount % LANES, 1)


def shift_rows(value, amount):
    return pltpu.roll(value, amount % value.shape[0], 0)


def low_of(axis, size, first, second):
    place = lax.axis_index(axis)
    odd = place % 2 == 1
    zero = jnp.zeros_like(first)
    if second is None:
        return jnp.where(odd, first, zero)
    return jnp.where(odd, first, jnp.where(place > 0, second, zero))


def high_of(axis, size, first, second):
    place = lax.axis_index(axis)
    even = place % 2 == 0
    zero = jnp.zeros_like(first)
    if second is None:
        return jnp.where(even, first, zero)
    return jnp.where(even, first, jnp.where(place < size - 1, second, zero))


def from_below(axis, value):
    return jnp.where(lax.axis_index(axis) > 0, value, jnp.zeros_like(value))


def from_above(axis, size, value):
    return jnp.where(lax.axis_index(axis) < size - 1, value, jnp.zeros_like(value))


def ring(value, axis, step):
    size = lax.axis_size(axis)
    return lax.ppermute(value, axis, [(i, (i + step) % size) for i in range(size)])


def swap(values, axis):
    size = lax.axis_size(axis)
    even = [(i, i ^ 1) for i in range(size)]
    out = [lax.ppermute(values[0], axis, even)]
    if len(values) > 1:
        odd = [(i, (i + 1) % size if i % 2 else (i - 1) % size) for i in range(size)]
        out.append(lax.ppermute(values[1], axis, odd))
    return out


def write_sides(axis, refs, up, down):
    even = lax.axis_index(axis) % 2 == 0

    @pl.when(even)
    def _():
        up(refs[0])
        if len(refs) > 1:
            down(refs[1])

    @pl.when(jnp.logical_not(even))
    def _():
        down(refs[0])
        if len(refs) > 1:
            up(refs[1])


def call(body, outs, name, scratch=(), **kwargs):
    return pl.pallas_call(
        body,
        out_shape=[jax.ShapeDtypeStruct(shape, F32) for shape in outs],
        scratch_shapes=[pltpu.VMEM(shape, F32) for shape in scratch],
        name=name,
        **kwargs,
    )


def vmem(count):
    return [pl.BlockSpec(memory_space=pltpu.VMEM)] * count


def edge_stage(residual, edge_diag):
    _, nz, nx, ny = residual.shape
    step = 4
    steps = nz // step

    def body(res, diag, part, up_z, up_x, up_y, low_z, low_x, low_y, last):
        block = pl.program_id(0)
        lane = lane_ids(nx)
        row = row_ids(nx)

        @pl.when(block == 0)
        def _():
            last[...] = jnp.zeros_like(last)
            up_y[...] = jnp.zeros_like(up_y)
            low_y[...] = jnp.zeros_like(low_y)

        before = last[...]
        high = up_y[...]
        low = low_y[...]
        for j in range(step):
            z = block * step + j
            s = [res[k, j] / diag[k, j] for k in range(3)]
            total = before - s[0]
            total += jnp.where(row == 0, 0.0, shift_rows(s[1], 1)) - s[1]
            total += jnp.where(lane == 0, 0.0, shift_lanes(s[2], 1)) - s[2]
            part[j] = total
            before = s[0]
            for k in range(3):
                up_x[pl.ds(k * nz + z, 1), :] = s[k][nx - 1 :, :]
                low_x[pl.ds(k * nz + z, 1), :] = s[k][:1, :]
                spot = k * nz + z
                high = jnp.where(lane == spot, pltpu.roll(s[k], spot + 1, 1), high)
                low = jnp.where(lane == spot, pltpu.roll(s[k], spot, 1), low)
            if j == 0:

                @pl.when(block == 0)
                def _():
                    for k in range(3):
                        low_z[k] = s[k]

            if j == step - 1:

                @pl.when(block == steps - 1)
                def _():
                    for k in range(3):
                        up_z[k] = s[k]

        last[...] = before
        up_y[...] = high
        low_y[...] = low

    whole = lambda *shape: pl.BlockSpec(shape, lambda i: (0,) * len(shape))
    spec = pl.BlockSpec((3, step, nx, ny), lambda i: (0, i, 0, 0))
    faces = [(3, nx, ny), (3 * nz, ny), (nx, LANES)] * 2
    return call(
        body,
        [(nz, nx, ny)] + faces,
        "edge_stage",
        scratch=[(nx, ny)],
        grid=(steps,),
        in_specs=[spec, spec],
        out_specs=[pl.BlockSpec((step, nx, ny), lambda i: (i, 0, 0))] + [whole(*f) for f in faces],
    )(residual, edge_diag)


def plane(values, row_count):
    return jnp.concatenate([values, jnp.zeros((row_count - values.shape[0], LANES), F32)], axis=0)


def nodal_stage(part, node_shift, coarse_shift, got_z, got_x, got_y, low_z, z_count):
    nz, nx, ny = part.shape
    cz, cx, cy = nz // 2, nx // 2, ny // 2
    rows = cx + 8
    sends = 1 if z_count == 2 else 2

    def body(part, shift, coarse, gz, gx, gy, low_z, fg, rhs, xb, yb, w, *rest):
        out, (pair, s_, xl_, yl_, zl_, zh_) = rest[:sends], rest[sends:]
        lane = lane_ids(nx)
        row = row_ids(nx)
        lane_c = lane_ids(rows)
        row_c = row_ids(rows)
        below_z = from_below("gz", gz[0])
        below_y = from_below("gy", gy[...])
        fine = lax.broadcasted_iota(jnp.int32, (ny, 2 * LANES), 0)
        coarse_lane = lax.broadcasted_iota(jnp.int32, (ny, 2 * LANES), 1)
        miss = jnp.where(
            coarse_lane < LANES, fine // 2 - coarse_lane, fine - 2 * (coarse_lane - LANES)
        )
        gather = jnp.where(miss == 0, 1.0, 0.0)
        for c in range(cz):
            both = []
            for z in (2 * c, 2 * c + 1):
                total = part[z]
                if z == 0:
                    total += below_z
                total += jnp.where(row == 0, from_below("gx", gx[nz + z : nz + z + 1, :]), 0.0)
                total += jnp.where(lane == 0, shift_lanes(below_y, -(2 * nz + z)), 0.0)
                guess = total / (6.0 + shift[z])
                fg[z] = guess
                both.append(guess)
            pair[c % 2] = both[0] + both[1]
            low = pair[c % 2, pl.ds(0, cx, 2), :]
            high = pair[c % 2, pl.ds(1, cx, 2), :]
            first = fg[2 * c, pl.ds(0, cx, 2), :] + fg[2 * c, pl.ds(1, cx, 2), :]
            stacked = jnp.concatenate([low + high, low, first], axis=0)
            sums = jnp.dot(stacked, gather, precision=HIGHEST, preferred_element_type=F32)
            s = sums[:cx, :LANES]
            z_low = sums[2 * cx :, :LANES]
            s_[c] = plane(s, rows)
            yl_[c] = plane(sums[:cx, LANES:], rows)
            xl_[c] = plane(sums[cx : 2 * cx, :LANES], rows)
            zl_[c] = plane(z_low, rows)
            zh_[c] = plane(s - z_low, rows)
            w[c] = jnp.zeros((rows, LANES), F32)
            w[c, :cx, :cy] = 1.0 / (6.0 + coarse[c])
        for c in range(cz):
            s, x_low, y_low = s_[c], xl_[c], yl_[c]
            x_high = s - x_low
            y_high = s - y_low
            total = 3.0 * s
            total += shift_rows(x_low, -1) + shift_rows(x_high, 1)
            total += shift_lanes(y_low, -1) + shift_lanes(y_high, 1)
            if c > 0:
                total += zh_[c - 1]
            if c < cz - 1:
                total += zl_[c + 1]
            rhs[c] = total
            xb[c] = jnp.where(row_c < cx // 2, x_low, x_high)
            yb[c] = jnp.where(lane_c < cy // 2, y_low, y_high)
        rhs[cz] = zh_[cz - 1]
        rhs[cz + 1] = jnp.zeros((rows, LANES), F32)
        rhs[cz + 2] = jnp.zeros((rows, LANES), F32)
        rhs[cz + 3] = zl_[0]

        def fill(ref, near, far, half, face):
            planes = [rhs[near], rhs[far], w[near], w[far], half]
            planes += [xb[near], xb[far], yb[near], yb[far]]
            for i, value in enumerate(planes):
                ref[i * rows : (i + 1) * rows, :] = value
            ref[9 * rows : 9 * rows + nx, :] = face

        def up(ref):
            fill(ref, cz - 1, cz - 2, zh_[cz - 1], fg[nz - 1])
            for k in range(3):
                at = 9 * rows + nx + k * nx
                ref[at : at + nx, :] = jnp.zeros((nx, LANES), F32)

        def down(ref):
            fill(ref, 0, 1, zl_[0], fg[0])
            for k in range(3):
                at = 9 * rows + nx + k * nx
                ref[at : at + nx, :] = low_z[k]

        write_sides("gz", out, up, down)

    coarse = (cz, rows, LANES)
    send = (9 * rows + 4 * nx, LANES)
    return call(
        body,
        [(nz, nx, ny), (cz + 4, rows, LANES), coarse, coarse, coarse] + [send] * sends,
        "nodal_stage",
        scratch=[(2, nx, ny), coarse, coarse, coarse, coarse, coarse],
        in_specs=vmem(7),
        out_specs=vmem(5 + sends),
    )(part, node_shift, coarse_shift, got_z, got_x, got_y, low_z)


def x_stage(got, rhs, xb, yb, w, fg, low_x, z_count, x_count):
    planes, rows, _ = rhs.shape
    cz, cx = planes - 4, rows - 8
    nz, nx, _ = fg.shape
    sends = 1 if x_count == 2 else 2
    gots = len(got)

    def body(*refs):
        got = refs[:gots]
        rhs, xb, yb, w, fg, low_x, rhs2, yb2, w2 = refs[gots : gots + 9]
        out, (xb2,) = refs[gots + 9 : gots + 9 + sends], refs[gots + 9 + sends :]

        def take(pick, i):
            at = slice(i * rows, (i + 1) * rows)
            values = [ref[at, :] for ref in got]
            return pick("gz", z_count, values[0], values[1] if gots > 1 else None)

        for c in range(1, cz - 1):
            rhs2[c] = rhs[c]
        rhs2[0] = rhs[0] + take(low_of, 4)
        rhs2[cz - 1] = rhs[cz - 1] + take(high_of, 4)
        rhs2[cz] = rhs[cz] + take(high_of, 0)
        rhs2[cz + 1] = take(high_of, 1)
        rhs2[cz + 2] = take(low_of, 1)
        rhs2[cz + 3] = rhs[cz + 3] + take(low_of, 0)
        for here, there, i in ((w, w2, 2), (xb, xb2, 5), (yb, yb2, 7)):
            for c in range(cz):
                there[c] = here[c]
            there[cz] = take(high_of, i)
            there[cz + 1] = take(high_of, i + 1)
            there[cz + 2] = take(low_of, i + 1)
            there[cz + 3] = take(low_of, i)

        def fill(ref, near, far, fine):
            pieces = [rhs2[:, near, :], rhs2[:, far, :], w2[:, near, :], w2[:, far, :]]
            pieces += [xb2[:, near, :], yb2[:, near, :], yb2[:, far, :]]
            for i, value in enumerate(pieces):
                ref[i * 16 : i * 16 + planes, :] = value
                if planes < 16:
                    ref[i * 16 + planes : i * 16 + 16, :] = jnp.zeros((16 - planes, LANES), F32)
            ref[112 : 112 + nz, :] = fg[:, fine, :]

        def up(ref):
            fill(ref, cx - 1, cx - 2, nx - 1)
            ref[112 + nz : 112 + 4 * nz, :] = jnp.zeros((3 * nz, LANES), F32)

        def down(ref):
            fill(ref, 0, 1, 0)
            ref[112 + nz : 112 + 4 * nz, :] = low_x[...]

        write_sides("gx", out, up, down)

    whole = (planes, rows, LANES)
    return call(
        body,
        [whole, whole, whole] + [(112 + 4 * nz, LANES)] * sends,
        "x_stage",
        scratch=[whole],
        in_specs=vmem(gots + 6),
        out_specs=vmem(3 + sends),
    )(*got, rhs, xb, yb, w, fg, low_x)


def y_stage(got, rhs, yb, w, fg, low_y, x_count, y_count):
    planes, rows, _ = rhs.shape
    cx = rows - 8
    nz, nx, ny = fg.shape
    cy = ny // 2
    sends = 1 if y_count == 2 else 2
    gots = len(got)

    def body(*refs):
        got = refs[:gots]
        rhs, yb, w, fg, low_y, rhs3, w3 = refs[gots : gots + 7]
        out, (yb3, add) = refs[gots + 7 : gots + 7 + sends], refs[gots + 7 + sends :]

        def take(pick, i):
            at = slice(i * 16, i * 16 + planes)
            values = [ref[at, :] for ref in got]
            return pick("gx", x_count, values[0], values[1] if gots > 1 else None)

        add[...] = jnp.zeros_like(add)
        add[:, cx, :] = take(high_of, 0)
        add[:, cx + 1, :] = take(high_of, 1)
        add[:, rows - 1, :] = take(low_of, 0)
        add[:, rows - 2, :] = take(low_of, 1)
        add[:, cx - 1, :] = take(high_of, 4)
        add[:, 0, :] = take(low_of, 4)
        for c in range(planes):
            rhs3[c] = rhs[c] + add[c]
            w3[c] = w[c]
            yb3[c] = yb[c]
        for there, i in ((w3, 2), (yb3, 5)):
            there[:, cx, :] = take(high_of, i)
            there[:, cx + 1, :] = take(high_of, i + 1)
            there[:, rows - 1, :] = take(low_of, i)
            there[:, rows - 2, :] = take(low_of, i + 1)

        lane_c = lane_ids(rows)
        lane = lane_ids(nx)

        def fill(ref, near, far, fine, tail):
            acc = jnp.zeros((rows, LANES), F32)
            jobs = ((rhs3, near), (rhs3, far), (w3, near), (w3, far), (yb3, near))
            for i, (field, at) in enumerate(jobs):
                for z in range(planes):
                    spot = i * planes + z
                    acc = jnp.where(lane_c == spot, shift_lanes(field[z], spot - at), acc)
            acc = plane(acc, nx)
            base = 5 * planes
            for z in range(nz):
                acc = jnp.where(lane == base + z, shift_lanes(fg[z], base + z - fine), acc)
            if tail is not None:
                at = base + nz
                moved = shift_lanes(tail, at)
                acc = jnp.where((lane >= at) & (lane < at + 3 * nz), moved, acc)
            ref[...] = acc

        def up(ref):
            fill(ref, cy - 1, cy - 2, ny - 1, None)

        def down(ref):
            fill(ref, 0, 1, 0, low_y[...])

        write_sides("gy", out, up, down)

    whole = (planes, rows, LANES)
    return call(
        body,
        [whole, whole] + [(nx, LANES)] * sends,
        "y_stage",
        scratch=[whole, whole],
        in_specs=vmem(gots + 5),
        out_specs=vmem(2 + sends),
    )(*got, rhs, yb, w, fg, low_y)


def coarse_stage(got, rhs, w, y_count, devices):
    planes, rows, _ = rhs.shape
    cz, cx = planes - 4, rows - 8
    cy = LANES // 2
    gots = len(got)

    def body(*refs):
        got = refs[:gots]
        rhs, w, v1, v2, sums, tot, inv_, image_ = refs[gots:]
        values = [ref[:rows, :] for ref in got]
        second = values[1] if gots > 1 else None
        low = low_of("gy", y_count, values[0], second)
        high = high_of("gy", y_count, values[0], second)
        lane = lane_ids(rows)
        spots_r = ((cy, high, 0), (cy + 1, high, 1), (LANES - 1, low, 0), (LANES - 2, low, 1))
        spots_r += ((cy - 1, high, 4), (0, low, 4))
        for z in range(planes):
            right = rhs[z]
            for at, source, i in spots_r:
                moved = shift_lanes(source, at - (i * planes + z))
                right += jnp.where(lane == at, moved, 0.0)
            inv = w[z]
            for at, source, i in spots_r[:4]:
                moved = shift_lanes(source, at - ((i + 2) * planes + z))
                inv = jnp.where(lane == at, moved, inv)
            inv_[z] = inv
            tot[z] = right
            v1[z] = right * inv

        def near(field, z):
            here = field[z]
            total = field[(z + 1) % planes] + field[(z - 1) % planes]
            total += shift_rows(here, 1) + shift_rows(here, -1)
            return total + shift_lanes(here, 1) + shift_lanes(here, -1)

        v2[cz + 1] = jnp.zeros((rows, LANES), F32)
        v2[cz + 2] = jnp.zeros((rows, LANES), F32)
        for z in list(range(cz + 1)) + [planes - 1]:
            image = tot[z] - near(v1, z)
            if z < cz:
                image_[z] = image
            v2[z] = image * inv_[z]
        parts = [jnp.zeros((cx, LANES), F32)] * 5
        for z in range(cz):
            first, second_, right, image = v1[z], v2[z], tot[z], image_[z]
            third = image - near(v2, z)
            terms = (first * right, second_ * right, first * image, second_ * image, second_ * third)
            parts = [a + b[:cx, :] for a, b in zip(parts, terms)]
        keep = lane_ids(1) < cy
        lines = [jnp.where(keep, jnp.sum(a, axis=0, keepdims=True), 0.0) for a in parts]
        tile = jnp.concatenate(lines + [jnp.zeros((3, LANES), F32)], axis=0)
        column = jnp.sum(tile, axis=1, keepdims=True)
        spread = jnp.where(lane_ids(8) == row_ids(8), column, 0.0)
        line = jnp.sum(spread, axis=0, keepdims=True)
        sums[...] = jnp.broadcast_to(line[None], (devices, 1, LANES))

    whole = (planes, rows, LANES)
    return call(
        body,
        [whole, whole, (devices, 1, LANES)],
        "coarse_stage",
        scratch=[whole, whole, whole],
        in_specs=vmem(gots + 2),
        out_specs=vmem(3),
    )(*got, rhs, w)


def final_stage(sums, v1, v2, fg, node_shift, got_z, got_x, got_y, counts):
    planes, rows, _ = v1.shape
    cz, cx = planes - 4, rows - 8
    nz, nx, ny = fg.shape
    n_z, n_x, n_y = len(got_z), len(got_x), len(got_y)

    def body(*refs):
        sums, v1, v2, fg, shift = refs[:5]
        gz = refs[5 : 5 + n_z]
        gx = refs[5 + n_z : 5 + n_z + n_x]
        gy = refs[5 + n_z + n_x : 5 + n_z + n_x + n_y]
        fn, down_z, down_x, down_y, dup, inter = refs[5 + n_z + n_x + n_y :]

        def both(refs, axis, size, at):
            values = [ref[at, :] for ref in refs]
            second = values[1] if len(values) > 1 else None
            return low_of(axis, size, values[0], second), high_of(axis, size, values[0], second)

        total = jnp.sum(sums[...], axis=0)
        lane1 = lane_ids(1)
        gone, gtwo, hone, hmix, htwo = [
            jnp.sum(jnp.where(lane1 == i, total, 0.0), axis=1, keepdims=True) for i in range(5)
        ]
        two = (gtwo - hmix * gone / hone) / (htwo - hmix * hmix / hone)
        one = (gone - hmix * two) / hone
        source = lax.broadcasted_iota(jnp.int32, (LANES, 2 * LANES), 0)
        target = lax.broadcasted_iota(jnp.int32, (LANES, 2 * LANES), 1)
        fine = target - LANES
        side = jnp.where(fine % 2 == 1, fine // 2 + 1, (fine // 2 + LANES - 1) % LANES)
        spread = jnp.where(jnp.where(target < LANES, target // 2, side) == source, 1.0, 0.0)
        for z in list(range(cz + 1)) + [planes - 1]:
            sol = one * v1[z] + two * v2[z]
            dup[z] = jnp.dot(sol, spread, precision=HIGHEST, preferred_element_type=F32)

        z_face = slice(9 * rows, 9 * rows + nx)
        z_low, z_high = both(gz, "gz", counts[0], z_face)
        x_low, x_high = both(gx, "gx", counts[1], slice(112, 112 + nz))
        y_low, y_high = both(gy, "gy", counts[2], slice(0, nx))
        lane = lane_ids(nx)
        row = row_ids(nx)
        base = 5 * planes
        acc = jnp.zeros((nx, LANES), F32)
        for z in range(nz):
            c, odd = z // 2, z % 2
            here = dup[c, :, :LANES]
            same = 3.0 * here + dup[c, :, LANES:]
            same += dup[(c + 1 if odd else c - 1) % planes, :, :LANES]
            slot = z % 2
            inter[slot, pl.ds(0, cx, 2), :] = (same + shift_rows(here, 1))[:cx, :]
            inter[slot, pl.ds(1, cx, 2), :] = (same + shift_rows(here, -1))[:cx, :]
            guess = fg[z]
            around = inter[slot]
            around += fg[z - 1] if z > 0 else z_low
            around += fg[z + 1] if z < nz - 1 else z_high
            around += jnp.where(row == 0, x_low[z : z + 1, :], shift_rows(guess, 1))
            around += jnp.where(row == nx - 1, x_high[z : z + 1, :], shift_rows(guess, -1))
            left = shift_lanes(y_low, -(base + z))
            right = shift_lanes(y_high, -(base + z) - 1)
            around += jnp.where(lane == 0, left, shift_lanes(guess, 1))
            around += jnp.where(lane == LANES - 1, right, shift_lanes(guess, -1))
            value = guess + around / (6.0 + shift[z])
            fn[z] = value
            if z == 0:
                down_z[...] = value
            down_x[z : z + 1, :] = value[:1, :]
            acc = jnp.where(lane == z, shift_lanes(value, z), acc)
        down_y[...] = acc

    return call(
        body,
        [(nz, nx, ny), (nx, ny), (nz, ny), (nx, LANES)],
        "final_stage",
        scratch=[(planes, rows, 2 * LANES), (2, nx, LANES)],
        in_specs=vmem(5 + n_z + n_x + n_y),
        out_specs=vmem(4),
    )(sums, v1, v2, fg, node_shift, *got_z, *got_x, *got_y)


def output_stage(residual, edge_diag, fn, above, below, got_z, got_x, got_y, planes, counts):
    _, nz, nx, ny = residual.shape
    n_z, n_x, n_y = len(got_z), len(got_x), len(got_y)
    rows = nx // 2 + 8

    def body(*refs):
        res, diag, fn, fz, fx, fy, lz, lx, ly = refs[:9]
        gz = refs[9 : 9 + n_z]
        gx = refs[9 + n_z : 9 + n_z + n_x]
        gy = refs[9 + n_z + n_x : 9 + n_z + n_x + n_y]
        out, s = refs[9 + n_z + n_x + n_y :]
        k = pl.program_id(0)
        lane = lane_ids(nx)
        row = row_ids(nx)

        def above_of(refs, axis, size, at):
            values = [ref[at, :] for ref in refs]
            return high_of(axis, size, values[0], values[1] if len(values) > 1 else None)

        for z in range(nz):
            s[z] = res[0, z] / diag[0, z]
        z_low = from_below("gz", lz[k])
        z_high = above_of(gz, "gz", counts[0], pl.ds(9 * rows + nx + k * nx, nx))
        x_low = from_below("gx", lx[pl.ds(k * nz, nz), :])
        x_high = above_of(gx, "gx", counts[1], pl.ds(112 + nz + k * nz, nz))
        y_low = pltpu.roll(from_below("gy", ly[...]), (LANES - k * nz) % LANES, 1)
        y_high = above_of(gy, "gy", counts[2], pl.ds(0, nx))
        y_high = pltpu.roll(y_high, (2 * LANES - 5 * planes - nz - k * nz) % LANES, 1)
        for z in range(nz):
            here = s[z]
            around = s[z - 1] if z > 0 else z_low
            around += s[z + 1] if z < nz - 1 else z_high
            around += jnp.where(row == 0, x_low[z : z + 1, :], shift_rows(here, 1))
            around += jnp.where(row == nx - 1, x_high[z : z + 1, :], shift_rows(here, -1))
            left = shift_lanes(y_low, -z)
            right = shift_lanes(y_high, -z - 1)
            around += jnp.where(lane == 0, left, shift_lanes(here, 1))
            around += jnp.where(lane == LANES - 1, right, shift_lanes(here, -1))
            out[0, z] = here + around / diag[0, z] - fn[z]

        @pl.when(k == 0)
        def _():
            for z in range(nz - 1):
                out[0, z] += fn[z + 1]
            out[0, nz - 1] += from_above("gz", counts[0], fz[...])

        @pl.when(k == 1)
        def _():
            face = from_above("gx", counts[1], fx[...])
            for z in range(nz):
                out[0, z] += jnp.where(row == nx - 1, face[z : z + 1, :], shift_rows(fn[z], -1))

        @pl.when(k == 2)
        def _():
            face = from_above("gy", counts[2], fy[...])
            for z in range(nz):
                moved = shift_lanes(face, -z - 1)
                out[0, z] += jnp.where(lane == LANES - 1, moved, shift_lanes(fn[z], -1))

    spec = pl.BlockSpec((1, nz, nx, ny), lambda k: (k, 0, 0, 0))
    args = (fn, *above, *below, *got_z, *got_x, *got_y)
    whole = [pl.BlockSpec(a.shape, lambda k, n=a.ndim: (0,) * n) for a in args]
    return call(
        body,
        [residual.shape],
        "output_stage",
        scratch=[(nz, nx, ny)],
        grid=(3,),
        in_specs=[spec, spec] + whole,
        out_specs=[spec],
    )(residual, edge_diag, *args)[0]


def local(residual, edge_diag, node_shift, coarse_shift):
    axes = ("gz", "gx", "gy")
    counts = tuple(lax.axis_size(a) for a in axes)
    devices = counts[0] * counts[1] * counts[2]
    part, up_z, up_x, up_y, low_z, low_x, low_y = edge_stage(residual, edge_diag)
    below = (ring(up_z, "gz", 1), ring(up_x, "gx", 1), ring(up_y, "gy", 1))
    fg, rhs, xb, yb, w, *send = nodal_stage(part, node_shift, coarse_shift, *below, low_z, counts[0])
    got_z = swap(send, "gz")
    rhs, yb, w, *send = x_stage(got_z, rhs, xb, yb, w, fg, low_x, counts[0], counts[1])
    got_x = swap(send, "gx")
    planes = rhs.shape[0]
    rhs, w, *send = y_stage(got_x, rhs, yb, w, fg, low_y, counts[1], counts[2])
    got_y = swap(send, "gy")
    v1, v2, sums = coarse_stage(got_y, rhs, w, counts[2], devices)
    sums = lax.all_to_all(sums, ("gx", "gy", "gz"), 0, 0)
    fn, down_z, down_x, down_y = final_stage(
        sums, v1, v2, fg, node_shift, got_z, got_x, got_y, counts
    )
    above = (ring(down_z, "gz", -1), ring(down_x, "gx", -1), ring(down_y, "gy", -1))
    return output_stage(
        residual, edge_diag, fn, above, below, got_z, got_x, got_y, planes, counts
    )


def solution(mesh):
    placed = (
        P(None, "gz", "gx", "gy"),
        P(None, "gz", "gx", "gy"),
        P("gz", "gx", "gy"),
        P("gz", "gx", "gy"),
    )
    return jax.shard_map(
        local, mesh=mesh, in_specs=placed, out_specs=P(None, "gz", "gx", "gy"), check_vma=False
    )
```

time: 313 us -> 69.1 us (0.22)
  local copies, waits for them, and re-layouts: 96.2 us -> 3.23 us
  starting transfers between devices: 80.9 us -> 13 us
  waiting for transfers between devices: 54.6 us -> 16.8 us
  other arithmetic: 34.1 us -> 0 us
  blocking collectives: 38 us -> 10.3 us
  Pallas kernels: 0 us -> 25.5 us
  between operations: 7.79 us -> 0.05 us
    ppermute x35 -> x11, starting transfers between devices: 80.9 us -> 13 us  [the longest x6 5.96 us: ring(): lax.ppermute(value, axis, [(i, (i + step) % size) for i in range(size)])]
    reshape x2 -> x0, local copies, waits for them, and re-layouts: 58.9 us -> none  [the longest x1 34.9 us: local(): node_res.reshape(sx // 2, 2, sy // 2, 2, sz // 2, 2).sum(axis=(1, 3, 5))]
    psum x1 -> x0, blocking collectives: 38 us -> none  [local(): lax.psum((jnp.sum(first_dir * coarse_rhs), jnp.sum(second_dir * coarse_rh...]
    ppermute x35 -> x11, waiting for transfers between devices: 54.6 us -> 16.8 us  [the longest x6 6.72 us: ring(): lax.ppermute(value, axis, [(i, (i + step) % size) for i in range(size)])]
    pallas_call x0 -> x7, Pallas kernels: none -> 25.5 us  [the longest x1 5.5 us: output_stage(): call(body, [residual.shape], 'output_stage', scratch=[(nz, nx, ny)], grid...]
    slice x20 -> x0, local copies, waits for them, and re-layouts: 14.9 us -> none  [the longest x12 9.78 us: with_halo(): lax.slice_in_dim(block, block.shape[dim] - width, None, axis=dim)]
    reduce_sum x3 -> x0, other arithmetic: 14.2 us -> none  [the longest x1 12.2 us: local(): node_res.reshape(sx // 2, 2, sy // 2, 2, sz // 2, 2).sum(axis=(1, 3, 5))]
    broadcast_in_dim x1 -> x0, local copies, waits for them, and re-layouts: 11.4 us -> none  [local(): jnp.broadcast_to(coarse_sol[:, None, :, None, :, None], (sx // 2, 2, sy /...]
  transfers between devices with their start and end apart: 35 -> 11, of which waited for: 22 -> 7; matrix products, arithmetic and copies ran while one was open for 4% -> 0% of each run, Pallas kernels for 0% -> 0%
where the time goes in v1:
time: 69.1 us; the launch traced here: 68.8 us
  Pallas kernels  25.5 us (37%)
  waiting for transfers between devices  16.8 us (24%)
  starting transfers between devices  13 us (19%)
  blocking collectives  10.3 us (15%)
  local copies, waits for them, and re-layouts  3.23 us (5%)
    all_to_all x1, blocking collectives, local(): sums = lax.all_to_all(sums, ('gx', 'gy', 'gz'), 0, 0)  10.3 us
    ppermute x6, waiting for transfers between devices, ring(): lax.ppermute(value, axis, [(i, (i + step) % size) for i in range(size)])  6.72 us
    ppermute x6, starting transfers between devices, ring(): lax.ppermute(value, axis, [(i, (i + step) % size) for i in range(size)])  5.96 us
    ppermute x2, waiting for transfers between devices, swap(): out.append(lax.ppermute(values[1], axis, odd))  5.9 us
    pallas_call x1, Pallas kernels, output_stage(): call(body, [residual.shape], 'output_stage', scratch=[(nz, nx, ny)], grid...  5.5 us
    ppermute x2, starting transfers between devices, swap(): out.append(lax.ppermute(values[1], axis, odd))  4.56 us
    pallas_call x1, Pallas kernels, edge_stage(): call(body, [(nz, nx, ny)] + faces, 'edge_stage', scratch=[(nx, ny)], grid...  4.47 us
    ppermute x3, waiting for transfers between devices, swap(): out = [lax.ppermute(values[0], axis, even)]  4.14 us
  transfers between devices with their start and end apart: 11, of which 7 were waited for; matrix products, arithmetic and copies ran while one was open for 0% of the time, Pallas kernels for 0%

profile of v1, /device:TPU:0, one launch (start us, length us, event | category | flops | bytes accessed | tf_op | source)
XLA Modules:
  0.0 68.8 jit_solution(8164852832272152907)
XLA Ops:
  0.0 4.5 %edge_stage.1 = (f32[16,64,128]{2,1,0:T(8,128)}, f32[3,64,128]{2,1,0:T(8,128)}, f32[48,128]{1,0:T(8,128)}, f32[64,128]{1,0:T(8,128)}, f32[3,64,128]{2,1,0:T(8,12...) custom-call(f32[3,16,64,128]{3,2,1,0:T(8,128)} %refs_0_.1, f32[3,16,64,128]{3,2,1,0:T(8,128)} %refs_1_.1), custom_call_target="tpu_custom_call" | custom-call | tf_op jit(solution)/shard_map/edge_stage/pallas_call | solution.py:154
  5.0 2.6 %collective-permute-start.2 = (f32[64,128]{1,0:T(8,128)}, f32[64,128]{1,0:T(8,128)S(1)}, u32[]{:S(2)}, u32[]{:S(2)}) collective-permute-start(f32[64,128]{1,0:T(8,128)} %get-tuple-element.37), channel_id=1, source_target_pairs={{0,2},{2,4},{4,6},{6,0},{1,3},{3,5},{5,7},{7,1},{8,10},{10,12},{12... | collective-permute-start | bytes 98312 | tf_op jit(solution)/shard_map/ppermute | solution.py:57
  7.7 1.5 %collective-permute-start.1 = (f32[48,128]{1,0:T(8,128)}, f32[48,128]{1,0:T(8,128)S(1)}, u32[]{:S(2)}, u32[]{:S(2)}) collective-permute-start(f32[48,128]{1,0:T(8,128)} %get-tuple-element.36), channel_id=1, source_target_pairs={{0,8},{8,16},{16,24},{24,0},{1,9},{9,17},{17,25},{25,1},{2,10},{10... | collective-permute-start | bytes 73736 | tf_op jit(solution)/shard_map/ppermute | solution.py:57
  9.1 3.4 %collective-permute-done.1.gx.refs_7_ = f32[48,128]{1,0:T(8,128)S(1)} collective-permute-done((f32[48,128]{1,0:T(8,128)}, f32[48,128]{1,0:T(8,128)S(1)}, u32[]{:S(2)}, u32[]{:S(2)}) %collective-permute-start.1) | collective-permute-done | bytes 24608 | tf_op jit(solution)/shard_map/ppermute | solution.py:57
  13.3 3.4 %nodal_stage.1 = (f32[16,64,128]{2,1,0:T(8,128)}, f32[12,40,128]{2,1,0:T(8,128)}, f32[8,40,128]{2,1,0:T(8,128)}, f32[8,40,128]{2,1,0:T(8,128)}, f32[8,40,128]{2,1,0:T(8,128)}, /*index=5*/f32[616,128]{1,0:T(8,128)}) custom-call(f32[16,64,128]{2,1,0:T(8,128)} %get-tuple-element.34.part, f32[16,64,128]{2,1,0:T(8,128)} %refs_4_.1, f32[8,32,64]{2,1,0:T(8,128)} %coarse.1, ...), custom_call_target="tpu_custom_call" | custom-call | tf_op jit(solution)/shard_map/nodal_stage/pallas_call | solution.py:257
  16.7 1.8 %collective-permute-done.3.refs_0_.refs_5_.refs_9_ = f32[616,128]{1,0:T(8,128)S(1)} collective-permute-done((f32[616,128]{1,0:T(8,128)}, f32[616,128]{1,0:T(8,128)S(1)}, u32[]{:S(2)}, u32[]{:S(2)}) %collective-permute-start.3) | collective-permute-done | bytes 315424 | tf_op jit(solution)/shard_map/ppermute | solution.py:63
  18.5 0.7 %copy-done = f32[616,128]{1,0:T(8,128)} copy-done((f32[616,128]{1,0:T(8,128)}, f32[616,128]{1,0:T(8,128)S(1)}, u32[]{:S(2)}) %copy-start) | copy-done | bytes 315416
  19.2 2.5 %x_stage.1 = (f32[12,40,128]{2,1,0:T(8,128)}, f32[12,40,128]{2,1,0:T(8,128)}, f32[12,40,128]{2,1,0:T(8,128)}, f32[176,128]{1,0:T(8,128)}, f32[176,128]{1,0:T(8,128)}) custom-call(f32[616,128]{1,0:T(8,128)} %copy-done, f32[12,40,128]{2,1,0:T(8,128)} %get-tuple-element.40.refs_1_, f32[8,40,128]{2,1,0:T(8,128)} %get-tuple-element.41.refs_2_, ...), custom_call_target="tpu_custom_call" | custom-call | tf_op jit(solution)/shard_map/x_stage/pallas_call | solution.py:320
  21.7 0.9 %collective-permute-start.4 = (f32[176,128]{1,0:T(8,128)}, f32[176,128]{1,0:T(8,128)S(1)}, u32[]{:S(2)}, u32[]{:S(2)}) collective-permute-start(f32[176,128]{1,0:T(8,128)} %get-tuple-element.46), channel_id=1, source_target_pairs={{0,8},{8,0},{16,24},{24,16},{1,9},{9,1},{17,25},{25,17},{2,10},{10... | collective-permute-start | bytes 270344 | tf_op jit(solution)/shard_map/ppermute | solution.py:63
  22.6 2.1 %collective-permute-start.5 = (f32[176,128]{1,0:T(8,128)}, f32[176,128]{1,0:T(8,128)S(1)}, u32[]{:S(2)}, u32[]{:S(2)}) collective-permute-start(f32[176,128]{1,0:T(8,128)} %get-tuple-element.47), channel_id=1, source_target_pairs={{0,24},{8,16},{16,8},{24,0},{1,25},{9,17},{17,9},{25,1},{2,26},{10... | collective-permute-start | bytes 270344 | tf_op jit(solution)/shard_map/ppermute | solution.py:66
  24.7 2.2 %collective-permute-done.4.refs_0_.refs_6_.refs_10_ = f32[176,128]{1,0:T(8,128)S(1)} collective-permute-done((f32[176,128]{1,0:T(8,128)}, f32[176,128]{1,0:T(8,128)S(1)}, u32[]{:S(2)}, u32[]{:S(2)}) %collective-permute-start.4) | collective-permute-done | bytes 90144 | tf_op jit(solution)/shard_map/ppermute | solution.py:63
  26.9 2.5 %collective-permute-done.5.refs_1_.refs_7_.refs_11_ = f32[176,128]{1,0:T(8,128)S(1)} collective-permute-done((f32[176,128]{1,0:T(8,128)}, f32[176,128]{1,0:T(8,128)S(1)}, u32[]{:S(2)}, u32[]{:S(2)}) %collective-permute-start.5) | collective-permute-done | bytes 90144 | tf_op jit(solution)/shard_map/ppermute | solution.py:66
  29.5 0.6 copy-done.2
  30.1 3.4 %y_stage.1 = (f32[12,40,128]{2,1,0:T(8,128)}, f32[12,40,128]{2,1,0:T(8,128)}, f32[64,128]{1,0:T(8,128)}, f32[64,128]{1,0:T(8,128)}) custom-call(f32[176,128]{1,0:T(8,128)} %copy-done.1, f32[176,128]{1,0:T(8,128)} %copy-done.2, f32[12,40,128]{2,1,0:T(8,128)} %get-tuple-element.48.refs_2_, f32[12,40,128]{2,1,0:T(8,128)} %get-tuple-element.49.refs_3_, ...), custom_call_target="tpu_custom_call" | custom-call | tf_op jit(solution)/shard_map/y_stage/pallas_call | solution.py:394
  33.5 1.6 %collective-permute-start.6 = (f32[64,128]{1,0:T(8,128)}, f32[64,128]{1,0:T(8,128)S(1)}, u32[]{:S(2)}, u32[]{:S(2)}) collective-permute-start(f32[64,128]{1,0:T(8,128)} %get-tuple-element.52), channel_id=1, source_target_pairs={{0,2},{2,0},{4,6},{6,4},{1,3},{3,1},{5,7},{7,5},{8,10},{10,8},{12,... | collective-permute-start | bytes 98312 | tf_op jit(solution)/shard_map/ppermute | solution.py:63
  35.1 2.5 %collective-permute-start.7 = (f32[64,128]{1,0:T(8,128)}, f32[64,128]{1,0:T(8,128)S(1)}, u32[]{:S(2)}, u32[]{:S(2)}) collective-permute-start(f32[64,128]{1,0:T(8,128)} %get-tuple-element.53), channel_id=1, source_target_pairs={{0,6},{2,4},{4,2},{6,0},{1,7},{3,5},{5,3},{7,1},{8,14},{10,12},{12... | collective-permute-start | bytes 98312 | tf_op jit(solution)/shard_map/ppermute | solution.py:66
  37.6 3.4 %collective-permute-done.7.refs_1_.refs_9_.refs_13_ = f32[64,128]{1,0:T(8,128)S(1)} collective-permute-done((f32[64,128]{1,0:T(8,128)}, f32[64,128]{1,0:T(8,128)S(1)}, u32[]{:S(2)}, u32[]{:S(2)}) %collective-permute-start.7) | collective-permute-done | bytes 32800 | tf_op jit(solution)/shard_map/ppermute | solution.py:66
  41.0 0.6 copy-done.5
  41.6 2.7 %coarse_stage.1 = (f32[12,40,128]{2,1,0:T(8,128)}, f32[12,40,128]{2,1,0:T(8,128)}, f32[32,1,128]{2,1,0:T(1,128)}) custom-call(f32[64,128]{1,0:T(8,128)} %copy-done.4, f32[64,128]{1,0:T(8,128)} %copy-done.5, f32[12,40,128]{2,1,0:T(8,128)} %get-tuple-element.54.refs_2_, f32[12,40,128]{2,1,0:T(8,128)} %get-tuple-element.55.refs_3_), custom_call_target="tpu_custom_call" | custom-call | tf_op jit(solution)/shard_map/coarse_stage/pallas_call | solution.py:461
  44.3 10.3 %all_to_all.5.refs_0_ = f32[32,1,128]{2,1,0:T(1,128)} all-to-all(f32[32,1,128]{2,1,0:T(1,128)} %get-tuple-element.56), channel_id=1, replica_groups=mesh['gx'=4,'gy'=4,'gz'=2] {'gx','gy','gz'}, dimensions={0} | all-to-all | bytes 32768 | tf_op jit(solution)/shard_map/all_to_all | solution.py:636
  54.5 3.5 %final_stage.1 = (f32[16,64,128]{2,1,0:T(8,128)}, f32[64,128]{1,0:T(8,128)}, f32[16,128]{1,0:T(8,128)}, f32[64,128]{1,0:T(8,128)}) custom-call(f32[32,1,128]{2,1,0:T(1,128)} %all_to_all.5.refs_0_, f32[12,40,128]{2,1,0:T(8,128)} %get-tuple-element.57.refs_1_, f32[12,40,128]{2,1,0:T(8,128)} %get-tuple-element.58.refs_2_, ...), custom_call_target="tpu_custom_call" | custom-call | tf_op jit(solution)/shard_map/final_stage/pallas_call | solution.py:539
  58.1 0.6 collective-permute-start.10
  59.4 3.3 %collective-permute-done.9.refs_4_ = f32[16,128]{1,0:T(8,128)S(1)} collective-permute-done((f32[16,128]{1,0:T(8,128)}, f32[16,128]{1,0:T(8,128)S(1)}, u32[]{:S(2)}, u32[]{:S(2)}) %collective-permute-start.9) | collective-permute-done | bytes 8224 | tf_op jit(solution)/shard_map/ppermute | solution.py:57
  63.2 5.5 %output_stage.1 = f32[3,16,64,128]{3,2,1,0:T(8,128)} custom-call(f32[3,16,64,128]{3,2,1,0:T(8,128)} %refs_0_.1, f32[3,16,64,128]{3,2,1,0:T(8,128)} %refs_1_.1, f32[16,64,128]{2,1,0:T(8,128)} %get-tuple-element.59.refs_2_, f32[64,128]{1,0:T(8,128)} %copy-done.8, f32[16,128]{1,0:T(8,128)} %copy-done.10, f32[64,128]{1,0:T(8,128)} %copy-done.9, ...), custom_call_target="tpu_custom_call" | custom-call | tf_op jit(solution)/shard_map/output_stage/pallas_call | solution.py:611
  (28 shorter events, 2.6 us)
Async XLA Ops:
  4.5 8.1 %collective-permute-start = (f32[3,64,128]{2,1,0:T(8,128)}, f32[3,64,128]{2,1,0:T(8,128)S(1)}, u32[]{:S(2)}, u32[]{:S(2)}) collective-permute-start(f32[3,64,128]{2,1,0:T(8,128)} %get-tuple-element.35), channel_id=1, source_target_pairs={{0,1},{1,0},{2,3},{3,2},{4,5},{5,4},{6,7},{7,6},{8,9},{9,8},{10,11... | collective-permute-start | bytes 294920 | tf_op jit(solution)/shard_map/ppermute | solution.py:57
  5.0 7.6 %collective-permute-start.2 = (f32[64,128]{1,0:T(8,128)}, f32[64,128]{1,0:T(8,128)S(1)}, u32[]{:S(2)}, u32[]{:S(2)}) collective-permute-start(f32[64,128]{1,0:T(8,128)} %get-tuple-element.37), channel_id=1, source_target_pairs={{0,2},{2,4},{4,6},{6,0},{1,3},{3,5},{5,7},{7,1},{8,10},{10,12},{12... | collective-permute-start | bytes 98312 | tf_op jit(solution)/shard_map/ppermute | solution.py:57
  7.7 4.9 %collective-permute-start.1 = (f32[48,128]{1,0:T(8,128)}, f32[48,128]{1,0:T(8,128)S(1)}, u32[]{:S(2)}, u32[]{:S(2)}) collective-permute-start(f32[48,128]{1,0:T(8,128)} %get-tuple-element.36), channel_id=1, source_target_pairs={{0,8},{8,16},{16,24},{24,0},{1,9},{9,17},{17,25},{25,1},{2,10},{10... | collective-permute-start | bytes 73736 | tf_op jit(solution)/shard_map/ppermute | solution.py:57
  12.6 0.6 copy-start.7
  12.6 0.6 copy-start.6
  12.6 0.6 copy-start.3
  16.7 1.8 %collective-permute-start.3 = (f32[616,128]{1,0:T(8,128)}, f32[616,128]{1,0:T(8,128)S(1)}, u32[]{:S(2)}, u32[]{:S(2)}) collective-permute-start(f32[616,128]{1,0:T(8,128)} %get-tuple-element.39), channel_id=1, source_target_pairs={{0,1},{1,0},{2,3},{3,2},{4,5},{5,4},{6,7},{7,6},{8,9},{9,8},{10,11... | collective-permute-start | bytes 946184 | tf_op jit(solution)/shard_map/ppermute | solution.py:63
  18.5 0.7 %copy-start = (f32[616,128]{1,0:T(8,128)}, f32[616,128]{1,0:T(8,128)S(1)}, u32[]{:S(2)}) copy-start(f32[616,128]{1,0:T(8,128)S(1)} %collective-permute-done.3.refs_0_.refs_5_.refs_9_) | copy-start | bytes 946180
  21.7 5.2 %collective-permute-start.4 = (f32[176,128]{1,0:T(8,128)}, f32[176,128]{1,0:T(8,128)S(1)}, u32[]{:S(2)}, u32[]{:S(2)}) collective-permute-start(f32[176,128]{1,0:T(8,128)} %get-tuple-element.46), channel_id=1, source_target_pairs={{0,8},{8,0},{16,24},{24,16},{1,9},{9,1},{17,25},{25,17},{2,10},{10... | collective-permute-start | bytes 270344 | tf_op jit(solution)/shard_map/ppermute | solution.py:63
  22.6 6.9 %collective-permute-start.5 = (f32[176,128]{1,0:T(8,128)}, f32[176,128]{1,0:T(8,128)S(1)}, u32[]{:S(2)}, u32[]{:S(2)}) collective-permute-start(f32[176,128]{1,0:T(8,128)} %get-tuple-element.47), channel_id=1, source_target_pairs={{0,24},{8,16},{16,8},{24,0},{1,25},{9,17},{17,9},{25,1},{2,26},{10... | collective-permute-start | bytes 270344 | tf_op jit(solution)/shard_map/ppermute | solution.py:66
  26.9 2.5 %copy-start.1 = (f32[176,128]{1,0:T(8,128)}, f32[176,128]{1,0:T(8,128)S(1)}, u32[]{:S(2)}) copy-start(f32[176,128]{1,0:T(8,128)S(1)} %collective-permute-done.4.refs_0_.refs_6_.refs_10_) | copy-start | bytes 270340
  29.5 0.6 copy-start.2
  33.5 4.1 %collective-permute-start.6 = (f32[64,128]{1,0:T(8,128)}, f32[64,128]{1,0:T(8,128)S(1)}, u32[]{:S(2)}, u32[]{:S(2)}) collective-permute-start(f32[64,128]{1,0:T(8,128)} %get-tuple-element.52), channel_id=1, source_target_pairs={{0,2},{2,0},{4,6},{6,4},{1,3},{3,1},{5,7},{7,5},{8,10},{10,8},{12,... | collective-permute-start | bytes 98312 | tf_op jit(solution)/shard_map/ppermute | solution.py:63
  35.1 5.9 %collective-permute-start.7 = (f32[64,128]{1,0:T(8,128)}, f32[64,128]{1,0:T(8,128)S(1)}, u32[]{:S(2)}, u32[]{:S(2)}) collective-permute-start(f32[64,128]{1,0:T(8,128)} %get-tuple-element.53), channel_id=1, source_target_pairs={{0,6},{2,4},{4,2},{6,0},{1,7},{3,5},{5,3},{7,1},{8,14},{10,12},{12... | collective-permute-start | bytes 98312 | tf_op jit(solution)/shard_map/ppermute | solution.py:66
  37.6 3.4 %copy-start.4 = (f32[64,128]{1,0:T(8,128)}, f32[64,128]{1,0:T(8,128)S(1)}, u32[]{:S(2)}) copy-start(f32[64,128]{1,0:T(8,128)S(1)} %collective-permute-done.6.refs_0_.refs_8_.refs_12_) | copy-start | bytes 98308
  41.0 0.6 copy-start.5
  58.1 4.6 %collective-permute-start.8 = (f32[64,128]{1,0:T(8,128)}, f32[64,128]{1,0:T(8,128)S(1)}, u32[]{:S(2)}, u32[]{:S(2)}) collective-permute-start(f32[64,128]{1,0:T(8,128)} %get-tuple-element.60), channel_id=1, source_target_pairs={{0,1},{1,0},{2,3},{3,2},{4,5},{5,4},{6,7},{7,6},{8,9},{9,8},{10,11... | collective-permute-start | bytes 98312 | tf_op jit(solution)/shard_map/ppermute | solution.py:57
  58.1 4.5 %collective-permute-start.10 = (f32[64,128]{1,0:T(8,128)}, f32[64,128]{1,0:T(8,128)S(1)}, u32[]{:S(2)}, u32[]{:S(2)}) collective-permute-start(f32[64,128]{1,0:T(8,128)} %get-tuple-element.62), channel_id=1, source_target_pairs={{0,6},{2,0},{4,2},{6,4},{1,7},{3,1},{5,3},{7,5},{8,14},{10,8},{12,... | collective-permute-start | bytes 98312 | tf_op jit(solution)/shard_map/ppermute | solution.py:57
  58.8 3.9 %collective-permute-start.9 = (f32[16,128]{1,0:T(8,128)}, f32[16,128]{1,0:T(8,128)S(1)}, u32[]{:S(2)}, u32[]{:S(2)}) collective-permute-start(f32[16,128]{1,0:T(8,128)} %get-tuple-element.61), channel_id=1, source_target_pairs={{0,24},{8,0},{16,8},{24,16},{1,25},{9,1},{17,9},{25,17},{2,26},{10... | collective-permute-start | bytes 24584 | tf_op jit(solution)/shard_map/ppermute | solution.py:57
  62.6 0.6 copy-start.10
  62.6 0.6 copy-start.8
  62.6 0.6 copy-start.9

commit v2 on v1

--- a/solution.py
+++ b/solution.py
@@ -83,14 +83,24 @@
             up(refs[1])
 
 
-def call(body, outs, name, scratch=(), **kwargs):
-    return pl.pallas_call(
-        body,
-        out_shape=[jax.ShapeDtypeStruct(shape, F32) for shape in outs],
+def call(body, outs, name, scratch=(), far=(), far_out=False, **kwargs):
+    kind = jax.ShapeDtypeStruct if far_out else pltpu.VMEM
+    run = pl.pallas_call(
+        body,
+        out_shape=[kind(shape, F32) for shape in outs],
         scratch_shapes=[pltpu.VMEM(shape, F32) for shape in scratch],
         name=name,
         **kwargs,
     )
+
+    def apply(*args):
+        near = [
+            a if i in far else pltpu.with_memory_space_constraint(a, pltpu.VMEM)
+            for i, a in enumerate(args)
+        ]
+        return run(*near)
+
+    return apply
 
 
 def vmem(count):
@@ -156,6 +166,7 @@
         [(nz, nx, ny)] + faces,
         "edge_stage",
         scratch=[(nx, ny)],
+        far=(0, 1),
         grid=(steps,),
         in_specs=[spec, spec],
         out_specs=[pl.BlockSpec((step, nx, ny), lambda i: (i, 0, 0))] + [whole(*f) for f in faces],
@@ -613,6 +624,8 @@
         [residual.shape],
         "output_stage",
         scratch=[(nz, nx, ny)],
+        far=(0, 1),
+        far_out=True,
         grid=(3,),
         in_specs=[spec, spec] + whole,
         out_specs=[spec],

time: 69.1 us -> 64.7 us (0.936)
  Pallas kernels: 25.5 us -> 13.3 us
  local copies, waits for them, and re-layouts: 3.23 us -> 11.8 us
  waiting for transfers between devices: 16.8 us -> 15.8 us
    pallas_call x7, Pallas kernels: 25.5 us -> 13.3 us  [apply(): return run(*near)]
    unnamed x22 -> x48, local copies, waits for them, and re-layouts: 3.23 us -> 11.8 us
  transfers between devices with their start and end apart: 11 -> 11, of which waited for: 7 -> 6; matrix products, arithmetic and copies ran while one was open for 0% -> 0% of each run, Pallas kernels for 0% -> 0%
where the time goes in v2:
time: 64.7 us; the launch traced here: 64.1 us
  waiting for transfers between devices  15.8 us (24%)
  Pallas kernels  13.3 us (21%)
  starting transfers between devices  13 us (20%)
  local copies, waits for them, and re-layouts  11.8 us (18%)
  blocking collectives  10.1 us (16%)
    pallas_call x7, Pallas kernels, apply(): return run(*near)  13.3 us
    unnamed x48, local copies, waits for them, and re-layouts  11.8 us
    all_to_all x1, blocking collectives, local(): sums = lax.all_to_all(sums, ('gx', 'gy', 'gz'), 0, 0)  10.1 us
    ppermute x6, waiting for transfers between devices, ring(): lax.ppermute(value, axis, [(i, (i + step) % size) for i in range(size)])  6.34 us
    ppermute x6, starting transfers between devices, ring(): lax.ppermute(value, axis, [(i, (i + step) % size) for i in range(size)])  5.81 us
    ppermute x2, waiting for transfers between devices, swap(): out.append(lax.ppermute(values[1], axis, odd))  5.75 us
    ppermute x2, starting transfers between devices, swap(): out.append(lax.ppermute(values[1], axis, odd))  4.58 us
    ppermute x3, waiting for transfers between devices, swap(): out = [lax.ppermute(values[0], axis, even)]  3.66 us
  transfers between devices with their start and end apart: 11, of which 6 were waited for; matrix products, arithmetic and copies ran while one was open for 0% of the time, Pallas kernels for 0%

profile of v2, /device:TPU:0, one launch (start us, length us, event | category | flops | bytes accessed | tf_op | source)
XLA Modules:
  0.0 64.1 jit_solution(6225628182933378029)
XLA Ops:
  0.0 3.6 %edge_stage.1 = (f32[16,64,128]{2,1,0:T(8,128)S(1)}, f32[3,64,128]{2,1,0:T(8,128)S(1)}, f32[48,128]{1,0:T(8,128)S(1)}, f32[64,128]{1,0:T(8,128)S(1)}, f32[3,64,1...) custom-call(f32[3,16,64,128]{3,2,1,0:T(8,128)} %refs_0_.1, f32[3,16,64,128]{3,2,1,0:T(8,128)} %refs_1_.1), custom_call_target="tpu_custom_call" | custom-call | tf_op jit(solution)/shard_map/edge_stage/pallas_call | solution.py:101
  4.7 2.6 %collective-permute-start.2 = (f32[64,128]{1,0:T(8,128)S(1)}, f32[64,128]{1,0:T(8,128)S(1)}, u32[]{:S(2)}, u32[]{:S(2)}) collective-permute-start(f32[64,128]{1,0:T(8,128)S(1)} %get-tuple-element.37), channel_id=1, source_target_pairs={{0,2},{2,4},{4,6},{6,0},{1,3},{3,5},{5,7},{7,1},{8,10},{10,12},{12... | collective-permute-start | bytes 98312 | tf_op jit(solution)/shard_map/ppermute | solution.py:57
  7.3 1.5 %collective-permute-start.1 = (f32[48,128]{1,0:T(8,128)S(1)}, f32[48,128]{1,0:T(8,128)S(1)}, u32[]{:S(2)}, u32[]{:S(2)}) collective-permute-start(f32[48,128]{1,0:T(8,128)S(1)} %get-tuple-element.36), channel_id=1, source_target_pairs={{0,8},{8,16},{16,24},{24,0},{1,9},{9,17},{17,25},{25,1},{2,10},{10... | collective-permute-start | bytes 73736 | tf_op jit(solution)/shard_map/ppermute | solution.py:57
  8.8 3.2 %collective-permute-done.1.gx.refs_7_ = f32[48,128]{1,0:T(8,128)S(1)} collective-permute-done((f32[48,128]{1,0:T(8,128)S(1)}, f32[48,128]{1,0:T(8,128)S(1)}, u32[]{:S(2)}, u32[]{:S(2)}) %collective-permute-start.1) | collective-permute-done | bytes 24608 | tf_op jit(solution)/shard_map/ppermute | solution.py:57
  12.0 1.0 %nodal_stage.1 = (f32[16,64,128]{2,1,0:T(8,128)S(1)}, f32[12,40,128]{2,1,0:T(8,128)S(1)}, f32[8,40,128]{2,1,0:T(8,128)S(1)}, f32[8,40,128]{2,1,0:T(8,128)S(1)}, ...) custom-call(f32[16,64,128]{2,1,0:T(8,128)S(1)} %get-tuple-element.34.part, f32[16,64,128]{2,1,0:T(8,128)S(1)} %copy-done.3, ...), custom_call_target="tpu_custom_call" | custom-call | tf_op jit(solution)/shard_map/nodal_stage/pallas_call | solution.py:101
  14.4 1.6 %collective-permute-done.3.refs_0_.refs_5_.refs_9_ = f32[616,128]{1,0:T(8,128)S(1)} collective-permute-done((f32[616,128]{1,0:T(8,128)S(1)}, f32[616,128]{1,0:T(8,128)S(1)}, u32[]{:S(2)}, u32[]{:S(2)}) %collective-permute-start.3) | collective-permute-done | bytes 315424 | tf_op jit(solution)/shard_map/ppermute | solution.py:63
  16.0 1.0 %copy-done.10 = f32[12,40,128]{2,1,0:T(8,128)S(1)} copy-done((f32[12,40,128]{2,1,0:T(8,128)S(1)}, f32[12,40,128]{2,1,0:T(8,128)}, u32[]{:S(2)}) %copy-start.10) | copy-done | bytes 245784
  18.8 0.9 %collective-permute-start.4 = (f32[176,128]{1,0:T(8,128)S(1)}, f32[176,128]{1,0:T(8,128)S(1)}, u32[]{:S(2)}, u32[]{:S(2)}) collective-permute-start(f32[176,128]{1,0:T(8,128)S(1)} %get-tuple-element.46), channel_id=1, source_target_pairs={{0,8},{8,0},{16,24},{24,16},{1,9},{9,1},{17,25},{25,17},{2,10},{10... | collective-permute-start | bytes 270344 | tf_op jit(solution)/shard_map/ppermute | solution.py:63
  19.8 2.1 %collective-permute-start.5 = (f32[176,128]{1,0:T(8,128)S(1)}, f32[176,128]{1,0:T(8,128)S(1)}, u32[]{:S(2)}, u32[]{:S(2)}) collective-permute-start(f32[176,128]{1,0:T(8,128)S(1)} %get-tuple-element.47), channel_id=1, source_target_pairs={{0,24},{8,16},{16,8},{24,0},{1,25},{9,17},{17,9},{25,1},{2,26},{10... | collective-permute-start | bytes 270344 | tf_op jit(solution)/shard_map/ppermute | solution.py:66
  21.9 2.0 %collective-permute-done.4.refs_0_.refs_6_.refs_10_ = f32[176,128]{1,0:T(8,128)S(1)} collective-permute-done((f32[176,128]{1,0:T(8,128)S(1)}, f32[176,128]{1,0:T(8,128)S(1)}, u32[]{:S(2)}, u32[]{:S(2)}) %collective-permute-start.4) | collective-permute-done | bytes 90144 | tf_op jit(solution)/shard_map/ppermute | solution.py:63
  23.9 2.5 %collective-permute-done.5.refs_1_.refs_7_.refs_11_ = f32[176,128]{1,0:T(8,128)S(1)} collective-permute-done((f32[176,128]{1,0:T(8,128)S(1)}, f32[176,128]{1,0:T(8,128)S(1)}, u32[]{:S(2)}, u32[]{:S(2)}) %collective-permute-start.5) | collective-permute-done | bytes 90144 | tf_op jit(solution)/shard_map/ppermute | solution.py:66
  26.5 1.2 %y_stage.1 = (f32[12,40,128]{2,1,0:T(8,128)S(1)}, f32[12,40,128]{2,1,0:T(8,128)S(1)}, f32[64,128]{1,0:T(8,128)S(1)}, f32[64,128]{1,0:T(8,128)S(1)}) custom-call(f32[176,128]{1,0:T(8,128)S(1)} %collective-permute-done.4.refs_0_.refs_6_.refs_10_, f32[176,128]{1,0:T(8,128)S(1)} %collective-permute-done.5.refs_1_.refs_7_.refs_11_, ...), custom_call_target="tpu_custom_call" | custom-call | tf_op jit(solution)/shard_map/y_stage/pallas_call | solution.py:101
  27.7 1.6 %collective-permute-start.6 = (f32[64,128]{1,0:T(8,128)S(1)}, f32[64,128]{1,0:T(8,128)S(1)}, u32[]{:S(2)}, u32[]{:S(2)}) collective-permute-start(f32[64,128]{1,0:T(8,128)S(1)} %get-tuple-element.52), channel_id=1, source_target_pairs={{0,2},{2,0},{4,6},{6,4},{1,3},{3,1},{5,7},{7,5},{8,10},{10,8},{12,... | collective-permute-start | bytes 98312 | tf_op jit(solution)/shard_map/ppermute | solution.py:63
  29.3 2.5 %collective-permute-start.7 = (f32[64,128]{1,0:T(8,128)S(1)}, f32[64,128]{1,0:T(8,128)S(1)}, u32[]{:S(2)}, u32[]{:S(2)}) collective-permute-start(f32[64,128]{1,0:T(8,128)S(1)} %get-tuple-element.53), channel_id=1, source_target_pairs={{0,6},{2,4},{4,2},{6,0},{1,7},{3,5},{5,3},{7,1},{8,14},{10,12},{12... | collective-permute-start | bytes 98312 | tf_op jit(solution)/shard_map/ppermute | solution.py:66
  31.8 3.2 %collective-permute-done.7.refs_1_.refs_9_.refs_13_ = f32[64,128]{1,0:T(8,128)S(1)} collective-permute-done((f32[64,128]{1,0:T(8,128)S(1)}, f32[64,128]{1,0:T(8,128)S(1)}, u32[]{:S(2)}, u32[]{:S(2)}) %collective-permute-start.7) | collective-permute-done | bytes 32800 | tf_op jit(solution)/shard_map/ppermute | solution.py:66
  35.0 1.0 %coarse_stage.1 = (f32[12,40,128]{2,1,0:T(8,128)S(1)}, f32[12,40,128]{2,1,0:T(8,128)S(1)}, f32[32,1,128]{2,1,0:T(1,128)S(1)}) custom-call(f32[64,128]{1,0:T(8,128)S(1)} %collective-permute-done.6.refs_0_.refs_8_.refs_12_, f32[64,128]{1,0:T(8,128)S(1)} %collective-permute-done.7.refs_1_.refs_9_.refs_13_, f32[12,40,128]{2,1,0:T(8,128)S(1)} %get-tuple-element.54.refs_2_, ...), custom_call_target="tpu_custom_call" | custom-call | tf_op jit(solution)/shard_map/coarse_stage/pallas_call | solution.py:101
  37.4 10.1 %all_to_all.5.refs_0_ = f32[32,1,128]{2,1,0:T(1,128)S(1)} all-to-all(f32[32,1,128]{2,1,0:T(1,128)S(1)} %get-tuple-element.56), channel_id=1, replica_groups=mesh['gx'=4,'gy'=4,'gz'=2] {'gx','gy','gz'}, dimensions={0} | all-to-all | bytes 32768 | tf_op jit(solution)/shard_map/all_to_all | solution.py:649
  47.5 1.0 %copy-done.1 = f32[616,128]{1,0:T(8,128)S(1)} copy-done((f32[616,128]{1,0:T(8,128)S(1)}, f32[616,128]{1,0:T(8,128)}, u32[]{:S(2)}) %copy-start.1) | copy-done | bytes 315416
  48.5 1.0 %copy-done.4 = f32[16,64,128]{2,1,0:T(8,128)S(1)} copy-done((f32[16,64,128]{2,1,0:T(8,128)S(1)}, f32[16,64,128]{2,1,0:T(8,128)}, u32[]{:S(2)}) %copy-start.4) | copy-done | bytes 524312
  49.5 0.9 %copy-done.12 = f32[12,40,128]{2,1,0:T(8,128)S(1)} copy-done((f32[12,40,128]{2,1,0:T(8,128)S(1)}, f32[12,40,128]{2,1,0:T(8,128)}, u32[]{:S(2)}) %copy-start.12) | copy-done | bytes 245784
  51.4 1.2 %final_stage.1 = (f32[16,64,128]{2,1,0:T(8,128)S(1)}, f32[64,128]{1,0:T(8,128)S(1)}, f32[16,128]{1,0:T(8,128)S(1)}, f32[64,128]{1,0:T(8,128)S(1)}) custom-call(f32[32,1,128]{2,1,0:T(1,128)S(1)} %all_to_all.5.refs_0_, f32[12,40,128]{2,1,0:T(8,128)S(1)} %copy-done.12, f32[12,40,128]{2,1,0:T(8,128)S(1)} %copy-done.14, ...), custom_call_target="tpu_custom_call" | custom-call | tf_op jit(solution)/shard_map/final_stage/pallas_call | solution.py:101
  54.0 3.1 %collective-permute-done.9.refs_4_ = f32[16,128]{1,0:T(8,128)S(1)} collective-permute-done((f32[16,128]{1,0:T(8,128)S(1)}, f32[16,128]{1,0:T(8,128)S(1)}, u32[]{:S(2)}, u32[]{:S(2)}) %collective-permute-start.9) | collective-permute-done | bytes 8224 | tf_op jit(solution)/shard_map/ppermute | solution.py:57
  57.1 1.0 %copy-done.2 = f32[616,128]{1,0:T(8,128)S(1)} copy-done((f32[616,128]{1,0:T(8,128)S(1)}, f32[616,128]{1,0:T(8,128)}, u32[]{:S(2)}) %copy-start.2) | copy-done | bytes 315416
  58.9 5.2 %output_stage.1 = f32[3,16,64,128]{3,2,1,0:T(8,128)} custom-call(f32[3,16,64,128]{3,2,1,0:T(8,128)} %refs_0_.1, f32[3,16,64,128]{3,2,1,0:T(8,128)} %refs_1_.1, f32[16,64,128]{2,1,0:T(8,128)S(1)} %get-tuple-element.59.refs_2_, f32[64,128]{1,0:T(8,128)S(1)} %collective-permute-done.8.refs_3_, f32[16,128]{1,0:T(8,128)S(1)} %collective-permute-done.9.refs_4_, ...), custom_call_target="tpu_custom_call" | custom-call | tf_op jit(solution)/shard_map/output_stage/pallas_call | solution.py:101
  (54 shorter events, 8.8 us)
Async XLA Ops:
  0.0 12.0 %copy-start.3 = (f32[16,64,128]{2,1,0:T(8,128)S(1)}, f32[16,64,128]{2,1,0:T(8,128)}, u32[]{:S(2)}) copy-start(f32[16,64,128]{2,1,0:T(8,128)} %refs_4_.1) | copy-start | bytes 1572868
  0.0 12.0 %copy-start.17 = (f32[8,32,64]{2,1,0:T(8,128)S(1)}, f32[8,32,64]{2,1,0:T(8,128)}, u32[]{:S(2)}) copy-start(f32[8,32,64]{2,1,0:T(8,128)} %coarse.1) | copy-start | bytes 196612
  4.2 11.8 %copy-start.20 = (f32[64,128]{1,0:T(8,128)}, f32[64,128]{1,0:T(8,128)S(1)}, u32[]{:S(2)}) copy-start(f32[64,128]{1,0:T(8,128)S(1)} %get-tuple-element.51.refs_6_) | copy-start | bytes 98308
  4.2 7.8 %collective-permute-start = (f32[3,64,128]{2,1,0:T(8,128)S(1)}, f32[3,64,128]{2,1,0:T(8,128)S(1)}, u32[]{:S(2)}, u32[]{:S(2)}) collective-permute-start(f32[3,64,128]{2,1,0:T(8,128)S(1)} %get-tuple-element.35), channel_id=1, source_target_pairs={{0,1},{1,0},{2,3},{3,2},{4,5},{5,4},{6,7},{7,6},{8,9},{9,8},{10,11... | collective-permute-start | bytes 294920 | tf_op jit(solution)/shard_map/ppermute | solution.py:57
  4.7 7.3 %collective-permute-start.2 = (f32[64,128]{1,0:T(8,128)S(1)}, f32[64,128]{1,0:T(8,128)S(1)}, u32[]{:S(2)}, u32[]{:S(2)}) collective-permute-start(f32[64,128]{1,0:T(8,128)S(1)} %get-tuple-element.37), channel_id=1, source_target_pairs={{0,2},{2,4},{4,6},{6,0},{1,3},{3,5},{5,7},{7,1},{8,10},{10,12},{12... | collective-permute-start | bytes 98312 | tf_op jit(solution)/shard_map/ppermute | solution.py:57
  7.3 4.7 %collective-permute-start.1 = (f32[48,128]{1,0:T(8,128)S(1)}, f32[48,128]{1,0:T(8,128)S(1)}, u32[]{:S(2)}, u32[]{:S(2)}) collective-permute-start(f32[48,128]{1,0:T(8,128)S(1)} %get-tuple-element.36), channel_id=1, source_target_pairs={{0,8},{8,16},{16,24},{24,0},{1,9},{9,17},{17,25},{25,1},{2,10},{10... | collective-permute-start | bytes 73736 | tf_op jit(solution)/shard_map/ppermute | solution.py:57
  12.0 4.0 %copy-start.18 = (f32[48,128]{1,0:T(8,128)}, f32[48,128]{1,0:T(8,128)S(1)}, u32[]{:S(2)}) copy-start(f32[48,128]{1,0:T(8,128)S(1)} %collective-permute-done.1.gx.refs_7_) | copy-start | bytes 73732
  12.0 4.0 %copy-start.7 = (f32[3,64,128]{2,1,0:T(8,128)}, f32[3,64,128]{2,1,0:T(8,128)S(1)}, u32[]{:S(2)}) copy-start(f32[3,64,128]{2,1,0:T(8,128)S(1)} %collective-permute-done.gz.refs_6_) | copy-start | bytes 294916
  14.4 1.6 %collective-permute-start.3 = (f32[616,128]{1,0:T(8,128)S(1)}, f32[616,128]{1,0:T(8,128)S(1)}, u32[]{:S(2)}, u32[]{:S(2)}) collective-permute-start(f32[616,128]{1,0:T(8,128)S(1)} %get-tuple-element.39), channel_id=1, source_target_pairs={{0,1},{1,0},{2,3},{3,2},{4,5},{5,4},{6,7},{7,6},{8,9},{9,8},{10,11... | collective-permute-start | bytes 946184 | tf_op jit(solution)/shard_map/ppermute | solution.py:63
  16.0 20.0 %copy-start = (f32[616,128]{1,0:T(8,128)}, f32[616,128]{1,0:T(8,128)S(1)}, u32[]{:S(2)}) copy-start(f32[616,128]{1,0:T(8,128)S(1)} %collective-permute-done.3.refs_0_.refs_5_.refs_9_) | copy-start | bytes 946180
  16.0 1.1 %copy-start.10 = (f32[12,40,128]{2,1,0:T(8,128)S(1)}, f32[12,40,128]{2,1,0:T(8,128)}, u32[]{:S(2)}) copy-start(f32[12,40,128]{2,1,0:T(8,128)} %copy-done.9) | copy-start | bytes 737284
  18.7 7.7 %copy-start.21 = (f32[64,128]{1,0:T(8,128)S(1)}, f32[64,128]{1,0:T(8,128)}, u32[]{:S(2)}) copy-start(f32[64,128]{1,0:T(8,128)} %copy-done.20) | copy-start | bytes 98308
  18.8 5.1 %collective-permute-start.4 = (f32[176,128]{1,0:T(8,128)S(1)}, f32[176,128]{1,0:T(8,128)S(1)}, u32[]{:S(2)}, u32[]{:S(2)}) collective-permute-start(f32[176,128]{1,0:T(8,128)S(1)} %get-tuple-element.46), channel_id=1, source_target_pairs={{0,8},{8,0},{16,24},{24,16},{1,9},{9,1},{17,25},{25,17},{2,10},{10... | collective-permute-start | bytes 270344 | tf_op jit(solution)/shard_map/ppermute | solution.py:63
  19.8 6.7 %collective-permute-start.5 = (f32[176,128]{1,0:T(8,128)S(1)}, f32[176,128]{1,0:T(8,128)S(1)}, u32[]{:S(2)}, u32[]{:S(2)}) collective-permute-start(f32[176,128]{1,0:T(8,128)S(1)} %get-tuple-element.47), channel_id=1, source_target_pairs={{0,24},{8,16},{16,8},{24,0},{1,25},{9,17},{17,9},{25,1},{2,26},{10... | collective-permute-start | bytes 270344 | tf_op jit(solution)/shard_map/ppermute | solution.py:66
  26.5 26.2 %copy-start.5 = (f32[176,128]{1,0:T(8,128)}, f32[176,128]{1,0:T(8,128)S(1)}, u32[]{:S(2)}) copy-start(f32[176,128]{1,0:T(8,128)S(1)} %collective-permute-done.5.refs_1_.refs_7_.refs_11_) | copy-start | bytes 270340
  27.7 29.4 %copy-start.8 = (f32[3,64,128]{2,1,0:T(8,128)S(1)}, f32[3,64,128]{2,1,0:T(8,128)}, u32[]{:S(2)}) copy-start(f32[3,64,128]{2,1,0:T(8,128)} %copy-done.7) | copy-start | bytes 294916
  27.7 29.4 %copy-start.19 = (f32[48,128]{1,0:T(8,128)S(1)}, f32[48,128]{1,0:T(8,128)}, u32[]{:S(2)}) copy-start(f32[48,128]{1,0:T(8,128)} %copy-done.18) | copy-start | bytes 73732
  27.7 4.1 %collective-permute-start.6 = (f32[64,128]{1,0:T(8,128)S(1)}, f32[64,128]{1,0:T(8,128)S(1)}, u32[]{:S(2)}, u32[]{:S(2)}) collective-permute-start(f32[64,128]{1,0:T(8,128)S(1)} %get-tuple-element.52), channel_id=1, source_target_pairs={{0,2},{2,0},{4,6},{6,4},{1,3},{3,1},{5,7},{7,5},{8,10},{10,8},{12,... | collective-permute-start | bytes 98312 | tf_op jit(solution)/shard_map/ppermute | solution.py:63
  29.3 5.7 %collective-permute-start.7 = (f32[64,128]{1,0:T(8,128)S(1)}, f32[64,128]{1,0:T(8,128)S(1)}, u32[]{:S(2)}, u32[]{:S(2)}) collective-permute-start(f32[64,128]{1,0:T(8,128)S(1)} %get-tuple-element.53), channel_id=1, source_target_pairs={{0,6},{2,4},{4,2},{6,0},{1,7},{3,5},{5,3},{7,1},{8,14},{10,12},{12... | collective-permute-start | bytes 98312 | tf_op jit(solution)/shard_map/ppermute | solution.py:66
  48.5 1.0 %copy-start.4 = (f32[16,64,128]{2,1,0:T(8,128)S(1)}, f32[16,64,128]{2,1,0:T(8,128)}, u32[]{:S(2)}) copy-start(f32[16,64,128]{2,1,0:T(8,128)} %refs_4_.1) | copy-start | bytes 1572868
  52.7 4.4 %collective-permute-start.8 = (f32[64,128]{1,0:T(8,128)S(1)}, f32[64,128]{1,0:T(8,128)S(1)}, u32[]{:S(2)}, u32[]{:S(2)}) collective-permute-start(f32[64,128]{1,0:T(8,128)S(1)} %get-tuple-element.60), channel_id=1, source_target_pairs={{0,1},{1,0},{2,3},{3,2},{4,5},{5,4},{6,7},{7,6},{8,9},{9,8},{10,11... | collective-permute-start | bytes 98312 | tf_op jit(solution)/shard_map/ppermute | solution.py:57
  52.8 4.3 %collective-permute-start.10 = (f32[64,128]{1,0:T(8,128)S(1)}, f32[64,128]{1,0:T(8,128)S(1)}, u32[]{:S(2)}, u32[]{:S(2)}) collective-permute-start(f32[64,128]{1,0:T(8,128)S(1)} %get-tuple-element.62), channel_id=1, source_target_pairs={{0,6},{2,0},{4,2},{6,4},{1,7},{3,1},{5,3},{7,5},{8,14},{10,8},{12,... | collective-permute-start | bytes 98312 | tf_op jit(solution)/shard_map/ppermute | solution.py:57
  53.4 3.7 %collective-permute-start.9 = (f32[16,128]{1,0:T(8,128)S(1)}, f32[16,128]{1,0:T(8,128)S(1)}, u32[]{:S(2)}, u32[]{:S(2)}) collective-permute-start(f32[16,128]{1,0:T(8,128)S(1)} %get-tuple-element.61), channel_id=1, source_target_pairs={{0,24},{8,0},{16,8},{24,16},{1,25},{9,1},{17,9},{25,17},{2,26},{10... | collective-permute-start | bytes 24584 | tf_op jit(solution)/shard_map/ppermute | solution.py:57
  57.1 1.0 %copy-start.2 = (f32[616,128]{1,0:T(8,128)S(1)}, f32[616,128]{1,0:T(8,128)}, u32[]{:S(2)}) copy-start(f32[616,128]{1,0:T(8,128)} %copy-done) | copy-start | bytes 946180
  (11 other events, 8.8 us)

commit v3 on v2

--- a/solution.py
+++ b/solution.py
@@ -90,6 +90,7 @@
         out_shape=[kind(shape, F32) for shape in outs],
         scratch_shapes=[pltpu.VMEM(shape, F32) for shape in scratch],
         name=name,
+        compiler_params=pltpu.CompilerParams(vmem_limit_bytes=12 * 2**20),
         **kwargs,
     )
 

time: 64.7 us -> 52.1 us (0.81)
  local copies, waits for them, and re-layouts: 11.8 us -> 2.83 us
  Pallas kernels: 13.3 us -> 9.92 us
    unnamed x48 -> x12, local copies, waits for them, and re-layouts: 11.8 us -> 2.83 us
    pallas_call x7, Pallas kernels: 13.3 us -> 9.92 us  [apply(): return run(*near)]
where the time goes in v3:
time: 52.1 us; the launch traced here: 51.9 us
  waiting for transfers between devices  15.7 us (30%)
  starting transfers between devices  13.2 us (25%)
  blocking collectives  10.1 us (19%)
  Pallas kernels  9.92 us (19%)
  local copies, waits for them, and re-layouts  2.83 us (5%)
    all_to_all x1, blocking collectives, local(): sums = lax.all_to_all(sums, ('gx', 'gy', 'gz'), 0, 0)  10.1 us
    pallas_call x7, Pallas kernels, apply(): return run(*near)  9.92 us
    ppermute x6, waiting for transfers between devices, ring(): lax.ppermute(value, axis, [(i, (i + step) % size) for i in range(size)])  6.34 us
    ppermute x6, starting transfers between devices, ring(): lax.ppermute(value, axis, [(i, (i + step) % size) for i in range(size)])  5.93 us
    ppermute x2, waiting for transfers between devices, swap(): out.append(lax.ppermute(values[1], axis, odd))  5.75 us
    ppermute x2, starting transfers between devices, swap(): out.append(lax.ppermute(values[1], axis, odd))  4.57 us
    ppermute x3, waiting for transfers between devices, swap(): out = [lax.ppermute(values[0], axis, even)]  3.64 us
    unnamed x12, local copies, waits for them, and re-layouts  2.83 us
  transfers between devices with their start and end apart: 11, of which 6 were waited for; matrix products, arithmetic and copies ran while one was open for 0% of the time, Pallas kernels for 0%

profile of v3, /device:TPU:0, one launch (start us, length us, event | category | flops | bytes accessed | tf_op | source)
XLA Modules:
  0.0 51.9 jit_solution(11977394371384040064)
XLA Ops:
  0.0 1.4 %copy-done = f32[3,16,64,128]{3,2,1,0:T(8,128)S(1)} copy-done((f32[3,16,64,128]{3,2,1,0:T(8,128)S(1)}, f32[3,16,64,128]{3,2,1,0:T(8,128)}, u32[]{:S(2)}) %copy-start) | copy-done | bytes 1572888
  1.4 1.4 %copy-done.2 = f32[3,16,64,128]{3,2,1,0:T(8,128)S(1)} copy-done((f32[3,16,64,128]{3,2,1,0:T(8,128)S(1)}, f32[3,16,64,128]{3,2,1,0:T(8,128)}, u32[]{:S(2)}) %copy-start.2) | copy-done | bytes 1572888
  2.8 1.9 %edge_stage.1 = (f32[16,64,128]{2,1,0:T(8,128)S(1)}, f32[3,64,128]{2,1,0:T(8,128)S(1)}, f32[48,128]{1,0:T(8,128)S(1)}, f32[64,128]{1,0:T(8,128)S(1)}, f32[3,64,1...) custom-call(f32[3,16,64,128]{3,2,1,0:T(8,128)S(1)} %copy-done, f32[3,16,64,128]{3,2,1,0:T(8,128)S(1)} %copy-done.2), custom_call_target="tpu_custom_call" | custom-call | tf_op jit(solution)/shard_map/edge_stage/pallas_call | solution.py:102
  4.7 0.6 %collective-permute-start = (f32[3,64,128]{2,1,0:T(8,128)S(1)}, f32[3,64,128]{2,1,0:T(8,128)S(1)}, u32[]{:S(2)}, u32[]{:S(2)}) collective-permute-start(f32[3,64,128]{2,1,0:T(8,128)S(1)} %get-tuple-element.35), channel_id=1, source_target_pairs={{0,1},{1,0},{2,3},{3,2},{4,5},{5,4},{6,7},{7,6},{8,9},{9,8},{10,11... | collective-permute-start | bytes 294920 | tf_op jit(solution)/shard_map/ppermute | solution.py:57
  5.3 2.6 %collective-permute-start.2 = (f32[64,128]{1,0:T(8,128)S(1)}, f32[64,128]{1,0:T(8,128)S(1)}, u32[]{:S(2)}, u32[]{:S(2)}) collective-permute-start(f32[64,128]{1,0:T(8,128)S(1)} %get-tuple-element.37), channel_id=1, source_target_pairs={{0,2},{2,4},{4,6},{6,0},{1,3},{3,5},{5,7},{7,1},{8,10},{10,12},{12... | collective-permute-start | bytes 98312 | tf_op jit(solution)/shard_map/ppermute | solution.py:57
  7.9 1.5 %collective-permute-start.1 = (f32[48,128]{1,0:T(8,128)S(1)}, f32[48,128]{1,0:T(8,128)S(1)}, u32[]{:S(2)}, u32[]{:S(2)}) collective-permute-start(f32[48,128]{1,0:T(8,128)S(1)} %get-tuple-element.36), channel_id=1, source_target_pairs={{0,8},{8,16},{16,24},{24,0},{1,9},{9,17},{17,25},{25,1},{2,10},{10... | collective-permute-start | bytes 73736 | tf_op jit(solution)/shard_map/ppermute | solution.py:57
  9.4 3.2 %collective-permute-done.1.gx.refs_7_ = f32[48,128]{1,0:T(8,128)S(1)} collective-permute-done((f32[48,128]{1,0:T(8,128)S(1)}, f32[48,128]{1,0:T(8,128)S(1)}, u32[]{:S(2)}, u32[]{:S(2)}) %collective-permute-start.1) | collective-permute-done | bytes 24608 | tf_op jit(solution)/shard_map/ppermute | solution.py:57
  12.6 1.0 %nodal_stage.1 = (f32[16,64,128]{2,1,0:T(8,128)S(1)}, f32[12,40,128]{2,1,0:T(8,128)S(1)}, f32[8,40,128]{2,1,0:T(8,128)S(1)}, f32[8,40,128]{2,1,0:T(8,128)S(1)}, ...) custom-call(f32[16,64,128]{2,1,0:T(8,128)S(1)} %get-tuple-element.34.part, f32[16,64,128]{2,1,0:T(8,128)S(1)} %copy-done.4, ...), custom_call_target="tpu_custom_call" | custom-call | tf_op jit(solution)/shard_map/nodal_stage/pallas_call | solution.py:102
  13.7 1.6 %collective-permute-done.3.refs_0_.refs_5_.refs_9_ = f32[616,128]{1,0:T(8,128)S(1)} collective-permute-done((f32[616,128]{1,0:T(8,128)S(1)}, f32[616,128]{1,0:T(8,128)S(1)}, u32[]{:S(2)}, u32[]{:S(2)}) %collective-permute-start.3) | collective-permute-done | bytes 315424 | tf_op jit(solution)/shard_map/ppermute | solution.py:63
  15.4 1.0 %collective-permute-start.4 = (f32[176,128]{1,0:T(8,128)S(1)}, f32[176,128]{1,0:T(8,128)S(1)}, u32[]{:S(2)}, u32[]{:S(2)}) collective-permute-start(f32[176,128]{1,0:T(8,128)S(1)} %get-tuple-element.46), channel_id=1, source_target_pairs={{0,8},{8,0},{16,24},{24,16},{1,9},{9,1},{17,25},{25,17},{2,10},{10... | collective-permute-start | bytes 270344 | tf_op jit(solution)/shard_map/ppermute | solution.py:63
  16.4 2.1 %collective-permute-start.5 = (f32[176,128]{1,0:T(8,128)S(1)}, f32[176,128]{1,0:T(8,128)S(1)}, u32[]{:S(2)}, u32[]{:S(2)}) collective-permute-start(f32[176,128]{1,0:T(8,128)S(1)} %get-tuple-element.47), channel_id=1, source_target_pairs={{0,24},{8,16},{16,8},{24,0},{1,25},{9,17},{17,9},{25,1},{2,26},{10... | collective-permute-start | bytes 270344 | tf_op jit(solution)/shard_map/ppermute | solution.py:66
  18.5 2.0 %collective-permute-done.4.refs_0_.refs_6_.refs_10_ = f32[176,128]{1,0:T(8,128)S(1)} collective-permute-done((f32[176,128]{1,0:T(8,128)S(1)}, f32[176,128]{1,0:T(8,128)S(1)}, u32[]{:S(2)}, u32[]{:S(2)}) %collective-permute-start.4) | collective-permute-done | bytes 90144 | tf_op jit(solution)/shard_map/ppermute | solution.py:63
  20.5 2.5 %collective-permute-done.5.refs_1_.refs_7_.refs_11_ = f32[176,128]{1,0:T(8,128)S(1)} collective-permute-done((f32[176,128]{1,0:T(8,128)S(1)}, f32[176,128]{1,0:T(8,128)S(1)}, u32[]{:S(2)}, u32[]{:S(2)}) %collective-permute-start.5) | collective-permute-done | bytes 90144 | tf_op jit(solution)/shard_map/ppermute | solution.py:66
  23.0 1.2 %y_stage.1 = (f32[12,40,128]{2,1,0:T(8,128)S(1)}, f32[12,40,128]{2,1,0:T(8,128)S(1)}, f32[64,128]{1,0:T(8,128)S(1)}, f32[64,128]{1,0:T(8,128)S(1)}) custom-call(f32[176,128]{1,0:T(8,128)S(1)} %collective-permute-done.4.refs_0_.refs_6_.refs_10_, f32[176,128]{1,0:T(8,128)S(1)} %collective-permute-done.5.refs_1_.refs_7_.refs_11_, ...), custom_call_target="tpu_custom_call" | custom-call | tf_op jit(solution)/shard_map/y_stage/pallas_call | solution.py:102
  24.2 1.6 %collective-permute-start.6 = (f32[64,128]{1,0:T(8,128)S(1)}, f32[64,128]{1,0:T(8,128)S(1)}, u32[]{:S(2)}, u32[]{:S(2)}) collective-permute-start(f32[64,128]{1,0:T(8,128)S(1)} %get-tuple-element.52), channel_id=1, source_target_pairs={{0,2},{2,0},{4,6},{6,4},{1,3},{3,1},{5,7},{7,5},{8,10},{10,8},{12,... | collective-permute-start | bytes 98312 | tf_op jit(solution)/shard_map/ppermute | solution.py:63
  25.9 2.5 %collective-permute-start.7 = (f32[64,128]{1,0:T(8,128)S(1)}, f32[64,128]{1,0:T(8,128)S(1)}, u32[]{:S(2)}, u32[]{:S(2)}) collective-permute-start(f32[64,128]{1,0:T(8,128)S(1)} %get-tuple-element.53), channel_id=1, source_target_pairs={{0,6},{2,4},{4,2},{6,0},{1,7},{3,5},{5,3},{7,1},{8,14},{10,12},{12... | collective-permute-start | bytes 98312 | tf_op jit(solution)/shard_map/ppermute | solution.py:66
  28.4 3.2 %collective-permute-done.7.refs_1_.refs_9_.refs_13_ = f32[64,128]{1,0:T(8,128)S(1)} collective-permute-done((f32[64,128]{1,0:T(8,128)S(1)}, f32[64,128]{1,0:T(8,128)S(1)}, u32[]{:S(2)}, u32[]{:S(2)}) %collective-permute-start.7) | collective-permute-done | bytes 32800 | tf_op jit(solution)/shard_map/ppermute | solution.py:66
  31.6 1.0 %coarse_stage.1 = (f32[12,40,128]{2,1,0:T(8,128)S(1)}, f32[12,40,128]{2,1,0:T(8,128)S(1)}, f32[32,1,128]{2,1,0:T(1,128)S(1)}) custom-call(f32[64,128]{1,0:T(8,128)S(1)} %collective-permute-done.6.refs_0_.refs_8_.refs_12_, f32[64,128]{1,0:T(8,128)S(1)} %collective-permute-done.7.refs_1_.refs_9_.refs_13_, f32[12,40,128]{2,1,0:T(8,128)S(1)} %get-tuple-element.54.refs_2_, ...), custom_call_target="tpu_custom_call" | custom-call | tf_op jit(solution)/shard_map/coarse_stage/pallas_call | solution.py:102
  32.6 10.1 %all_to_all.5.refs_0_ = f32[32,1,128]{2,1,0:T(1,128)S(1)} all-to-all(f32[32,1,128]{2,1,0:T(1,128)S(1)} %get-tuple-element.56), channel_id=1, replica_groups=mesh['gx'=4,'gy'=4,'gz'=2] {'gx','gy','gz'}, dimensions={0} | all-to-all | bytes 32768 | tf_op jit(solution)/shard_map/all_to_all | solution.py:650
  42.7 1.3 %final_stage.1 = (f32[16,64,128]{2,1,0:T(8,128)S(1)}, f32[64,128]{1,0:T(8,128)S(1)}, f32[16,128]{1,0:T(8,128)S(1)}, f32[64,128]{1,0:T(8,128)S(1)}) custom-call(f32[32,1,128]{2,1,0:T(1,128)S(1)} %all_to_all.5.refs_0_, f32[12,40,128]{2,1,0:T(8,128)S(1)} %get-tuple-element.57.refs_1_, f32[12,40,128]{2,1,0:T(8,128)S(1)} %get-tuple-element.58.refs_2_, ...), custom_call_target="tpu_custom_call" | custom-call | tf_op jit(solution)/shard_map/final_stage/pallas_call | solution.py:102
  44.1 0.6 %collective-permute-start.10 = (f32[64,128]{1,0:T(8,128)S(1)}, f32[64,128]{1,0:T(8,128)S(1)}, u32[]{:S(2)}, u32[]{:S(2)}) collective-permute-start(f32[64,128]{1,0:T(8,128)S(1)} %get-tuple-element.62), channel_id=1, source_target_pairs={{0,6},{2,0},{4,2},{6,4},{1,7},{3,1},{5,3},{7,5},{8,14},{10,8},{12,... | collective-permute-start | bytes 98312 | tf_op jit(solution)/shard_map/ppermute | solution.py:57
  44.7 0.6 %collective-permute-start.9 = (f32[16,128]{1,0:T(8,128)S(1)}, f32[16,128]{1,0:T(8,128)S(1)}, u32[]{:S(2)}, u32[]{:S(2)}) collective-permute-start(f32[16,128]{1,0:T(8,128)S(1)} %get-tuple-element.61), channel_id=1, source_target_pairs={{0,24},{8,0},{16,8},{24,16},{1,25},{9,1},{17,9},{25,17},{2,26},{10... | collective-permute-start | bytes 24584 | tf_op jit(solution)/shard_map/ppermute | solution.py:57
  45.3 3.1 %collective-permute-done.9.refs_4_ = f32[16,128]{1,0:T(8,128)S(1)} collective-permute-done((f32[16,128]{1,0:T(8,128)S(1)}, f32[16,128]{1,0:T(8,128)S(1)}, u32[]{:S(2)}, u32[]{:S(2)}) %collective-permute-start.9) | collective-permute-done | bytes 8224 | tf_op jit(solution)/shard_map/ppermute | solution.py:57
  48.4 3.5 %output_stage.1 = f32[3,16,64,128]{3,2,1,0:T(8,128)} custom-call(f32[3,16,64,128]{3,2,1,0:T(8,128)S(1)} %copy-done.1, f32[3,16,64,128]{3,2,1,0:T(8,128)S(1)} %copy-done.3, f32[16,64,128]{2,1,0:T(8,128)S(1)} %get-tuple-element.59.refs_2_, f32[64,128]{1,0:T(8,128)S(1)} %collective-permute-done.8.refs_3_, f32[16,128]{1,0:T(8,128)S(1)} %collective-permute-done.9.refs_4_, ...), custom_call_target="tpu_custom_call" | custom-call | tf_op jit(solution)/shard_map/output_stage/pallas_call | solution.py:102
  (18 shorter events, 0.3 us)
Async XLA Ops:
  0.0 1.4 %copy-start = (f32[3,16,64,128]{3,2,1,0:T(8,128)S(1)}, f32[3,16,64,128]{3,2,1,0:T(8,128)}, u32[]{:S(2)}) copy-start(f32[3,16,64,128]{3,2,1,0:T(8,128)} %refs_0_.1) | copy-start | bytes 4718596
  1.4 1.4 %copy-start.2 = (f32[3,16,64,128]{3,2,1,0:T(8,128)S(1)}, f32[3,16,64,128]{3,2,1,0:T(8,128)}, u32[]{:S(2)}) copy-start(f32[3,16,64,128]{3,2,1,0:T(8,128)} %refs_1_.1) | copy-start | bytes 4718596
  2.8 9.8 %copy-start.4 = (f32[16,64,128]{2,1,0:T(8,128)S(1)}, f32[16,64,128]{2,1,0:T(8,128)}, u32[]{:S(2)}) copy-start(f32[16,64,128]{2,1,0:T(8,128)} %refs_4_.1) | copy-start | bytes 1572868
  2.8 9.8 %copy-start.5 = (f32[8,32,64]{2,1,0:T(8,128)S(1)}, f32[8,32,64]{2,1,0:T(8,128)}, u32[]{:S(2)}) copy-start(f32[8,32,64]{2,1,0:T(8,128)} %coarse.1) | copy-start | bytes 196612
  4.7 7.9 %collective-permute-start = (f32[3,64,128]{2,1,0:T(8,128)S(1)}, f32[3,64,128]{2,1,0:T(8,128)S(1)}, u32[]{:S(2)}, u32[]{:S(2)}) collective-permute-start(f32[3,64,128]{2,1,0:T(8,128)S(1)} %get-tuple-element.35), channel_id=1, source_target_pairs={{0,1},{1,0},{2,3},{3,2},{4,5},{5,4},{6,7},{7,6},{8,9},{9,8},{10,11... | collective-permute-start | bytes 294920 | tf_op jit(solution)/shard_map/ppermute | solution.py:57
  5.3 7.4 %collective-permute-start.2 = (f32[64,128]{1,0:T(8,128)S(1)}, f32[64,128]{1,0:T(8,128)S(1)}, u32[]{:S(2)}, u32[]{:S(2)}) collective-permute-start(f32[64,128]{1,0:T(8,128)S(1)} %get-tuple-element.37), channel_id=1, source_target_pairs={{0,2},{2,4},{4,6},{6,0},{1,3},{3,5},{5,7},{7,1},{8,10},{10,12},{12... | collective-permute-start | bytes 98312 | tf_op jit(solution)/shard_map/ppermute | solution.py:57
  7.9 4.7 %collective-permute-start.1 = (f32[48,128]{1,0:T(8,128)S(1)}, f32[48,128]{1,0:T(8,128)S(1)}, u32[]{:S(2)}, u32[]{:S(2)}) collective-permute-start(f32[48,128]{1,0:T(8,128)S(1)} %get-tuple-element.36), channel_id=1, source_target_pairs={{0,8},{8,16},{16,24},{24,0},{1,9},{9,17},{17,25},{25,1},{2,10},{10... | collective-permute-start | bytes 73736 | tf_op jit(solution)/shard_map/ppermute | solution.py:57
  13.6 1.7 %collective-permute-start.3 = (f32[616,128]{1,0:T(8,128)S(1)}, f32[616,128]{1,0:T(8,128)S(1)}, u32[]{:S(2)}, u32[]{:S(2)}) collective-permute-start(f32[616,128]{1,0:T(8,128)S(1)} %get-tuple-element.39), channel_id=1, source_target_pairs={{0,1},{1,0},{2,3},{3,2},{4,5},{5,4},{6,7},{7,6},{8,9},{9,8},{10,11... | collective-permute-start | bytes 946184 | tf_op jit(solution)/shard_map/ppermute | solution.py:63
  15.4 5.1 %collective-permute-start.4 = (f32[176,128]{1,0:T(8,128)S(1)}, f32[176,128]{1,0:T(8,128)S(1)}, u32[]{:S(2)}, u32[]{:S(2)}) collective-permute-start(f32[176,128]{1,0:T(8,128)S(1)} %get-tuple-element.46), channel_id=1, source_target_pairs={{0,8},{8,0},{16,24},{24,16},{1,9},{9,1},{17,25},{25,17},{2,10},{10... | collective-permute-start | bytes 270344 | tf_op jit(solution)/shard_map/ppermute | solution.py:63
  16.4 6.7 %collective-permute-start.5 = (f32[176,128]{1,0:T(8,128)S(1)}, f32[176,128]{1,0:T(8,128)S(1)}, u32[]{:S(2)}, u32[]{:S(2)}) collective-permute-start(f32[176,128]{1,0:T(8,128)S(1)} %get-tuple-element.47), channel_id=1, source_target_pairs={{0,24},{8,16},{16,8},{24,0},{1,25},{9,17},{17,9},{25,1},{2,26},{10... | collective-permute-start | bytes 270344 | tf_op jit(solution)/shard_map/ppermute | solution.py:66
  23.0 25.4 %copy-start.3 = (f32[3,16,64,128]{3,2,1,0:T(8,128)S(1)}, f32[3,16,64,128]{3,2,1,0:T(8,128)}, u32[]{:S(2)}) copy-start(f32[3,16,64,128]{3,2,1,0:T(8,128)} %refs_1_.1) | copy-start | bytes 4718596
  24.2 24.1 %copy-start.1 = (f32[3,16,64,128]{3,2,1,0:T(8,128)S(1)}, f32[3,16,64,128]{3,2,1,0:T(8,128)}, u32[]{:S(2)}) copy-start(f32[3,16,64,128]{3,2,1,0:T(8,128)} %refs_0_.1) | copy-start | bytes 4718596
  24.2 4.1 %collective-permute-start.6 = (f32[64,128]{1,0:T(8,128)S(1)}, f32[64,128]{1,0:T(8,128)S(1)}, u32[]{:S(2)}, u32[]{:S(2)}) collective-permute-start(f32[64,128]{1,0:T(8,128)S(1)} %get-tuple-element.52), channel_id=1, source_target_pairs={{0,2},{2,0},{4,6},{6,4},{1,3},{3,1},{5,7},{7,5},{8,10},{10,8},{12,... | collective-permute-start | bytes 98312 | tf_op jit(solution)/shard_map/ppermute | solution.py:63
  25.9 5.7 %collective-permute-start.7 = (f32[64,128]{1,0:T(8,128)S(1)}, f32[64,128]{1,0:T(8,128)S(1)}, u32[]{:S(2)}, u32[]{:S(2)}) collective-permute-start(f32[64,128]{1,0:T(8,128)S(1)} %get-tuple-element.53), channel_id=1, source_target_pairs={{0,6},{2,4},{4,2},{6,0},{1,7},{3,5},{5,3},{7,1},{8,14},{10,12},{12... | collective-permute-start | bytes 98312 | tf_op jit(solution)/shard_map/ppermute | solution.py:66
  44.0 4.4 %collective-permute-start.8 = (f32[64,128]{1,0:T(8,128)S(1)}, f32[64,128]{1,0:T(8,128)S(1)}, u32[]{:S(2)}, u32[]{:S(2)}) collective-permute-start(f32[64,128]{1,0:T(8,128)S(1)} %get-tuple-element.60), channel_id=1, source_target_pairs={{0,1},{1,0},{2,3},{3,2},{4,5},{5,4},{6,7},{7,6},{8,9},{9,8},{10,11... | collective-permute-start | bytes 98312 | tf_op jit(solution)/shard_map/ppermute | solution.py:57
  44.1 4.3 %collective-permute-start.10 = (f32[64,128]{1,0:T(8,128)S(1)}, f32[64,128]{1,0:T(8,128)S(1)}, u32[]{:S(2)}, u32[]{:S(2)}) collective-permute-start(f32[64,128]{1,0:T(8,128)S(1)} %get-tuple-element.62), channel_id=1, source_target_pairs={{0,6},{2,0},{4,2},{6,4},{1,7},{3,1},{5,3},{7,5},{8,14},{10,8},{12,... | collective-permute-start | bytes 98312 | tf_op jit(solution)/shard_map/ppermute | solution.py:57
  44.7 3.7 %collective-permute-start.9 = (f32[16,128]{1,0:T(8,128)S(1)}, f32[16,128]{1,0:T(8,128)S(1)}, u32[]{:S(2)}, u32[]{:S(2)}) collective-permute-start(f32[16,128]{1,0:T(8,128)S(1)} %get-tuple-element.61), channel_id=1, source_target_pairs={{0,24},{8,0},{16,8},{24,16},{1,25},{9,1},{17,9},{25,17},{2,26},{10... | collective-permute-start | bytes 24584 | tf_op jit(solution)/shard_map/ppermute | solution.py:57

commit v4 on v3

--- a/solution.py
+++ b/solution.py
@@ -83,23 +83,25 @@
             up(refs[1])
 
 
-def call(body, outs, name, scratch=(), far=(), far_out=False, **kwargs):
+def call(body, outs, name, scratch=(), far=(), free=(), far_out=False, **kwargs):
     kind = jax.ShapeDtypeStruct if far_out else pltpu.VMEM
     run = pl.pallas_call(
         body,
         out_shape=[kind(shape, F32) for shape in outs],
-        scratch_shapes=[pltpu.VMEM(shape, F32) for shape in scratch],
+        scratch_shapes=[pltpu.VMEM(s, F32) if isinstance(s, tuple) else s for s in scratch],
         name=name,
         compiler_params=pltpu.CompilerParams(vmem_limit_bytes=12 * 2**20),
         **kwargs,
     )
 
     def apply(*args):
-        near = [
-            a if i in far else pltpu.with_memory_space_constraint(a, pltpu.VMEM)
-            for i, a in enumerate(args)
-        ]
-        return run(*near)
+        spaces = [pltpu.HBM if i in far else pltpu.VMEM for i in range(len(args))]
+        return run(
+            *(
+                a if i in free else pltpu.with_memory_space_constraint(a, space)
+                for i, (a, space) in enumerate(zip(args, spaces))
+            )
+        )
 
     return apply
 
@@ -250,22 +252,29 @@
                 ref[i * rows : (i + 1) * rows, :] = value
             ref[9 * rows : 9 * rows + nx, :] = face
 
+        def tail(ref, values):
+            for i, value in enumerate(values):
+                at = 9 * rows + nx + i * nx
+                ref[at : at + nx, :] = value
+
         def up(ref):
             fill(ref, cz - 1, cz - 2, zh_[cz - 1], fg[nz - 1])
-            for k in range(3):
-                at = 9 * rows + nx + k * nx
-                ref[at : at + nx, :] = jnp.zeros((nx, LANES), F32)
+            tail(ref, [jnp.zeros((nx, LANES), F32)] * 5)
 
         def down(ref):
             fill(ref, 0, 1, zl_[0], fg[0])
-            for k in range(3):
-                at = 9 * rows + nx + k * nx
-                ref[at : at + nx, :] = low_z[k]
+            here = fg[0]
+            around = fg[1] + jnp.where(row == 0, 0.0, shift_rows(here, 1))
+            around += jnp.where(row == nx - 1, 0.0, shift_rows(here, -1))
+            around += jnp.where(lane == 0, 0.0, shift_lanes(here, 1))
+            around += jnp.where(lane == ny - 1, 0.0, shift_lanes(here, -1))
+            inverse = 1.0 / (6.0 + shift[0])
+            tail(ref, [low_z[0], low_z[1], low_z[2], here + inverse * around, inverse])
 
         write_sides("gz", out, up, down)
 
     coarse = (cz, rows, LANES)
-    send = (9 * rows + 4 * nx, LANES)
+    send = (9 * rows + 6 * nx, LANES)
     return call(
         body,
         [(nz, nx, ny), (cz + 4, rows, LANES), coarse, coarse, coarse] + [send] * sends,
@@ -276,22 +285,25 @@
     )(part, node_shift, coarse_shift, got_z, got_x, got_y, low_z)
 
 
-def x_stage(got, rhs, xb, yb, w, fg, low_x, z_count, x_count):
+def x_stage(got, rhs, xb, yb, w, fg, low_x, node_shift, z_count, x_count):
     planes, rows, _ = rhs.shape
     cz, cx = planes - 4, rows - 8
-    nz, nx, _ = fg.shape
+    nz, nx, ny = fg.shape
+    cy = ny // 2
     sends = 1 if x_count == 2 else 2
     gots = len(got)
 
     def body(*refs):
         got = refs[:gots]
-        rhs, xb, yb, w, fg, low_x, rhs2, yb2, w2 = refs[gots : gots + 9]
-        out, (xb2,) = refs[gots + 9 : gots + 9 + sends], refs[gots + 9 + sends :]
-
-        def take(pick, i):
-            at = slice(i * rows, (i + 1) * rows)
+        rhs, xb, yb, w, fg, low_x, shift, rhs2, yb2, w2 = refs[gots : gots + 10]
+        out, (xb2,) = refs[gots + 10 : gots + 10 + sends], refs[gots + 10 + sends :]
+
+        def take_at(pick, at):
             values = [ref[at, :] for ref in got]
             return pick("gz", z_count, values[0], values[1] if gots > 1 else None)
+
+        def take(pick, i):
+            return take_at(pick, slice(i * rows, (i + 1) * rows))
 
         for c in range(1, cz - 1):
             rhs2[c] = rhs[c]
@@ -309,73 +321,126 @@
             there[cz + 2] = take(low_of, i + 1)
             there[cz + 3] = take(low_of, i)
 
+        lane = lane_ids(planes)
+
         def fill(ref, near, far, fine):
-            pieces = [rhs2[:, near, :], rhs2[:, far, :], w2[:, near, :], w2[:, far, :]]
-            pieces += [xb2[:, near, :], yb2[:, near, :], yb2[:, far, :]]
-            for i, value in enumerate(pieces):
+            halves = lane < cy
+            first = jnp.where(halves, rhs2[:, near, :], shift_lanes(rhs2[:, far, :], cy))
+            second = jnp.where(halves, w2[:, near, :], shift_lanes(w2[:, far, :], cy))
+            edge = yb2[:, far, :]
+            third = jnp.where(halves, xb2[:, near, :], shift_lanes(yb2[:, near, :], cy))
+            third = jnp.where(lane == cy + 1, shift_lanes(edge, cy + 1), third)
+            third = jnp.where(lane == LANES - 2, shift_lanes(edge, cy - 1), third)
+            for i, value in enumerate((first, second, third)):
                 ref[i * 16 : i * 16 + planes, :] = value
-                if planes < 16:
-                    ref[i * 16 + planes : i * 16 + 16, :] = jnp.zeros((16 - planes, LANES), F32)
-            ref[112 : 112 + nz, :] = fg[:, fine, :]
+                ref[i * 16 + planes : i * 16 + 16, :] = jnp.zeros((16 - planes, LANES), F32)
+            ref[48 : 48 + nz, :] = fg[:, fine, :]
+            at = 9 * rows + fine
+            ref[48 + nz : 49 + nz, :] = take_at(high_of, slice(at, at + 1))
+            ref[49 + nz : 56 + nz, :] = jnp.zeros((7, LANES), F32)
+
+        tail = 56 + nz
 
         def up(ref):
             fill(ref, cx - 1, cx - 2, nx - 1)
-            ref[112 + nz : 112 + 4 * nz, :] = jnp.zeros((3 * nz, LANES), F32)
+            ref[tail : tail + 5 * nz, :] = jnp.zeros((5 * nz, LANES), F32)
 
         def down(ref):
             fill(ref, 0, 1, 0)
-            ref[112 + nz : 112 + 4 * nz, :] = low_x[...]
+            ref[tail : tail + 3 * nz, :] = low_x[...]
+            here = fg[:, 0, :]
+            lane_z = lane_ids(nz)
+            row_z = row_ids(nz)
+            at = 9 * rows
+            below = take_at(low_of, slice(at, at + 1))
+            above = take_at(high_of, slice(at, at + 1))
+            around = fg[:, 1, :] + jnp.where(row_z == 0, below, shift_rows(here, 1))
+            around += jnp.where(row_z == nz - 1, above, shift_rows(here, -1))
+            around += jnp.where(lane_z == 0, 0.0, shift_lanes(here, 1))
+            around += jnp.where(lane_z == ny - 1, 0.0, shift_lanes(here, -1))
+            inverse = 1.0 / (6.0 + shift[:, 0, :])
+            ref[tail + 3 * nz : tail + 4 * nz, :] = here + inverse * around
+            ref[tail + 4 * nz : tail + 5 * nz, :] = inverse
 
         write_sides("gx", out, up, down)
 
     whole = (planes, rows, LANES)
     return call(
         body,
-        [whole, whole, whole] + [(112 + 4 * nz, LANES)] * sends,
+        [whole, whole, whole] + [(56 + 6 * nz, LANES)] * sends,
         "x_stage",
         scratch=[whole],
-        in_specs=vmem(gots + 6),
+        in_specs=vmem(gots + 7),
         out_specs=vmem(3 + sends),
-    )(*got, rhs, xb, yb, w, fg, low_x)
-
-
-def y_stage(got, rhs, yb, w, fg, low_y, x_count, y_count):
+    )(*got, rhs, xb, yb, w, fg, low_x, node_shift)
+
+
+def y_stage(got_z, got, rhs, yb, w, fg, low_y, node_shift, counts):
     planes, rows, _ = rhs.shape
     cx = rows - 8
     nz, nx, ny = fg.shape
     cy = ny // 2
+    z_count, x_count, y_count = counts
     sends = 1 if y_count == 2 else 2
-    gots = len(got)
+    n_z, gots = len(got_z), len(got)
 
     def body(*refs):
-        got = refs[:gots]
-        rhs, yb, w, fg, low_y, rhs3, w3 = refs[gots : gots + 7]
-        out, (yb3, add) = refs[gots + 7 : gots + 7 + sends], refs[gots + 7 + sends :]
-
-        def take(pick, i):
-            at = slice(i * 16, i * 16 + planes)
+        gz, got = refs[:n_z], refs[n_z : n_z + gots]
+        rhs, yb, w, fg, low_y, shift, rhs3, w3 = refs[n_z + gots : n_z + gots + 8]
+        rest = refs[n_z + gots + 8 :]
+        out, (yb3, add) = rest[:sends], rest[sends:]
+        lane_p = lane_ids(planes)
+
+        def take_at(pick, at):
             values = [ref[at, :] for ref in got]
             return pick("gx", x_count, values[0], values[1] if gots > 1 else None)
 
+        def take(pick, i):
+            return take_at(pick, slice(i * 16, i * 16 + planes))
+
+        def z_face(pick):
+            values = [ref[9 * rows : 9 * rows + nx, :] for ref in gz]
+            return pick("gz", z_count, values[0], values[1] if n_z > 1 else None)
+
         add[...] = jnp.zeros_like(add)
-        add[:, cx, :] = take(high_of, 0)
-        add[:, cx + 1, :] = take(high_of, 1)
-        add[:, rows - 1, :] = take(low_of, 0)
-        add[:, rows - 2, :] = take(low_of, 1)
-        add[:, cx - 1, :] = take(high_of, 4)
-        add[:, 0, :] = take(low_of, 4)
+        for c in range(planes):
+            w3[c] = w[c]
+            yb3[c] = yb[c]
+        for pick, near, far, edge in ((high_of, cx, cx + 1, cx - 1), (low_of, rows - 1, rows - 2, 0)):
+            first, second, third = take(pick, 0), take(pick, 1), take(pick, 2)
+            other = shift_lanes(third, -cy)
+            one = jnp.where((lane_p == 0) | (lane_p == cy - 1), other, 0.0)
+            two = jnp.where(lane_p == 0, shift_lanes(third, -cy - 1), 0.0)
+            two = jnp.where(lane_p == cy - 1, shift_lanes(third, 1 - cy), two)
+            yb3[:, near, :] = one
+            yb3[:, far, :] = two
+            for at, value, ends in ((near, first, one), (far, shift_lanes(first, -cy), two)):
+                value = jnp.where(lane_p < cy, value, 0.0)
+                value += jnp.where(lane_p == cy, shift_lanes(ends, 1), 0.0)
+                value += jnp.where(lane_p == LANES - 1, shift_lanes(ends, -1), 0.0)
+                add[:, at, :] = value
+            w3[:, near, :] = jnp.where(lane_p < cy, second, 0.0)
+            w3[:, far, :] = jnp.where(lane_p < cy, shift_lanes(second, -cy), 0.0)
+            add[:, edge, :] = jnp.where(lane_p < cy, third, 0.0)
         for c in range(planes):
             rhs3[c] = rhs[c] + add[c]
-            w3[c] = w[c]
-            yb3[c] = yb[c]
-        for there, i in ((w3, 2), (yb3, 5)):
-            there[:, cx, :] = take(high_of, i)
-            there[:, cx + 1, :] = take(high_of, i + 1)
-            there[:, rows - 1, :] = take(low_of, i)
-            there[:, rows - 2, :] = take(low_of, i + 1)
 
         lane_c = lane_ids(rows)
         lane = lane_ids(nx)
+        row = row_ids(nx)
+        lane8 = lane_ids(8)
+        base = 5 * planes
+        above = z_face(high_of)
+        below = z_face(low_of)
+        x_high = take_at(high_of, slice(48, 48 + nz))
+        x_low = take_at(low_of, slice(48, 48 + nz))
+
+        def line(source, fine, at):
+            acc = jnp.zeros((8, LANES), F32)
+            for z in range(nz):
+                moved = jnp.broadcast_to(source[z : z + 1, :], (8, LANES))
+                acc = jnp.where(lane8 == at + z, shift_lanes(moved, at + z - fine), acc)
+            return acc
 
         def fill(ref, near, far, fine, tail):
             acc = jnp.zeros((rows, LANES), F32)
@@ -385,35 +450,55 @@
                     spot = i * planes + z
                     acc = jnp.where(lane_c == spot, shift_lanes(field[z], spot - at), acc)
             acc = plane(acc, nx)
-            base = 5 * planes
             for z in range(nz):
                 acc = jnp.where(lane == base + z, shift_lanes(fg[z], base + z - fine), acc)
+            acc = jnp.where(lane == base + nz, shift_lanes(above, base + nz - fine), acc)
+            at = base + nz + 1
             if tail is not None:
-                at = base + nz
                 moved = shift_lanes(tail, at)
                 acc = jnp.where((lane >= at) & (lane < at + 3 * nz), moved, acc)
-            ref[...] = acc
+            ref[:nx, :] = acc
+            ref[nx : nx + 8, :] = line(x_high, fine, base)
+            return acc
 
         def up(ref):
             fill(ref, cy - 1, cy - 2, ny - 1, None)
+            ref[nx + 8 :, :] = jnp.zeros((nx // 2, LANES), F32)
 
         def down(ref):
-            fill(ref, 0, 1, 0, low_y[...])
+            acc = fill(ref, 0, 1, 0, low_y[...])
+            here = jnp.where(lane < nz + 1, shift_lanes(acc, -base), 0.0)
+            here = jnp.where(lane == LANES - 1, shift_lanes(below, -1), here)
+            around = shift_lanes(here, 1) + shift_lanes(here, -1)
+            around += jnp.where(row == 0, line(x_low, 0, 0)[:1, :], shift_rows(here, 1))
+            around += jnp.where(row == nx - 1, line(x_high, 0, 0)[:1, :], shift_rows(here, -1))
+            inverse = jnp.ones((nx, LANES), F32)
+            for z in range(nz):
+                inverse = jnp.where(lane == z, shift_lanes(6.0 + shift[z], z), inverse)
+                around += jnp.where(lane == z, shift_lanes(fg[z], z - 1), 0.0)
+            inverse = 1.0 / inverse
+            value = here + inverse * around
+            half = nx // 2
+            packed = jnp.zeros((half, LANES), F32)
+            for i, source in enumerate((value[:half], value[half:], inverse[:half], inverse[half:])):
+                there = lane_ids(half) // nz == i
+                packed = jnp.where(there, shift_lanes(source, i * nz), packed)
+            ref[nx + 8 :, :] = packed
 
         write_sides("gy", out, up, down)
 
     whole = (planes, rows, LANES)
     return call(
         body,
-        [whole, whole] + [(nx, LANES)] * sends,
+        [whole, whole] + [(nx + 8 + nx // 2, LANES)] * sends,
         "y_stage",
         scratch=[whole, whole],
-        in_specs=vmem(gots + 5),
+        in_specs=vmem(n_z + gots + 6),
         out_specs=vmem(2 + sends),
-    )(*got, rhs, yb, w, fg, low_y)
-
-
-def coarse_stage(got, rhs, w, y_count, devices):
+    )(*got_z, *got, rhs, yb, w, fg, low_y, node_shift)
+
+
+def coarse_stage(got, rhs, w, after, y_count, devices):
     planes, rows, _ = rhs.shape
     cz, cx = planes - 4, rows - 8
     cy = LANES // 2
@@ -421,7 +506,7 @@
 
     def body(*refs):
         got = refs[:gots]
-        rhs, w, v1, v2, sums, tot, inv_, image_ = refs[gots:]
+        rhs, w, _, v1, v2, sums, tot, inv_, image_ = refs[gots:]
         values = [ref[:rows, :] for ref in got]
         second = values[1] if gots > 1 else None
         low = low_of("gy", y_count, values[0], second)
@@ -475,28 +560,84 @@
         [whole, whole, (devices, 1, LANES)],
         "coarse_stage",
         scratch=[whole, whole, whole],
-        in_specs=vmem(gots + 2),
+        in_specs=vmem(gots + 3),
         out_specs=vmem(3),
-    )(*got, rhs, w)
-
-
-def final_stage(sums, v1, v2, fg, node_shift, got_z, got_x, got_y, counts):
+    )(*got, rhs, w, after)
+
+
+def smooth_stage(residual, edge_diag, below, got_z, got_x, after, counts):
+    _, nz, nx, ny = residual.shape
+    n_z, n_x = len(got_z), len(got_x)
+    rows = nx // 2 + 8
+
+    def body(*refs):
+        res, diag, lz, lx, ly = refs[:5]
+        gz = refs[5 : 5 + n_z]
+        gx = refs[5 + n_z : 5 + n_z + n_x]
+        _, out, last, s = refs[5 + n_z + n_x :]
+        lane = lane_ids(nx)
+        row = row_ids(nx)
+        y_low = from_below("gy", ly[...])
+
+        def above_of(refs, axis, size, at):
+            values = [ref[at, :] for ref in refs]
+            return high_of(axis, size, values[0], values[1] if len(values) > 1 else None)
+
+        acc = jnp.zeros((nx, LANES), F32)
+        for k in range(3):
+            for z in range(nz):
+                s[z] = res[k, z] / diag[k, z]
+            z_low = from_below("gz", lz[k])
+            at = 9 * rows + nx + k * nx
+            z_high = above_of(gz, "gz", counts[0], slice(at, at + nx))
+            x_low = from_below("gx", lx[k * nz : (k + 1) * nz, :])
+            at = 56 + nz + k * nz
+            x_high = above_of(gx, "gx", counts[1], slice(at, at + nz))
+            for z in range(nz):
+                here = s[z]
+                around = s[z - 1] if z > 0 else z_low
+                around += s[z + 1] if z < nz - 1 else z_high
+                around += jnp.where(row == 0, x_low[z : z + 1, :], shift_rows(here, 1))
+                around += jnp.where(row == nx - 1, x_high[z : z + 1, :], shift_rows(here, -1))
+                spot = k * nz + z
+                around += jnp.where(lane == 0, shift_lanes(y_low, -spot), shift_lanes(here, 1))
+                around += jnp.where(lane == LANES - 1, 0.0, shift_lanes(here, -1))
+                inverse = 1.0 / diag[k, z]
+                acc = jnp.where(lane == spot, shift_lanes(inverse, spot + 1), acc)
+                out[k, z] = here + around * inverse
+        last[...] = acc
+
+    return call(
+        body,
+        [residual.shape, (nx, LANES)],
+        "smooth_stage",
+        scratch=[(nz, nx, ny)],
+        free=(0, 1),
+        in_specs=vmem(6 + n_z + n_x),
+        out_specs=vmem(2),
+    )(residual, edge_diag, *below, *got_z, *got_x, after)
+
+
+def final_stage(sums, v1, v2, fg, node_shift, smooth, last, got_z, got_x, got_y, counts):
     planes, rows, _ = v1.shape
-    cz, cx = planes - 4, rows - 8
+    cz, cx, cy = planes - 4, rows - 8, LANES // 2
     nz, nx, ny = fg.shape
     n_z, n_x, n_y = len(got_z), len(got_x), len(got_y)
+    gots = n_z + n_x + n_y
 
     def body(*refs):
-        sums, v1, v2, fg, shift = refs[:5]
-        gz = refs[5 : 5 + n_z]
-        gx = refs[5 + n_z : 5 + n_z + n_x]
-        gy = refs[5 + n_z + n_x : 5 + n_z + n_x + n_y]
-        fn, down_z, down_x, down_y, dup, inter = refs[5 + n_z + n_x + n_y :]
+        sums, v1, v2, fg, shift, smooth, last = refs[:7]
+        gz = refs[7 : 7 + n_z]
+        gx = refs[7 + n_z : 7 + n_z + n_x]
+        gy = refs[7 + n_z + n_x : 7 + gots]
+        out, sol, dup, inter, small, lines, buf, sem = refs[7 + gots :]
+
+        def one_side(pick, refs, axis, size, at):
+            values = [ref[at, :] for ref in refs]
+            return pick(axis, size, values[0], values[1] if len(values) > 1 else None)
 
         def both(refs, axis, size, at):
-            values = [ref[at, :] for ref in refs]
-            second = values[1] if len(values) > 1 else None
-            return low_of(axis, size, values[0], second), high_of(axis, size, values[0], second)
+            return [one_side(pick, refs, axis, size, at) for pick in (low_of, high_of)]
 
         total = jnp.sum(sums[...], axis=0)
         lane1 = lane_ids(1)
@@ -511,18 +652,27 @@
         side = jnp.where(fine % 2 == 1, fine // 2 + 1, (fine // 2 + LANES - 1) % LANES)
         spread = jnp.where(jnp.where(target < LANES, target // 2, side) == source, 1.0, 0.0)
         for z in list(range(cz + 1)) + [planes - 1]:
-            sol = one * v1[z] + two * v2[z]
-            dup[z] = jnp.dot(sol, spread, precision=HIGHEST, preferred_element_type=F32)
-
-        z_face = slice(9 * rows, 9 * rows + nx)
-        z_low, z_high = both(gz, "gz", counts[0], z_face)
-        x_low, x_high = both(gx, "gx", counts[1], slice(112, 112 + nz))
+            sol[z] = one * v1[z] + two * v2[z]
+            dup[z] = jnp.dot(sol[z], spread, precision=HIGHEST, preferred_element_type=F32)
+
+        z_at = 9 * rows
+        z_low, z_high = both(gz, "gz", counts[0], slice(z_at, z_at + nx))
+        z_base = one_side(high_of, gz, "gz", counts[0], slice(z_at + 4 * nx, z_at + 5 * nx))
+        z_inverse = one_side(high_of, gz, "gz", counts[0], slice(z_at + 5 * nx, z_at + 6 * nx))
+        x_low, x_high = both(gx, "gx", counts[1], slice(48, 48 + nz + 1))
+        x_at = 56 + nz
+        x_base = one_side(high_of, gx, "gx", counts[1], slice(x_at + 3 * nz, x_at + 4 * nz))
+        x_inverse = one_side(high_of, gx, "gx", counts[1], slice(x_at + 4 * nz, x_at + 5 * nz))
         y_low, y_high = both(gy, "gy", counts[2], slice(0, nx))
+        y_row_low, y_row_high = both(gy, "gy", counts[2], slice(nx, nx + 1))
+        half = nx // 2
+        y_pack = one_side(high_of, gy, "gy", counts[2], slice(nx + 8, nx + 8 + half))
         lane = lane_ids(nx)
         row = row_ids(nx)
         base = 5 * planes
-        acc = jnp.zeros((nx, LANES), F32)
-        for z in range(nz):
+        tail = base + nz + 1
+
+        def spread_around(z):
             c, odd = z // 2, z % 2
             here = dup[c, :, :LANES]
             same = 3.0 * here + dup[c, :, LANES:]
@@ -530,107 +680,102 @@
             slot = z % 2
             inter[slot, pl.ds(0, cx, 2), :] = (same + shift_rows(here, 1))[:cx, :]
             inter[slot, pl.ds(1, cx, 2), :] = (same + shift_rows(here, -1))[:cx, :]
+            return inter[slot]
+
+        def edges(z, guess):
+            left = shift_lanes(y_low, -(base + z))
+            right = shift_lanes(y_high, -(base + z) - 1)
+            if guess is None:
+                around = jnp.where(row == 0, x_low[z : z + 1, :], 0.0)
+                around += jnp.where(row == nx - 1, x_high[z : z + 1, :], 0.0)
+                around += jnp.where(lane == 0, left, 0.0)
+                return around + jnp.where(lane == LANES - 1, right, 0.0)
+            around = jnp.where(row == 0, x_low[z : z + 1, :], shift_rows(guess, 1))
+            around += jnp.where(row == nx - 1, x_high[z : z + 1, :], shift_rows(guess, -1))
+            around += jnp.where(lane == 0, left, shift_lanes(guess, 1))
+            return around + jnp.where(lane == LANES - 1, right, shift_lanes(guess, -1))
+
+        def nodal(z):
+            if z == nz:
+                around = spread_around(z) + edges(z, None) + fg[nz - 1]
+                value = z_base + z_inverse * around
+                return from_above("gz", counts[0], value)
             guess = fg[z]
-            around = inter[slot]
+            around = spread_around(z) + edges(z, guess)
             around += fg[z - 1] if z > 0 else z_low
             around += fg[z + 1] if z < nz - 1 else z_high
-            around += jnp.where(row == 0, x_low[z : z + 1, :], shift_rows(guess, 1))
-            around += jnp.where(row == nx - 1, x_high[z : z + 1, :], shift_rows(guess, -1))
-            left = shift_lanes(y_low, -(base + z))
-            right = shift_lanes(y_high, -(base + z) - 1)
-            around += jnp.where(lane == 0, left, shift_lanes(guess, 1))
-            around += jnp.where(lane == LANES - 1, right, shift_lanes(guess, -1))
-            value = guess + around / (6.0 + shift[z])
-            fn[z] = value
-            if z == 0:
-                down_z[...] = value
-            down_x[z : z + 1, :] = value[:1, :]
-            acc = jnp.where(lane == z, shift_lanes(value, z), acc)
-        down_y[...] = acc
+            return guess + around / (6.0 + shift[z])
+
+        here = dup[:cz, cx, :LANES]
+        same = 3.0 * here + dup[:cz, cx, LANES:] + dup[:cz, cx - 1, :LANES]
+        small[pl.ds(0, cz, 2), :] = same + jnp.concatenate(
+            [dup[planes - 1, cx : cx + 1, :LANES], here[: cz - 1]], axis=0
+        )
+        small[pl.ds(1, cz, 2), :] = same + dup[1 : cz + 1, cx, :LANES]
+        for z in range(nz):
+            left = shift_lanes(y_row_low, -(base + z))
+            right = shift_lanes(y_row_high, -(base + z) - 1)
+            value = jnp.where(lane1 == 0, left, 0.0)
+            lines[z : z + 1, :] = jnp.where(lane1 == LANES - 1, right, value)
+        x_value = x_base + x_inverse * (fg[:, nx - 1, :] + small[...] + lines[...])
+        x_value = from_above("gx", counts[1], x_value)
+
+        lane_c = lane_ids(rows)
+        even = jnp.zeros((rows, LANES), F32)
+        odd = jnp.zeros((rows, LANES), F32)
+        own = jnp.zeros((nx, LANES), F32)
+        for z in range(nz):
+            c = z // 2
+            here = sol[c]
+            same = 3.0 * here + shift_lanes(here, 1) + sol[(c + 1 if z % 2 else c - 1) % planes]
+            even = jnp.where(lane_c == z, shift_lanes(same + shift_rows(here, 1), z - cy), even)
+            odd = jnp.where(lane_c == z, shift_lanes(same + shift_rows(here, -1), z - cy), odd)
+            own = jnp.where(lane == z, shift_lanes(fg[z], z + 1), own)
+        inter[0, pl.ds(0, cx, 2), :] = even[:cx, :]
+        inter[0, pl.ds(1, cx, 2), :] = odd[:cx, :]
+        y_base = jnp.concatenate([y_pack, shift_lanes(y_pack, -nz)], axis=0)
+        y_inverse = jnp.concatenate(
+            [shift_lanes(y_pack, -2 * nz), shift_lanes(y_pack, -3 * nz)], axis=0
+        )
+        y_value = y_base + y_inverse * (own + inter[0])
+        y_value = from_above("gy", counts[2], y_value)
+        y_fix = shift_lanes(y_high, -tail) * last[...]
+
+        def copy(z):
+            return pltpu.make_async_copy(buf.at[:, z], out.at[:, z], sem.at[z])
+
+        value = nodal(0)
+        for z in range(nz):
+            after = nodal(z + 1)
+            steps = [after, jnp.where(row == nx - 1, x_value[z : z + 1, :], shift_rows(value, -1))]
+            steps.append(
+                jnp.where(lane == LANES - 1, shift_lanes(y_value, -z - 1), shift_lanes(value, -1))
+            )
+            for k in range(3):
+                fixed = jnp.where(lane == LANES - 1, shift_lanes(y_fix, -(k * nz + z) - 1), 0.0)
+                buf[k, z] = (smooth[k, z] + fixed) + (steps[k] - value)
+            copy(z).start()
+            value = after
+        for z in range(nz):
+            copy(z).wait()
 
     return call(
         body,
-        [(nz, nx, ny), (nx, ny), (nz, ny), (nx, LANES)],
+        [smooth.shape],
         "final_stage",
-        scratch=[(planes, rows, 2 * LANES), (2, nx, LANES)],
-        in_specs=vmem(5 + n_z + n_x + n_y),
-        out_specs=vmem(4),
-    )(sums, v1, v2, fg, node_shift, *got_z, *got_x, *got_y)
-
-
-def output_stage(residual, edge_diag, fn, above, below, got_z, got_x, got_y, planes, counts):
-    _, nz, nx, ny = residual.shape
-    n_z, n_x, n_y = len(got_z), len(got_x), len(got_y)
-    rows = nx // 2 + 8
-
-    def body(*refs):
-        res, diag, fn, fz, fx, fy, lz, lx, ly = refs[:9]
-        gz = refs[9 : 9 + n_z]
-        gx = refs[9 + n_z : 9 + n_z + n_x]
-        gy = refs[9 + n_z + n_x : 9 + n_z + n_x + n_y]
-        out, s = refs[9 + n_z + n_x + n_y :]
-        k = pl.program_id(0)
-        lane = lane_ids(nx)
-        row = row_ids(nx)
-
-        def above_of(refs, axis, size, at):
-            values = [ref[at, :] for ref in refs]
-            return high_of(axis, size, values[0], values[1] if len(values) > 1 else None)
-
-        for z in range(nz):
-            s[z] = res[0, z] / diag[0, z]
-        z_low = from_below("gz", lz[k])
-        z_high = above_of(gz, "gz", counts[0], pl.ds(9 * rows + nx + k * nx, nx))
-        x_low = from_below("gx", lx[pl.ds(k * nz, nz), :])
-        x_high = above_of(gx, "gx", counts[1], pl.ds(112 + nz + k * nz, nz))
-        y_low = pltpu.roll(from_below("gy", ly[...]), (LANES - k * nz) % LANES, 1)
-        y_high = above_of(gy, "gy", counts[2], pl.ds(0, nx))
-        y_high = pltpu.roll(y_high, (2 * LANES - 5 * planes - nz - k * nz) % LANES, 1)
-        for z in range(nz):
-            here = s[z]
-            around = s[z - 1] if z > 0 else z_low
-            around += s[z + 1] if z < nz - 1 else z_high
-            around += jnp.where(row == 0, x_low[z : z + 1, :], shift_rows(here, 1))
-            around += jnp.where(row == nx - 1, x_high[z : z + 1, :], shift_rows(here, -1))
-            left = shift_lanes(y_low, -z)
-            right = shift_lanes(y_high, -z - 1)
-            around += jnp.where(lane == 0, left, shift_lanes(here, 1))
-            around += jnp.where(lane == LANES - 1, right, shift_lanes(here, -1))
-            out[0, z] = here + around / diag[0, z] - fn[z]
-
-        @pl.when(k == 0)
-        def _():
-            for z in range(nz - 1):
-                out[0, z] += fn[z + 1]
-            out[0, nz - 1] += from_above("gz", counts[0], fz[...])
-
-        @pl.when(k == 1)
-        def _():
-            face = from_above("gx", counts[1], fx[...])
-            for z in range(nz):
-                out[0, z] += jnp.where(row == nx - 1, face[z : z + 1, :], shift_rows(fn[z], -1))
-
-        @pl.when(k == 2)
-        def _():
-            face = from_above("gy", counts[2], fy[...])
-            for z in range(nz):
-                moved = shift_lanes(face, -z - 1)
-                out[0, z] += jnp.where(lane == LANES - 1, moved, shift_lanes(fn[z], -1))
-
-    spec = pl.BlockSpec((1, nz, nx, ny), lambda k: (k, 0, 0, 0))
-    args = (fn, *above, *below, *got_z, *got_x, *got_y)
-    whole = [pl.BlockSpec(a.shape, lambda k, n=a.ndim: (0,) * n) for a in args]
-    return call(
-        body,
-        [residual.shape],
-        "output_stage",
-        scratch=[(nz, nx, ny)],
-        far=(0, 1),
+        scratch=[
+            (planes, rows, LANES),
+            (planes, rows, 2 * LANES),
+            (2, nx, LANES),
+            (nz, LANES),
+            (nz, LANES),
+            smooth.shape,
+            pltpu.SemaphoreType.DMA((nz,)),
+        ],
         far_out=True,
-        grid=(3,),
-        in_specs=[spec, spec] + whole,
-        out_specs=[spec],
-    )(residual, edge_diag, *args)[0]
+        in_specs=vmem(7 + gots),
+        out_specs=[pl.BlockSpec(memory_space=pltpu.HBM)],
+    )(sums, v1, v2, fg, node_shift, smooth, last, *got_z, *got_x, *got_y)[0]
 
 
 def local(residual, edge_diag, node_shift, coarse_shift):
@@ -641,19 +786,17 @@
     below = (ring(up_z, "gz", 1), ring(up_x, "gx", 1), ring(up_y, "gy", 1))
     fg, rhs, xb, yb, w, *send = nodal_stage(part, node_shift, coarse_shift, *below, low_z, counts[0])
     got_z = swap(send, "gz")
-    rhs, yb, w, *send = x_stage(got_z, rhs, xb, yb, w, fg, low_x, counts[0], counts[1])
+    rhs, yb, w, *send = x_stage(
+        got_z, rhs, xb, yb, w, fg, low_x, node_shift, counts[0], counts[1]
+    )
     got_x = swap(send, "gx")
-    planes = rhs.shape[0]
-    rhs, w, *send = y_stage(got_x, rhs, yb, w, fg, low_y, counts[1], counts[2])
+    rhs, w, *send = y_stage(got_z, got_x, rhs, yb, w, fg, low_y, node_shift, counts)
     got_y = swap(send, "gy")
-    v1, v2, sums = coarse_stage(got_y, rhs, w, counts[2], devices)
+    smooth, last = smooth_stage(residual, edge_diag, below, got_z, got_x, w, counts)
+    v1, v2, sums = coarse_stage(got_y, rhs, w, last, counts[2], devices)
     sums = lax.all_to_all(sums, ("gx", "gy", "gz"), 0, 0)
-    fn, down_z, down_x, down_y = final_stage(
-        sums, v1, v2, fg, node_shift, got_z, got_x, got_y, counts
-    )
-    above = (ring(down_z, "gz", -1), ring(down_x, "gx", -1), ring(down_y, "gy", -1))
-    return output_stage(
-        residual, edge_diag, fn, above, below, got_z, got_x, got_y, planes, counts
+    return final_stage(
+        sums, v1, v2, fg, node_shift, smooth, last, got_z, got_x, got_y, counts
     )
 
 

time: 52.1 us -> 45.7 us (0.88)
  waiting for transfers between devices: 15.7 us -> 10.7 us
  local copies, waits for them, and re-layouts: 2.83 us -> 0.02 us
  Pallas kernels: 9.92 us -> 12.4 us
  starting transfers between devices: 13.2 us -> 11.9 us
    ppermute x6 -> x3, waiting for transfers between devices: 6.34 us -> 3.24 us  [ring(): lax.ppermute(value, axis, [(i, (i + step) % size) for i in range(size)])]
    unnamed x12 -> x8, local copies, waits for them, and re-layouts: 2.83 us -> 0.02 us
    pallas_call x7, Pallas kernels: 9.92 us -> 12.4 us  [apply(): run(*(a if i in free else pltpu.with_memory_space_constraint(a, space) fo...]
    ppermute x2, waiting for transfers between devices: 5.75 us -> 4.21 us  [swap(): out.append(lax.ppermute(values[1], axis, odd))]
    ppermute x6 -> x3, starting transfers between devices: 5.93 us -> 4.68 us  [ring(): lax.ppermute(value, axis, [(i, (i + step) % size) for i in range(size)])]
  transfers between devices with their start and end apart: 11 -> 8, of which waited for: 6 -> 5; matrix products, arithmetic and copies ran while one was open for 0% -> 0% of each run, Pallas kernels for 0% -> 4%
where the time goes in v4:
time: 45.7 us; the launch traced here: 45.5 us
  Pallas kernels  12.4 us (27%)
  starting transfers between devices  11.9 us (26%)
  waiting for transfers between devices  10.7 us (23%)
  blocking collectives  10.5 us (23%)
    pallas_call x7, Pallas kernels, apply(): run(*(a if i in free else pltpu.with_memory_space_constraint(a, space) fo...  12.4 us
    all_to_all x1, blocking collectives, local(): sums = lax.all_to_all(sums, ('gx', 'gy', 'gz'), 0, 0)  10.5 us
    ppermute x3, starting transfers between devices, ring(): lax.ppermute(value, axis, [(i, (i + step) % size) for i in range(size)])  4.68 us
    ppermute x2, starting transfers between devices, swap(): out.append(lax.ppermute(values[1], axis, odd))  4.53 us
    ppermute x2, waiting for transfers between devices, swap(): out.append(lax.ppermute(values[1], axis, odd))  4.21 us
    ppermute x3, waiting for transfers between devices, ring(): lax.ppermute(value, axis, [(i, (i + step) % size) for i in range(size)])  3.24 us
    ppermute x3, waiting for transfers between devices, swap(): out = [lax.ppermute(values[0], axis, even)]  3.21 us
    ppermute x3, starting transfers between devices, swap(): out = [lax.ppermute(values[0], axis, even)]  2.7 us
  transfers between devices with their start and end apart: 8, of which 5 were waited for; matrix products, arithmetic and copies ran while one was open for 0% of the time, Pallas kernels for 4%

profile of v4, /device:TPU:0, one launch (start us, length us, event | category | flops | bytes accessed | tf_op | source)
XLA Modules:
  0.0 45.5 jit_solution(4271732328811373601)
XLA Ops:
  0.0 3.6 %edge_stage.1 = (f32[16,64,128]{2,1,0:T(8,128)S(1)}, f32[3,64,128]{2,1,0:T(8,128)S(1)}, f32[48,128]{1,0:T(8,128)S(1)}, f32[64,128]{1,0:T(8,128)S(1)}, f32[3,64,1...) custom-call(f32[3,16,64,128]{3,2,1,0:T(8,128)} %refs_0_.1, f32[3,16,64,128]{3,2,1,0:T(8,128)} %refs_1_.1), custom_call_target="tpu_custom_call" | custom-call | tf_op jit(solution)/shard_map/edge_stage/pallas_call | solution.py:99
  3.6 0.6 %collective-permute-start = (f32[3,64,128]{2,1,0:T(8,128)S(1)}, f32[3,64,128]{2,1,0:T(8,128)S(1)}, u32[]{:S(2)}, u32[]{:S(2)}) collective-permute-start(f32[3,64,128]{2,1,0:T(8,128)S(1)} %get-tuple-element.33), channel_id=1, source_target_pairs={{0,1},{1,0},{2,3},{3,2},{4,5},{5,4},{6,7},{7,6},{8,9},{9,8},{10,11... | collective-permute-start | bytes 294920 | tf_op jit(solution)/shard_map/ppermute | solution.py:57
  4.2 2.6 %collective-permute-start.2 = (f32[64,128]{1,0:T(8,128)S(1)}, f32[64,128]{1,0:T(8,128)S(1)}, u32[]{:S(2)}, u32[]{:S(2)}) collective-permute-start(f32[64,128]{1,0:T(8,128)S(1)} %get-tuple-element.35), channel_id=1, source_target_pairs={{0,2},{2,4},{4,6},{6,0},{1,3},{3,5},{5,7},{7,1},{8,10},{10,12},{12... | collective-permute-start | bytes 98312 | tf_op jit(solution)/shard_map/ppermute | solution.py:57
  6.8 1.5 %collective-permute-start.1 = (f32[48,128]{1,0:T(8,128)S(1)}, f32[48,128]{1,0:T(8,128)S(1)}, u32[]{:S(2)}, u32[]{:S(2)}) collective-permute-start(f32[48,128]{1,0:T(8,128)S(1)} %get-tuple-element.34), channel_id=1, source_target_pairs={{0,8},{8,16},{16,24},{24,0},{1,9},{9,17},{17,25},{25,1},{2,10},{10... | collective-permute-start | bytes 73736 | tf_op jit(solution)/shard_map/ppermute | solution.py:57
  8.3 3.2 %collective-permute-done.1.gx.refs_3_ = f32[48,128]{1,0:T(8,128)S(1)} collective-permute-done((f32[48,128]{1,0:T(8,128)S(1)}, f32[48,128]{1,0:T(8,128)S(1)}, u32[]{:S(2)}, u32[]{:S(2)}) %collective-permute-start.1) | collective-permute-done | bytes 24608 | tf_op jit(solution)/shard_map/ppermute | solution.py:57
  11.5 0.0 collective-permute-done.2.gy.refs_4_
  11.5 0.0 collective-permute-done.gz.refs_2_
  11.5 1.0 %nodal_stage.1 = (f32[16,64,128]{2,1,0:T(8,128)S(1)}, f32[12,40,128]{2,1,0:T(8,128)S(1)}, f32[8,40,128]{2,1,0:T(8,128)S(1)}, f32[8,40,128]{2,1,0:T(8,128)S(1)}, ...) custom-call(f32[16,64,128]{2,1,0:T(8,128)S(1)} %get-tuple-element.32.part, f32[16,64,128]{2,1,0:T(8,128)S(1)} %copy-done, ...), custom_call_target="tpu_custom_call" | custom-call | tf_op jit(solution)/shard_map/nodal_stage/pallas_call | solution.py:99
  12.5 0.1 collective-permute-start.3
  12.6 1.7 %collective-permute-done.3.refs_0_.refs_5_.refs_7_ = f32[744,128]{1,0:T(8,128)S(1)} collective-permute-done((f32[744,128]{1,0:T(8,128)S(1)}, f32[744,128]{1,0:T(8,128)S(1)}, u32[]{:S(2)}, u32[]{:S(2)}) %collective-permute-start.3) | collective-permute-done | bytes 380960 | tf_op jit(solution)/shard_map/ppermute | solution.py:63
  14.3 0.2 x_stage.1
  14.5 0.0 copy-start.1
  14.5 1.0 %collective-permute-start.4 = (f32[152,128]{1,0:T(8,128)S(1)}, f32[152,128]{1,0:T(8,128)S(1)}, u32[]{:S(2)}, u32[]{:S(2)}) collective-permute-start(f32[152,128]{1,0:T(8,128)S(1)} %get-tuple-element.44), channel_id=1, source_target_pairs={{0,8},{8,0},{16,24},{24,16},{1,9},{9,1},{17,25},{25,17},{2,10},{10... | collective-permute-start | bytes 233480 | tf_op jit(solution)/shard_map/ppermute | solution.py:63
  15.4 2.1 %collective-permute-start.5 = (f32[152,128]{1,0:T(8,128)S(1)}, f32[152,128]{1,0:T(8,128)S(1)}, u32[]{:S(2)}, u32[]{:S(2)}) collective-permute-start(f32[152,128]{1,0:T(8,128)S(1)} %get-tuple-element.45), channel_id=1, source_target_pairs={{0,24},{8,16},{16,8},{24,0},{1,25},{9,17},{17,9},{25,1},{2,26},{10... | collective-permute-start | bytes 233480 | tf_op jit(solution)/shard_map/ppermute | solution.py:66
  17.5 1.5 %collective-permute-done.4.refs_1_.refs_6_.refs_8_ = f32[152,128]{1,0:T(8,128)S(1)} collective-permute-done((f32[152,128]{1,0:T(8,128)S(1)}, f32[152,128]{1,0:T(8,128)S(1)}, u32[]{:S(2)}, u32[]{:S(2)}) %collective-permute-start.4) | collective-permute-done | bytes 77856 | tf_op jit(solution)/shard_map/ppermute | solution.py:63
  19.0 2.5 %collective-permute-done.5.refs_2_.refs_7_.refs_9_ = f32[152,128]{1,0:T(8,128)S(1)} collective-permute-done((f32[152,128]{1,0:T(8,128)S(1)}, f32[152,128]{1,0:T(8,128)S(1)}, u32[]{:S(2)}, u32[]{:S(2)}) %collective-permute-start.5) | collective-permute-done | bytes 77856 | tf_op jit(solution)/shard_map/ppermute | solution.py:66
  21.6 1.9 %y_stage.1 = (f32[12,40,128]{2,1,0:T(8,128)S(1)}, f32[12,40,128]{2,1,0:T(8,128)S(1)}, f32[104,128]{1,0:T(8,128)S(1)}, f32[104,128]{1,0:T(8,128)S(1)}) custom-call(f32[744,128]{1,0:T(8,128)S(1)} %collective-permute-done.3.refs_0_.refs_5_.refs_7_, f32[152,128]{1,0:T(8,128)S(1)} %collective-permute-done.4.refs_1_.refs_6_.refs_8_, ...), custom_call_target="tpu_custom_call" | custom-call | tf_op jit(solution)/shard_map/y_stage/pallas_call | solution.py:99
  23.4 1.7 %collective-permute-start.6 = (f32[104,128]{1,0:T(8,128)S(1)}, f32[104,128]{1,0:T(8,128)S(1)}, u32[]{:S(2)}, u32[]{:S(2)}) collective-permute-start(f32[104,128]{1,0:T(8,128)S(1)} %get-tuple-element.50), channel_id=1, source_target_pairs={{0,2},{2,0},{4,6},{6,4},{1,3},{3,1},{5,7},{7,5},{8,10},{10,8},{12,... | collective-permute-start | bytes 159752 | tf_op jit(solution)/shard_map/ppermute | solution.py:63
  25.1 2.4 %collective-permute-start.7 = (f32[104,128]{1,0:T(8,128)S(1)}, f32[104,128]{1,0:T(8,128)S(1)}, u32[]{:S(2)}, u32[]{:S(2)}) collective-permute-start(f32[104,128]{1,0:T(8,128)S(1)} %get-tuple-element.51), channel_id=1, source_target_pairs={{0,6},{2,4},{4,2},{6,0},{1,7},{3,5},{5,3},{7,1},{8,14},{10,12},{12... | collective-permute-start | bytes 159752 | tf_op jit(solution)/shard_map/ppermute | solution.py:66
  27.6 1.8 %smooth_stage.1 = (f32[3,16,64,128]{3,2,1,0:T(8,128)S(1)}, f32[64,128]{1,0:T(8,128)S(1)}) custom-call(f32[3,16,64,128]{3,2,1,0:T(8,128)S(1)} %copy-done.1, f32[3,16,64,128]{3,2,1,0:T(8,128)S(1)} %copy-done.2, f32[3,64,128]{2,1,0:T(8,128)S(1)} %collective-permute-done.gz.refs_2_, f32[48,128]{1,0:T(8,128)S(1)} %collective-permute-done.1.gx.refs_3_, ...), custom_call_target="tpu_custom_call" | custom-call | tf_op jit(solution)/shard_map/smooth_stage/pallas_call | solution.py:99
  29.4 1.7 %collective-permute-done.7.refs_1_.refs_11_ = f32[104,128]{1,0:T(8,128)S(1)} collective-permute-done((f32[104,128]{1,0:T(8,128)S(1)}, f32[104,128]{1,0:T(8,128)S(1)}, u32[]{:S(2)}, u32[]{:S(2)}) %collective-permute-start.7) | collective-permute-done | bytes 53280 | tf_op jit(solution)/shard_map/ppermute | solution.py:66
  31.0 1.0 %coarse_stage.1 = (f32[12,40,128]{2,1,0:T(8,128)S(1)}, f32[12,40,128]{2,1,0:T(8,128)S(1)}, f32[32,1,128]{2,1,0:T(1,128)S(1)}) custom-call(f32[104,128]{1,0:T(8,128)S(1)} %collective-permute-done.6.refs_0_.refs_10_, f32[104,128]{1,0:T(8,128)S(1)} %collective-permute-done.7.refs_1_.refs_11_, f32[12,40,128]{2,1,0:T(8,128)S(1)} %get-tuple-element.52.refs_2_, ...), custom_call_target="tpu_custom_call" | custom-call | tf_op jit(solution)/shard_map/coarse_stage/pallas_call | solution.py:99
  32.0 10.5 %all_to_all.5.refs_0_ = f32[32,1,128]{2,1,0:T(1,128)S(1)} all-to-all(f32[32,1,128]{2,1,0:T(1,128)S(1)} %get-tuple-element.55), channel_id=1, replica_groups=mesh['gx'=4,'gy'=4,'gz'=2] {'gx','gy','gz'}, dimensions={0} | all-to-all | bytes 32768 | tf_op jit(solution)/shard_map/all_to_all | solution.py:797
  42.5 3.0 %final_stage.1 = f32[3,16,64,128]{3,2,1,0:T(8,128)} custom-call(f32[32,1,128]{2,1,0:T(1,128)S(1)} %all_to_all.5.refs_0_, f32[12,40,128]{2,1,0:T(8,128)S(1)} %get-tuple-element.56.refs_1_, f32[12,40,128]{2,1,0:T(8,128)S(1)} %get-tuple-element.57.refs_2_, f32[16,64,128]{2,1,0:T(8,128)S(1)} %get-tuple-element.42.refs_5_.refs_6_.refs_3_, ...), custom_call_target="tpu_custom_call" | custom-call | tf_op jit(solution)/shard_map/final_stage/pallas_call | solution.py:99
  (8 shorter events, 0.0 us)
Async XLA Ops:
  0.0 11.5 %copy-start = (f32[16,64,128]{2,1,0:T(8,128)S(1)}, f32[16,64,128]{2,1,0:T(8,128)}, u32[]{:S(2)}) copy-start(f32[16,64,128]{2,1,0:T(8,128)} %refs_4_.1) | copy-start | bytes 1572868
  0.0 11.5 %copy-start.3 = (f32[8,32,64]{2,1,0:T(8,128)S(1)}, f32[8,32,64]{2,1,0:T(8,128)}, u32[]{:S(2)}) copy-start(f32[8,32,64]{2,1,0:T(8,128)} %coarse.1) | copy-start | bytes 196612
  3.6 7.9 %collective-permute-start = (f32[3,64,128]{2,1,0:T(8,128)S(1)}, f32[3,64,128]{2,1,0:T(8,128)S(1)}, u32[]{:S(2)}, u32[]{:S(2)}) collective-permute-start(f32[3,64,128]{2,1,0:T(8,128)S(1)} %get-tuple-element.33), channel_id=1, source_target_pairs={{0,1},{1,0},{2,3},{3,2},{4,5},{5,4},{6,7},{7,6},{8,9},{9,8},{10,11... | collective-permute-start | bytes 294920 | tf_op jit(solution)/shard_map/ppermute | solution.py:57
  4.2 7.4 %collective-permute-start.2 = (f32[64,128]{1,0:T(8,128)S(1)}, f32[64,128]{1,0:T(8,128)S(1)}, u32[]{:S(2)}, u32[]{:S(2)}) collective-permute-start(f32[64,128]{1,0:T(8,128)S(1)} %get-tuple-element.35), channel_id=1, source_target_pairs={{0,2},{2,4},{4,6},{6,0},{1,3},{3,5},{5,7},{7,1},{8,10},{10,12},{12... | collective-permute-start | bytes 98312 | tf_op jit(solution)/shard_map/ppermute | solution.py:57
  6.8 4.7 %collective-permute-start.1 = (f32[48,128]{1,0:T(8,128)S(1)}, f32[48,128]{1,0:T(8,128)S(1)}, u32[]{:S(2)}, u32[]{:S(2)}) collective-permute-start(f32[48,128]{1,0:T(8,128)S(1)} %get-tuple-element.34), channel_id=1, source_target_pairs={{0,8},{8,16},{16,24},{24,0},{1,9},{9,17},{17,25},{25,1},{2,10},{10... | collective-permute-start | bytes 73736 | tf_op jit(solution)/shard_map/ppermute | solution.py:57
  12.5 1.8 %collective-permute-start.3 = (f32[744,128]{1,0:T(8,128)S(1)}, f32[744,128]{1,0:T(8,128)S(1)}, u32[]{:S(2)}, u32[]{:S(2)}) collective-permute-start(f32[744,128]{1,0:T(8,128)S(1)} %get-tuple-element.37), channel_id=1, source_target_pairs={{0,1},{1,0},{2,3},{3,2},{4,5},{5,4},{6,7},{7,6},{8,9},{9,8},{10,11... | collective-permute-start | bytes 1142792 | tf_op jit(solution)/shard_map/ppermute | solution.py:63
  14.3 13.3 %copy-start.2 = (f32[3,16,64,128]{3,2,1,0:T(8,128)S(1)}, f32[3,16,64,128]{3,2,1,0:T(8,128)}, u32[]{:S(2)}) copy-start(f32[3,16,64,128]{3,2,1,0:T(8,128)} %refs_1_.1) | copy-start | bytes 4718596
  14.5 13.1 %copy-start.1 = (f32[3,16,64,128]{3,2,1,0:T(8,128)S(1)}, f32[3,16,64,128]{3,2,1,0:T(8,128)}, u32[]{:S(2)}) copy-start(f32[3,16,64,128]{3,2,1,0:T(8,128)} %refs_0_.1) | copy-start | bytes 4718596
  14.5 4.6 %collective-permute-start.4 = (f32[152,128]{1,0:T(8,128)S(1)}, f32[152,128]{1,0:T(8,128)S(1)}, u32[]{:S(2)}, u32[]{:S(2)}) collective-permute-start(f32[152,128]{1,0:T(8,128)S(1)} %get-tuple-element.44), channel_id=1, source_target_pairs={{0,8},{8,0},{16,24},{24,16},{1,9},{9,1},{17,25},{25,17},{2,10},{10... | collective-permute-start | bytes 233480 | tf_op jit(solution)/shard_map/ppermute | solution.py:63
  15.4 6.1 %collective-permute-start.5 = (f32[152,128]{1,0:T(8,128)S(1)}, f32[152,128]{1,0:T(8,128)S(1)}, u32[]{:S(2)}, u32[]{:S(2)}) collective-permute-start(f32[152,128]{1,0:T(8,128)S(1)} %get-tuple-element.45), channel_id=1, source_target_pairs={{0,24},{8,16},{16,8},{24,0},{1,25},{9,17},{17,9},{25,1},{2,26},{10... | collective-permute-start | bytes 233480 | tf_op jit(solution)/shard_map/ppermute | solution.py:66
  23.4 5.9 %collective-permute-start.6 = (f32[104,128]{1,0:T(8,128)S(1)}, f32[104,128]{1,0:T(8,128)S(1)}, u32[]{:S(2)}, u32[]{:S(2)}) collective-permute-start(f32[104,128]{1,0:T(8,128)S(1)} %get-tuple-element.50), channel_id=1, source_target_pairs={{0,2},{2,0},{4,6},{6,4},{1,3},{3,1},{5,7},{7,5},{8,10},{10,8},{12,... | collective-permute-start | bytes 159752 | tf_op jit(solution)/shard_map/ppermute | solution.py:63
  25.1 5.9 %collective-permute-start.7 = (f32[104,128]{1,0:T(8,128)S(1)}, f32[104,128]{1,0:T(8,128)S(1)}, u32[]{:S(2)}, u32[]{:S(2)}) collective-permute-start(f32[104,128]{1,0:T(8,128)S(1)} %get-tuple-element.51), channel_id=1, source_target_pairs={{0,6},{2,4},{4,2},{6,0},{1,7},{3,5},{5,3},{7,1},{8,14},{10,12},{12... | collective-permute-start | bytes 159752 | tf_op jit(solution)/shard_map/ppermute | solution.py:66

commit v5 on v4

--- a/solution.py
+++ b/solution.py
@@ -4,6 +4,7 @@
 from jax.experimental import pallas as pl
 from jax.experimental.pallas import tpu as pltpu
 from jax.sharding import PartitionSpec as P
+
 
 F32 = jnp.float32
 HIGHEST = lax.Precision.HIGHEST
@@ -83,13 +84,12 @@
             up(refs[1])
 
 
-def call(body, outs, name, scratch=(), far=(), free=(), far_out=False, **kwargs):
+def call(body, outs, scratch=(), far=(), free=(), far_out=False, **kwargs):
     kind = jax.ShapeDtypeStruct if far_out else pltpu.VMEM
     run = pl.pallas_call(
         body,
         out_shape=[kind(shape, F32) for shape in outs],
         scratch_shapes=[pltpu.VMEM(s, F32) if isinstance(s, tuple) else s for s in scratch],
-        name=name,
         compiler_params=pltpu.CompilerParams(vmem_limit_bytes=12 * 2**20),
         **kwargs,
     )
@@ -167,7 +167,6 @@
     return call(
         body,
         [(nz, nx, ny)] + faces,
-        "edge_stage",
         scratch=[(nx, ny)],
         far=(0, 1),
         grid=(steps,),
@@ -278,25 +277,25 @@
     return call(
         body,
         [(nz, nx, ny), (cz + 4, rows, LANES), coarse, coarse, coarse] + [send] * sends,
-        "nodal_stage",
         scratch=[(2, nx, ny), coarse, coarse, coarse, coarse, coarse],
         in_specs=vmem(7),
         out_specs=vmem(5 + sends),
     )(part, node_shift, coarse_shift, got_z, got_x, got_y, low_z)
 
 
-def x_stage(got, rhs, xb, yb, w, fg, low_x, node_shift, z_count, x_count):
+def x_stage(got, rhs, xb, yb, w, fg, z_count, x_count):
     planes, rows, _ = rhs.shape
     cz, cx = planes - 4, rows - 8
     nz, nx, ny = fg.shape
     cy = ny // 2
     sends = 1 if x_count == 2 else 2
     gots = len(got)
+    size = -(-(3 * planes + nz + 1) // 8) * 8
 
     def body(*refs):
         got = refs[:gots]
-        rhs, xb, yb, w, fg, low_x, shift, rhs2, yb2, w2 = refs[gots : gots + 10]
-        out, (xb2,) = refs[gots + 10 : gots + 10 + sends], refs[gots + 10 + sends :]
+        rhs, xb, yb, w, fg, rhs2, yb2, w2 = refs[gots : gots + 8]
+        out, (xb2,) = refs[gots + 8 : gots + 8 + sends], refs[gots + 8 + sends :]
 
         def take_at(pick, at):
             values = [ref[at, :] for ref in got]
@@ -332,62 +331,113 @@
             third = jnp.where(lane == cy + 1, shift_lanes(edge, cy + 1), third)
             third = jnp.where(lane == LANES - 2, shift_lanes(edge, cy - 1), third)
             for i, value in enumerate((first, second, third)):
-                ref[i * 16 : i * 16 + planes, :] = value
-                ref[i * 16 + planes : i * 16 + 16, :] = jnp.zeros((16 - planes, LANES), F32)
-            ref[48 : 48 + nz, :] = fg[:, fine, :]
+                ref[i * planes : (i + 1) * planes, :] = value
+            ref[3 * planes : 3 * planes + nz, :] = fg[:, fine, :]
             at = 9 * rows + fine
-            ref[48 + nz : 49 + nz, :] = take_at(high_of, slice(at, at + 1))
-            ref[49 + nz : 56 + nz, :] = jnp.zeros((7, LANES), F32)
-
-        tail = 56 + nz
+            last = 3 * planes + nz
+            ref[last : last + 1, :] = take_at(high_of, slice(at, at + 1))
+            ref[last + 1 :, :] = jnp.zeros((size - last - 1, LANES), F32)
 
         def up(ref):
             fill(ref, cx - 1, cx - 2, nx - 1)
-            ref[tail : tail + 5 * nz, :] = jnp.zeros((5 * nz, LANES), F32)
 
         def down(ref):
             fill(ref, 0, 1, 0)
-            ref[tail : tail + 3 * nz, :] = low_x[...]
-            here = fg[:, 0, :]
-            lane_z = lane_ids(nz)
-            row_z = row_ids(nz)
-            at = 9 * rows
-            below = take_at(low_of, slice(at, at + 1))
-            above = take_at(high_of, slice(at, at + 1))
-            around = fg[:, 1, :] + jnp.where(row_z == 0, below, shift_rows(here, 1))
-            around += jnp.where(row_z == nz - 1, above, shift_rows(here, -1))
-            around += jnp.where(lane_z == 0, 0.0, shift_lanes(here, 1))
-            around += jnp.where(lane_z == ny - 1, 0.0, shift_lanes(here, -1))
-            inverse = 1.0 / (6.0 + shift[:, 0, :])
-            ref[tail + 3 * nz : tail + 4 * nz, :] = here + inverse * around
-            ref[tail + 4 * nz : tail + 5 * nz, :] = inverse
 
         write_sides("gx", out, up, down)
 
     whole = (planes, rows, LANES)
     return call(
         body,
-        [whole, whole, whole] + [(56 + 6 * nz, LANES)] * sends,
-        "x_stage",
+        [whole, whole, whole] + [(size, LANES)] * sends,
         scratch=[whole],
-        in_specs=vmem(gots + 7),
+        in_specs=vmem(gots + 5),
         out_specs=vmem(3 + sends),
-    )(*got, rhs, xb, yb, w, fg, low_x, node_shift)
-
-
-def y_stage(got_z, got, rhs, yb, w, fg, low_y, node_shift, counts):
+    )(*got, rhs, xb, yb, w, fg)
+
+
+def x_tail(got, fg, node_shift, low_x, after, z_count):
+    nz, nx, ny = fg.shape
+    z_at = 9 * (nx // 2 + 8)
+    gots = len(got)
+
+    def body(*refs):
+        got = refs[:gots]
+        fg, shift, low_x, _, out = refs[gots:]
+        lane = lane_ids(nz)
+        row = row_ids(nz)
+
+        def z_row(pick):
+            values = [ref[z_at : z_at + 1, :] for ref in got]
+            return pick("gz", z_count, values[0], values[1] if gots > 1 else None)
+
+        here = fg[:, 0, :]
+        around = fg[:, 1, :] + jnp.where(row == 0, z_row(low_of), shift_rows(here, 1))
+        around += jnp.where(row == nz - 1, z_row(high_of), shift_rows(here, -1))
+        around += jnp.where(lane == 0, 0.0, shift_lanes(here, 1))
+        around += jnp.where(lane == ny - 1, 0.0, shift_lanes(here, -1))
+        inverse = 1.0 / (6.0 + shift[:, 0, :])
+        out[: 3 * nz, :] = low_x[...]
+        out[3 * nz : 4 * nz, :] = here + inverse * around
+        out[4 * nz :, :] = inverse
+
+    return call(
+        body, [(5 * nz, LANES)], in_specs=vmem(gots + 4), out_specs=vmem(1)
+    )(*got, fg, node_shift, low_x, after)[0]
+
+
+def part_stage(got, fg, node_shift, after, z_count):
+    nz, nx, ny = fg.shape
+    z_at = 9 * (nx // 2 + 8)
+    gots = len(got)
+
+    def body(*refs):
+        got = refs[:gots]
+        fg, shift, _, part, inv = refs[gots:]
+        lane = lane_ids(nx)
+        row = row_ids(nx)
+
+        def z_face(pick):
+            values = [ref[z_at : z_at + nx, :] for ref in got]
+            return pick("gz", z_count, values[0], values[1] if gots > 1 else None)
+
+        for z in range(nz):
+            guess = fg[z]
+            around = fg[z - 1] if z > 0 else z_face(low_of)
+            around += fg[z + 1] if z < nz - 1 else z_face(high_of)
+            around += jnp.where(row == 0, 0.0, shift_rows(guess, 1))
+            around += jnp.where(row == nx - 1, 0.0, shift_rows(guess, -1))
+            around += jnp.where(lane == 0, 0.0, shift_lanes(guess, 1))
+            around += jnp.where(lane == ny - 1, 0.0, shift_lanes(guess, -1))
+            inverse = 1.0 / (6.0 + shift[z])
+            inv[z] = inverse
+            part[z] = guess + inverse * around
+
+    return call(
+        body, [fg.shape, fg.shape], in_specs=vmem(gots + 3), out_specs=vmem(2)
+    )(*got, fg, node_shift, after)
+
+
+def line(source, lane, fine, at):
+    acc = jnp.zeros(lane.shape, F32)
+    for z in range(source.shape[0]):
+        moved = jnp.broadcast_to(source[z : z + 1, :], lane.shape)
+        acc = jnp.where(lane == at + z, shift_lanes(moved, at + z - fine), acc)
+    return acc
+
+
+def y_stage(got, rhs, yb, w, early, x_count, y_count):
     planes, rows, _ = rhs.shape
     cx = rows - 8
-    nz, nx, ny = fg.shape
-    cy = ny // 2
-    z_count, x_count, y_count = counts
+    nx, cy = 2 * cx, LANES // 2
+    nz, half = 2 * (planes - 4), nx // 2
     sends = 1 if y_count == 2 else 2
-    n_z, gots = len(got_z), len(got)
+    gots = len(got)
 
     def body(*refs):
-        gz, got = refs[:n_z], refs[n_z : n_z + gots]
-        rhs, yb, w, fg, low_y, shift, rhs3, w3 = refs[n_z + gots : n_z + gots + 8]
-        rest = refs[n_z + gots + 8 :]
+        got = refs[:gots]
+        rhs, yb, w, up_, down_, part, inv, _, _, rhs3, w3 = refs[gots : gots + 11]
+        rest = refs[gots + 11 :]
         out, (yb3, add) = rest[:sends], rest[sends:]
         lane_p = lane_ids(planes)
 
@@ -396,11 +446,7 @@
             return pick("gx", x_count, values[0], values[1] if gots > 1 else None)
 
         def take(pick, i):
-            return take_at(pick, slice(i * 16, i * 16 + planes))
-
-        def z_face(pick):
-            values = [ref[9 * rows : 9 * rows + nx, :] for ref in gz]
-            return pick("gz", z_count, values[0], values[1] if n_z > 1 else None)
+            return take_at(pick, slice(i * planes, (i + 1) * planes))
 
         add[...] = jnp.zeros_like(add)
         for c in range(planes):
@@ -426,59 +472,32 @@
             rhs3[c] = rhs[c] + add[c]
 
         lane_c = lane_ids(rows)
-        lane = lane_ids(nx)
-        row = row_ids(nx)
         lane8 = lane_ids(8)
         base = 5 * planes
-        above = z_face(high_of)
-        below = z_face(low_of)
-        x_high = take_at(high_of, slice(48, 48 + nz))
-        x_low = take_at(low_of, slice(48, 48 + nz))
-
-        def line(source, fine, at):
-            acc = jnp.zeros((8, LANES), F32)
-            for z in range(nz):
-                moved = jnp.broadcast_to(source[z : z + 1, :], (8, LANES))
-                acc = jnp.where(lane8 == at + z, shift_lanes(moved, at + z - fine), acc)
-            return acc
-
-        def fill(ref, near, far, fine, tail):
+        x_face = slice(3 * planes, 3 * planes + nz)
+        x_high = take_at(high_of, x_face)
+
+        def fill(ref, near, far, fine, early):
             acc = jnp.zeros((rows, LANES), F32)
             jobs = ((rhs3, near), (rhs3, far), (w3, near), (w3, far), (yb3, near))
             for i, (field, at) in enumerate(jobs):
                 for z in range(planes):
                     spot = i * planes + z
                     acc = jnp.where(lane_c == spot, shift_lanes(field[z], spot - at), acc)
-            acc = plane(acc, nx)
-            for z in range(nz):
-                acc = jnp.where(lane == base + z, shift_lanes(fg[z], base + z - fine), acc)
-            acc = jnp.where(lane == base + nz, shift_lanes(above, base + nz - fine), acc)
-            at = base + nz + 1
-            if tail is not None:
-                moved = shift_lanes(tail, at)
-                acc = jnp.where((lane >= at) & (lane < at + 3 * nz), moved, acc)
-            ref[:nx, :] = acc
-            ref[nx : nx + 8, :] = line(x_high, fine, base)
-            return acc
+            ref[:nx, :] = plane(acc, nx) + early[...]
+            ref[nx : nx + 8, :] = line(x_high, lane8, fine, base)
 
         def up(ref):
-            fill(ref, cy - 1, cy - 2, ny - 1, None)
-            ref[nx + 8 :, :] = jnp.zeros((nx // 2, LANES), F32)
+            fill(ref, cy - 1, cy - 2, 2 * cy - 1, up_)
+            ref[nx + 8 :, :] = jnp.zeros((half, LANES), F32)
 
         def down(ref):
-            acc = fill(ref, 0, 1, 0, low_y[...])
-            here = jnp.where(lane < nz + 1, shift_lanes(acc, -base), 0.0)
-            here = jnp.where(lane == LANES - 1, shift_lanes(below, -1), here)
-            around = shift_lanes(here, 1) + shift_lanes(here, -1)
-            around += jnp.where(row == 0, line(x_low, 0, 0)[:1, :], shift_rows(here, 1))
-            around += jnp.where(row == nx - 1, line(x_high, 0, 0)[:1, :], shift_rows(here, -1))
-            inverse = jnp.ones((nx, LANES), F32)
-            for z in range(nz):
-                inverse = jnp.where(lane == z, shift_lanes(6.0 + shift[z], z), inverse)
-                around += jnp.where(lane == z, shift_lanes(fg[z], z - 1), 0.0)
-            inverse = 1.0 / inverse
-            value = here + inverse * around
-            half = nx // 2
+            fill(ref, 0, 1, 0, down_)
+            row = row_ids(nx)
+            ends = jnp.where(row == 0, line(take_at(low_of, x_face), lane8, 0, 0)[:1, :], 0.0)
+            ends += jnp.where(row == nx - 1, line(x_high, lane8, 0, 0)[:1, :], 0.0)
+            inverse = inv[...]
+            value = part[...] + inverse * ends
             packed = jnp.zeros((half, LANES), F32)
             for i, source in enumerate((value[:half], value[half:], inverse[:half], inverse[half:])):
                 there = lane_ids(half) // nz == i
@@ -490,12 +509,55 @@
     whole = (planes, rows, LANES)
     return call(
         body,
-        [whole, whole] + [(nx + 8 + nx // 2, LANES)] * sends,
-        "y_stage",
+        [whole, whole] + [(nx + 8 + half, LANES)] * sends,
         scratch=[whole, whole],
-        in_specs=vmem(n_z + gots + 6),
+        in_specs=vmem(gots + 9),
         out_specs=vmem(2 + sends),
-    )(*got_z, *got, rhs, yb, w, fg, low_y, node_shift)
+    )(*got, rhs, yb, w, *early)
+
+
+def y_early(got_z, fg, node_shift, low_y, after, planes, z_count):
+    nz, nx, _ = fg.shape
+    z_at = 9 * (nx // 2 + 8)
+    base = 5 * planes
+    n_z = len(got_z)
+
+    def body(*refs):
+        gz = refs[:n_z]
+        fg, shift, low_y, _, up, down, part, inv = refs[n_z:]
+        lane = lane_ids(nx)
+        row = row_ids(nx)
+
+        def side(pick):
+            values = [ref[z_at : z_at + nx, :] for ref in gz]
+            return pick("gz", z_count, values[0], values[1] if n_z > 1 else None)
+
+        above = side(high_of)
+        here = jnp.where(lane == nz, shift_lanes(above, nz), 0.0)
+        here = jnp.where(lane == LANES - 1, shift_lanes(side(low_of), -1), here)
+        high = jnp.where(lane == base + nz, shift_lanes(above, base + nz + 1), 0.0)
+        inverse = jnp.ones((nx, LANES), F32)
+        inner = jnp.zeros((nx, LANES), F32)
+        for z in range(nz):
+            guess = fg[z]
+            here = jnp.where(lane == z, shift_lanes(guess, z), here)
+            inner = jnp.where(lane == z, shift_lanes(guess, z - 1), inner)
+            high = jnp.where(lane == base + z, shift_lanes(guess, base + z + 1), high)
+            inverse = jnp.where(lane == z, shift_lanes(6.0 + shift[z], z), inverse)
+        inverse = 1.0 / inverse
+        around = inner + shift_lanes(here, 1) + shift_lanes(here, -1)
+        around += jnp.where(row == 0, 0.0, shift_rows(here, 1))
+        around += jnp.where(row == nx - 1, 0.0, shift_rows(here, -1))
+        up[...] = high
+        at = base + nz + 1
+        low = jnp.where((lane >= base) & (lane < at), shift_lanes(here, base), 0.0)
+        down[...] = jnp.where((lane >= at) & (lane < at + 3 * nz), shift_lanes(low_y[...], at), low)
+        part[...] = here + inverse * around
+        inv[...] = inverse
+
+    return call(
+        body, [(nx, LANES)] * 4, in_specs=vmem(n_z + 4), out_specs=vmem(4)
+    )(*got_z, fg, node_shift, low_y, after)
 
 
 def coarse_stage(got, rhs, w, after, y_count, devices):
@@ -558,23 +620,21 @@
     return call(
         body,
         [whole, whole, (devices, 1, LANES)],
-        "coarse_stage",
         scratch=[whole, whole, whole],
         in_specs=vmem(gots + 3),
         out_specs=vmem(3),
-    )(*got, rhs, w, after)
-
-
-def smooth_stage(residual, edge_diag, below, got_z, got_x, after, counts):
+    )(*got, rhs, w, *after)
+
+
+def smooth_stage(residual, edge_diag, below, got_z, tail_x, after, counts):
     _, nz, nx, ny = residual.shape
-    n_z, n_x = len(got_z), len(got_x)
+    n_z = len(got_z)
     rows = nx // 2 + 8
 
     def body(*refs):
         res, diag, lz, lx, ly = refs[:5]
         gz = refs[5 : 5 + n_z]
-        gx = refs[5 + n_z : 5 + n_z + n_x]
-        _, out, last, s = refs[5 + n_z + n_x :]
+        gx, _, out, last, s = refs[5 + n_z :]
         lane = lane_ids(nx)
         row = row_ids(nx)
         y_low = from_below("gy", ly[...])
@@ -586,13 +646,14 @@
         acc = jnp.zeros((nx, LANES), F32)
         for k in range(3):
             for z in range(nz):
-                s[z] = res[k, z] / diag[k, z]
+                inverse = 1.0 / diag[k, z]
+                out[k, z] = inverse
+                s[z] = res[k, z] * inverse
             z_low = from_below("gz", lz[k])
             at = 9 * rows + nx + k * nx
             z_high = above_of(gz, "gz", counts[0], slice(at, at + nx))
             x_low = from_below("gx", lx[k * nz : (k + 1) * nz, :])
-            at = 56 + nz + k * nz
-            x_high = above_of(gx, "gx", counts[1], slice(at, at + nz))
+            x_high = from_above("gx", counts[1], gx[k * nz : (k + 1) * nz, :])
             for z in range(nz):
                 here = s[z]
                 around = s[z - 1] if z > 0 else z_low
@@ -602,7 +663,7 @@
                 spot = k * nz + z
                 around += jnp.where(lane == 0, shift_lanes(y_low, -spot), shift_lanes(here, 1))
                 around += jnp.where(lane == LANES - 1, 0.0, shift_lanes(here, -1))
-                inverse = 1.0 / diag[k, z]
+                inverse = out[k, z]
                 acc = jnp.where(lane == spot, shift_lanes(inverse, spot + 1), acc)
                 out[k, z] = here + around * inverse
         last[...] = acc
@@ -610,27 +671,26 @@
     return call(
         body,
         [residual.shape, (nx, LANES)],
-        "smooth_stage",
         scratch=[(nz, nx, ny)],
         free=(0, 1),
-        in_specs=vmem(6 + n_z + n_x),
+        in_specs=vmem(7 + n_z),
         out_specs=vmem(2),
-    )(residual, edge_diag, *below, *got_z, *got_x, after)
-
-
-def final_stage(sums, v1, v2, fg, node_shift, smooth, last, got_z, got_x, got_y, counts):
+    )(residual, edge_diag, *below, *got_z, tail_x, after)
+
+
+def final_stage(sums, v1, v2, fg, mid, smooth, last, tail_x, got_z, got_x, got_y, counts):
     planes, rows, _ = v1.shape
     cz, cx, cy = planes - 4, rows - 8, LANES // 2
-    nz, nx, ny = fg.shape
+    nz, nx, _ = fg.shape
     n_z, n_x, n_y = len(got_z), len(got_x), len(got_y)
     gots = n_z + n_x + n_y
 
     def body(*refs):
-        sums, v1, v2, fg, shift, smooth, last = refs[:7]
-        gz = refs[7 : 7 + n_z]
-        gx = refs[7 + n_z : 7 + n_z + n_x]
-        gy = refs[7 + n_z + n_x : 7 + gots]
-        out, sol, dup, inter, small, lines, buf, sem = refs[7 + gots :]
+        sums, v1, v2, fg, part, inv, smooth, last, tx = refs[:9]
+        gz = refs[9 : 9 + n_z]
+        gx = refs[9 + n_z : 9 + n_z + n_x]
+        gy = refs[9 + n_z + n_x : 9 + gots]
+        out, sol, dup, inter, small, lines, buf, sem = refs[9 + gots :]
 
         def one_side(pick, refs, axis, size, at):
             values = [ref[at, :] for ref in refs]
@@ -656,13 +716,9 @@
             dup[z] = jnp.dot(sol[z], spread, precision=HIGHEST, preferred_element_type=F32)
 
         z_at = 9 * rows
-        z_low, z_high = both(gz, "gz", counts[0], slice(z_at, z_at + nx))
         z_base = one_side(high_of, gz, "gz", counts[0], slice(z_at + 4 * nx, z_at + 5 * nx))
         z_inverse = one_side(high_of, gz, "gz", counts[0], slice(z_at + 5 * nx, z_at + 6 * nx))
-        x_low, x_high = both(gx, "gx", counts[1], slice(48, 48 + nz + 1))
-        x_at = 56 + nz
-        x_base = one_side(high_of, gx, "gx", counts[1], slice(x_at + 3 * nz, x_at + 4 * nz))
-        x_inverse = one_side(high_of, gx, "gx", counts[1], slice(x_at + 4 * nz, x_at + 5 * nz))
+        x_low, x_high = both(gx, "gx", counts[1], slice(3 * planes, 3 * planes + nz + 1))
         y_low, y_high = both(gy, "gy", counts[2], slice(0, nx))
         y_row_low, y_row_high = both(gy, "gy", counts[2], slice(nx, nx + 1))
         half = nx // 2
@@ -670,7 +726,6 @@
         lane = lane_ids(nx)
         row = row_ids(nx)
         base = 5 * planes
-        tail = base + nz + 1
 
         def spread_around(z):
             c, odd = z // 2, z % 2
@@ -682,29 +737,15 @@
             inter[slot, pl.ds(1, cx, 2), :] = (same + shift_rows(here, -1))[:cx, :]
             return inter[slot]
 
-        def edges(z, guess):
-            left = shift_lanes(y_low, -(base + z))
-            right = shift_lanes(y_high, -(base + z) - 1)
-            if guess is None:
-                around = jnp.where(row == 0, x_low[z : z + 1, :], 0.0)
-                around += jnp.where(row == nx - 1, x_high[z : z + 1, :], 0.0)
-                around += jnp.where(lane == 0, left, 0.0)
-                return around + jnp.where(lane == LANES - 1, right, 0.0)
-            around = jnp.where(row == 0, x_low[z : z + 1, :], shift_rows(guess, 1))
-            around += jnp.where(row == nx - 1, x_high[z : z + 1, :], shift_rows(guess, -1))
-            around += jnp.where(lane == 0, left, shift_lanes(guess, 1))
-            return around + jnp.where(lane == LANES - 1, right, shift_lanes(guess, -1))
-
         def nodal(z):
+            around = spread_around(z) + jnp.where(row == 0, x_low[z : z + 1, :], 0.0)
+            around += jnp.where(row == nx - 1, x_high[z : z + 1, :], 0.0)
+            around += jnp.where(lane == 0, shift_lanes(y_low, -(base + z)), 0.0)
+            around += jnp.where(lane == LANES - 1, shift_lanes(y_high, -(base + z) - 1), 0.0)
             if z == nz:
-                around = spread_around(z) + edges(z, None) + fg[nz - 1]
-                value = z_base + z_inverse * around
+                value = z_base + z_inverse * (around + fg[nz - 1])
                 return from_above("gz", counts[0], value)
-            guess = fg[z]
-            around = spread_around(z) + edges(z, guess)
-            around += fg[z - 1] if z > 0 else z_low
-            around += fg[z + 1] if z < nz - 1 else z_high
-            return guess + around / (6.0 + shift[z])
+            return part[z] + inv[z] * around
 
         here = dup[:cz, cx, :LANES]
         same = 3.0 * here + dup[:cz, cx, LANES:] + dup[:cz, cx - 1, :LANES]
@@ -717,7 +758,9 @@
             right = shift_lanes(y_row_high, -(base + z) - 1)
             value = jnp.where(lane1 == 0, left, 0.0)
             lines[z : z + 1, :] = jnp.where(lane1 == LANES - 1, right, value)
-        x_value = x_base + x_inverse * (fg[:, nx - 1, :] + small[...] + lines[...])
+        x_value = tx[3 * nz : 4 * nz, :] + tx[4 * nz :, :] * (
+            fg[:, nx - 1, :] + small[...] + lines[...]
+        )
         x_value = from_above("gx", counts[1], x_value)
 
         lane_c = lane_ids(rows)
@@ -739,7 +782,7 @@
         )
         y_value = y_base + y_inverse * (own + inter[0])
         y_value = from_above("gy", counts[2], y_value)
-        y_fix = shift_lanes(y_high, -tail) * last[...]
+        y_fix = shift_lanes(y_high, -(base + nz + 1)) * last[...]
 
         def copy(z):
             return pltpu.make_async_copy(buf.at[:, z], out.at[:, z], sem.at[z])
@@ -762,7 +805,6 @@
     return call(
         body,
         [smooth.shape],
-        "final_stage",
         scratch=[
             (planes, rows, LANES),
             (planes, rows, 2 * LANES),
@@ -773,9 +815,9 @@
             pltpu.SemaphoreType.DMA((nz,)),
         ],
         far_out=True,
-        in_specs=vmem(7 + gots),
+        in_specs=vmem(9 + gots),
         out_specs=[pl.BlockSpec(memory_space=pltpu.HBM)],
-    )(sums, v1, v2, fg, node_shift, smooth, last, *got_z, *got_x, *got_y)[0]
+    )(sums, v1, v2, fg, *mid, smooth, last, tail_x, *got_z, *got_x, *got_y)[0]
 
 
 def local(residual, edge_diag, node_shift, coarse_shift):
@@ -786,18 +828,20 @@
     below = (ring(up_z, "gz", 1), ring(up_x, "gx", 1), ring(up_y, "gy", 1))
     fg, rhs, xb, yb, w, *send = nodal_stage(part, node_shift, coarse_shift, *below, low_z, counts[0])
     got_z = swap(send, "gz")
-    rhs, yb, w, *send = x_stage(
-        got_z, rhs, xb, yb, w, fg, low_x, node_shift, counts[0], counts[1]
-    )
+    rhs, yb, w, *send = x_stage(got_z, rhs, xb, yb, w, fg, counts[0], counts[1])
     got_x = swap(send, "gx")
-    rhs, w, *send = y_stage(got_z, got_x, rhs, yb, w, fg, low_y, node_shift, counts)
+    planes = rhs.shape[0]
+    tail_x = x_tail(got_z, fg, node_shift, low_x, w, counts[0])
+    mid = part_stage(got_z, fg, node_shift, w, counts[0])
+    early = y_early(got_z, fg, node_shift, low_y, w, planes, counts[0])
+    early = (*early, tail_x, mid[1])
+    tail_x = ring(tail_x, "gx", -1)
+    rhs, w, *send = y_stage(got_x, rhs, yb, w, early, counts[1], counts[2])
     got_y = swap(send, "gy")
-    smooth, last = smooth_stage(residual, edge_diag, below, got_z, got_x, w, counts)
-    v1, v2, sums = coarse_stage(got_y, rhs, w, last, counts[2], devices)
+    smooth, last = smooth_stage(residual, edge_diag, below, got_z, tail_x, w, counts)
+    v1, v2, sums = coarse_stage(got_y, rhs, w, (last,), counts[2], devices)
     sums = lax.all_to_all(sums, ("gx", "gy", "gz"), 0, 0)
-    return final_stage(
-        sums, v1, v2, fg, node_shift, smooth, last, got_z, got_x, got_y, counts
-    )
+    return final_stage(sums, v1, v2, fg, mid, smooth, last, tail_x, got_z, got_x, got_y, counts)
 
 
 def solution(mesh):
@@ -807,6 +851,7 @@
         P("gz", "gx", "gy"),
         P("gz", "gx", "gy"),
     )
+
     return jax.shard_map(
         local, mesh=mesh, in_specs=placed, out_specs=P(None, "gz", "gx", "gy"), check_vma=False
     )

time: 45.7 us -> 46.3 us (1.013)
  waiting for transfers between devices: 10.7 us -> 8.14 us
  starting transfers between devices: 11.9 us -> 14 us
  blocking collectives: 10.5 us -> 11.4 us
    ppermute x2, waiting for transfers between devices: 4.21 us -> 1.53 us  [swap(): out.append(lax.ppermute(values[1], axis, odd))]
    ppermute x3 -> x4, starting transfers between devices: 4.68 us -> 7.07 us  [ring(): lax.ppermute(value, axis, [(i, (i + step) % size) for i in range(size)])]
    ppermute x3 -> x4, waiting for transfers between devices: 3.24 us -> 4.91 us  [ring(): lax.ppermute(value, axis, [(i, (i + step) % size) for i in range(size)])]
    ppermute x3, waiting for transfers between devices: 3.21 us -> 1.7 us  [swap(): out = [lax.ppermute(values[0], axis, even)]]
    all_to_all x1, blocking collectives: 10.5 us -> 11.4 us  [local(): sums = lax.all_to_all(sums, ('gx', 'gy', 'gz'), 0, 0)]
    pallas_call x7 -> x10, Pallas kernels: 12.4 us -> 12.4 us  [apply(): run(*(a if i in free else pltpu.with_memory_space_constraint(a, space) fo...]
  transfers between devices with their start and end apart: 8 -> 9, of which waited for: 5 -> 4; matrix products, arithmetic and copies ran while one was open for 0% -> 0% of each run, Pallas kernels for 4% -> 6%
where the time goes in v5:
time: 46.3 us; the launch traced here: 46.1 us
  starting transfers between devices  14 us (30%)
  Pallas kernels  12.4 us (27%)
  blocking collectives  11.4 us (25%)
  waiting for transfers between devices  8.14 us (18%)
    pallas_call x10, Pallas kernels, apply(): run(*(a if i in free else pltpu.with_memory_space_constraint(a, space) fo...  12.4 us
    all_to_all x1, blocking collectives, local(): sums = lax.all_to_all(sums, ('gx', 'gy', 'gz'), 0, 0)  11.4 us
    ppermute x4, starting transfers between devices, ring(): lax.ppermute(value, axis, [(i, (i + step) % size) for i in range(size)])  7.07 us
    ppermute x4, waiting for transfers between devices, ring(): lax.ppermute(value, axis, [(i, (i + step) % size) for i in range(size)])  4.91 us
    ppermute x2, starting transfers between devices, swap(): out.append(lax.ppermute(values[1], axis, odd))  4.59 us
    ppermute x3, starting transfers between devices, swap(): out = [lax.ppermute(values[0], axis, even)]  2.35 us
    ppermute x3, waiting for transfers between devices, swap(): out = [lax.ppermute(values[0], axis, even)]  1.7 us
    ppermute x2, waiting for transfers between devices, swap(): out.append(lax.ppermute(values[1], axis, odd))  1.53 us
  transfers between devices with their start and end apart: 9, of which 4 were waited for; matrix products, arithmetic and copies ran while one was open for 0% of the time, Pallas kernels for 6%

profile of v5, /device:TPU:0, one launch (start us, length us, event | category | flops | bytes accessed | tf_op | source)
XLA Modules:
  0.0 46.1 jit_solution(9585299244349937212)
XLA Ops:
  0.0 3.6 %shard_map.46 = (f32[16,64,128]{2,1,0:T(8,128)S(1)}, f32[3,64,128]{2,1,0:T(8,128)S(1)}, f32[48,128]{1,0:T(8,128)S(1)}, f32[64,128]{1,0:T(8,128)S(1)}, f32[3,64,1...) custom-call(f32[3,16,64,128]{3,2,1,0:T(8,128)} %refs_0_.1, f32[3,16,64,128]{3,2,1,0:T(8,128)} %refs_1_.1), custom_call_target="tpu_custom_call" | custom-call | tf_op jit(solution)/shard_map/pallas_call | solution.py:99
  3.6 0.6 %collective-permute-start = (f32[3,64,128]{2,1,0:T(8,128)S(1)}, f32[3,64,128]{2,1,0:T(8,128)S(1)}, u32[]{:S(2)}, u32[]{:S(2)}) collective-permute-start(f32[3,64,128]{2,1,0:T(8,128)S(1)} %get-tuple-element.39), channel_id=1, source_target_pairs={{0,1},{1,0},{2,3},{3,2},{4,5},{5,4},{6,7},{7,6},{8,9},{9,8},{10,11... | collective-permute-start | bytes 294920 | tf_op jit(solution)/shard_map/ppermute | solution.py:58
  4.2 2.6 %collective-permute-start.2 = (f32[64,128]{1,0:T(8,128)S(1)}, f32[64,128]{1,0:T(8,128)S(1)}, u32[]{:S(2)}, u32[]{:S(2)}) collective-permute-start(f32[64,128]{1,0:T(8,128)S(1)} %get-tuple-element.41), channel_id=1, source_target_pairs={{0,2},{2,4},{4,6},{6,0},{1,3},{3,5},{5,7},{7,1},{8,10},{10,12},{12... | collective-permute-start | bytes 98312 | tf_op jit(solution)/shard_map/ppermute | solution.py:58
  6.8 1.5 %collective-permute-start.1 = (f32[48,128]{1,0:T(8,128)S(1)}, f32[48,128]{1,0:T(8,128)S(1)}, u32[]{:S(2)}, u32[]{:S(2)}) collective-permute-start(f32[48,128]{1,0:T(8,128)S(1)} %get-tuple-element.40), channel_id=1, source_target_pairs={{0,8},{8,16},{16,24},{24,0},{1,9},{9,17},{17,25},{25,1},{2,10},{10... | collective-permute-start | bytes 73736 | tf_op jit(solution)/shard_map/ppermute | solution.py:58
  8.3 3.2 %collective-permute-done.1.gx.refs_3_ = f32[48,128]{1,0:T(8,128)S(1)} collective-permute-done((f32[48,128]{1,0:T(8,128)S(1)}, f32[48,128]{1,0:T(8,128)S(1)}, u32[]{:S(2)}, u32[]{:S(2)}) %collective-permute-start.1) | collective-permute-done | bytes 24608 | tf_op jit(solution)/shard_map/ppermute | solution.py:58
  11.5 1.0 %shard_map.47 = (f32[16,64,128]{2,1,0:T(8,128)S(1)}, f32[12,40,128]{2,1,0:T(8,128)S(1)}, f32[8,40,128]{2,1,0:T(8,128)S(1)}, f32[8,40,128]{2,1,0:T(8,128)S(1)}, f...) custom-call(f32[16,64,128]{2,1,0:T(8,128)S(1)} %get-tuple-element.38.part, f32[16,64,128]{2,1,0:T(8,128)S(1)} %copy-done, ...), custom_call_target="tpu_custom_call" | custom-call | tf_op jit(solution)/shard_map/pallas_call | solution.py:99
  12.5 0.1 collective-permute-start.3
  12.6 1.7 %collective-permute-done.3.refs_0_.refs_5_.refs_9_ = f32[744,128]{1,0:T(8,128)S(1)} collective-permute-done((f32[744,128]{1,0:T(8,128)S(1)}, f32[744,128]{1,0:T(8,128)S(1)}, u32[]{:S(2)}, u32[]{:S(2)}) %collective-permute-start.3) | collective-permute-done | bytes 380960 | tf_op jit(solution)/shard_map/ppermute | solution.py:64
  14.3 0.2 shard_map.48
  14.5 1.0 %collective-permute-start.4 = (f32[56,128]{1,0:T(8,128)S(1)}, f32[56,128]{1,0:T(8,128)S(1)}, u32[]{:S(2)}, u32[]{:S(2)}) collective-permute-start(f32[56,128]{1,0:T(8,128)S(1)} %get-tuple-element.49), channel_id=1, source_target_pairs={{0,8},{8,0},{16,24},{24,16},{1,9},{9,1},{17,25},{25,17},{2,10},{10... | collective-permute-start | bytes 86024 | tf_op jit(solution)/shard_map/ppermute | solution.py:64
  15.4 2.1 %collective-permute-start.5 = (f32[56,128]{1,0:T(8,128)S(1)}, f32[56,128]{1,0:T(8,128)S(1)}, u32[]{:S(2)}, u32[]{:S(2)}) collective-permute-start(f32[56,128]{1,0:T(8,128)S(1)} %get-tuple-element.50), channel_id=1, source_target_pairs={{0,24},{8,16},{16,8},{24,0},{1,25},{9,17},{17,9},{25,1},{2,26},{10... | collective-permute-start | bytes 86024 | tf_op jit(solution)/shard_map/ppermute | solution.py:67
  17.5 0.4 shard_map.51
  17.9 0.1 shard_map.50.refs_9_
  18.0 0.7 %shard_map.49 = (f32[64,128]{1,0:T(8,128)S(1)}, f32[64,128]{1,0:T(8,128)S(1)}, f32[64,128]{1,0:T(8,128)S(1)}, f32[64,128]{1,0:T(8,128)S(1)}) custom-call(f32[744,128]{1,0:T(8,128)S(1)} %collective-permute-done.3.refs_0_.refs_5_.refs_9_, f32[16,64,128]{2,1,0:T(8,128)S(1)} %get-tuple-element.48.refs_5_.refs_1_.refs_3_, f32[16,64,128]{2,1,0:T(8,128)S(1)} %copy-done, ...), custom_call_target="tpu_custom_call" | custom-call | tf_op jit(solution)/shard_map/pallas_call | solution.py:99
  18.7 1.5 %collective-permute-done.5.refs_1_.refs_11_ = f32[56,128]{1,0:T(8,128)S(1)} collective-permute-done((f32[56,128]{1,0:T(8,128)S(1)}, f32[56,128]{1,0:T(8,128)S(1)}, u32[]{:S(2)}, u32[]{:S(2)}) %collective-permute-start.5) | collective-permute-done | bytes 28704 | tf_op jit(solution)/shard_map/ppermute | solution.py:67
  20.2 1.1 %shard_map.52 = (f32[12,40,128]{2,1,0:T(8,128)S(1)}, f32[12,40,128]{2,1,0:T(8,128)S(1)}, f32[104,128]{1,0:T(8,128)S(1)}, f32[104,128]{1,0:T(8,128)S(1)}) custom-call(f32[56,128]{1,0:T(8,128)S(1)} %collective-permute-done.4.refs_0_.refs_10_, f32[56,128]{1,0:T(8,128)S(1)} %collective-permute-done.5.refs_1_.refs_11_, ...), custom_call_target="tpu_custom_call" | custom-call | tf_op jit(solution)/shard_map/pallas_call | solution.py:99
  21.3 1.3 %collective-permute-start.6 = (f32[104,128]{1,0:T(8,128)S(1)}, f32[104,128]{1,0:T(8,128)S(1)}, u32[]{:S(2)}, u32[]{:S(2)}) collective-permute-start(f32[104,128]{1,0:T(8,128)S(1)} %get-tuple-element.61), channel_id=1, source_target_pairs={{0,2},{2,0},{4,6},{6,4},{1,3},{3,1},{5,7},{7,5},{8,10},{10,8},{12,... | collective-permute-start | bytes 159752 | tf_op jit(solution)/shard_map/ppermute | solution.py:64
  22.6 2.5 %collective-permute-start.7 = (f32[104,128]{1,0:T(8,128)S(1)}, f32[104,128]{1,0:T(8,128)S(1)}, u32[]{:S(2)}, u32[]{:S(2)}) collective-permute-start(f32[104,128]{1,0:T(8,128)S(1)} %get-tuple-element.62), channel_id=1, source_target_pairs={{0,6},{2,4},{4,2},{6,0},{1,7},{3,5},{5,3},{7,1},{8,14},{10,12},{12... | collective-permute-start | bytes 159752 | tf_op jit(solution)/shard_map/ppermute | solution.py:67
  25.1 2.4 %collective-permute-start.8 = (f32[80,128]{1,0:T(8,128)S(1)}, f32[80,128]{1,0:T(8,128)S(1)}, u32[]{:S(2)}, u32[]{:S(2)}) collective-permute-start(f32[80,128]{1,0:T(8,128)S(1)} %shard_map.50.refs_9_), channel_id=1, source_target_pairs={{0,24},{8,0},{16,8},{24,16},{1,25},{9,1},{17,9},{25,17},{2,26},{10... | collective-permute-start | bytes 122888 | tf_op jit(solution)/shard_map/ppermute | solution.py:58
  27.5 1.7 %collective-permute-done.8.refs_6_.refs_8_ = f32[80,128]{1,0:T(8,128)S(1)} collective-permute-done((f32[80,128]{1,0:T(8,128)S(1)}, f32[80,128]{1,0:T(8,128)S(1)}, u32[]{:S(2)}, u32[]{:S(2)}) %collective-permute-start.8) | collective-permute-done | bytes 40992 | tf_op jit(solution)/shard_map/ppermute | solution.py:58
  29.2 1.8 %shard_map.53 = (f32[3,16,64,128]{3,2,1,0:T(8,128)S(1)}, f32[64,128]{1,0:T(8,128)S(1)}) custom-call(f32[3,16,64,128]{3,2,1,0:T(8,128)S(1)} %copy-done.1, f32[3,16,64,128]{3,2,1,0:T(8,128)S(1)} %copy-done.2, f32[3,64,128]{2,1,0:T(8,128)S(1)} %collective-permute-done.gz.refs_2_, f32[48,128]{1,0:T(8,128)S(1)} %collective-permute-done.1.gx.refs_3_, ...), custom_call_target="tpu_custom_call" | custom-call | tf_op jit(solution)/shard_map/pallas_call | solution.py:99
  31.0 1.0 %shard_map.54 = (f32[12,40,128]{2,1,0:T(8,128)S(1)}, f32[12,40,128]{2,1,0:T(8,128)S(1)}, f32[32,1,128]{2,1,0:T(1,128)S(1)}) custom-call(f32[104,128]{1,0:T(8,128)S(1)} %collective-permute-done.6.refs_0_.refs_12_, f32[104,128]{1,0:T(8,128)S(1)} %collective-permute-done.7.refs_1_.refs_13_, f32[12,40,128]{2,1,0:T(8,128)S(1)} %get-tuple-element.63.refs_2_, ...), custom_call_target="tpu_custom_call" | custom-call | tf_op jit(solution)/shard_map/pallas_call | solution.py:99
  32.0 11.4 %all_to_all.5.refs_0_ = f32[32,1,128]{2,1,0:T(1,128)S(1)} all-to-all(f32[32,1,128]{2,1,0:T(1,128)S(1)} %get-tuple-element.66), channel_id=1, replica_groups=mesh['gx'=4,'gy'=4,'gz'=2] {'gx','gy','gz'}, dimensions={0} | all-to-all | bytes 32768 | tf_op jit(solution)/shard_map/all_to_all | solution.py:843
  43.4 2.7 %shard_map.55 = f32[3,16,64,128]{3,2,1,0:T(8,128)} custom-call(f32[32,1,128]{2,1,0:T(1,128)S(1)} %all_to_all.5.refs_0_, f32[12,40,128]{2,1,0:T(8,128)S(1)} %get-tuple-element.67.refs_1_, f32[12,40,128]{2,1,0:T(8,128)S(1)} %get-tuple-element.68.refs_2_, f32[16,64,128]{2,1,0:T(8,128)S(1)} %get-tuple-element.48.refs_5_.refs_1_.refs_3_, ...), custom_call_target="tpu_custom_call" | custom-call | tf_op jit(solution)/shard_map/pallas_call | solution.py:99
  (13 shorter events, 0.0 us)
Async XLA Ops:
  0.0 11.5 %copy-start = (f32[16,64,128]{2,1,0:T(8,128)S(1)}, f32[16,64,128]{2,1,0:T(8,128)}, u32[]{:S(2)}) copy-start(f32[16,64,128]{2,1,0:T(8,128)} %refs_2_.5) | copy-start | bytes 1572868
  0.0 11.5 %copy-start.3 = (f32[8,32,64]{2,1,0:T(8,128)S(1)}, f32[8,32,64]{2,1,0:T(8,128)}, u32[]{:S(2)}) copy-start(f32[8,32,64]{2,1,0:T(8,128)} %coarse.1) | copy-start | bytes 196612
  3.6 7.9 %collective-permute-start = (f32[3,64,128]{2,1,0:T(8,128)S(1)}, f32[3,64,128]{2,1,0:T(8,128)S(1)}, u32[]{:S(2)}, u32[]{:S(2)}) collective-permute-start(f32[3,64,128]{2,1,0:T(8,128)S(1)} %get-tuple-element.39), channel_id=1, source_target_pairs={{0,1},{1,0},{2,3},{3,2},{4,5},{5,4},{6,7},{7,6},{8,9},{9,8},{10,11... | collective-permute-start | bytes 294920 | tf_op jit(solution)/shard_map/ppermute | solution.py:58
  4.2 7.4 %collective-permute-start.2 = (f32[64,128]{1,0:T(8,128)S(1)}, f32[64,128]{1,0:T(8,128)S(1)}, u32[]{:S(2)}, u32[]{:S(2)}) collective-permute-start(f32[64,128]{1,0:T(8,128)S(1)} %get-tuple-element.41), channel_id=1, source_target_pairs={{0,2},{2,4},{4,6},{6,0},{1,3},{3,5},{5,7},{7,1},{8,10},{10,12},{12... | collective-permute-start | bytes 98312 | tf_op jit(solution)/shard_map/ppermute | solution.py:58
  6.8 4.7 %collective-permute-start.1 = (f32[48,128]{1,0:T(8,128)S(1)}, f32[48,128]{1,0:T(8,128)S(1)}, u32[]{:S(2)}, u32[]{:S(2)}) collective-permute-start(f32[48,128]{1,0:T(8,128)S(1)} %get-tuple-element.40), channel_id=1, source_target_pairs={{0,8},{8,16},{16,24},{24,0},{1,9},{9,17},{17,25},{25,1},{2,10},{10... | collective-permute-start | bytes 73736 | tf_op jit(solution)/shard_map/ppermute | solution.py:58
  12.5 1.8 %collective-permute-start.3 = (f32[744,128]{1,0:T(8,128)S(1)}, f32[744,128]{1,0:T(8,128)S(1)}, u32[]{:S(2)}, u32[]{:S(2)}) collective-permute-start(f32[744,128]{1,0:T(8,128)S(1)} %get-tuple-element.43), channel_id=1, source_target_pairs={{0,1},{1,0},{2,3},{3,2},{4,5},{5,4},{6,7},{7,6},{8,9},{9,8},{10,11... | collective-permute-start | bytes 1142792 | tf_op jit(solution)/shard_map/ppermute | solution.py:64
  14.5 4.2 %collective-permute-start.4 = (f32[56,128]{1,0:T(8,128)S(1)}, f32[56,128]{1,0:T(8,128)S(1)}, u32[]{:S(2)}, u32[]{:S(2)}) collective-permute-start(f32[56,128]{1,0:T(8,128)S(1)} %get-tuple-element.49), channel_id=1, source_target_pairs={{0,8},{8,0},{16,24},{24,16},{1,9},{9,1},{17,25},{25,17},{2,10},{10... | collective-permute-start | bytes 86024 | tf_op jit(solution)/shard_map/ppermute | solution.py:64
  15.4 4.8 %collective-permute-start.5 = (f32[56,128]{1,0:T(8,128)S(1)}, f32[56,128]{1,0:T(8,128)S(1)}, u32[]{:S(2)}, u32[]{:S(2)}) collective-permute-start(f32[56,128]{1,0:T(8,128)S(1)} %get-tuple-element.50), channel_id=1, source_target_pairs={{0,24},{8,16},{16,8},{24,0},{1,25},{9,17},{17,9},{25,1},{2,26},{10... | collective-permute-start | bytes 86024 | tf_op jit(solution)/shard_map/ppermute | solution.py:67
  18.0 11.2 %copy-start.1 = (f32[3,16,64,128]{3,2,1,0:T(8,128)S(1)}, f32[3,16,64,128]{3,2,1,0:T(8,128)}, u32[]{:S(2)}) copy-start(f32[3,16,64,128]{3,2,1,0:T(8,128)} %refs_0_.1) | copy-start | bytes 4718596
  18.0 11.2 %copy-start.2 = (f32[3,16,64,128]{3,2,1,0:T(8,128)S(1)}, f32[3,16,64,128]{3,2,1,0:T(8,128)}, u32[]{:S(2)}) copy-start(f32[3,16,64,128]{3,2,1,0:T(8,128)} %refs_1_.1) | copy-start | bytes 4718596
  21.3 9.7 %collective-permute-start.6 = (f32[104,128]{1,0:T(8,128)S(1)}, f32[104,128]{1,0:T(8,128)S(1)}, u32[]{:S(2)}, u32[]{:S(2)}) collective-permute-start(f32[104,128]{1,0:T(8,128)S(1)} %get-tuple-element.61), channel_id=1, source_target_pairs={{0,2},{2,0},{4,6},{6,4},{1,3},{3,1},{5,7},{7,5},{8,10},{10,8},{12,... | collective-permute-start | bytes 159752 | tf_op jit(solution)/shard_map/ppermute | solution.py:64
  22.6 8.4 %collective-permute-start.7 = (f32[104,128]{1,0:T(8,128)S(1)}, f32[104,128]{1,0:T(8,128)S(1)}, u32[]{:S(2)}, u32[]{:S(2)}) collective-permute-start(f32[104,128]{1,0:T(8,128)S(1)} %get-tuple-element.62), channel_id=1, source_target_pairs={{0,6},{2,4},{4,2},{6,0},{1,7},{3,5},{5,3},{7,1},{8,14},{10,12},{12... | collective-permute-start | bytes 159752 | tf_op jit(solution)/shard_map/ppermute | solution.py:67
  25.1 4.1 %collective-permute-start.8 = (f32[80,128]{1,0:T(8,128)S(1)}, f32[80,128]{1,0:T(8,128)S(1)}, u32[]{:S(2)}, u32[]{:S(2)}) collective-permute-start(f32[80,128]{1,0:T(8,128)S(1)} %shard_map.50.refs_9_), channel_id=1, source_target_pairs={{0,24},{8,0},{16,8},{24,16},{1,25},{9,1},{17,9},{25,17},{2,26},{10... | collective-permute-start | bytes 122888 | tf_op jit(solution)/shard_map/ppermute | solution.py:58

commit v6 on v5

--- a/solution.py
+++ b/solution.py
@@ -60,8 +60,7 @@
 
 def swap(values, axis):
     size = lax.axis_size(axis)
-    even = [(i, i ^ 1) for i in range(size)]
-    out = [lax.ppermute(values[0], axis, even)]
+    out = [lax.ppermute(values[0], axis, [(i, i ^ 1) for i in range(size)])]
     if len(values) > 1:
         odd = [(i, (i + 1) % size if i % 2 else (i - 1) % size) for i in range(size)]
         out.append(lax.ppermute(values[1], axis, odd))
@@ -84,7 +83,7 @@
             up(refs[1])
 
 
-def call(body, outs, scratch=(), far=(), free=(), far_out=False, **kwargs):
+def call(body, outs, scratch=(), far=(), far_out=False, **kwargs):
     kind = jax.ShapeDtypeStruct if far_out else pltpu.VMEM
     run = pl.pallas_call(
         body,
@@ -98,8 +97,8 @@
         spaces = [pltpu.HBM if i in far else pltpu.VMEM for i in range(len(args))]
         return run(
             *(
-                a if i in free else pltpu.with_memory_space_constraint(a, space)
-                for i, (a, space) in enumerate(zip(args, spaces))
+                pltpu.with_memory_space_constraint(a, space)
+                for a, space in zip(args, spaces)
             )
         )
 
@@ -112,66 +111,62 @@
 
 def edge_stage(residual, edge_diag):
     _, nz, nx, ny = residual.shape
-    step = 4
+    step = 2
     steps = nz // step
 
-    def body(res, diag, part, up_z, up_x, up_y, low_z, low_x, low_y, last):
-        block = pl.program_id(0)
+    def body(res, diag, part, up_z, up_x, up_y, low_z, low_x, low_y, scaled, inv, near, sems):
         lane = lane_ids(nx)
         row = row_ids(nx)
 
-        @pl.when(block == 0)
-        def _():
-            last[...] = jnp.zeros_like(last)
-            up_y[...] = jnp.zeros_like(up_y)
-            low_y[...] = jnp.zeros_like(low_y)
-
-        before = last[...]
-        high = up_y[...]
-        low = low_y[...]
-        for j in range(step):
-            z = block * step + j
-            s = [res[k, j] / diag[k, j] for k in range(3)]
+        def copies(block):
+            at = pl.ds(block * step, step)
+            return [
+                pltpu.make_async_copy(source.at[:, at], target.at[:, at], sems.at[i, block])
+                for i, (source, target) in enumerate(((res, near), (diag, inv)))
+            ]
+
+        for block in range(steps):
+            for copy in copies(block):
+                copy.start()
+        before = jnp.zeros((nx, ny), F32)
+        high = jnp.zeros((nx, LANES), F32)
+        low = jnp.zeros((nx, LANES), F32)
+        for z in range(nz):
+            if z % step == 0:
+                for copy in copies(z // step):
+                    copy.wait()
+            s = []
+            for k in range(3):
+                inverse = 1.0 / inv[k, z]
+                inv[k, z] = inverse
+                s.append(near[k, z] * inverse)
+                scaled[k, z] = s[k]
             total = before - s[0]
             total += jnp.where(row == 0, 0.0, shift_rows(s[1], 1)) - s[1]
             total += jnp.where(lane == 0, 0.0, shift_lanes(s[2], 1)) - s[2]
-            part[j] = total
+            part[z] = total
             before = s[0]
             for k in range(3):
-                up_x[pl.ds(k * nz + z, 1), :] = s[k][nx - 1 :, :]
-                low_x[pl.ds(k * nz + z, 1), :] = s[k][:1, :]
                 spot = k * nz + z
-                high = jnp.where(lane == spot, pltpu.roll(s[k], spot + 1, 1), high)
-                low = jnp.where(lane == spot, pltpu.roll(s[k], spot, 1), low)
-            if j == 0:
-
-                @pl.when(block == 0)
-                def _():
-                    for k in range(3):
-                        low_z[k] = s[k]
-
-            if j == step - 1:
-
-                @pl.when(block == steps - 1)
-                def _():
-                    for k in range(3):
-                        up_z[k] = s[k]
-
-        last[...] = before
+                up_x[spot : spot + 1, :] = s[k][nx - 1 :, :]
+                low_x[spot : spot + 1, :] = s[k][:1, :]
+                high = jnp.where(lane == spot, shift_lanes(s[k], spot + 1), high)
+                low = jnp.where(lane == spot, shift_lanes(s[k], spot), low)
+                if z == 0:
+                    low_z[k] = s[k]
+                if z == nz - 1:
+                    up_z[k] = s[k]
         up_y[...] = high
         low_y[...] = low
 
-    whole = lambda *shape: pl.BlockSpec(shape, lambda i: (0,) * len(shape))
-    spec = pl.BlockSpec((3, step, nx, ny), lambda i: (0, i, 0, 0))
     faces = [(3, nx, ny), (3 * nz, ny), (nx, LANES)] * 2
     return call(
         body,
-        [(nz, nx, ny)] + faces,
-        scratch=[(nx, ny)],
+        [(nz, nx, ny)] + faces + [residual.shape] * 2,
+        scratch=[residual.shape, pltpu.SemaphoreType.DMA((2, steps))],
         far=(0, 1),
-        grid=(steps,),
-        in_specs=[spec, spec],
-        out_specs=[pl.BlockSpec((step, nx, ny), lambda i: (i, 0, 0))] + [whole(*f) for f in faces],
+        in_specs=[pl.BlockSpec(memory_space=pltpu.HBM)] * 2,
+        out_specs=vmem(9),
     )(residual, edge_diag)
 
 
@@ -626,15 +621,15 @@
     )(*got, rhs, w, *after)
 
 
-def smooth_stage(residual, edge_diag, below, got_z, tail_x, after, counts):
-    _, nz, nx, ny = residual.shape
+def smooth_stage(scaled, inverses, below, got_z, tail_x, after, counts):
+    _, nz, nx, _ = scaled.shape
     n_z = len(got_z)
     rows = nx // 2 + 8
 
     def body(*refs):
-        res, diag, lz, lx, ly = refs[:5]
+        s, inv, lz, lx, ly = refs[:5]
         gz = refs[5 : 5 + n_z]
-        gx, _, out, last, s = refs[5 + n_z :]
+        gx, _, out, last = refs[5 + n_z :]
         lane = lane_ids(nx)
         row = row_ids(nx)
         y_low = from_below("gy", ly[...])
@@ -645,37 +640,28 @@
 
         acc = jnp.zeros((nx, LANES), F32)
         for k in range(3):
-            for z in range(nz):
-                inverse = 1.0 / diag[k, z]
-                out[k, z] = inverse
-                s[z] = res[k, z] * inverse
             z_low = from_below("gz", lz[k])
             at = 9 * rows + nx + k * nx
             z_high = above_of(gz, "gz", counts[0], slice(at, at + nx))
             x_low = from_below("gx", lx[k * nz : (k + 1) * nz, :])
             x_high = from_above("gx", counts[1], gx[k * nz : (k + 1) * nz, :])
             for z in range(nz):
-                here = s[z]
-                around = s[z - 1] if z > 0 else z_low
-                around += s[z + 1] if z < nz - 1 else z_high
+                here = s[k, z]
+                around = s[k, z - 1] if z > 0 else z_low
+                around += s[k, z + 1] if z < nz - 1 else z_high
                 around += jnp.where(row == 0, x_low[z : z + 1, :], shift_rows(here, 1))
                 around += jnp.where(row == nx - 1, x_high[z : z + 1, :], shift_rows(here, -1))
                 spot = k * nz + z
                 around += jnp.where(lane == 0, shift_lanes(y_low, -spot), shift_lanes(here, 1))
                 around += jnp.where(lane == LANES - 1, 0.0, shift_lanes(here, -1))
-                inverse = out[k, z]
+                inverse = inv[k, z]
                 acc = jnp.where(lane == spot, shift_lanes(inverse, spot + 1), acc)
                 out[k, z] = here + around * inverse
         last[...] = acc
 
     return call(
-        body,
-        [residual.shape, (nx, LANES)],
-        scratch=[(nz, nx, ny)],
-        free=(0, 1),
-        in_specs=vmem(7 + n_z),
-        out_specs=vmem(2),
-    )(residual, edge_diag, *below, *got_z, tail_x, after)
+        body, [scaled.shape, (nx, LANES)], in_specs=vmem(7 + n_z), out_specs=vmem(2)
+    )(scaled, inverses, *below, *got_z, tail_x, after)
 
 
 def final_stage(sums, v1, v2, fg, mid, smooth, last, tail_x, got_z, got_x, got_y, counts):
@@ -824,7 +810,8 @@
     axes = ("gz", "gx", "gy")
     counts = tuple(lax.axis_size(a) for a in axes)
     devices = counts[0] * counts[1] * counts[2]
-    part, up_z, up_x, up_y, low_z, low_x, low_y = edge_stage(residual, edge_diag)
+    part, *faces, scaled, inverses = edge_stage(residual, edge_diag)
+    up_z, up_x, up_y, low_z, low_x, low_y = faces
     below = (ring(up_z, "gz", 1), ring(up_x, "gx", 1), ring(up_y, "gy", 1))
     fg, rhs, xb, yb, w, *send = nodal_stage(part, node_shift, coarse_shift, *below, low_z, counts[0])
     got_z = swap(send, "gz")
@@ -838,7 +825,7 @@
     tail_x = ring(tail_x, "gx", -1)
     rhs, w, *send = y_stage(got_x, rhs, yb, w, early, counts[1], counts[2])
     got_y = swap(send, "gy")
-    smooth, last = smooth_stage(residual, edge_diag, below, got_z, tail_x, w, counts)
+    smooth, last = smooth_stage(scaled, inverses, below, got_z, tail_x, w, counts)
     v1, v2, sums = coarse_stage(got_y, rhs, w, (last,), counts[2], devices)
     sums = lax.all_to_all(sums, ("gx", "gy", "gz"), 0, 0)
     return final_stage(sums, v1, v2, fg, mid, smooth, last, tail_x, got_z, got_x, got_y, counts)

time: 46.3 us -> 45.5 us (0.983)
  Pallas kernels: 12.4 us -> 11.7 us
    pallas_call x10, Pallas kernels: 12.4 us -> 11.7 us  [apply(): run(*(pltpu.with_memory_space_constraint(a, space) for a, space in zip(ar...]
where the time goes in v6:
time: 45.5 us; the launch traced here: 45.3 us
  starting transfers between devices  14 us (31%)
  Pallas kernels  11.7 us (26%)
  blocking collectives  11.3 us (25%)
  waiting for transfers between devices  8.14 us (18%)
    pallas_call x10, Pallas kernels, apply(): run(*(pltpu.with_memory_space_constraint(a, space) for a, space in zip(ar...  11.7 us
    all_to_all x1, blocking collectives, local(): sums = lax.all_to_all(sums, ('gx', 'gy', 'gz'), 0, 0)  11.3 us
    ppermute x4, starting transfers between devices, ring(): lax.ppermute(value, axis, [(i, (i + step) % size) for i in range(size)])  7.07 us
    ppermute x4, waiting for transfers between devices, ring(): lax.ppermute(value, axis, [(i, (i + step) % size) for i in range(size)])  4.91 us
    ppermute x2, starting transfers between devices, swap(): out.append(lax.ppermute(values[1], axis, odd))  4.59 us
    ppermute x3, starting transfers between devices, swap(): out = [lax.ppermute(values[0], axis, [(i, i ^ 1) for i in range(size)])]  2.36 us
    ppermute x3, waiting for transfers between devices, swap(): out = [lax.ppermute(values[0], axis, [(i, i ^ 1) for i in range(size)])]  1.7 us
    ppermute x2, waiting for transfers between devices, swap(): out.append(lax.ppermute(values[1], axis, odd))  1.53 us
  transfers between devices with their start and end apart: 9, of which 4 were waited for; matrix products, arithmetic and copies ran while one was open for 0% of the time, Pallas kernels for 6%

profile of v6, /device:TPU:0, one launch (start us, length us, event | category | flops | bytes accessed | tf_op | source)
XLA Modules:
  0.0 45.3 jit_solution(13048733801541654777)
XLA Ops:
  0.0 2.8 %shard_map.46 = (f32[16,64,128]{2,1,0:T(8,128)S(1)}, f32[3,64,128]{2,1,0:T(8,128)S(1)}, f32[48,128]{1,0:T(8,128)S(1)}, f32[64,128]{1,0:T(8,128)S(1)}, f32[3,64,1...) custom-call(f32[3,16,64,128]{3,2,1,0:T(8,128)} %res.1, ...), custom_call_target="tpu_custom_call" | custom-call | tf_op jit(solution)/shard_map/pallas_call | solution.py:98
  2.8 0.6 %collective-permute-start = (f32[3,64,128]{2,1,0:T(8,128)S(1)}, f32[3,64,128]{2,1,0:T(8,128)S(1)}, u32[]{:S(2)}, u32[]{:S(2)}) collective-permute-start(f32[3,64,128]{2,1,0:T(8,128)S(1)} %get-tuple-element.41), channel_id=1, source_target_pairs={{0,1},{1,0},{2,3},{3,2},{4,5},{5,4},{6,7},{7,6},{8,9},{9,8},{10,11... | collective-permute-start | bytes 294920 | tf_op jit(solution)/shard_map/ppermute | solution.py:58
  3.4 2.6 %collective-permute-start.2 = (f32[64,128]{1,0:T(8,128)S(1)}, f32[64,128]{1,0:T(8,128)S(1)}, u32[]{:S(2)}, u32[]{:S(2)}) collective-permute-start(f32[64,128]{1,0:T(8,128)S(1)} %get-tuple-element.43), channel_id=1, source_target_pairs={{0,2},{2,4},{4,6},{6,0},{1,3},{3,5},{5,7},{7,1},{8,10},{10,12},{12... | collective-permute-start | bytes 98312 | tf_op jit(solution)/shard_map/ppermute | solution.py:58
  6.0 1.5 %collective-permute-start.1 = (f32[48,128]{1,0:T(8,128)S(1)}, f32[48,128]{1,0:T(8,128)S(1)}, u32[]{:S(2)}, u32[]{:S(2)}) collective-permute-start(f32[48,128]{1,0:T(8,128)S(1)} %get-tuple-element.42), channel_id=1, source_target_pairs={{0,8},{8,16},{16,24},{24,0},{1,9},{9,17},{17,25},{25,1},{2,10},{10... | collective-permute-start | bytes 73736 | tf_op jit(solution)/shard_map/ppermute | solution.py:58
  7.5 3.2 %collective-permute-done.1.gx.refs_3_ = f32[48,128]{1,0:T(8,128)S(1)} collective-permute-done((f32[48,128]{1,0:T(8,128)S(1)}, f32[48,128]{1,0:T(8,128)S(1)}, u32[]{:S(2)}, u32[]{:S(2)}) %collective-permute-start.1) | collective-permute-done | bytes 24608 | tf_op jit(solution)/shard_map/ppermute | solution.py:58
  10.8 1.0 %shard_map.47 = (f32[16,64,128]{2,1,0:T(8,128)S(1)}, f32[12,40,128]{2,1,0:T(8,128)S(1)}, f32[8,40,128]{2,1,0:T(8,128)S(1)}, f32[8,40,128]{2,1,0:T(8,128)S(1)}, f...) custom-call(f32[16,64,128]{2,1,0:T(8,128)S(1)} %get-tuple-element.40.part, f32[16,64,128]{2,1,0:T(8,128)S(1)} %copy-done, ...), custom_call_target="tpu_custom_call" | custom-call | tf_op jit(solution)/shard_map/pallas_call | solution.py:98
  11.7 0.1 collective-permute-start.3
  11.8 1.7 %collective-permute-done.3.refs_0_.refs_5_.refs_9_ = f32[744,128]{1,0:T(8,128)S(1)} collective-permute-done((f32[744,128]{1,0:T(8,128)S(1)}, f32[744,128]{1,0:T(8,128)S(1)}, u32[]{:S(2)}, u32[]{:S(2)}) %collective-permute-start.3) | collective-permute-done | bytes 380960 | tf_op jit(solution)/shard_map/ppermute | solution.py:63
  13.5 0.2 shard_map.48
  13.7 1.0 %collective-permute-start.4 = (f32[56,128]{1,0:T(8,128)S(1)}, f32[56,128]{1,0:T(8,128)S(1)}, u32[]{:S(2)}, u32[]{:S(2)}) collective-permute-start(f32[56,128]{1,0:T(8,128)S(1)} %get-tuple-element.51), channel_id=1, source_target_pairs={{0,8},{8,0},{16,24},{24,16},{1,9},{9,1},{17,25},{25,17},{2,10},{10... | collective-permute-start | bytes 86024 | tf_op jit(solution)/shard_map/ppermute | solution.py:63
  14.6 2.1 %collective-permute-start.5 = (f32[56,128]{1,0:T(8,128)S(1)}, f32[56,128]{1,0:T(8,128)S(1)}, u32[]{:S(2)}, u32[]{:S(2)}) collective-permute-start(f32[56,128]{1,0:T(8,128)S(1)} %get-tuple-element.52), channel_id=1, source_target_pairs={{0,24},{8,16},{16,8},{24,0},{1,25},{9,17},{17,9},{25,1},{2,26},{10... | collective-permute-start | bytes 86024 | tf_op jit(solution)/shard_map/ppermute | solution.py:66
  16.7 0.4 shard_map.51
  17.1 0.1 shard_map.50.refs_9_
  17.2 0.7 %shard_map.49 = (f32[64,128]{1,0:T(8,128)S(1)}, f32[64,128]{1,0:T(8,128)S(1)}, f32[64,128]{1,0:T(8,128)S(1)}, f32[64,128]{1,0:T(8,128)S(1)}) custom-call(f32[744,128]{1,0:T(8,128)S(1)} %collective-permute-done.3.refs_0_.refs_5_.refs_9_, f32[16,64,128]{2,1,0:T(8,128)S(1)} %get-tuple-element.50.refs_5_.refs_1_.refs_3_, f32[16,64,128]{2,1,0:T(8,128)S(1)} %copy-done, ...), custom_call_target="tpu_custom_call" | custom-call | tf_op jit(solution)/shard_map/pallas_call | solution.py:98
  17.9 1.5 %collective-permute-done.5.refs_1_.refs_11_ = f32[56,128]{1,0:T(8,128)S(1)} collective-permute-done((f32[56,128]{1,0:T(8,128)S(1)}, f32[56,128]{1,0:T(8,128)S(1)}, u32[]{:S(2)}, u32[]{:S(2)}) %collective-permute-start.5) | collective-permute-done | bytes 28704 | tf_op jit(solution)/shard_map/ppermute | solution.py:66
  19.4 1.1 %shard_map.52 = (f32[12,40,128]{2,1,0:T(8,128)S(1)}, f32[12,40,128]{2,1,0:T(8,128)S(1)}, f32[104,128]{1,0:T(8,128)S(1)}, f32[104,128]{1,0:T(8,128)S(1)}) custom-call(f32[56,128]{1,0:T(8,128)S(1)} %collective-permute-done.4.refs_0_.refs_10_, f32[56,128]{1,0:T(8,128)S(1)} %collective-permute-done.5.refs_1_.refs_11_, ...), custom_call_target="tpu_custom_call" | custom-call | tf_op jit(solution)/shard_map/pallas_call | solution.py:98
  20.5 1.3 %collective-permute-start.6 = (f32[104,128]{1,0:T(8,128)S(1)}, f32[104,128]{1,0:T(8,128)S(1)}, u32[]{:S(2)}, u32[]{:S(2)}) collective-permute-start(f32[104,128]{1,0:T(8,128)S(1)} %get-tuple-element.63), channel_id=1, source_target_pairs={{0,2},{2,0},{4,6},{6,4},{1,3},{3,1},{5,7},{7,5},{8,10},{10,8},{12,... | collective-permute-start | bytes 159752 | tf_op jit(solution)/shard_map/ppermute | solution.py:63
  21.8 2.5 %collective-permute-start.7 = (f32[104,128]{1,0:T(8,128)S(1)}, f32[104,128]{1,0:T(8,128)S(1)}, u32[]{:S(2)}, u32[]{:S(2)}) collective-permute-start(f32[104,128]{1,0:T(8,128)S(1)} %get-tuple-element.64), channel_id=1, source_target_pairs={{0,6},{2,4},{4,2},{6,0},{1,7},{3,5},{5,3},{7,1},{8,14},{10,12},{12... | collective-permute-start | bytes 159752 | tf_op jit(solution)/shard_map/ppermute | solution.py:66
  24.3 2.4 %collective-permute-start.8 = (f32[80,128]{1,0:T(8,128)S(1)}, f32[80,128]{1,0:T(8,128)S(1)}, u32[]{:S(2)}, u32[]{:S(2)}) collective-permute-start(f32[80,128]{1,0:T(8,128)S(1)} %shard_map.50.refs_9_), channel_id=1, source_target_pairs={{0,24},{8,0},{16,8},{24,16},{1,25},{9,1},{17,9},{25,17},{2,26},{10... | collective-permute-start | bytes 122888 | tf_op jit(solution)/shard_map/ppermute | solution.py:58
  26.7 1.7 %collective-permute-done.8.refs_6_.refs_8_ = f32[80,128]{1,0:T(8,128)S(1)} collective-permute-done((f32[80,128]{1,0:T(8,128)S(1)}, f32[80,128]{1,0:T(8,128)S(1)}, u32[]{:S(2)}, u32[]{:S(2)}) %collective-permute-start.8) | collective-permute-done | bytes 40992 | tf_op jit(solution)/shard_map/ppermute | solution.py:58
  28.4 1.8 %shard_map.53 = (f32[3,16,64,128]{3,2,1,0:T(8,128)S(1)}, f32[64,128]{1,0:T(8,128)S(1)}) custom-call(f32[3,16,64,128]{3,2,1,0:T(8,128)S(1)} %get-tuple-element.67.refs_0_, f32[3,16,64,128]{3,2,1,0:T(8,128)S(1)} %get-tuple-element.68.refs_1_, f32[3,64,128]{2,1,0:T(8,128)S(1)} %collective-permute-done.gz.refs_2_, ...), custom_call_target="tpu_custom_call" | custom-call | tf_op jit(solution)/shard_map/pallas_call | solution.py:98
  30.2 1.0 %shard_map.54 = (f32[12,40,128]{2,1,0:T(8,128)S(1)}, f32[12,40,128]{2,1,0:T(8,128)S(1)}, f32[32,1,128]{2,1,0:T(1,128)S(1)}) custom-call(f32[104,128]{1,0:T(8,128)S(1)} %collective-permute-done.6.refs_0_.refs_12_, f32[104,128]{1,0:T(8,128)S(1)} %collective-permute-done.7.refs_1_.refs_13_, f32[12,40,128]{2,1,0:T(8,128)S(1)} %get-tuple-element.65.refs_2_, ...), custom_call_target="tpu_custom_call" | custom-call | tf_op jit(solution)/shard_map/pallas_call | solution.py:98
  31.2 11.3 %all_to_all.5.refs_0_ = f32[32,1,128]{2,1,0:T(1,128)S(1)} all-to-all(f32[32,1,128]{2,1,0:T(1,128)S(1)} %get-tuple-element.70), channel_id=1, replica_groups=mesh['gx'=4,'gy'=4,'gz'=2] {'gx','gy','gz'}, dimensions={0} | all-to-all | bytes 32768 | tf_op jit(solution)/shard_map/all_to_all | solution.py:830
  42.5 2.7 %shard_map.55 = f32[3,16,64,128]{3,2,1,0:T(8,128)} custom-call(f32[32,1,128]{2,1,0:T(1,128)S(1)} %all_to_all.5.refs_0_, f32[12,40,128]{2,1,0:T(8,128)S(1)} %get-tuple-element.71.refs_1_, f32[12,40,128]{2,1,0:T(8,128)S(1)} %get-tuple-element.72.refs_2_, f32[16,64,128]{2,1,0:T(8,128)S(1)} %get-tuple-element.50.refs_5_.refs_1_.refs_3_, ...), custom_call_target="tpu_custom_call" | custom-call | tf_op jit(solution)/shard_map/pallas_call | solution.py:98
  (9 shorter events, 0.0 us)
Async XLA Ops:
  0.0 10.7 %copy-start = (f32[16,64,128]{2,1,0:T(8,128)S(1)}, f32[16,64,128]{2,1,0:T(8,128)}, u32[]{:S(2)}) copy-start(f32[16,64,128]{2,1,0:T(8,128)} %refs_2_.5) | copy-start | bytes 1572868
  0.0 10.8 %copy-start.1 = (f32[8,32,64]{2,1,0:T(8,128)S(1)}, f32[8,32,64]{2,1,0:T(8,128)}, u32[]{:S(2)}) copy-start(f32[8,32,64]{2,1,0:T(8,128)} %coarse.1) | copy-start | bytes 196612
  2.8 7.9 %collective-permute-start = (f32[3,64,128]{2,1,0:T(8,128)S(1)}, f32[3,64,128]{2,1,0:T(8,128)S(1)}, u32[]{:S(2)}, u32[]{:S(2)}) collective-permute-start(f32[3,64,128]{2,1,0:T(8,128)S(1)} %get-tuple-element.41), channel_id=1, source_target_pairs={{0,1},{1,0},{2,3},{3,2},{4,5},{5,4},{6,7},{7,6},{8,9},{9,8},{10,11... | collective-permute-start | bytes 294920 | tf_op jit(solution)/shard_map/ppermute | solution.py:58
  3.4 7.4 %collective-permute-start.2 = (f32[64,128]{1,0:T(8,128)S(1)}, f32[64,128]{1,0:T(8,128)S(1)}, u32[]{:S(2)}, u32[]{:S(2)}) collective-permute-start(f32[64,128]{1,0:T(8,128)S(1)} %get-tuple-element.43), channel_id=1, source_target_pairs={{0,2},{2,4},{4,6},{6,0},{1,3},{3,5},{5,7},{7,1},{8,10},{10,12},{12... | collective-permute-start | bytes 98312 | tf_op jit(solution)/shard_map/ppermute | solution.py:58
  6.0 4.7 %collective-permute-start.1 = (f32[48,128]{1,0:T(8,128)S(1)}, f32[48,128]{1,0:T(8,128)S(1)}, u32[]{:S(2)}, u32[]{:S(2)}) collective-permute-start(f32[48,128]{1,0:T(8,128)S(1)} %get-tuple-element.42), channel_id=1, source_target_pairs={{0,8},{8,16},{16,24},{24,0},{1,9},{9,17},{17,25},{25,1},{2,10},{10... | collective-permute-start | bytes 73736 | tf_op jit(solution)/shard_map/ppermute | solution.py:58
  11.7 1.8 %collective-permute-start.3 = (f32[744,128]{1,0:T(8,128)S(1)}, f32[744,128]{1,0:T(8,128)S(1)}, u32[]{:S(2)}, u32[]{:S(2)}) collective-permute-start(f32[744,128]{1,0:T(8,128)S(1)} %get-tuple-element.45), channel_id=1, source_target_pairs={{0,1},{1,0},{2,3},{3,2},{4,5},{5,4},{6,7},{7,6},{8,9},{9,8},{10,11... | collective-permute-start | bytes 1142792 | tf_op jit(solution)/shard_map/ppermute | solution.py:63
  13.7 4.2 %collective-permute-start.4 = (f32[56,128]{1,0:T(8,128)S(1)}, f32[56,128]{1,0:T(8,128)S(1)}, u32[]{:S(2)}, u32[]{:S(2)}) collective-permute-start(f32[56,128]{1,0:T(8,128)S(1)} %get-tuple-element.51), channel_id=1, source_target_pairs={{0,8},{8,0},{16,24},{24,16},{1,9},{9,1},{17,25},{25,17},{2,10},{10... | collective-permute-start | bytes 86024 | tf_op jit(solution)/shard_map/ppermute | solution.py:63
  14.6 4.8 %collective-permute-start.5 = (f32[56,128]{1,0:T(8,128)S(1)}, f32[56,128]{1,0:T(8,128)S(1)}, u32[]{:S(2)}, u32[]{:S(2)}) collective-permute-start(f32[56,128]{1,0:T(8,128)S(1)} %get-tuple-element.52), channel_id=1, source_target_pairs={{0,24},{8,16},{16,8},{24,0},{1,25},{9,17},{17,9},{25,1},{2,26},{10... | collective-permute-start | bytes 86024 | tf_op jit(solution)/shard_map/ppermute | solution.py:66
  20.5 9.7 %collective-permute-start.6 = (f32[104,128]{1,0:T(8,128)S(1)}, f32[104,128]{1,0:T(8,128)S(1)}, u32[]{:S(2)}, u32[]{:S(2)}) collective-permute-start(f32[104,128]{1,0:T(8,128)S(1)} %get-tuple-element.63), channel_id=1, source_target_pairs={{0,2},{2,0},{4,6},{6,4},{1,3},{3,1},{5,7},{7,5},{8,10},{10,8},{12,... | collective-permute-start | bytes 159752 | tf_op jit(solution)/shard_map/ppermute | solution.py:63
  21.8 8.4 %collective-permute-start.7 = (f32[104,128]{1,0:T(8,128)S(1)}, f32[104,128]{1,0:T(8,128)S(1)}, u32[]{:S(2)}, u32[]{:S(2)}) collective-permute-start(f32[104,128]{1,0:T(8,128)S(1)} %get-tuple-element.64), channel_id=1, source_target_pairs={{0,6},{2,4},{4,2},{6,0},{1,7},{3,5},{5,3},{7,1},{8,14},{10,12},{12... | collective-permute-start | bytes 159752 | tf_op jit(solution)/shard_map/ppermute | solution.py:66
  24.3 4.1 %collective-permute-start.8 = (f32[80,128]{1,0:T(8,128)S(1)}, f32[80,128]{1,0:T(8,128)S(1)}, u32[]{:S(2)}, u32[]{:S(2)}) collective-permute-start(f32[80,128]{1,0:T(8,128)S(1)} %shard_map.50.refs_9_), channel_id=1, source_target_pairs={{0,24},{8,0},{16,8},{24,16},{1,25},{9,1},{17,9},{25,17},{2,26},{10... | collective-permute-start | bytes 122888 | tf_op jit(solution)/shard_map/ppermute | solution.py:58

commit v7 on v6

--- a/solution.py
+++ b/solution.py
@@ -1,3 +1,5 @@
+import itertools
+
 import jax
 import jax.numpy as jnp
 from jax import lax
@@ -58,12 +60,26 @@
     return lax.ppermute(value, axis, [(i, (i + step) % size) for i in range(size)])
 
 
-def swap(values, axis):
+def swap(values, axis, names=None):
     size = lax.axis_size(axis)
     out = [lax.ppermute(values[0], axis, [(i, i ^ 1) for i in range(size)])]
-    if len(values) > 1:
-        odd = [(i, (i + 1) % size if i % 2 else (i - 1) % size) for i in range(size)]
-        out.append(lax.ppermute(values[1], axis, odd))
+    if len(values) == 1:
+        return out
+    odd = [(i + 1) % size if i % 2 else (i - 1) % size for i in range(size)]
+    if names is None:
+        out.append(lax.ppermute(values[1], axis, list(enumerate(odd))))
+        return out
+    main = names.index(axis)
+    pairs = []
+    sizes = [lax.axis_size(name) for name in names]
+    for at in itertools.product(*(range(n) for n in sizes)):
+        to = list(at)
+        if at[main] in (0, size - 1):
+            to[1 - main] ^= 1
+        else:
+            to[main] = odd[at[main]]
+        pairs.append(tuple(p[0] * sizes[1] + p[1] for p in (at, to)))
+    out.append(lax.ppermute(values[1], names, pairs))
     return out
 
 
@@ -812,11 +828,13 @@
     devices = counts[0] * counts[1] * counts[2]
     part, *faces, scaled, inverses = edge_stage(residual, edge_diag)
     up_z, up_x, up_y, low_z, low_x, low_y = faces
-    below = (ring(up_z, "gz", 1), ring(up_x, "gx", 1), ring(up_y, "gy", 1))
+    below = []
+    for value, axis in ((up_z, "gz"), (up_x, "gx"), (up_y, "gy")):
+        below.append(ring(value, axis, 1))
     fg, rhs, xb, yb, w, *send = nodal_stage(part, node_shift, coarse_shift, *below, low_z, counts[0])
     got_z = swap(send, "gz")
     rhs, yb, w, *send = x_stage(got_z, rhs, xb, yb, w, fg, counts[0], counts[1])
-    got_x = swap(send, "gx")
+    got_x = swap(send, "gx", ("gx", "gy"))
     planes = rhs.shape[0]
     tail_x = x_tail(got_z, fg, node_shift, low_x, w, counts[0])
     mid = part_stage(got_z, fg, node_shift, w, counts[0])
@@ -824,7 +842,7 @@
     early = (*early, tail_x, mid[1])
     tail_x = ring(tail_x, "gx", -1)
     rhs, w, *send = y_stage(got_x, rhs, yb, w, early, counts[1], counts[2])
-    got_y = swap(send, "gy")
+    got_y = swap(send, "gy", ("gx", "gy"))
     smooth, last = smooth_stage(scaled, inverses, below, got_z, tail_x, w, counts)
     v1, v2, sums = coarse_stage(got_y, rhs, w, (last,), counts[2], devices)
     sums = lax.all_to_all(sums, ("gx", "gy", "gz"), 0, 0)

time: 45.5 us -> 44.7 us (0.982)
  starting transfers between devices: 14 us -> 12.2 us
  waiting for transfers between devices: 8.14 us -> 8.84 us
    ppermute x2, starting transfers between devices: 4.59 us -> 3.62 us  [swap(): out.append(lax.ppermute(values[1], names, pairs))]
    ppermute x4, starting transfers between devices: 7.07 us -> 6.22 us  [ring(): lax.ppermute(value, axis, [(i, (i + step) % size) for i in range(size)])]
    ppermute x4, waiting for transfers between devices: 4.91 us -> 5.7 us  [ring(): lax.ppermute(value, axis, [(i, (i + step) % size) for i in range(size)])]
    ppermute x2, waiting for transfers between devices: 1.53 us -> 0.89 us  [swap(): out.append(lax.ppermute(values[1], names, pairs))]
    ppermute x3, waiting for transfers between devices: 1.7 us -> 2.25 us  [swap(): out = [lax.ppermute(values[0], axis, [(i, i ^ 1) for i in range(size)])]]
  transfers between devices with their start and end apart: 9 -> 9, of which waited for: 4 -> 5; matrix products, arithmetic and copies ran while one was open for 0% -> 0% of each run, Pallas kernels for 6% -> 7%
where the time goes in v7:
time: 44.7 us; the launch traced here: 44.6 us
  starting transfers between devices  12.2 us (27%)
  Pallas kernels  11.7 us (26%)
  blocking collectives  11.7 us (26%)
  waiting for transfers between devices  8.84 us (20%)
    all_to_all x1, blocking collectives, local(): sums = lax.all_to_all(sums, ('gx', 'gy', 'gz'), 0, 0)  11.7 us
    pallas_call x10, Pallas kernels, apply(): run(*(pltpu.with_memory_space_constraint(a, space) for a, space in zip(ar...  11.7 us
    ppermute x4, starting transfers between devices, ring(): lax.ppermute(value, axis, [(i, (i + step) % size) for i in range(size)])  6.22 us
    ppermute x4, waiting for transfers between devices, ring(): lax.ppermute(value, axis, [(i, (i + step) % size) for i in range(size)])  5.7 us
    ppermute x2, starting transfers between devices, swap(): out.append(lax.ppermute(values[1], names, pairs))  3.62 us
    ppermute x3, starting transfers between devices, swap(): out = [lax.ppermute(values[0], axis, [(i, i ^ 1) for i in range(size)])]  2.36 us
    ppermute x3, waiting for transfers between devices, swap(): out = [lax.ppermute(values[0], axis, [(i, i ^ 1) for i in range(size)])]  2.25 us
  transfers between devices with their start and end apart: 9, of which 5 were waited for; matrix products, arithmetic and copies ran while one was open for 0% of the time, Pallas kernels for 7%

profile of v7, /device:TPU:0, one launch (start us, length us, event | category | flops | bytes accessed | tf_op | source)
XLA Modules:
  0.0 44.6 jit_solution(9040762122809791095)
XLA Ops:
  0.0 2.8 %shard_map.46 = (f32[16,64,128]{2,1,0:T(8,128)S(1)}, f32[3,64,128]{2,1,0:T(8,128)S(1)}, f32[48,128]{1,0:T(8,128)S(1)}, f32[64,128]{1,0:T(8,128)S(1)}, f32[3,64,1...) custom-call(f32[3,16,64,128]{3,2,1,0:T(8,128)} %res.1, ...), custom_call_target="tpu_custom_call" | custom-call | tf_op jit(solution)/shard_map/pallas_call | solution.py:114
  2.8 0.6 %collective-permute-start = (f32[3,64,128]{2,1,0:T(8,128)S(1)}, f32[3,64,128]{2,1,0:T(8,128)S(1)}, u32[]{:S(2)}, u32[]{:S(2)}) collective-permute-start(f32[3,64,128]{2,1,0:T(8,128)S(1)} %get-tuple-element.41), channel_id=1, source_target_pairs={{0,1},{1,0},{2,3},{3,2},{4,5},{5,4},{6,7},{7,6},{8,9},{9,8},{10,11... | collective-permute-start | bytes 294920 | tf_op jit(solution)/shard_map/ppermute | solution.py:60
  3.4 2.6 %collective-permute-start.2 = (f32[64,128]{1,0:T(8,128)S(1)}, f32[64,128]{1,0:T(8,128)S(1)}, u32[]{:S(2)}, u32[]{:S(2)}) collective-permute-start(f32[64,128]{1,0:T(8,128)S(1)} %get-tuple-element.43), channel_id=1, source_target_pairs={{0,2},{2,4},{4,6},{6,0},{1,3},{3,5},{5,7},{7,1},{8,10},{10,12},{12... | collective-permute-start | bytes 98312 | tf_op jit(solution)/shard_map/ppermute | solution.py:60
  6.0 1.5 %collective-permute-start.1 = (f32[48,128]{1,0:T(8,128)S(1)}, f32[48,128]{1,0:T(8,128)S(1)}, u32[]{:S(2)}, u32[]{:S(2)}) collective-permute-start(f32[48,128]{1,0:T(8,128)S(1)} %get-tuple-element.42), channel_id=1, source_target_pairs={{0,8},{8,16},{16,24},{24,0},{1,9},{9,17},{17,25},{25,1},{2,10},{10... | collective-permute-start | bytes 73736 | tf_op jit(solution)/shard_map/ppermute | solution.py:60
  7.5 3.2 %collective-permute-done.1.gx.refs_3_ = f32[48,128]{1,0:T(8,128)S(1)} collective-permute-done((f32[48,128]{1,0:T(8,128)S(1)}, f32[48,128]{1,0:T(8,128)S(1)}, u32[]{:S(2)}, u32[]{:S(2)}) %collective-permute-start.1) | collective-permute-done | bytes 24608 | tf_op jit(solution)/shard_map/ppermute | solution.py:60
  10.8 1.0 %shard_map.47 = (f32[16,64,128]{2,1,0:T(8,128)S(1)}, f32[12,40,128]{2,1,0:T(8,128)S(1)}, f32[8,40,128]{2,1,0:T(8,128)S(1)}, f32[8,40,128]{2,1,0:T(8,128)S(1)}, f...) custom-call(f32[16,64,128]{2,1,0:T(8,128)S(1)} %get-tuple-element.40.part, f32[16,64,128]{2,1,0:T(8,128)S(1)} %copy-done, ...), custom_call_target="tpu_custom_call" | custom-call | tf_op jit(solution)/shard_map/pallas_call | solution.py:114
  11.8 1.7 %collective-permute-done.3.refs_0_.refs_5_.refs_9_ = f32[744,128]{1,0:T(8,128)S(1)} collective-permute-done((f32[744,128]{1,0:T(8,128)S(1)}, f32[744,128]{1,0:T(8,128)S(1)}, u32[]{:S(2)}, u32[]{:S(2)}) %collective-permute-start.3) | collective-permute-done | bytes 380960 | tf_op jit(solution)/shard_map/ppermute | solution.py:65
  13.5 0.2 shard_map.48
  13.7 1.0 %collective-permute-start.4 = (f32[56,128]{1,0:T(8,128)S(1)}, f32[56,128]{1,0:T(8,128)S(1)}, u32[]{:S(2)}, u32[]{:S(2)}) collective-permute-start(f32[56,128]{1,0:T(8,128)S(1)} %get-tuple-element.51), channel_id=1, source_target_pairs={{0,8},{8,0},{16,24},{24,16},{1,9},{9,1},{17,25},{25,17},{2,10},{10... | collective-permute-start | bytes 86024 | tf_op jit(solution)/shard_map/ppermute | solution.py:65
  14.6 1.3 %collective-permute-start.5 = (f32[56,128]{1,0:T(8,128)S(1)}, f32[56,128]{1,0:T(8,128)S(1)}, u32[]{:S(2)}, u32[]{:S(2)}) collective-permute-start(f32[56,128]{1,0:T(8,128)S(1)} %get-tuple-element.52), channel_id=1, source_target_pairs={{0,2},{2,0},{4,6},{6,4},{8,16},{10,18},{12,20},{14,22},{16,8},{18,... | collective-permute-start | bytes 86024 | tf_op jit(solution)/shard_map/ppermute | solution.py:82
  15.9 0.4 shard_map.51
  16.3 0.1 shard_map.50.refs_9_
  16.4 0.7 %shard_map.49 = (f32[64,128]{1,0:T(8,128)S(1)}, f32[64,128]{1,0:T(8,128)S(1)}, f32[64,128]{1,0:T(8,128)S(1)}, f32[64,128]{1,0:T(8,128)S(1)}) custom-call(f32[744,128]{1,0:T(8,128)S(1)} %collective-permute-done.3.refs_0_.refs_5_.refs_9_, f32[16,64,128]{2,1,0:T(8,128)S(1)} %get-tuple-element.50.refs_5_.refs_1_.refs_3_, f32[16,64,128]{2,1,0:T(8,128)S(1)} %copy-done, ...), custom_call_target="tpu_custom_call" | custom-call | tf_op jit(solution)/shard_map/pallas_call | solution.py:114
  17.1 0.6 %collective-permute-done.4.refs_0_.refs_10_ = f32[56,128]{1,0:T(8,128)S(1)} collective-permute-done((f32[56,128]{1,0:T(8,128)S(1)}, f32[56,128]{1,0:T(8,128)S(1)}, u32[]{:S(2)}, u32[]{:S(2)}) %collective-permute-start.4) | collective-permute-done | bytes 28704 | tf_op jit(solution)/shard_map/ppermute | solution.py:65
  17.6 0.9 %collective-permute-done.5.refs_1_.refs_11_ = f32[56,128]{1,0:T(8,128)S(1)} collective-permute-done((f32[56,128]{1,0:T(8,128)S(1)}, f32[56,128]{1,0:T(8,128)S(1)}, u32[]{:S(2)}, u32[]{:S(2)}) %collective-permute-start.5) | collective-permute-done | bytes 28704 | tf_op jit(solution)/shard_map/ppermute | solution.py:82
  18.5 1.1 %shard_map.52 = (f32[12,40,128]{2,1,0:T(8,128)S(1)}, f32[12,40,128]{2,1,0:T(8,128)S(1)}, f32[104,128]{1,0:T(8,128)S(1)}, f32[104,128]{1,0:T(8,128)S(1)}) custom-call(f32[56,128]{1,0:T(8,128)S(1)} %collective-permute-done.4.refs_0_.refs_10_, f32[56,128]{1,0:T(8,128)S(1)} %collective-permute-done.5.refs_1_.refs_11_, ...), custom_call_target="tpu_custom_call" | custom-call | tf_op jit(solution)/shard_map/pallas_call | solution.py:114
  19.6 1.3 %collective-permute-start.6 = (f32[104,128]{1,0:T(8,128)S(1)}, f32[104,128]{1,0:T(8,128)S(1)}, u32[]{:S(2)}, u32[]{:S(2)}) collective-permute-start(f32[104,128]{1,0:T(8,128)S(1)} %get-tuple-element.63), channel_id=1, source_target_pairs={{0,2},{2,0},{4,6},{6,4},{1,3},{3,1},{5,7},{7,5},{8,10},{10,8},{12,... | collective-permute-start | bytes 159752 | tf_op jit(solution)/shard_map/ppermute | solution.py:65
  20.9 2.3 %collective-permute-start.7 = (f32[104,128]{1,0:T(8,128)S(1)}, f32[104,128]{1,0:T(8,128)S(1)}, u32[]{:S(2)}, u32[]{:S(2)}) collective-permute-start(f32[104,128]{1,0:T(8,128)S(1)} %get-tuple-element.64), channel_id=1, source_target_pairs={{0,8},{2,4},{4,2},{6,14},{8,0},{10,12},{12,10},{14,6},{16,24},{18,... | collective-permute-start | bytes 159752 | tf_op jit(solution)/shard_map/ppermute | solution.py:82
  23.3 1.5 %collective-permute-start.8 = (f32[80,128]{1,0:T(8,128)S(1)}, f32[80,128]{1,0:T(8,128)S(1)}, u32[]{:S(2)}, u32[]{:S(2)}) collective-permute-start(f32[80,128]{1,0:T(8,128)S(1)} %shard_map.50.refs_9_), channel_id=1, source_target_pairs={{0,24},{8,0},{16,8},{24,16},{1,25},{9,1},{17,9},{25,17},{2,26},{10... | collective-permute-start | bytes 122888 | tf_op jit(solution)/shard_map/ppermute | solution.py:60
  24.8 2.5 %collective-permute-done.8.refs_6_.refs_8_ = f32[80,128]{1,0:T(8,128)S(1)} collective-permute-done((f32[80,128]{1,0:T(8,128)S(1)}, f32[80,128]{1,0:T(8,128)S(1)}, u32[]{:S(2)}, u32[]{:S(2)}) %collective-permute-start.8) | collective-permute-done | bytes 40992 | tf_op jit(solution)/shard_map/ppermute | solution.py:60
  27.3 1.8 %shard_map.53 = (f32[3,16,64,128]{3,2,1,0:T(8,128)S(1)}, f32[64,128]{1,0:T(8,128)S(1)}) custom-call(f32[3,16,64,128]{3,2,1,0:T(8,128)S(1)} %get-tuple-element.67.refs_0_, f32[3,16,64,128]{3,2,1,0:T(8,128)S(1)} %get-tuple-element.68.refs_1_, f32[3,64,128]{2,1,0:T(8,128)S(1)} %collective-permute-done.gz.refs_2_, ...), custom_call_target="tpu_custom_call" | custom-call | tf_op jit(solution)/shard_map/pallas_call | solution.py:114
  29.1 1.0 %shard_map.54 = (f32[12,40,128]{2,1,0:T(8,128)S(1)}, f32[12,40,128]{2,1,0:T(8,128)S(1)}, f32[32,1,128]{2,1,0:T(1,128)S(1)}) custom-call(f32[104,128]{1,0:T(8,128)S(1)} %collective-permute-done.6.refs_0_.refs_12_, f32[104,128]{1,0:T(8,128)S(1)} %collective-permute-done.7.refs_1_.refs_13_, f32[12,40,128]{2,1,0:T(8,128)S(1)} %get-tuple-element.65.refs_2_, ...), custom_call_target="tpu_custom_call" | custom-call | tf_op jit(solution)/shard_map/pallas_call | solution.py:114
  30.1 11.7 %all_to_all.5.refs_0_ = f32[32,1,128]{2,1,0:T(1,128)S(1)} all-to-all(f32[32,1,128]{2,1,0:T(1,128)S(1)} %get-tuple-element.70), channel_id=1, replica_groups=mesh['gx'=4,'gy'=4,'gz'=2] {'gx','gy','gz'}, dimensions={0} | all-to-all | bytes 32768 | tf_op jit(solution)/shard_map/all_to_all | solution.py:848
  41.8 2.7 %shard_map.55 = f32[3,16,64,128]{3,2,1,0:T(8,128)} custom-call(f32[32,1,128]{2,1,0:T(1,128)S(1)} %all_to_all.5.refs_0_, f32[12,40,128]{2,1,0:T(8,128)S(1)} %get-tuple-element.71.refs_1_, f32[12,40,128]{2,1,0:T(8,128)S(1)} %get-tuple-element.72.refs_2_, f32[16,64,128]{2,1,0:T(8,128)S(1)} %get-tuple-element.50.refs_5_.refs_1_.refs_3_, ...), custom_call_target="tpu_custom_call" | custom-call | tf_op jit(solution)/shard_map/pallas_call | solution.py:114
  (9 shorter events, 0.1 us)
Async XLA Ops:
  0.0 10.7 %copy-start = (f32[16,64,128]{2,1,0:T(8,128)S(1)}, f32[16,64,128]{2,1,0:T(8,128)}, u32[]{:S(2)}) copy-start(f32[16,64,128]{2,1,0:T(8,128)} %refs_2_.5) | copy-start | bytes 1572868
  0.0 10.8 %copy-start.1 = (f32[8,32,64]{2,1,0:T(8,128)S(1)}, f32[8,32,64]{2,1,0:T(8,128)}, u32[]{:S(2)}) copy-start(f32[8,32,64]{2,1,0:T(8,128)} %coarse.1) | copy-start | bytes 196612
  2.8 7.9 %collective-permute-start = (f32[3,64,128]{2,1,0:T(8,128)S(1)}, f32[3,64,128]{2,1,0:T(8,128)S(1)}, u32[]{:S(2)}, u32[]{:S(2)}) collective-permute-start(f32[3,64,128]{2,1,0:T(8,128)S(1)} %get-tuple-element.41), channel_id=1, source_target_pairs={{0,1},{1,0},{2,3},{3,2},{4,5},{5,4},{6,7},{7,6},{8,9},{9,8},{10,11... | collective-permute-start | bytes 294920 | tf_op jit(solution)/shard_map/ppermute | solution.py:60
  3.4 7.4 %collective-permute-start.2 = (f32[64,128]{1,0:T(8,128)S(1)}, f32[64,128]{1,0:T(8,128)S(1)}, u32[]{:S(2)}, u32[]{:S(2)}) collective-permute-start(f32[64,128]{1,0:T(8,128)S(1)} %get-tuple-element.43), channel_id=1, source_target_pairs={{0,2},{2,4},{4,6},{6,0},{1,3},{3,5},{5,7},{7,1},{8,10},{10,12},{12... | collective-permute-start | bytes 98312 | tf_op jit(solution)/shard_map/ppermute | solution.py:60
  6.0 4.7 %collective-permute-start.1 = (f32[48,128]{1,0:T(8,128)S(1)}, f32[48,128]{1,0:T(8,128)S(1)}, u32[]{:S(2)}, u32[]{:S(2)}) collective-permute-start(f32[48,128]{1,0:T(8,128)S(1)} %get-tuple-element.42), channel_id=1, source_target_pairs={{0,8},{8,16},{16,24},{24,0},{1,9},{9,17},{17,25},{25,1},{2,10},{10... | collective-permute-start | bytes 73736 | tf_op jit(solution)/shard_map/ppermute | solution.py:60
  11.7 1.8 %collective-permute-start.3 = (f32[744,128]{1,0:T(8,128)S(1)}, f32[744,128]{1,0:T(8,128)S(1)}, u32[]{:S(2)}, u32[]{:S(2)}) collective-permute-start(f32[744,128]{1,0:T(8,128)S(1)} %get-tuple-element.45), channel_id=1, source_target_pairs={{0,1},{1,0},{2,3},{3,2},{4,5},{5,4},{6,7},{7,6},{8,9},{9,8},{10,11... | collective-permute-start | bytes 1142792 | tf_op jit(solution)/shard_map/ppermute | solution.py:65
  13.7 3.9 %collective-permute-start.4 = (f32[56,128]{1,0:T(8,128)S(1)}, f32[56,128]{1,0:T(8,128)S(1)}, u32[]{:S(2)}, u32[]{:S(2)}) collective-permute-start(f32[56,128]{1,0:T(8,128)S(1)} %get-tuple-element.51), channel_id=1, source_target_pairs={{0,8},{8,0},{16,24},{24,16},{1,9},{9,1},{17,25},{25,17},{2,10},{10... | collective-permute-start | bytes 86024 | tf_op jit(solution)/shard_map/ppermute | solution.py:65
  14.6 3.9 %collective-permute-start.5 = (f32[56,128]{1,0:T(8,128)S(1)}, f32[56,128]{1,0:T(8,128)S(1)}, u32[]{:S(2)}, u32[]{:S(2)}) collective-permute-start(f32[56,128]{1,0:T(8,128)S(1)} %get-tuple-element.52), channel_id=1, source_target_pairs={{0,2},{2,0},{4,6},{6,4},{8,16},{10,18},{12,20},{14,22},{16,8},{18,... | collective-permute-start | bytes 86024 | tf_op jit(solution)/shard_map/ppermute | solution.py:82
  19.6 9.5 %collective-permute-start.6 = (f32[104,128]{1,0:T(8,128)S(1)}, f32[104,128]{1,0:T(8,128)S(1)}, u32[]{:S(2)}, u32[]{:S(2)}) collective-permute-start(f32[104,128]{1,0:T(8,128)S(1)} %get-tuple-element.63), channel_id=1, source_target_pairs={{0,2},{2,0},{4,6},{6,4},{1,3},{3,1},{5,7},{7,5},{8,10},{10,8},{12,... | collective-permute-start | bytes 159752 | tf_op jit(solution)/shard_map/ppermute | solution.py:65
  20.9 8.2 %collective-permute-start.7 = (f32[104,128]{1,0:T(8,128)S(1)}, f32[104,128]{1,0:T(8,128)S(1)}, u32[]{:S(2)}, u32[]{:S(2)}) collective-permute-start(f32[104,128]{1,0:T(8,128)S(1)} %get-tuple-element.64), channel_id=1, source_target_pairs={{0,8},{2,4},{4,2},{6,14},{8,0},{10,12},{12,10},{14,6},{16,24},{18,... | collective-permute-start | bytes 159752 | tf_op jit(solution)/shard_map/ppermute | solution.py:82
  23.3 4.0 %collective-permute-start.8 = (f32[80,128]{1,0:T(8,128)S(1)}, f32[80,128]{1,0:T(8,128)S(1)}, u32[]{:S(2)}, u32[]{:S(2)}) collective-permute-start(f32[80,128]{1,0:T(8,128)S(1)} %shard_map.50.refs_9_), channel_id=1, source_target_pairs={{0,24},{8,0},{16,8},{24,16},{1,25},{9,1},{17,9},{25,17},{2,26},{10... | collective-permute-start | bytes 122888 | tf_op jit(solution)/shard_map/ppermute | solution.py:60

commit v8 on v7

--- a/solution.py
+++ b/solution.py
@@ -190,13 +190,13 @@
     return jnp.concatenate([values, jnp.zeros((row_count - values.shape[0], LANES), F32)], axis=0)
 
 
-def nodal_stage(part, node_shift, coarse_shift, got_z, got_x, got_y, low_z, z_count):
+def nodal_stage(part, node_shift, coarse_shift, got_z, got_x, got_y, z_count):
     nz, nx, ny = part.shape
     cz, cx, cy = nz // 2, nx // 2, ny // 2
     rows = cx + 8
     sends = 1 if z_count == 2 else 2
 
-    def body(part, shift, coarse, gz, gx, gy, low_z, fg, rhs, xb, yb, w, *rest):
+    def body(part, shift, coarse, gz, gx, gy, fg, rhs, xb, yb, w, *rest):
         out, (pair, s_, xl_, yl_, zl_, zh_) = rest[:sends], rest[sends:]
         lane = lane_ids(nx)
         row = row_ids(nx)
@@ -262,36 +262,23 @@
                 ref[i * rows : (i + 1) * rows, :] = value
             ref[9 * rows : 9 * rows + nx, :] = face
 
-        def tail(ref, values):
-            for i, value in enumerate(values):
-                at = 9 * rows + nx + i * nx
-                ref[at : at + nx, :] = value
-
         def up(ref):
             fill(ref, cz - 1, cz - 2, zh_[cz - 1], fg[nz - 1])
-            tail(ref, [jnp.zeros((nx, LANES), F32)] * 5)
 
         def down(ref):
             fill(ref, 0, 1, zl_[0], fg[0])
-            here = fg[0]
-            around = fg[1] + jnp.where(row == 0, 0.0, shift_rows(here, 1))
-            around += jnp.where(row == nx - 1, 0.0, shift_rows(here, -1))
-            around += jnp.where(lane == 0, 0.0, shift_lanes(here, 1))
-            around += jnp.where(lane == ny - 1, 0.0, shift_lanes(here, -1))
-            inverse = 1.0 / (6.0 + shift[0])
-            tail(ref, [low_z[0], low_z[1], low_z[2], here + inverse * around, inverse])
 
         write_sides("gz", out, up, down)
 
     coarse = (cz, rows, LANES)
-    send = (9 * rows + 6 * nx, LANES)
+    send = (9 * rows + nx, LANES)
     return call(
         body,
         [(nz, nx, ny), (cz + 4, rows, LANES), coarse, coarse, coarse] + [send] * sends,
         scratch=[(2, nx, ny), coarse, coarse, coarse, coarse, coarse],
-        in_specs=vmem(7),
+        in_specs=vmem(6),
         out_specs=vmem(5 + sends),
-    )(part, node_shift, coarse_shift, got_z, got_x, got_y, low_z)
+    )(part, node_shift, coarse_shift, got_z, got_x, got_y)
 
 
 def x_stage(got, rhs, xb, yb, w, fg, z_count, x_count):
@@ -305,8 +292,8 @@
 
     def body(*refs):
         got = refs[:gots]
-        rhs, xb, yb, w, fg, rhs2, yb2, w2 = refs[gots : gots + 8]
-        out, (xb2,) = refs[gots + 8 : gots + 8 + sends], refs[gots + 8 + sends :]
+        rhs, xb, yb, w, fg, rhs2, w2 = refs[gots : gots + 7]
+        out, (xb2, yb2) = refs[gots + 7 : gots + 7 + sends], refs[gots + 7 + sends :]
 
         def take_at(pick, at):
             values = [ref[at, :] for ref in got]
@@ -360,10 +347,10 @@
     whole = (planes, rows, LANES)
     return call(
         body,
-        [whole, whole, whole] + [(size, LANES)] * sends,
-        scratch=[whole],
+        [whole, whole] + [(size, LANES)] * sends,
+        scratch=[whole, whole],
         in_specs=vmem(gots + 5),
-        out_specs=vmem(3 + sends),
+        out_specs=vmem(2 + sends),
     )(*got, rhs, xb, yb, w, fg)
 
 
@@ -397,14 +384,14 @@
     )(*got, fg, node_shift, low_x, after)[0]
 
 
-def part_stage(got, fg, node_shift, after, z_count):
+def part_stage(got, fg, node_shift, low_z, after, z_count):
     nz, nx, ny = fg.shape
     z_at = 9 * (nx // 2 + 8)
     gots = len(got)
 
     def body(*refs):
         got = refs[:gots]
-        fg, shift, _, part, inv = refs[gots:]
+        fg, shift, low_z, _, part, inv, tail = refs[gots:]
         lane = lane_ids(nx)
         row = row_ids(nx)
 
@@ -414,19 +401,23 @@
 
         for z in range(nz):
             guess = fg[z]
-            around = fg[z - 1] if z > 0 else z_face(low_of)
-            around += fg[z + 1] if z < nz - 1 else z_face(high_of)
-            around += jnp.where(row == 0, 0.0, shift_rows(guess, 1))
-            around += jnp.where(row == nx - 1, 0.0, shift_rows(guess, -1))
-            around += jnp.where(lane == 0, 0.0, shift_lanes(guess, 1))
-            around += jnp.where(lane == ny - 1, 0.0, shift_lanes(guess, -1))
+            inner = fg[z + 1] if z < nz - 1 else z_face(high_of)
+            inner += jnp.where(row == 0, 0.0, shift_rows(guess, 1))
+            inner += jnp.where(row == nx - 1, 0.0, shift_rows(guess, -1))
+            inner += jnp.where(lane == 0, 0.0, shift_lanes(guess, 1))
+            inner += jnp.where(lane == ny - 1, 0.0, shift_lanes(guess, -1))
             inverse = 1.0 / (6.0 + shift[z])
             inv[z] = inverse
-            part[z] = guess + inverse * around
-
-    return call(
-        body, [fg.shape, fg.shape], in_specs=vmem(gots + 3), out_specs=vmem(2)
-    )(*got, fg, node_shift, after)
+            part[z] = guess + inverse * (inner + (fg[z - 1] if z > 0 else z_face(low_of)))
+            if z == 0:
+                for k in range(3):
+                    tail[k * nx : (k + 1) * nx, :] = low_z[k]
+                tail[3 * nx : 4 * nx, :] = guess + inverse * inner
+                tail[4 * nx :, :] = inverse
+
+    return call(
+        body, [fg.shape, fg.shape, (5 * nx, LANES)], in_specs=vmem(gots + 4), out_specs=vmem(3)
+    )(*got, fg, node_shift, low_z, after)
 
 
 def line(source, lane, fine, at):
@@ -437,7 +428,7 @@
     return acc
 
 
-def y_stage(got, rhs, yb, w, early, x_count, y_count):
+def y_stage(got, rhs, w, early, x_count, y_count):
     planes, rows, _ = rhs.shape
     cx = rows - 8
     nx, cy = 2 * cx, LANES // 2
@@ -447,9 +438,9 @@
 
     def body(*refs):
         got = refs[:gots]
-        rhs, yb, w, up_, down_, part, inv, _, _, rhs3, w3 = refs[gots : gots + 11]
-        rest = refs[gots + 11 :]
-        out, (yb3, add) = rest[:sends], rest[sends:]
+        rhs, w, up_, down_, part, inv, _, _, rhs3, w3 = refs[gots : gots + 10]
+        rest = refs[gots + 10 :]
+        out, (add,) = rest[:sends], rest[sends:]
         lane_p = lane_ids(planes)
 
         def take_at(pick, at):
@@ -462,15 +453,12 @@
         add[...] = jnp.zeros_like(add)
         for c in range(planes):
             w3[c] = w[c]
-            yb3[c] = yb[c]
         for pick, near, far, edge in ((high_of, cx, cx + 1, cx - 1), (low_of, rows - 1, rows - 2, 0)):
             first, second, third = take(pick, 0), take(pick, 1), take(pick, 2)
             other = shift_lanes(third, -cy)
             one = jnp.where((lane_p == 0) | (lane_p == cy - 1), other, 0.0)
             two = jnp.where(lane_p == 0, shift_lanes(third, -cy - 1), 0.0)
             two = jnp.where(lane_p == cy - 1, shift_lanes(third, 1 - cy), two)
-            yb3[:, near, :] = one
-            yb3[:, far, :] = two
             for at, value, ends in ((near, first, one), (far, shift_lanes(first, -cy), two)):
                 value = jnp.where(lane_p < cy, value, 0.0)
                 value += jnp.where(lane_p == cy, shift_lanes(ends, 1), 0.0)
@@ -488,22 +476,25 @@
         x_face = slice(3 * planes, 3 * planes + nz)
         x_high = take_at(high_of, x_face)
 
-        def fill(ref, near, far, fine, early):
+        def fill(ref, first, fine, early):
             acc = jnp.zeros((rows, LANES), F32)
-            jobs = ((rhs3, near), (rhs3, far), (w3, near), (w3, far), (yb3, near))
-            for i, (field, at) in enumerate(jobs):
-                for z in range(planes):
-                    spot = i * planes + z
-                    acc = jnp.where(lane_c == spot, shift_lanes(field[z], spot - at), acc)
+            inner = first if first > 0 else 0
+            for z in range(planes):
+                for field, width, at, source in (
+                    (rhs3, 3, 3 * z, first),
+                    (w3, 2, 3 * planes + 2 * z, inner),
+                ):
+                    there = (lane_c >= at) & (lane_c < at + width)
+                    acc = jnp.where(there, shift_lanes(field[z], at - source), acc)
             ref[:nx, :] = plane(acc, nx) + early[...]
             ref[nx : nx + 8, :] = line(x_high, lane8, fine, base)
 
         def up(ref):
-            fill(ref, cy - 1, cy - 2, 2 * cy - 1, up_)
+            fill(ref, cy - 2, 2 * cy - 1, up_)
             ref[nx + 8 :, :] = jnp.zeros((half, LANES), F32)
 
         def down(ref):
-            fill(ref, 0, 1, 0, down_)
+            fill(ref, -1, 0, down_)
             row = row_ids(nx)
             ends = jnp.where(row == 0, line(take_at(low_of, x_face), lane8, 0, 0)[:1, :], 0.0)
             ends += jnp.where(row == nx - 1, line(x_high, lane8, 0, 0)[:1, :], 0.0)
@@ -521,10 +512,10 @@
     return call(
         body,
         [whole, whole] + [(nx + 8 + half, LANES)] * sends,
-        scratch=[whole, whole],
-        in_specs=vmem(gots + 9),
+        scratch=[whole],
+        in_specs=vmem(gots + 8),
         out_specs=vmem(2 + sends),
-    )(*got, rhs, yb, w, *early)
+    )(*got, rhs, w, *early)
 
 
 def y_early(got_z, fg, node_shift, low_y, after, planes, z_count):
@@ -585,17 +576,15 @@
         low = low_of("gy", y_count, values[0], second)
         high = high_of("gy", y_count, values[0], second)
         lane = lane_ids(rows)
-        spots_r = ((cy, high, 0), (cy + 1, high, 1), (LANES - 1, low, 0), (LANES - 2, low, 1))
-        spots_r += ((cy - 1, high, 4), (0, low, 4))
+        above = (lane >= cy - 1) & (lane < cy + 2)
+        below = (lane >= LANES - 2) | (lane == 0)
         for z in range(planes):
-            right = rhs[z]
-            for at, source, i in spots_r:
-                moved = shift_lanes(source, at - (i * planes + z))
-                right += jnp.where(lane == at, moved, 0.0)
-            inv = w[z]
-            for at, source, i in spots_r[:4]:
-                moved = shift_lanes(source, at - ((i + 2) * planes + z))
-                inv = jnp.where(lane == at, moved, inv)
+            at = 3 * z
+            right = jnp.where(below, shift_lanes(low, LANES - 2 - at), 0.0)
+            right = rhs[z] + jnp.where(above, shift_lanes(high, cy - 1 - at), right)
+            at = 3 * planes + 2 * z
+            inv = jnp.where(lane >= LANES - 2, shift_lanes(low, LANES - 2 - at), w[z])
+            inv = jnp.where((lane >= cy) & (lane < cy + 2), shift_lanes(high, cy - at), inv)
             inv_[z] = inv
             tot[z] = right
             v1[z] = right * inv
@@ -637,28 +626,20 @@
     )(*got, rhs, w, *after)
 
 
-def smooth_stage(scaled, inverses, below, got_z, tail_x, after, counts):
+def smooth_stage(scaled, inverses, below, tail_z, tail_x, after, counts):
     _, nz, nx, _ = scaled.shape
-    n_z = len(got_z)
-    rows = nx // 2 + 8
 
     def body(*refs):
         s, inv, lz, lx, ly = refs[:5]
-        gz = refs[5 : 5 + n_z]
-        gx, _, out, last = refs[5 + n_z :]
+        tz, gx, _, out, last = refs[5:]
         lane = lane_ids(nx)
         row = row_ids(nx)
         y_low = from_below("gy", ly[...])
 
-        def above_of(refs, axis, size, at):
-            values = [ref[at, :] for ref in refs]
-            return high_of(axis, size, values[0], values[1] if len(values) > 1 else None)
-
         acc = jnp.zeros((nx, LANES), F32)
         for k in range(3):
             z_low = from_below("gz", lz[k])
-            at = 9 * rows + nx + k * nx
-            z_high = above_of(gz, "gz", counts[0], slice(at, at + nx))
+            z_high = from_above("gz", counts[0], tz[k * nx : (k + 1) * nx, :])
             x_low = from_below("gx", lx[k * nz : (k + 1) * nz, :])
             x_high = from_above("gx", counts[1], gx[k * nz : (k + 1) * nz, :])
             for z in range(nz):
@@ -676,23 +657,22 @@
         last[...] = acc
 
     return call(
-        body, [scaled.shape, (nx, LANES)], in_specs=vmem(7 + n_z), out_specs=vmem(2)
-    )(scaled, inverses, *below, *got_z, tail_x, after)
-
-
-def final_stage(sums, v1, v2, fg, mid, smooth, last, tail_x, got_z, got_x, got_y, counts):
+        body, [scaled.shape, (nx, LANES)], in_specs=vmem(8), out_specs=vmem(2)
+    )(scaled, inverses, *below, tail_z, tail_x, after)
+
+
+def final_stage(sums, v1, v2, fg, mid, smooth, last, early, tail_z, tail_x, got_x, got_y, counts):
     planes, rows, _ = v1.shape
     cz, cx, cy = planes - 4, rows - 8, LANES // 2
     nz, nx, _ = fg.shape
-    n_z, n_x, n_y = len(got_z), len(got_x), len(got_y)
-    gots = n_z + n_x + n_y
+    n_x, n_y = len(got_x), len(got_y)
+    gots = n_x + n_y
 
     def body(*refs):
-        sums, v1, v2, fg, part, inv, smooth, last, tx = refs[:9]
-        gz = refs[9 : 9 + n_z]
-        gx = refs[9 + n_z : 9 + n_z + n_x]
-        gy = refs[9 + n_z + n_x : 9 + gots]
-        out, sol, dup, inter, small, lines, buf, sem = refs[9 + gots :]
+        sums, v1, v2, fg, part, inv, smooth, last, early, tz, tx = refs[:11]
+        gx = refs[11 : 11 + n_x]
+        gy = refs[11 + n_x : 11 + gots]
+        out, sol, dup, inter, small, lines, buf, sem = refs[11 + gots :]
 
         def one_side(pick, refs, axis, size, at):
             values = [ref[at, :] for ref in refs]
@@ -717,9 +697,6 @@
             sol[z] = one * v1[z] + two * v2[z]
             dup[z] = jnp.dot(sol[z], spread, precision=HIGHEST, preferred_element_type=F32)
 
-        z_at = 9 * rows
-        z_base = one_side(high_of, gz, "gz", counts[0], slice(z_at + 4 * nx, z_at + 5 * nx))
-        z_inverse = one_side(high_of, gz, "gz", counts[0], slice(z_at + 5 * nx, z_at + 6 * nx))
         x_low, x_high = both(gx, "gx", counts[1], slice(3 * planes, 3 * planes + nz + 1))
         y_low, y_high = both(gy, "gy", counts[2], slice(0, nx))
         y_row_low, y_row_high = both(gy, "gy", counts[2], slice(nx, nx + 1))
@@ -745,7 +722,7 @@
             around += jnp.where(lane == 0, shift_lanes(y_low, -(base + z)), 0.0)
             around += jnp.where(lane == LANES - 1, shift_lanes(y_high, -(base + z) - 1), 0.0)
             if z == nz:
-                value = z_base + z_inverse * (around + fg[nz - 1])
+                value = tz[3 * nx : 4 * nx, :] + tz[4 * nx :, :] * (around + fg[nz - 1])
                 return from_above("gz", counts[0], value)
             return part[z] + inv[z] * around
 
@@ -768,23 +745,22 @@
         lane_c = lane_ids(rows)
         even = jnp.zeros((rows, LANES), F32)
         odd = jnp.zeros((rows, LANES), F32)
-        own = jnp.zeros((nx, LANES), F32)
         for z in range(nz):
             c = z // 2
             here = sol[c]
             same = 3.0 * here + shift_lanes(here, 1) + sol[(c + 1 if z % 2 else c - 1) % planes]
             even = jnp.where(lane_c == z, shift_lanes(same + shift_rows(here, 1), z - cy), even)
             odd = jnp.where(lane_c == z, shift_lanes(same + shift_rows(here, -1), z - cy), odd)
-            own = jnp.where(lane == z, shift_lanes(fg[z], z + 1), own)
         inter[0, pl.ds(0, cx, 2), :] = even[:cx, :]
         inter[0, pl.ds(1, cx, 2), :] = odd[:cx, :]
         y_base = jnp.concatenate([y_pack, shift_lanes(y_pack, -nz)], axis=0)
         y_inverse = jnp.concatenate(
             [shift_lanes(y_pack, -2 * nz), shift_lanes(y_pack, -3 * nz)], axis=0
         )
-        y_value = y_base + y_inverse * (own + inter[0])
+        y_value = y_base + y_inverse * (shift_lanes(early[...], -base) + inter[0])
         y_value = from_above("gy", counts[2], y_value)
         y_fix = shift_lanes(y_high, -(base + nz + 1)) * last[...]
+        y_value += shift_lanes(y_fix, -2 * nz)
 
         def copy(z):
             return pltpu.make_async_copy(buf.at[:, z], out.at[:, z], sem.at[z])
@@ -797,8 +773,11 @@
                 jnp.where(lane == LANES - 1, shift_lanes(y_value, -z - 1), shift_lanes(value, -1))
             )
             for k in range(3):
-                fixed = jnp.where(lane == LANES - 1, shift_lanes(y_fix, -(k * nz + z) - 1), 0.0)
-                buf[k, z] = (smooth[k, z] + fixed) + (steps[k] - value)
+                moved = smooth[k, z]
+                if k < 2:
+                    fixed = shift_lanes(y_fix, -(k * nz + z) - 1)
+                    moved += jnp.where(lane == LANES - 1, fixed, 0.0)
+                buf[k, z] = moved + (steps[k] - value)
             copy(z).start()
             value = after
         for z in range(nz):
@@ -817,9 +796,9 @@
             pltpu.SemaphoreType.DMA((nz,)),
         ],
         far_out=True,
-        in_specs=vmem(9 + gots),
+        in_specs=vmem(11 + gots),
         out_specs=[pl.BlockSpec(memory_space=pltpu.HBM)],
-    )(sums, v1, v2, fg, *mid, smooth, last, tail_x, *got_z, *got_x, *got_y)[0]
+    )(sums, v1, v2, fg, *mid, smooth, last, early, tail_z, tail_x, *got_x, *got_y)[0]
 
 
 def local(residual, edge_diag, node_shift, coarse_shift):
@@ -831,22 +810,26 @@
     below = []
     for value, axis in ((up_z, "gz"), (up_x, "gx"), (up_y, "gy")):
         below.append(ring(value, axis, 1))
-    fg, rhs, xb, yb, w, *send = nodal_stage(part, node_shift, coarse_shift, *below, low_z, counts[0])
+    fg, rhs, xb, yb, w, *send = nodal_stage(part, node_shift, coarse_shift, *below, counts[0])
     got_z = swap(send, "gz")
-    rhs, yb, w, *send = x_stage(got_z, rhs, xb, yb, w, fg, counts[0], counts[1])
+    rhs, w, *send = x_stage(got_z, rhs, xb, yb, w, fg, counts[0], counts[1])
     got_x = swap(send, "gx", ("gx", "gy"))
     planes = rhs.shape[0]
     tail_x = x_tail(got_z, fg, node_shift, low_x, w, counts[0])
-    mid = part_stage(got_z, fg, node_shift, w, counts[0])
+    *mid, tail_z = part_stage(got_z, fg, node_shift, low_z, w, counts[0])
     early = y_early(got_z, fg, node_shift, low_y, w, planes, counts[0])
     early = (*early, tail_x, mid[1])
+    tail_z = ring(tail_z, "gz", -1)
     tail_x = ring(tail_x, "gx", -1)
-    rhs, w, *send = y_stage(got_x, rhs, yb, w, early, counts[1], counts[2])
+    rhs, w, *send = y_stage(got_x, rhs, w, early, counts[1], counts[2])
     got_y = swap(send, "gy", ("gx", "gy"))
-    smooth, last = smooth_stage(scaled, inverses, below, got_z, tail_x, w, counts)
+    smooth, last = smooth_stage(scaled, inverses, below, tail_z, tail_x, w, counts)
     v1, v2, sums = coarse_stage(got_y, rhs, w, (last,), counts[2], devices)
     sums = lax.all_to_all(sums, ("gx", "gy", "gz"), 0, 0)
-    return final_stage(sums, v1, v2, fg, mid, smooth, last, tail_x, got_z, got_x, got_y, counts)
+    early = early[0]
+    return final_stage(
+        sums, v1, v2, fg, mid, smooth, last, early, tail_z, tail_x, got_x, got_y, counts
+    )
 
 
 def solution(mesh):

time: 44.7 us -> 43.9 us (0.982)
  Pallas kernels: 11.7 us -> 10.6 us
    pallas_call x10, Pallas kernels: 11.7 us -> 10.6 us  [apply(): run(*(pltpu.with_memory_space_constraint(a, space) for a, space in zip(ar...]
    ppermute x4 -> x5, starting transfers between devices: 6.22 us -> 6.41 us  [ring(): lax.ppermute(value, axis, [(i, (i + step) % size) for i in range(size)])]
    ppermute x4 -> x5, waiting for transfers between devices: 5.7 us -> 5.71 us  [ring(): lax.ppermute(value, axis, [(i, (i + step) % size) for i in range(size)])]
  transfers between devices with their start and end apart: 9 -> 10, of which waited for: 5 -> 5; matrix products, arithmetic and copies ran while one was open for 0% -> 0% of each run, Pallas kernels for 7% -> 7%
where the time goes in v8:
time: 43.9 us; the launch traced here: 43.7 us
  starting transfers between devices  12.4 us (28%)
  blocking collectives  11.7 us (27%)
  Pallas kernels  10.6 us (24%)
  waiting for transfers between devices  9 us (21%)
    all_to_all x1, blocking collectives, local(): sums = lax.all_to_all(sums, ('gx', 'gy', 'gz'), 0, 0)  11.7 us
    pallas_call x10, Pallas kernels, apply(): run(*(pltpu.with_memory_space_constraint(a, space) for a, space in zip(ar...  10.6 us
    ppermute x5, starting transfers between devices, ring(): lax.ppermute(value, axis, [(i, (i + step) % size) for i in range(size)])  6.41 us
    ppermute x5, waiting for transfers between devices, ring(): lax.ppermute(value, axis, [(i, (i + step) % size) for i in range(size)])  5.71 us
    ppermute x2, starting transfers between devices, swap(): out.append(lax.ppermute(values[1], names, pairs))  3.62 us
    ppermute x3, waiting for transfers between devices, swap(): out = [lax.ppermute(values[0], axis, [(i, i ^ 1) for i in range(size)])]  2.41 us
    ppermute x3, starting transfers between devices, swap(): out = [lax.ppermute(values[0], axis, [(i, i ^ 1) for i in range(size)])]  2.34 us
    ppermute x2, waiting for transfers between devices, swap(): out.append(lax.ppermute(values[1], names, pairs))  0.89 us
  transfers between devices with their start and end apart: 10, of which 5 were waited for; matrix products, arithmetic and copies ran while one was open for 0% of the time, Pallas kernels for 7%

profile of v8, /device:TPU:0, one launch (start us, length us, event | category | flops | bytes accessed | tf_op | source)
XLA Modules:
  0.0 43.7 jit_solution(6957521705347800350)
XLA Ops:
  0.0 2.8 %shard_map.46 = (f32[16,64,128]{2,1,0:T(8,128)S(1)}, f32[3,64,128]{2,1,0:T(8,128)S(1)}, f32[48,128]{1,0:T(8,128)S(1)}, f32[64,128]{1,0:T(8,128)S(1)}, f32[3,64,1...) custom-call(f32[3,16,64,128]{3,2,1,0:T(8,128)} %res.1, ...), custom_call_target="tpu_custom_call" | custom-call | tf_op jit(solution)/shard_map/pallas_call | solution.py:114
  2.8 0.6 %collective-permute-start = (f32[3,64,128]{2,1,0:T(8,128)S(1)}, f32[3,64,128]{2,1,0:T(8,128)S(1)}, u32[]{:S(2)}, u32[]{:S(2)}) collective-permute-start(f32[3,64,128]{2,1,0:T(8,128)S(1)} %get-tuple-element.41), channel_id=1, source_target_pairs={{0,1},{1,0},{2,3},{3,2},{4,5},{5,4},{6,7},{7,6},{8,9},{9,8},{10,11... | collective-permute-start | bytes 294920 | tf_op jit(solution)/shard_map/ppermute | solution.py:60
  3.4 2.6 %collective-permute-start.2 = (f32[64,128]{1,0:T(8,128)S(1)}, f32[64,128]{1,0:T(8,128)S(1)}, u32[]{:S(2)}, u32[]{:S(2)}) collective-permute-start(f32[64,128]{1,0:T(8,128)S(1)} %get-tuple-element.43), channel_id=1, source_target_pairs={{0,2},{2,4},{4,6},{6,0},{1,3},{3,5},{5,7},{7,1},{8,10},{10,12},{12... | collective-permute-start | bytes 98312 | tf_op jit(solution)/shard_map/ppermute | solution.py:60
  6.0 1.5 %collective-permute-start.1 = (f32[48,128]{1,0:T(8,128)S(1)}, f32[48,128]{1,0:T(8,128)S(1)}, u32[]{:S(2)}, u32[]{:S(2)}) collective-permute-start(f32[48,128]{1,0:T(8,128)S(1)} %get-tuple-element.42), channel_id=1, source_target_pairs={{0,8},{8,16},{16,24},{24,0},{1,9},{9,17},{17,25},{25,1},{2,10},{10... | collective-permute-start | bytes 73736 | tf_op jit(solution)/shard_map/ppermute | solution.py:60
  7.5 3.2 %collective-permute-done.1.gx.refs_3_ = f32[48,128]{1,0:T(8,128)S(1)} collective-permute-done((f32[48,128]{1,0:T(8,128)S(1)}, f32[48,128]{1,0:T(8,128)S(1)}, u32[]{:S(2)}, u32[]{:S(2)}) %collective-permute-start.1) | collective-permute-done | bytes 24608 | tf_op jit(solution)/shard_map/ppermute | solution.py:60
  10.7 1.0 %shard_map.47 = (f32[16,64,128]{2,1,0:T(8,128)S(1)}, f32[12,40,128]{2,1,0:T(8,128)S(1)}, f32[8,40,128]{2,1,0:T(8,128)S(1)}, f32[8,40,128]{2,1,0:T(8,128)S(1)}, f...) custom-call(f32[16,64,128]{2,1,0:T(8,128)S(1)} %get-tuple-element.40.part, f32[16,64,128]{2,1,0:T(8,128)S(1)} %copy-done, ...), custom_call_target="tpu_custom_call" | custom-call | tf_op jit(solution)/shard_map/pallas_call | solution.py:114
  11.8 1.5 %collective-permute-done.3.refs_0_ = f32[424,128]{1,0:T(8,128)S(1)} collective-permute-done((f32[424,128]{1,0:T(8,128)S(1)}, f32[424,128]{1,0:T(8,128)S(1)}, u32[]{:S(2)}, u32[]{:S(2)}) %collective-permute-start.3) | collective-permute-done | bytes 217120 | tf_op jit(solution)/shard_map/ppermute | solution.py:65
  13.2 0.2 shard_map.48
  13.4 0.3 shard_map.51
  13.7 0.2 collective-permute-start.8
  13.9 0.9 %collective-permute-start.4 = (f32[56,128]{1,0:T(8,128)S(1)}, f32[56,128]{1,0:T(8,128)S(1)}, u32[]{:S(2)}, u32[]{:S(2)}) collective-permute-start(f32[56,128]{1,0:T(8,128)S(1)} %get-tuple-element.50), channel_id=1, source_target_pairs={{0,8},{8,0},{16,24},{24,16},{1,9},{9,1},{17,25},{25,17},{2,10},{10... | collective-permute-start | bytes 86024 | tf_op jit(solution)/shard_map/ppermute | solution.py:65
  14.8 1.3 %collective-permute-start.5 = (f32[56,128]{1,0:T(8,128)S(1)}, f32[56,128]{1,0:T(8,128)S(1)}, u32[]{:S(2)}, u32[]{:S(2)}) collective-permute-start(f32[56,128]{1,0:T(8,128)S(1)} %get-tuple-element.51), channel_id=1, source_target_pairs={{0,2},{2,0},{4,6},{6,4},{8,16},{10,18},{12,20},{14,22},{16,8},{18,... | collective-permute-start | bytes 86024 | tf_op jit(solution)/shard_map/ppermute | solution.py:82
  16.2 0.7 %shard_map.49 = (f32[64,128]{1,0:T(8,128)S(1)}, f32[64,128]{1,0:T(8,128)S(1)}, f32[64,128]{1,0:T(8,128)S(1)}, f32[64,128]{1,0:T(8,128)S(1)}) custom-call(f32[424,128]{1,0:T(8,128)S(1)} %collective-permute-done.3.refs_0_, f32[16,64,128]{2,1,0:T(8,128)S(1)} %get-tuple-element.49.refs_5_.refs_1_.refs_3_, f32[16,64,128]{2,1,0:T(8,128)S(1)} %copy-done, ...), custom_call_target="tpu_custom_call" | custom-call | tf_op jit(solution)/shard_map/pallas_call | solution.py:114
  16.9 0.9 %collective-permute-done.4.refs_0_.refs_11_ = f32[56,128]{1,0:T(8,128)S(1)} collective-permute-done((f32[56,128]{1,0:T(8,128)S(1)}, f32[56,128]{1,0:T(8,128)S(1)}, u32[]{:S(2)}, u32[]{:S(2)}) %collective-permute-start.4) | collective-permute-done | bytes 28704 | tf_op jit(solution)/shard_map/ppermute | solution.py:65
  17.8 0.9 %collective-permute-done.5.refs_1_.refs_12_ = f32[56,128]{1,0:T(8,128)S(1)} collective-permute-done((f32[56,128]{1,0:T(8,128)S(1)}, f32[56,128]{1,0:T(8,128)S(1)}, u32[]{:S(2)}, u32[]{:S(2)}) %collective-permute-start.5) | collective-permute-done | bytes 28704 | tf_op jit(solution)/shard_map/ppermute | solution.py:82
  18.7 0.6 %shard_map.52 = (f32[12,40,128]{2,1,0:T(8,128)S(1)}, f32[12,40,128]{2,1,0:T(8,128)S(1)}, f32[104,128]{1,0:T(8,128)S(1)}, f32[104,128]{1,0:T(8,128)S(1)}) custom-call(f32[56,128]{1,0:T(8,128)S(1)} %collective-permute-done.4.refs_0_.refs_11_, f32[56,128]{1,0:T(8,128)S(1)} %collective-permute-done.5.refs_1_.refs_12_, ...), custom_call_target="tpu_custom_call" | custom-call | tf_op jit(solution)/shard_map/pallas_call | solution.py:114
  19.3 1.4 %collective-permute-start.6 = (f32[104,128]{1,0:T(8,128)S(1)}, f32[104,128]{1,0:T(8,128)S(1)}, u32[]{:S(2)}, u32[]{:S(2)}) collective-permute-start(f32[104,128]{1,0:T(8,128)S(1)} %get-tuple-element.62), channel_id=1, source_target_pairs={{0,2},{2,0},{4,6},{6,4},{1,3},{3,1},{5,7},{7,5},{8,10},{10,8},{12,... | collective-permute-start | bytes 159752 | tf_op jit(solution)/shard_map/ppermute | solution.py:65
  20.7 2.3 %collective-permute-start.7 = (f32[104,128]{1,0:T(8,128)S(1)}, f32[104,128]{1,0:T(8,128)S(1)}, u32[]{:S(2)}, u32[]{:S(2)}) collective-permute-start(f32[104,128]{1,0:T(8,128)S(1)} %get-tuple-element.63), channel_id=1, source_target_pairs={{0,8},{2,4},{4,2},{6,14},{8,0},{10,12},{12,10},{14,6},{16,24},{18,... | collective-permute-start | bytes 159752 | tf_op jit(solution)/shard_map/ppermute | solution.py:82
  23.1 1.5 %collective-permute-start.9 = (f32[80,128]{1,0:T(8,128)S(1)}, f32[80,128]{1,0:T(8,128)S(1)}, u32[]{:S(2)}, u32[]{:S(2)}) collective-permute-start(f32[80,128]{1,0:T(8,128)S(1)} %shard_map.50.refs_8_), channel_id=1, source_target_pairs={{0,24},{8,0},{16,8},{24,16},{1,25},{9,1},{17,9},{25,17},{2,26},{10... | collective-permute-start | bytes 122888 | tf_op jit(solution)/shard_map/ppermute | solution.py:60
  24.6 2.5 %collective-permute-done.9.refs_6_.refs_10_ = f32[80,128]{1,0:T(8,128)S(1)} collective-permute-done((f32[80,128]{1,0:T(8,128)S(1)}, f32[80,128]{1,0:T(8,128)S(1)}, u32[]{:S(2)}, u32[]{:S(2)}) %collective-permute-start.9) | collective-permute-done | bytes 40992 | tf_op jit(solution)/shard_map/ppermute | solution.py:60
  27.1 1.7 %shard_map.53 = (f32[3,16,64,128]{3,2,1,0:T(8,128)S(1)}, f32[64,128]{1,0:T(8,128)S(1)}) custom-call(f32[3,16,64,128]{3,2,1,0:T(8,128)S(1)} %get-tuple-element.66.refs_0_, f32[3,16,64,128]{3,2,1,0:T(8,128)S(1)} %get-tuple-element.67.refs_1_, f32[3,64,128]{2,1,0:T(8,128)S(1)} %collective-permute-done.gz.refs_2_, ...), custom_call_target="tpu_custom_call" | custom-call | tf_op jit(solution)/shard_map/pallas_call | solution.py:114
  28.8 0.6 %shard_map.54 = (f32[12,40,128]{2,1,0:T(8,128)S(1)}, f32[12,40,128]{2,1,0:T(8,128)S(1)}, f32[32,1,128]{2,1,0:T(1,128)S(1)}) custom-call(f32[104,128]{1,0:T(8,128)S(1)} %collective-permute-done.6.refs_0_.refs_13_, f32[104,128]{1,0:T(8,128)S(1)} %collective-permute-done.7.refs_1_.refs_14_, f32[12,40,128]{2,1,0:T(8,128)S(1)} %get-tuple-element.64.refs_2_, ...), custom_call_target="tpu_custom_call" | custom-call | tf_op jit(solution)/shard_map/pallas_call | solution.py:114
  29.5 11.7 %all_to_all.5.refs_0_ = f32[32,1,128]{2,1,0:T(1,128)S(1)} all-to-all(f32[32,1,128]{2,1,0:T(1,128)S(1)} %get-tuple-element.70), channel_id=1, replica_groups=mesh['gx'=4,'gy'=4,'gz'=2] {'gx','gy','gz'}, dimensions={0} | all-to-all | bytes 32768 | tf_op jit(solution)/shard_map/all_to_all | solution.py:828
  41.1 2.6 %shard_map.55 = f32[3,16,64,128]{3,2,1,0:T(8,128)} custom-call(f32[32,1,128]{2,1,0:T(1,128)S(1)} %all_to_all.5.refs_0_, f32[12,40,128]{2,1,0:T(8,128)S(1)} %get-tuple-element.71.refs_1_, f32[12,40,128]{2,1,0:T(8,128)S(1)} %get-tuple-element.72.refs_2_, f32[16,64,128]{2,1,0:T(8,128)S(1)} %get-tuple-element.49.refs_5_.refs_1_.refs_3_, ...), custom_call_target="tpu_custom_call" | custom-call | tf_op jit(solution)/shard_map/pallas_call | solution.py:114
  (11 shorter events, 0.2 us)
Async XLA Ops:
  0.0 10.7 %copy-start = (f32[16,64,128]{2,1,0:T(8,128)S(1)}, f32[16,64,128]{2,1,0:T(8,128)}, u32[]{:S(2)}) copy-start(f32[16,64,128]{2,1,0:T(8,128)} %refs_2_.5) | copy-start | bytes 1572868
  0.0 10.7 %copy-start.1 = (f32[8,32,64]{2,1,0:T(8,128)S(1)}, f32[8,32,64]{2,1,0:T(8,128)}, u32[]{:S(2)}) copy-start(f32[8,32,64]{2,1,0:T(8,128)} %coarse.1) | copy-start | bytes 196612
  2.8 7.9 %collective-permute-start = (f32[3,64,128]{2,1,0:T(8,128)S(1)}, f32[3,64,128]{2,1,0:T(8,128)S(1)}, u32[]{:S(2)}, u32[]{:S(2)}) collective-permute-start(f32[3,64,128]{2,1,0:T(8,128)S(1)} %get-tuple-element.41), channel_id=1, source_target_pairs={{0,1},{1,0},{2,3},{3,2},{4,5},{5,4},{6,7},{7,6},{8,9},{9,8},{10,11... | collective-permute-start | bytes 294920 | tf_op jit(solution)/shard_map/ppermute | solution.py:60
  3.4 7.4 %collective-permute-start.2 = (f32[64,128]{1,0:T(8,128)S(1)}, f32[64,128]{1,0:T(8,128)S(1)}, u32[]{:S(2)}, u32[]{:S(2)}) collective-permute-start(f32[64,128]{1,0:T(8,128)S(1)} %get-tuple-element.43), channel_id=1, source_target_pairs={{0,2},{2,4},{4,6},{6,0},{1,3},{3,5},{5,7},{7,1},{8,10},{10,12},{12... | collective-permute-start | bytes 98312 | tf_op jit(solution)/shard_map/ppermute | solution.py:60
  6.0 4.7 %collective-permute-start.1 = (f32[48,128]{1,0:T(8,128)S(1)}, f32[48,128]{1,0:T(8,128)S(1)}, u32[]{:S(2)}, u32[]{:S(2)}) collective-permute-start(f32[48,128]{1,0:T(8,128)S(1)} %get-tuple-element.42), channel_id=1, source_target_pairs={{0,8},{8,16},{16,24},{24,0},{1,9},{9,17},{17,25},{25,1},{2,10},{10... | collective-permute-start | bytes 73736 | tf_op jit(solution)/shard_map/ppermute | solution.py:60
  11.7 1.5 %collective-permute-start.3 = (f32[424,128]{1,0:T(8,128)S(1)}, f32[424,128]{1,0:T(8,128)S(1)}, u32[]{:S(2)}, u32[]{:S(2)}) collective-permute-start(f32[424,128]{1,0:T(8,128)S(1)} %get-tuple-element.44), channel_id=1, source_target_pairs={{0,1},{1,0},{2,3},{3,2},{4,5},{5,4},{6,7},{7,6},{8,9},{9,8},{10,11... | collective-permute-start | bytes 651272 | tf_op jit(solution)/shard_map/ppermute | solution.py:65
  13.7 13.3 %collective-permute-start.8 = (f32[320,128]{1,0:T(8,128)S(1)}, f32[320,128]{1,0:T(8,128)S(1)}, u32[]{:S(2)}, u32[]{:S(2)}) collective-permute-start(f32[320,128]{1,0:T(8,128)S(1)} %get-tuple-element.68), channel_id=1, source_target_pairs={{0,1},{1,0},{2,3},{3,2},{4,5},{5,4},{6,7},{7,6},{8,9},{9,8},{10,11... | collective-permute-start | bytes 491528 | tf_op jit(solution)/shard_map/ppermute | solution.py:60
  13.9 3.9 %collective-permute-start.4 = (f32[56,128]{1,0:T(8,128)S(1)}, f32[56,128]{1,0:T(8,128)S(1)}, u32[]{:S(2)}, u32[]{:S(2)}) collective-permute-start(f32[56,128]{1,0:T(8,128)S(1)} %get-tuple-element.50), channel_id=1, source_target_pairs={{0,8},{8,0},{16,24},{24,16},{1,9},{9,1},{17,25},{25,17},{2,10},{10... | collective-permute-start | bytes 86024 | tf_op jit(solution)/shard_map/ppermute | solution.py:65
  14.8 3.9 %collective-permute-start.5 = (f32[56,128]{1,0:T(8,128)S(1)}, f32[56,128]{1,0:T(8,128)S(1)}, u32[]{:S(2)}, u32[]{:S(2)}) collective-permute-start(f32[56,128]{1,0:T(8,128)S(1)} %get-tuple-element.51), channel_id=1, source_target_pairs={{0,2},{2,0},{4,6},{6,4},{8,16},{10,18},{12,20},{14,22},{16,8},{18,... | collective-permute-start | bytes 86024 | tf_op jit(solution)/shard_map/ppermute | solution.py:82
  19.3 9.5 %collective-permute-start.6 = (f32[104,128]{1,0:T(8,128)S(1)}, f32[104,128]{1,0:T(8,128)S(1)}, u32[]{:S(2)}, u32[]{:S(2)}) collective-permute-start(f32[104,128]{1,0:T(8,128)S(1)} %get-tuple-element.62), channel_id=1, source_target_pairs={{0,2},{2,0},{4,6},{6,4},{1,3},{3,1},{5,7},{7,5},{8,10},{10,8},{12,... | collective-permute-start | bytes 159752 | tf_op jit(solution)/shard_map/ppermute | solution.py:65
  20.7 8.1 %collective-permute-start.7 = (f32[104,128]{1,0:T(8,128)S(1)}, f32[104,128]{1,0:T(8,128)S(1)}, u32[]{:S(2)}, u32[]{:S(2)}) collective-permute-start(f32[104,128]{1,0:T(8,128)S(1)} %get-tuple-element.63), channel_id=1, source_target_pairs={{0,8},{2,4},{4,2},{6,14},{8,0},{10,12},{12,10},{14,6},{16,24},{18,... | collective-permute-start | bytes 159752 | tf_op jit(solution)/shard_map/ppermute | solution.py:82
  23.1 4.0 %collective-permute-start.9 = (f32[80,128]{1,0:T(8,128)S(1)}, f32[80,128]{1,0:T(8,128)S(1)}, u32[]{:S(2)}, u32[]{:S(2)}) collective-permute-start(f32[80,128]{1,0:T(8,128)S(1)} %shard_map.50.refs_8_), channel_id=1, source_target_pairs={{0,24},{8,0},{16,8},{24,16},{1,25},{9,1},{17,9},{25,17},{2,26},{10... | collective-permute-start | bytes 122888 | tf_op jit(solution)/shard_map/ppermute | solution.py:60

commit v9 on v8

--- a/solution.py
+++ b/solution.py
@@ -9,7 +9,6 @@
 
 
 F32 = jnp.float32
-HIGHEST = lax.Precision.HIGHEST
 LANES = 128
 
 
@@ -186,6 +185,17 @@
     )(residual, edge_diag)
 
 
+def select_sum(values, chosen):
+    first = values.astype(jnp.bfloat16)
+    left = values - first.astype(F32)
+    second = left.astype(jnp.bfloat16)
+    third = (left - second.astype(F32)).astype(jnp.bfloat16)
+    chosen = chosen.astype(jnp.bfloat16)
+    both = jnp.concatenate([first, second], axis=1)
+    total = jnp.dot(both, jnp.concatenate([chosen, chosen], axis=0), preferred_element_type=F32)
+    return total + jnp.dot(third, chosen, preferred_element_type=F32)
+
+
 def plane(values, row_count):
     return jnp.concatenate([values, jnp.zeros((row_count - values.shape[0], LANES), F32)], axis=0)
 
@@ -197,7 +207,7 @@
     sends = 1 if z_count == 2 else 2
 
     def body(part, shift, coarse, gz, gx, gy, fg, rhs, xb, yb, w, *rest):
-        out, (pair, s_, xl_, yl_, zl_, zh_) = rest[:sends], rest[sends:]
+        out, (pair, stack, s_, xl_, yl_, zl_, zh_) = rest[:sends], rest[sends:]
         lane = lane_ids(nx)
         row = row_ids(nx)
         lane_c = lane_ids(rows)
@@ -225,8 +235,12 @@
             low = pair[c % 2, pl.ds(0, cx, 2), :]
             high = pair[c % 2, pl.ds(1, cx, 2), :]
             first = fg[2 * c, pl.ds(0, cx, 2), :] + fg[2 * c, pl.ds(1, cx, 2), :]
-            stacked = jnp.concatenate([low + high, low, first], axis=0)
-            sums = jnp.dot(stacked, gather, precision=HIGHEST, preferred_element_type=F32)
+            stack[c, :cx, :] = low + high
+            stack[c, cx : 2 * cx, :] = low
+            stack[c, 2 * cx :, :] = first
+        every = select_sum(stack[...].reshape(3 * cx * cz, LANES), gather)
+        for c in range(cz):
+            sums = every[3 * cx * c : 3 * cx * (c + 1)]
             s = sums[:cx, :LANES]
             z_low = sums[2 * cx :, :LANES]
             s_[c] = plane(s, rows)
@@ -275,7 +289,7 @@
     return call(
         body,
         [(nz, nx, ny), (cz + 4, rows, LANES), coarse, coarse, coarse] + [send] * sends,
-        scratch=[(2, nx, ny), coarse, coarse, coarse, coarse, coarse],
+        scratch=[(2, nx, ny), (cz, 3 * cx, LANES), coarse, coarse, coarse, coarse, coarse],
         in_specs=vmem(6),
         out_specs=vmem(5 + sends),
     )(part, node_shift, coarse_shift, got_z, got_x, got_y)
@@ -693,9 +707,10 @@
         fine = target - LANES
         side = jnp.where(fine % 2 == 1, fine // 2 + 1, (fine // 2 + LANES - 1) % LANES)
         spread = jnp.where(jnp.where(target < LANES, target // 2, side) == source, 1.0, 0.0)
-        for z in list(range(cz + 1)) + [planes - 1]:
+        for z in range(planes):
             sol[z] = one * v1[z] + two * v2[z]
-            dup[z] = jnp.dot(sol[z], spread, precision=HIGHEST, preferred_element_type=F32)
+        every = select_sum(sol[...].reshape(planes * rows, LANES), spread)
+        dup[...] = every.reshape(planes, rows, 2 * LANES)
 
         x_low, x_high = both(gx, "gx", counts[1], slice(3 * planes, 3 * planes + nz + 1))
         y_low, y_high = both(gy, "gy", counts[2], slice(0, nx))

time: 43.9 us -> 43.1 us (0.982)
  Pallas kernels: 10.6 us -> 9.82 us
    pallas_call x10, Pallas kernels: 10.6 us -> 9.82 us  [apply(): run(*(pltpu.with_memory_space_constraint(a, space) for a, space in zip(ar...]
where the time goes in v9:
time: 43.1 us; the launch traced here: 43 us
  starting transfers between devices  12.4 us (29%)
  blocking collectives  11.7 us (27%)
  Pallas kernels  9.82 us (23%)
  waiting for transfers between devices  8.99 us (21%)
    all_to_all x1, blocking collectives, local(): sums = lax.all_to_all(sums, ('gx', 'gy', 'gz'), 0, 0)  11.7 us
    pallas_call x10, Pallas kernels, apply(): run(*(pltpu.with_memory_space_constraint(a, space) for a, space in zip(ar...  9.82 us
    ppermute x5, starting transfers between devices, ring(): lax.ppermute(value, axis, [(i, (i + step) % size) for i in range(size)])  6.42 us
    ppermute x5, waiting for transfers between devices, ring(): lax.ppermute(value, axis, [(i, (i + step) % size) for i in range(size)])  5.7 us
    ppermute x2, starting transfers between devices, swap(): out.append(lax.ppermute(values[1], names, pairs))  3.62 us
    ppermute x3, waiting for transfers between devices, swap(): out = [lax.ppermute(values[0], axis, [(i, i ^ 1) for i in range(size)])]  2.4 us
    ppermute x3, starting transfers between devices, swap(): out = [lax.ppermute(values[0], axis, [(i, i ^ 1) for i in range(size)])]  2.35 us
    ppermute x2, waiting for transfers between devices, swap(): out.append(lax.ppermute(values[1], names, pairs))  0.89 us
  transfers between devices with their start and end apart: 10, of which 5 were waited for; matrix products, arithmetic and copies ran while one was open for 0% of the time, Pallas kernels for 7%

profile of v9, /device:TPU:0, one launch (start us, length us, event | category | flops | bytes accessed | tf_op | source)
XLA Modules:
  0.0 43.0 jit_solution(5536019564214587360)
XLA Ops:
  0.0 2.8 %shard_map.46 = (f32[16,64,128]{2,1,0:T(8,128)S(1)}, f32[3,64,128]{2,1,0:T(8,128)S(1)}, f32[48,128]{1,0:T(8,128)S(1)}, f32[64,128]{1,0:T(8,128)S(1)}, f32[3,64,1...) custom-call(f32[3,16,64,128]{3,2,1,0:T(8,128)} %res.1, ...), custom_call_target="tpu_custom_call" | custom-call | tf_op jit(solution)/shard_map/pallas_call | solution.py:113
  2.8 0.6 %collective-permute-start = (f32[3,64,128]{2,1,0:T(8,128)S(1)}, f32[3,64,128]{2,1,0:T(8,128)S(1)}, u32[]{:S(2)}, u32[]{:S(2)}) collective-permute-start(f32[3,64,128]{2,1,0:T(8,128)S(1)} %get-tuple-element.41), channel_id=1, source_target_pairs={{0,1},{1,0},{2,3},{3,2},{4,5},{5,4},{6,7},{7,6},{8,9},{9,8},{10,11... | collective-permute-start | bytes 294920 | tf_op jit(solution)/shard_map/ppermute | solution.py:59
  3.4 2.6 %collective-permute-start.2 = (f32[64,128]{1,0:T(8,128)S(1)}, f32[64,128]{1,0:T(8,128)S(1)}, u32[]{:S(2)}, u32[]{:S(2)}) collective-permute-start(f32[64,128]{1,0:T(8,128)S(1)} %get-tuple-element.43), channel_id=1, source_target_pairs={{0,2},{2,4},{4,6},{6,0},{1,3},{3,5},{5,7},{7,1},{8,10},{10,12},{12... | collective-permute-start | bytes 98312 | tf_op jit(solution)/shard_map/ppermute | solution.py:59
  6.0 1.5 %collective-permute-start.1 = (f32[48,128]{1,0:T(8,128)S(1)}, f32[48,128]{1,0:T(8,128)S(1)}, u32[]{:S(2)}, u32[]{:S(2)}) collective-permute-start(f32[48,128]{1,0:T(8,128)S(1)} %get-tuple-element.42), channel_id=1, source_target_pairs={{0,8},{8,16},{16,24},{24,0},{1,9},{9,17},{17,25},{25,1},{2,10},{10... | collective-permute-start | bytes 73736 | tf_op jit(solution)/shard_map/ppermute | solution.py:59
  7.5 3.2 %collective-permute-done.1.gx.refs_3_ = f32[48,128]{1,0:T(8,128)S(1)} collective-permute-done((f32[48,128]{1,0:T(8,128)S(1)}, f32[48,128]{1,0:T(8,128)S(1)}, u32[]{:S(2)}, u32[]{:S(2)}) %collective-permute-start.1) | collective-permute-done | bytes 24608 | tf_op jit(solution)/shard_map/ppermute | solution.py:59
  10.7 0.5 %shard_map.47 = (f32[16,64,128]{2,1,0:T(8,128)S(1)}, f32[12,40,128]{2,1,0:T(8,128)S(1)}, f32[8,40,128]{2,1,0:T(8,128)S(1)}, f32[8,40,128]{2,1,0:T(8,128)S(1)}, f...) custom-call(f32[16,64,128]{2,1,0:T(8,128)S(1)} %get-tuple-element.40.part, f32[16,64,128]{2,1,0:T(8,128)S(1)} %copy-done, ...), custom_call_target="tpu_custom_call" | custom-call | tf_op jit(solution)/shard_map/pallas_call | solution.py:113
  11.3 1.5 %collective-permute-done.3.refs_0_ = f32[424,128]{1,0:T(8,128)S(1)} collective-permute-done((f32[424,128]{1,0:T(8,128)S(1)}, f32[424,128]{1,0:T(8,128)S(1)}, u32[]{:S(2)}, u32[]{:S(2)}) %collective-permute-start.3) | collective-permute-done | bytes 217120 | tf_op jit(solution)/shard_map/ppermute | solution.py:64
  12.8 0.2 shard_map.48
  13.0 0.3 shard_map.51
  13.3 0.2 collective-permute-start.8
  13.5 0.9 %collective-permute-start.4 = (f32[56,128]{1,0:T(8,128)S(1)}, f32[56,128]{1,0:T(8,128)S(1)}, u32[]{:S(2)}, u32[]{:S(2)}) collective-permute-start(f32[56,128]{1,0:T(8,128)S(1)} %get-tuple-element.50), channel_id=1, source_target_pairs={{0,8},{8,0},{16,24},{24,16},{1,9},{9,1},{17,25},{25,17},{2,10},{10... | collective-permute-start | bytes 86024 | tf_op jit(solution)/shard_map/ppermute | solution.py:64
  14.4 1.3 %collective-permute-start.5 = (f32[56,128]{1,0:T(8,128)S(1)}, f32[56,128]{1,0:T(8,128)S(1)}, u32[]{:S(2)}, u32[]{:S(2)}) collective-permute-start(f32[56,128]{1,0:T(8,128)S(1)} %get-tuple-element.51), channel_id=1, source_target_pairs={{0,2},{2,0},{4,6},{6,4},{8,16},{10,18},{12,20},{14,22},{16,8},{18,... | collective-permute-start | bytes 86024 | tf_op jit(solution)/shard_map/ppermute | solution.py:81
  15.8 0.7 %shard_map.49 = (f32[64,128]{1,0:T(8,128)S(1)}, f32[64,128]{1,0:T(8,128)S(1)}, f32[64,128]{1,0:T(8,128)S(1)}, f32[64,128]{1,0:T(8,128)S(1)}) custom-call(f32[424,128]{1,0:T(8,128)S(1)} %collective-permute-done.3.refs_0_, f32[16,64,128]{2,1,0:T(8,128)S(1)} %get-tuple-element.49.refs_5_.refs_1_.refs_3_, f32[16,64,128]{2,1,0:T(8,128)S(1)} %copy-done, ...), custom_call_target="tpu_custom_call" | custom-call | tf_op jit(solution)/shard_map/pallas_call | solution.py:113
  16.5 0.9 %collective-permute-done.4.refs_0_.refs_11_ = f32[56,128]{1,0:T(8,128)S(1)} collective-permute-done((f32[56,128]{1,0:T(8,128)S(1)}, f32[56,128]{1,0:T(8,128)S(1)}, u32[]{:S(2)}, u32[]{:S(2)}) %collective-permute-start.4) | collective-permute-done | bytes 28704 | tf_op jit(solution)/shard_map/ppermute | solution.py:64
  17.4 0.9 %collective-permute-done.5.refs_1_.refs_12_ = f32[56,128]{1,0:T(8,128)S(1)} collective-permute-done((f32[56,128]{1,0:T(8,128)S(1)}, f32[56,128]{1,0:T(8,128)S(1)}, u32[]{:S(2)}, u32[]{:S(2)}) %collective-permute-start.5) | collective-permute-done | bytes 28704 | tf_op jit(solution)/shard_map/ppermute | solution.py:81
  18.3 0.6 %shard_map.52 = (f32[12,40,128]{2,1,0:T(8,128)S(1)}, f32[12,40,128]{2,1,0:T(8,128)S(1)}, f32[104,128]{1,0:T(8,128)S(1)}, f32[104,128]{1,0:T(8,128)S(1)}) custom-call(f32[56,128]{1,0:T(8,128)S(1)} %collective-permute-done.4.refs_0_.refs_11_, f32[56,128]{1,0:T(8,128)S(1)} %collective-permute-done.5.refs_1_.refs_12_, ...), custom_call_target="tpu_custom_call" | custom-call | tf_op jit(solution)/shard_map/pallas_call | solution.py:113
  18.9 1.4 %collective-permute-start.6 = (f32[104,128]{1,0:T(8,128)S(1)}, f32[104,128]{1,0:T(8,128)S(1)}, u32[]{:S(2)}, u32[]{:S(2)}) collective-permute-start(f32[104,128]{1,0:T(8,128)S(1)} %get-tuple-element.62), channel_id=1, source_target_pairs={{0,2},{2,0},{4,6},{6,4},{1,3},{3,1},{5,7},{7,5},{8,10},{10,8},{12,... | collective-permute-start | bytes 159752 | tf_op jit(solution)/shard_map/ppermute | solution.py:64
  20.3 2.3 %collective-permute-start.7 = (f32[104,128]{1,0:T(8,128)S(1)}, f32[104,128]{1,0:T(8,128)S(1)}, u32[]{:S(2)}, u32[]{:S(2)}) collective-permute-start(f32[104,128]{1,0:T(8,128)S(1)} %get-tuple-element.63), channel_id=1, source_target_pairs={{0,8},{2,4},{4,2},{6,14},{8,0},{10,12},{12,10},{14,6},{16,24},{18,... | collective-permute-start | bytes 159752 | tf_op jit(solution)/shard_map/ppermute | solution.py:81
  22.6 1.5 %collective-permute-start.9 = (f32[80,128]{1,0:T(8,128)S(1)}, f32[80,128]{1,0:T(8,128)S(1)}, u32[]{:S(2)}, u32[]{:S(2)}) collective-permute-start(f32[80,128]{1,0:T(8,128)S(1)} %shard_map.50.refs_8_), channel_id=1, source_target_pairs={{0,24},{8,0},{16,8},{24,16},{1,25},{9,1},{17,9},{25,17},{2,26},{10... | collective-permute-start | bytes 122888 | tf_op jit(solution)/shard_map/ppermute | solution.py:59
  24.2 2.5 %collective-permute-done.9.refs_6_.refs_10_ = f32[80,128]{1,0:T(8,128)S(1)} collective-permute-done((f32[80,128]{1,0:T(8,128)S(1)}, f32[80,128]{1,0:T(8,128)S(1)}, u32[]{:S(2)}, u32[]{:S(2)}) %collective-permute-start.9) | collective-permute-done | bytes 40992 | tf_op jit(solution)/shard_map/ppermute | solution.py:59
  26.6 1.7 %shard_map.53 = (f32[3,16,64,128]{3,2,1,0:T(8,128)S(1)}, f32[64,128]{1,0:T(8,128)S(1)}) custom-call(f32[3,16,64,128]{3,2,1,0:T(8,128)S(1)} %get-tuple-element.66.refs_0_, f32[3,16,64,128]{3,2,1,0:T(8,128)S(1)} %get-tuple-element.67.refs_1_, f32[3,64,128]{2,1,0:T(8,128)S(1)} %collective-permute-done.gz.refs_2_, ...), custom_call_target="tpu_custom_call" | custom-call | tf_op jit(solution)/shard_map/pallas_call | solution.py:113
  28.4 0.6 %shard_map.54 = (f32[12,40,128]{2,1,0:T(8,128)S(1)}, f32[12,40,128]{2,1,0:T(8,128)S(1)}, f32[32,1,128]{2,1,0:T(1,128)S(1)}) custom-call(f32[104,128]{1,0:T(8,128)S(1)} %collective-permute-done.6.refs_0_.refs_13_, f32[104,128]{1,0:T(8,128)S(1)} %collective-permute-done.7.refs_1_.refs_14_, f32[12,40,128]{2,1,0:T(8,128)S(1)} %get-tuple-element.64.refs_2_, ...), custom_call_target="tpu_custom_call" | custom-call | tf_op jit(solution)/shard_map/pallas_call | solution.py:113
  29.0 11.7 %all_to_all.5.refs_0_ = f32[32,1,128]{2,1,0:T(1,128)S(1)} all-to-all(f32[32,1,128]{2,1,0:T(1,128)S(1)} %get-tuple-element.70), channel_id=1, replica_groups=mesh['gx'=4,'gy'=4,'gz'=2] {'gx','gy','gz'}, dimensions={0} | all-to-all | bytes 32768 | tf_op jit(solution)/shard_map/all_to_all | solution.py:843
  40.7 2.3 %shard_map.55 = f32[3,16,64,128]{3,2,1,0:T(8,128)} custom-call(f32[32,1,128]{2,1,0:T(1,128)S(1)} %all_to_all.5.refs_0_, f32[12,40,128]{2,1,0:T(8,128)S(1)} %get-tuple-element.71.refs_1_, f32[12,40,128]{2,1,0:T(8,128)S(1)} %get-tuple-element.72.refs_2_, f32[16,64,128]{2,1,0:T(8,128)S(1)} %get-tuple-element.49.refs_5_.refs_1_.refs_3_, ...), custom_call_target="tpu_custom_call" | custom-call | tf_op jit(solution)/shard_map/pallas_call | solution.py:113
  (11 shorter events, 0.2 us)
Async XLA Ops:
  0.0 10.7 %copy-start = (f32[16,64,128]{2,1,0:T(8,128)S(1)}, f32[16,64,128]{2,1,0:T(8,128)}, u32[]{:S(2)}) copy-start(f32[16,64,128]{2,1,0:T(8,128)} %refs_2_.5) | copy-start | bytes 1572868
  0.0 10.7 %copy-start.1 = (f32[8,32,64]{2,1,0:T(8,128)S(1)}, f32[8,32,64]{2,1,0:T(8,128)}, u32[]{:S(2)}) copy-start(f32[8,32,64]{2,1,0:T(8,128)} %coarse.1) | copy-start | bytes 196612
  2.8 7.9 %collective-permute-start = (f32[3,64,128]{2,1,0:T(8,128)S(1)}, f32[3,64,128]{2,1,0:T(8,128)S(1)}, u32[]{:S(2)}, u32[]{:S(2)}) collective-permute-start(f32[3,64,128]{2,1,0:T(8,128)S(1)} %get-tuple-element.41), channel_id=1, source_target_pairs={{0,1},{1,0},{2,3},{3,2},{4,5},{5,4},{6,7},{7,6},{8,9},{9,8},{10,11... | collective-permute-start | bytes 294920 | tf_op jit(solution)/shard_map/ppermute | solution.py:59
  3.4 7.4 %collective-permute-start.2 = (f32[64,128]{1,0:T(8,128)S(1)}, f32[64,128]{1,0:T(8,128)S(1)}, u32[]{:S(2)}, u32[]{:S(2)}) collective-permute-start(f32[64,128]{1,0:T(8,128)S(1)} %get-tuple-element.43), channel_id=1, source_target_pairs={{0,2},{2,4},{4,6},{6,0},{1,3},{3,5},{5,7},{7,1},{8,10},{10,12},{12... | collective-permute-start | bytes 98312 | tf_op jit(solution)/shard_map/ppermute | solution.py:59
  6.0 4.7 %collective-permute-start.1 = (f32[48,128]{1,0:T(8,128)S(1)}, f32[48,128]{1,0:T(8,128)S(1)}, u32[]{:S(2)}, u32[]{:S(2)}) collective-permute-start(f32[48,128]{1,0:T(8,128)S(1)} %get-tuple-element.42), channel_id=1, source_target_pairs={{0,8},{8,16},{16,24},{24,0},{1,9},{9,17},{17,25},{25,1},{2,10},{10... | collective-permute-start | bytes 73736 | tf_op jit(solution)/shard_map/ppermute | solution.py:59
  11.3 1.5 %collective-permute-start.3 = (f32[424,128]{1,0:T(8,128)S(1)}, f32[424,128]{1,0:T(8,128)S(1)}, u32[]{:S(2)}, u32[]{:S(2)}) collective-permute-start(f32[424,128]{1,0:T(8,128)S(1)} %get-tuple-element.44), channel_id=1, source_target_pairs={{0,1},{1,0},{2,3},{3,2},{4,5},{5,4},{6,7},{7,6},{8,9},{9,8},{10,11... | collective-permute-start | bytes 651272 | tf_op jit(solution)/shard_map/ppermute | solution.py:64
  13.3 13.3 %collective-permute-start.8 = (f32[320,128]{1,0:T(8,128)S(1)}, f32[320,128]{1,0:T(8,128)S(1)}, u32[]{:S(2)}, u32[]{:S(2)}) collective-permute-start(f32[320,128]{1,0:T(8,128)S(1)} %get-tuple-element.68), channel_id=1, source_target_pairs={{0,1},{1,0},{2,3},{3,2},{4,5},{5,4},{6,7},{7,6},{8,9},{9,8},{10,11... | collective-permute-start | bytes 491528 | tf_op jit(solution)/shard_map/ppermute | solution.py:59
  13.5 3.9 %collective-permute-start.4 = (f32[56,128]{1,0:T(8,128)S(1)}, f32[56,128]{1,0:T(8,128)S(1)}, u32[]{:S(2)}, u32[]{:S(2)}) collective-permute-start(f32[56,128]{1,0:T(8,128)S(1)} %get-tuple-element.50), channel_id=1, source_target_pairs={{0,8},{8,0},{16,24},{24,16},{1,9},{9,1},{17,25},{25,17},{2,10},{10... | collective-permute-start | bytes 86024 | tf_op jit(solution)/shard_map/ppermute | solution.py:64
  14.4 3.9 %collective-permute-start.5 = (f32[56,128]{1,0:T(8,128)S(1)}, f32[56,128]{1,0:T(8,128)S(1)}, u32[]{:S(2)}, u32[]{:S(2)}) collective-permute-start(f32[56,128]{1,0:T(8,128)S(1)} %get-tuple-element.51), channel_id=1, source_target_pairs={{0,2},{2,0},{4,6},{6,4},{8,16},{10,18},{12,20},{14,22},{16,8},{18,... | collective-permute-start | bytes 86024 | tf_op jit(solution)/shard_map/ppermute | solution.py:81
  18.9 9.5 %collective-permute-start.6 = (f32[104,128]{1,0:T(8,128)S(1)}, f32[104,128]{1,0:T(8,128)S(1)}, u32[]{:S(2)}, u32[]{:S(2)}) collective-permute-start(f32[104,128]{1,0:T(8,128)S(1)} %get-tuple-element.62), channel_id=1, source_target_pairs={{0,2},{2,0},{4,6},{6,4},{1,3},{3,1},{5,7},{7,5},{8,10},{10,8},{12,... | collective-permute-start | bytes 159752 | tf_op jit(solution)/shard_map/ppermute | solution.py:64
  20.3 8.1 %collective-permute-start.7 = (f32[104,128]{1,0:T(8,128)S(1)}, f32[104,128]{1,0:T(8,128)S(1)}, u32[]{:S(2)}, u32[]{:S(2)}) collective-permute-start(f32[104,128]{1,0:T(8,128)S(1)} %get-tuple-element.63), channel_id=1, source_target_pairs={{0,8},{2,4},{4,2},{6,14},{8,0},{10,12},{12,10},{14,6},{16,24},{18,... | collective-permute-start | bytes 159752 | tf_op jit(solution)/shard_map/ppermute | solution.py:81
  22.6 4.0 %collective-permute-start.9 = (f32[80,128]{1,0:T(8,128)S(1)}, f32[80,128]{1,0:T(8,128)S(1)}, u32[]{:S(2)}, u32[]{:S(2)}) collective-permute-start(f32[80,128]{1,0:T(8,128)S(1)} %shard_map.50.refs_8_), channel_id=1, source_target_pairs={{0,24},{8,0},{16,8},{24,16},{1,25},{9,1},{17,9},{25,17},{2,26},{10... | collective-permute-start | bytes 122888 | tf_op jit(solution)/shard_map/ppermute | solution.py:59

commit v10 on v9

--- a/solution.py
+++ b/solution.py
@@ -434,6 +434,10 @@
     )(*got, fg, node_shift, low_z, after)
 
 
+def fold_row(rows):
+    return (rows + 8) // 16 * 8
+
+
 def line(source, lane, fine, at):
     acc = jnp.zeros(lane.shape, F32)
     for z in range(source.shape[0]):
@@ -446,14 +450,14 @@
     planes, rows, _ = rhs.shape
     cx = rows - 8
     nx, cy = 2 * cx, LANES // 2
-    nz, half = 2 * (planes - 4), nx // 2
+    nz, half, cut = 2 * (planes - 4), nx // 2, fold_row(rows)
     sends = 1 if y_count == 2 else 2
     gots = len(got)
 
     def body(*refs):
         got = refs[:gots]
-        rhs, w, up_, down_, part, inv, _, _, rhs3, w3 = refs[gots : gots + 10]
-        rest = refs[gots + 10 :]
+        rhs, w, up_, down_, part, inv, _, _, _, rhs3, w3 = refs[gots : gots + 11]
+        rest = refs[gots + 11 :]
         out, (add,) = rest[:sends], rest[sends:]
         lane_p = lane_ids(planes)
 
@@ -500,47 +504,51 @@
                 ):
                     there = (lane_c >= at) & (lane_c < at + width)
                     acc = jnp.where(there, shift_lanes(field[z], at - source), acc)
-            ref[:nx, :] = plane(acc, nx) + early[...]
-            ref[nx : nx + 8, :] = line(x_high, lane8, fine, base)
+            ref[:cut, :] = acc[:cut]
+            ref[: rows - cut, :] += shift_lanes(acc[cut:], base)
+            ref[cut - 8 : cut, :] += line(x_high, lane8, fine, base)
+            ref[cut:, :] = early
 
         def up(ref):
-            fill(ref, cy - 2, 2 * cy - 1, up_)
-            ref[nx + 8 :, :] = jnp.zeros((half, LANES), F32)
+            fill(ref, cy - 2, 2 * cy - 1, up_[...])
 
         def down(ref):
-            fill(ref, -1, 0, down_)
             row = row_ids(nx)
             ends = jnp.where(row == 0, line(take_at(low_of, x_face), lane8, 0, 0)[:1, :], 0.0)
             ends += jnp.where(row == nx - 1, line(x_high, lane8, 0, 0)[:1, :], 0.0)
             inverse = inv[...]
             value = part[...] + inverse * ends
-            packed = jnp.zeros((half, LANES), F32)
-            for i, source in enumerate((value[:half], value[half:], inverse[:half], inverse[half:])):
+            packed = down_[...]
+            for i, source in (
+                (1, value[:half]),
+                (2, inverse[:half]),
+                (4, value[half:]),
+                (5, inverse[half:]),
+            ):
                 there = lane_ids(half) // nz == i
                 packed = jnp.where(there, shift_lanes(source, i * nz), packed)
-            ref[nx + 8 :, :] = packed
+            fill(ref, -1, 0, packed)
 
         write_sides("gy", out, up, down)
 
     whole = (planes, rows, LANES)
     return call(
         body,
-        [whole, whole] + [(nx + 8 + half, LANES)] * sends,
+        [whole, whole] + [(cut + half, LANES)] * sends,
         scratch=[whole],
-        in_specs=vmem(gots + 8),
+        in_specs=vmem(gots + 9),
         out_specs=vmem(2 + sends),
     )(*got, rhs, w, *early)
 
 
-def y_early(got_z, fg, node_shift, low_y, after, planes, z_count):
+def y_early(got_z, fg, node_shift, after, z_count):
     nz, nx, _ = fg.shape
     z_at = 9 * (nx // 2 + 8)
-    base = 5 * planes
     n_z = len(got_z)
 
     def body(*refs):
         gz = refs[:n_z]
-        fg, shift, low_y, _, up, down, part, inv = refs[n_z:]
+        fg, shift, _, up, down, part, inv, last = refs[n_z:]
         lane = lane_ids(nx)
         row = row_ids(nx)
 
@@ -551,29 +559,39 @@
         above = side(high_of)
         here = jnp.where(lane == nz, shift_lanes(above, nz), 0.0)
         here = jnp.where(lane == LANES - 1, shift_lanes(side(low_of), -1), here)
-        high = jnp.where(lane == base + nz, shift_lanes(above, base + nz + 1), 0.0)
+        high = jnp.where(lane == nz, shift_lanes(above, nz + 1), 0.0)
         inverse = jnp.ones((nx, LANES), F32)
         inner = jnp.zeros((nx, LANES), F32)
         for z in range(nz):
             guess = fg[z]
             here = jnp.where(lane == z, shift_lanes(guess, z), here)
             inner = jnp.where(lane == z, shift_lanes(guess, z - 1), inner)
-            high = jnp.where(lane == base + z, shift_lanes(guess, base + z + 1), high)
+            high = jnp.where(lane == z, shift_lanes(guess, z + 1), high)
             inverse = jnp.where(lane == z, shift_lanes(6.0 + shift[z], z), inverse)
         inverse = 1.0 / inverse
         around = inner + shift_lanes(here, 1) + shift_lanes(here, -1)
         around += jnp.where(row == 0, 0.0, shift_rows(here, 1))
         around += jnp.where(row == nx - 1, 0.0, shift_rows(here, -1))
-        up[...] = high
-        at = base + nz + 1
-        low = jnp.where((lane >= base) & (lane < at), shift_lanes(here, base), 0.0)
-        down[...] = jnp.where((lane >= at) & (lane < at + 3 * nz), shift_lanes(low_y[...], at), low)
+        last[...] = high
+        half = nx // 2
+        lane_h = lane_ids(half)
+
+        def fold(value):
+            first, second = value[:half], value[half:]
+            block = jnp.where(lane_h < nz, first, 0.0)
+            there = (lane_h >= 3 * nz) & (lane_h < 4 * nz)
+            block = jnp.where(there, shift_lanes(second, 3 * nz), block)
+            block = jnp.where(lane_h == 6 * nz, shift_lanes(first, 5 * nz), block)
+            return jnp.where(lane_h == 6 * nz + 1, shift_lanes(second, 5 * nz + 1), block)
+
+        up[...] = fold(high)
+        down[...] = fold(here)
         part[...] = here + inverse * around
         inv[...] = inverse
 
     return call(
-        body, [(nx, LANES)] * 4, in_specs=vmem(n_z + 4), out_specs=vmem(4)
-    )(*got_z, fg, node_shift, low_y, after)
+        body, [(nx // 2, LANES)] * 2 + [(nx, LANES)] * 3, in_specs=vmem(n_z + 3), out_specs=vmem(5)
+    )(*got_z, fg, node_shift, after)
 
 
 def coarse_stage(got, rhs, w, after, y_count, devices):
@@ -585,7 +603,9 @@
     def body(*refs):
         got = refs[:gots]
         rhs, w, _, v1, v2, sums, tot, inv_, image_ = refs[gots:]
-        values = [ref[:rows, :] for ref in got]
+        cut = fold_row(rows)
+        tail = [shift_lanes(ref[: rows - cut, :], -5 * planes) for ref in got]
+        values = [jnp.concatenate([ref[:cut, :], t], axis=0) for ref, t in zip(got, tail)]
         second = values[1] if gots > 1 else None
         low = low_of("gy", y_count, values[0], second)
         high = high_of("gy", y_count, values[0], second)
@@ -640,17 +660,17 @@
     )(*got, rhs, w, *after)
 
 
-def smooth_stage(scaled, inverses, below, tail_z, tail_x, after, counts):
+def smooth_stage(scaled, inverses, below, tail_z, tail_x, tail_y, after, counts):
     _, nz, nx, _ = scaled.shape
 
     def body(*refs):
         s, inv, lz, lx, ly = refs[:5]
-        tz, gx, _, out, last = refs[5:]
+        tz, gx, ty, _, out = refs[5:]
         lane = lane_ids(nx)
         row = row_ids(nx)
         y_low = from_below("gy", ly[...])
 
-        acc = jnp.zeros((nx, LANES), F32)
+        y_high = from_above("gy", counts[2], ty[...])
         for k in range(3):
             z_low = from_below("gz", lz[k])
             z_high = from_above("gz", counts[0], tz[k * nx : (k + 1) * nx, :])
@@ -664,18 +684,16 @@
                 around += jnp.where(row == nx - 1, x_high[z : z + 1, :], shift_rows(here, -1))
                 spot = k * nz + z
                 around += jnp.where(lane == 0, shift_lanes(y_low, -spot), shift_lanes(here, 1))
-                around += jnp.where(lane == LANES - 1, 0.0, shift_lanes(here, -1))
-                inverse = inv[k, z]
-                acc = jnp.where(lane == spot, shift_lanes(inverse, spot + 1), acc)
-                out[k, z] = here + around * inverse
-        last[...] = acc
-
-    return call(
-        body, [scaled.shape, (nx, LANES)], in_specs=vmem(8), out_specs=vmem(2)
-    )(scaled, inverses, *below, tail_z, tail_x, after)
-
-
-def final_stage(sums, v1, v2, fg, mid, smooth, last, early, tail_z, tail_x, got_x, got_y, counts):
+                right = shift_lanes(y_high, -spot - 1)
+                around += jnp.where(lane == LANES - 1, right, shift_lanes(here, -1))
+                out[k, z] = here + around * inv[k, z]
+
+    return call(
+        body, [scaled.shape], in_specs=vmem(9), out_specs=vmem(1)
+    )(scaled, inverses, *below, tail_z, tail_x, tail_y, after)[0]
+
+
+def final_stage(sums, v1, v2, fg, mid, smooth, early, tail_z, tail_x, got_x, got_y, counts):
     planes, rows, _ = v1.shape
     cz, cx, cy = planes - 4, rows - 8, LANES // 2
     nz, nx, _ = fg.shape
@@ -683,10 +701,10 @@
     gots = n_x + n_y
 
     def body(*refs):
-        sums, v1, v2, fg, part, inv, smooth, last, early, tz, tx = refs[:11]
-        gx = refs[11 : 11 + n_x]
-        gy = refs[11 + n_x : 11 + gots]
-        out, sol, dup, inter, small, lines, buf, sem = refs[11 + gots :]
+        sums, v1, v2, fg, part, inv, smooth, early, tz, tx = refs[:10]
+        gx = refs[10 : 10 + n_x]
+        gy = refs[10 + n_x : 10 + gots]
+        out, sol, dup, inter, small, lines, buf, sem = refs[10 + gots :]
 
         def one_side(pick, refs, axis, size, at):
             values = [ref[at, :] for ref in refs]
@@ -713,10 +731,19 @@
         dup[...] = every.reshape(planes, rows, 2 * LANES)
 
         x_low, x_high = both(gx, "gx", counts[1], slice(3 * planes, 3 * planes + nz + 1))
-        y_low, y_high = both(gy, "gy", counts[2], slice(0, nx))
-        y_row_low, y_row_high = both(gy, "gy", counts[2], slice(nx, nx + 1))
-        half = nx // 2
-        y_pack = one_side(high_of, gy, "gy", counts[2], slice(nx + 8, nx + 8 + half))
+        half, cut = nx // 2, fold_row(rows)
+        y_row_low, y_row_high = both(gy, "gy", counts[2], slice(cut - 8, cut - 7))
+        y_packs = both(gy, "gy", counts[2], slice(cut, cut + half))
+        lane_h = lane_ids(half)
+
+        def unfold(pack):
+            first = jnp.where(lane_h < nz, pack, shift_lanes(pack, -5 * nz))
+            second = shift_lanes(pack, -5 * nz - 1)
+            second = jnp.where(lane_h < nz, shift_lanes(pack, -3 * nz), second)
+            return jnp.concatenate([first, second], axis=0)
+
+        y_low, y_high = [unfold(pack) for pack in y_packs]
+        y_pack = y_packs[1]
         lane = lane_ids(nx)
         row = row_ids(nx)
         base = 5 * planes
@@ -734,8 +761,8 @@
         def nodal(z):
             around = spread_around(z) + jnp.where(row == 0, x_low[z : z + 1, :], 0.0)
             around += jnp.where(row == nx - 1, x_high[z : z + 1, :], 0.0)
-            around += jnp.where(lane == 0, shift_lanes(y_low, -(base + z)), 0.0)
-            around += jnp.where(lane == LANES - 1, shift_lanes(y_high, -(base + z) - 1), 0.0)
+            around += jnp.where(lane == 0, shift_lanes(y_low, -z), 0.0)
+            around += jnp.where(lane == LANES - 1, shift_lanes(y_high, -z - 1), 0.0)
             if z == nz:
                 value = tz[3 * nx : 4 * nx, :] + tz[4 * nx :, :] * (around + fg[nz - 1])
                 return from_above("gz", counts[0], value)
@@ -768,14 +795,14 @@
             odd = jnp.where(lane_c == z, shift_lanes(same + shift_rows(here, -1), z - cy), odd)
         inter[0, pl.ds(0, cx, 2), :] = even[:cx, :]
         inter[0, pl.ds(1, cx, 2), :] = odd[:cx, :]
-        y_base = jnp.concatenate([y_pack, shift_lanes(y_pack, -nz)], axis=0)
+        y_base = jnp.concatenate(
+            [shift_lanes(y_pack, -nz), shift_lanes(y_pack, -4 * nz)], axis=0
+        )
         y_inverse = jnp.concatenate(
-            [shift_lanes(y_pack, -2 * nz), shift_lanes(y_pack, -3 * nz)], axis=0
+            [shift_lanes(y_pack, -2 * nz), shift_lanes(y_pack, -5 * nz)], axis=0
         )
-        y_value = y_base + y_inverse * (shift_lanes(early[...], -base) + inter[0])
+        y_value = y_base + y_inverse * (early[...] + inter[0])
         y_value = from_above("gy", counts[2], y_value)
-        y_fix = shift_lanes(y_high, -(base + nz + 1)) * last[...]
-        y_value += shift_lanes(y_fix, -2 * nz)
 
         def copy(z):
             return pltpu.make_async_copy(buf.at[:, z], out.at[:, z], sem.at[z])
@@ -788,11 +815,7 @@
                 jnp.where(lane == LANES - 1, shift_lanes(y_value, -z - 1), shift_lanes(value, -1))
             )
             for k in range(3):
-                moved = smooth[k, z]
-                if k < 2:
-                    fixed = shift_lanes(y_fix, -(k * nz + z) - 1)
-                    moved += jnp.where(lane == LANES - 1, fixed, 0.0)
-                buf[k, z] = moved + (steps[k] - value)
+                buf[k, z] = smooth[k, z] + (steps[k] - value)
             copy(z).start()
             value = after
         for z in range(nz):
@@ -811,9 +834,9 @@
             pltpu.SemaphoreType.DMA((nz,)),
         ],
         far_out=True,
-        in_specs=vmem(11 + gots),
+        in_specs=vmem(10 + gots),
         out_specs=[pl.BlockSpec(memory_space=pltpu.HBM)],
-    )(sums, v1, v2, fg, *mid, smooth, last, early, tail_z, tail_x, *got_x, *got_y)[0]
+    )(sums, v1, v2, fg, *mid, smooth, early, tail_z, tail_x, *got_x, *got_y)[0]
 
 
 def local(residual, edge_diag, node_shift, coarse_shift):
@@ -825,25 +848,25 @@
     below = []
     for value, axis in ((up_z, "gz"), (up_x, "gx"), (up_y, "gy")):
         below.append(ring(value, axis, 1))
+    tail_y = ring(low_y, "gy", -1)
     fg, rhs, xb, yb, w, *send = nodal_stage(part, node_shift, coarse_shift, *below, counts[0])
     got_z = swap(send, "gz")
     rhs, w, *send = x_stage(got_z, rhs, xb, yb, w, fg, counts[0], counts[1])
     got_x = swap(send, "gx", ("gx", "gy"))
-    planes = rhs.shape[0]
     tail_x = x_tail(got_z, fg, node_shift, low_x, w, counts[0])
     *mid, tail_z = part_stage(got_z, fg, node_shift, low_z, w, counts[0])
-    early = y_early(got_z, fg, node_shift, low_y, w, planes, counts[0])
+    early = y_early(got_z, fg, node_shift, w, counts[0])
     early = (*early, tail_x, mid[1])
     tail_z = ring(tail_z, "gz", -1)
     tail_x = ring(tail_x, "gx", -1)
     rhs, w, *send = y_stage(got_x, rhs, w, early, counts[1], counts[2])
     got_y = swap(send, "gy", ("gx", "gy"))
-    smooth, last = smooth_stage(scaled, inverses, below, tail_z, tail_x, w, counts)
-    v1, v2, sums = coarse_stage(got_y, rhs, w, (last,), counts[2], devices)
+    smooth = smooth_stage(scaled, inverses, below, tail_z, tail_x, tail_y, w, counts)
+    v1, v2, sums = coarse_stage(got_y, rhs, w, (smooth,), counts[2], devices)
     sums = lax.all_to_all(sums, ("gx", "gy", "gz"), 0, 0)
-    early = early[0]
+    early = early[4]
     return final_stage(
-        sums, v1, v2, fg, mid, smooth, last, early, tail_z, tail_x, got_x, got_y, counts
+        sums, v1, v2, fg, mid, smooth, early, tail_z, tail_x, got_x, got_y, counts
     )
 
 

time: 43.1 us -> 38.9 us (0.903)
  waiting for transfers between devices: 8.99 us -> 6.37 us
  blocking collectives: 11.7 us -> 9.78 us
    ppermute x5 -> x6, starting transfers between devices: 6.42 us -> 9.75 us  [ring(): lax.ppermute(value, axis, [(i, (i + step) % size) for i in range(size)])]
    ppermute x5 -> x6, waiting for transfers between devices: 5.7 us -> 3.25 us  [ring(): lax.ppermute(value, axis, [(i, (i + step) % size) for i in range(size)])]
    all_to_all x1, blocking collectives: 11.7 us -> 9.78 us  [local(): sums = lax.all_to_all(sums, ('gx', 'gy', 'gz'), 0, 0)]
    ppermute x2, starting transfers between devices: 3.62 us -> 1.74 us  [swap(): out.append(lax.ppermute(values[1], names, pairs))]
    ppermute x3, starting transfers between devices: 2.35 us -> 1.03 us  [swap(): out = [lax.ppermute(values[0], axis, [(i, i ^ 1) for i in range(size)])]]
    ppermute x2, waiting for transfers between devices: 0.89 us -> 0.08 us  [swap(): out.append(lax.ppermute(values[1], names, pairs))]
    ppermute x3, waiting for transfers between devices: 2.4 us -> 3.05 us  [swap(): out = [lax.ppermute(values[0], axis, [(i, i ^ 1) for i in range(size)])]]
  transfers between devices with their start and end apart: 10 -> 11, of which waited for: 5 -> 4; matrix products, arithmetic and copies ran while one was open for 0% -> 0% of each run, Pallas kernels for 7% -> 9%
where the time goes in v10:
time: 38.9 us; the launch traced here: 38.8 us
  starting transfers between devices  12.5 us (32%)
  Pallas kernels  9.96 us (26%)
  blocking collectives  9.78 us (25%)
  waiting for transfers between devices  6.37 us (16%)
    pallas_call x10, Pallas kernels, apply(): run(*(pltpu.with_memory_space_constraint(a, space) for a, space in zip(ar...  9.96 us
    all_to_all x1, blocking collectives, local(): sums = lax.all_to_all(sums, ('gx', 'gy', 'gz'), 0, 0)  9.78 us
    ppermute x6, starting transfers between devices, ring(): lax.ppermute(value, axis, [(i, (i + step) % size) for i in range(size)])  9.75 us
    ppermute x6, waiting for transfers between devices, ring(): lax.ppermute(value, axis, [(i, (i + step) % size) for i in range(size)])  3.25 us
    ppermute x3, waiting for transfers between devices, swap(): out = [lax.ppermute(values[0], axis, [(i, i ^ 1) for i in range(size)])]  3.05 us
    ppermute x2, starting transfers between devices, swap(): out.append(lax.ppermute(values[1], names, pairs))  1.74 us
    ppermute x3, starting transfers between devices, swap(): out = [lax.ppermute(values[0], axis, [(i, i ^ 1) for i in range(size)])]  1.03 us
  transfers between devices with their start and end apart: 11, of which 4 were waited for; matrix products, arithmetic and copies ran while one was open for 0% of the time, Pallas kernels for 9%

profile of v10, /device:TPU:0, one launch (start us, length us, event | category | flops | bytes accessed | tf_op | source)
XLA Modules:
  0.0 38.8 jit_solution(5488144194568637423)
XLA Ops:
  0.0 2.8 %shard_map.46 = (f32[16,64,128]{2,1,0:T(8,128)S(1)}, f32[3,64,128]{2,1,0:T(8,128)S(1)}, f32[48,128]{1,0:T(8,128)S(1)}, f32[64,128]{1,0:T(8,128)S(1)}, f32[3,64,1...) custom-call(f32[3,16,64,128]{3,2,1,0:T(8,128)} %res.1, ...), custom_call_target="tpu_custom_call" | custom-call | tf_op jit(solution)/shard_map/pallas_call | solution.py:113
  2.8 0.6 %collective-permute-start = (f32[3,64,128]{2,1,0:T(8,128)S(1)}, f32[3,64,128]{2,1,0:T(8,128)S(1)}, u32[]{:S(2)}, u32[]{:S(2)}) collective-permute-start(f32[3,64,128]{2,1,0:T(8,128)S(1)} %get-tuple-element.40), channel_id=1, source_target_pairs={{0,1},{1,0},{2,3},{3,2},{4,5},{5,4},{6,7},{7,6},{8,9},{9,8},{10,11... | collective-permute-start | bytes 294920 | tf_op jit(solution)/shard_map/ppermute | solution.py:59
  3.4 2.6 %collective-permute-start.2 = (f32[64,128]{1,0:T(8,128)S(1)}, f32[64,128]{1,0:T(8,128)S(1)}, u32[]{:S(2)}, u32[]{:S(2)}) collective-permute-start(f32[64,128]{1,0:T(8,128)S(1)} %get-tuple-element.42), channel_id=1, source_target_pairs={{0,2},{2,4},{4,6},{6,0},{1,3},{3,5},{5,7},{7,1},{8,10},{10,12},{12... | collective-permute-start | bytes 98312 | tf_op jit(solution)/shard_map/ppermute | solution.py:59
  6.0 1.5 %collective-permute-start.1 = (f32[48,128]{1,0:T(8,128)S(1)}, f32[48,128]{1,0:T(8,128)S(1)}, u32[]{:S(2)}, u32[]{:S(2)}) collective-permute-start(f32[48,128]{1,0:T(8,128)S(1)} %get-tuple-element.41), channel_id=1, source_target_pairs={{0,8},{8,16},{16,24},{24,0},{1,9},{9,17},{17,25},{25,1},{2,10},{10... | collective-permute-start | bytes 73736 | tf_op jit(solution)/shard_map/ppermute | solution.py:59
  7.5 3.2 %collective-permute-done.1.gx.refs_3_ = f32[48,128]{1,0:T(8,128)S(1)} collective-permute-done((f32[48,128]{1,0:T(8,128)S(1)}, f32[48,128]{1,0:T(8,128)S(1)}, u32[]{:S(2)}, u32[]{:S(2)}) %collective-permute-start.1) | collective-permute-done | bytes 24608 | tf_op jit(solution)/shard_map/ppermute | solution.py:59
  10.8 0.5 %shard_map.47 = (f32[16,64,128]{2,1,0:T(8,128)S(1)}, f32[12,40,128]{2,1,0:T(8,128)S(1)}, f32[8,40,128]{2,1,0:T(8,128)S(1)}, f32[8,40,128]{2,1,0:T(8,128)S(1)}, f...) custom-call(f32[16,64,128]{2,1,0:T(8,128)S(1)} %get-tuple-element.39.part, f32[16,64,128]{2,1,0:T(8,128)S(1)} %copy-done, ...), custom_call_target="tpu_custom_call" | custom-call | tf_op jit(solution)/shard_map/pallas_call | solution.py:113
  11.4 1.5 %collective-permute-done.3.refs_0_ = f32[424,128]{1,0:T(8,128)S(1)} collective-permute-done((f32[424,128]{1,0:T(8,128)S(1)}, f32[424,128]{1,0:T(8,128)S(1)}, u32[]{:S(2)}, u32[]{:S(2)}) %collective-permute-start.3) | collective-permute-done | bytes 217120 | tf_op jit(solution)/shard_map/ppermute | solution.py:64
  12.8 0.2 shard_map.48
  13.0 0.4 shard_map.51
  13.4 0.2 collective-permute-start.8
  13.6 0.9 %collective-permute-start.4 = (f32[56,128]{1,0:T(8,128)S(1)}, f32[56,128]{1,0:T(8,128)S(1)}, u32[]{:S(2)}, u32[]{:S(2)}) collective-permute-start(f32[56,128]{1,0:T(8,128)S(1)} %get-tuple-element.49), channel_id=1, source_target_pairs={{0,8},{8,0},{16,24},{24,16},{1,9},{9,1},{17,25},{25,17},{2,10},{10... | collective-permute-start | bytes 86024 | tf_op jit(solution)/shard_map/ppermute | solution.py:64
  14.5 1.3 %collective-permute-start.5 = (f32[56,128]{1,0:T(8,128)S(1)}, f32[56,128]{1,0:T(8,128)S(1)}, u32[]{:S(2)}, u32[]{:S(2)}) collective-permute-start(f32[56,128]{1,0:T(8,128)S(1)} %get-tuple-element.50), channel_id=1, source_target_pairs={{0,2},{2,0},{4,6},{6,4},{8,16},{10,18},{12,20},{14,22},{16,8},{18,... | collective-permute-start | bytes 86024 | tf_op jit(solution)/shard_map/ppermute | solution.py:81
  15.7 0.1 shard_map.50.refs_9_
  15.8 2.4 %collective-permute-start.9 = (f32[80,128]{1,0:T(8,128)S(1)}, f32[80,128]{1,0:T(8,128)S(1)}, u32[]{:S(2)}, u32[]{:S(2)}) collective-permute-start(f32[80,128]{1,0:T(8,128)S(1)} %shard_map.50.refs_9_), channel_id=1, source_target_pairs={{0,24},{8,0},{16,8},{24,16},{1,25},{9,1},{17,9},{25,17},{2,26},{10... | collective-permute-start | bytes 122888 | tf_op jit(solution)/shard_map/ppermute | solution.py:59
  18.2 2.5 %collective-permute-start.10 = (f32[64,128]{1,0:T(8,128)S(1)}, f32[64,128]{1,0:T(8,128)S(1)}, u32[]{:S(2)}, u32[]{:S(2)}) collective-permute-start(f32[64,128]{1,0:T(8,128)S(1)} %get-tuple-element.68), channel_id=1, source_target_pairs={{0,6},{2,0},{4,2},{6,4},{1,7},{3,1},{5,3},{7,5},{8,14},{10,8},{12,... | collective-permute-start | bytes 98312 | tf_op jit(solution)/shard_map/ppermute | solution.py:59
  20.7 0.7 %shard_map.49 = (f32[32,128]{1,0:T(8,128)S(1)}, f32[32,128]{1,0:T(8,128)S(1)}, f32[64,128]{1,0:T(8,128)S(1)}, f32[64,128]{1,0:T(8,128)S(1)}, f32[64,128]{1,0:T(8,128)S(1)}) custom-call(f32[424,128]{1,0:T(8,128)S(1)} %collective-permute-done.3.refs_0_, f32[16,64,128]{2,1,0:T(8,128)S(1)} %get-tuple-element.48.refs_5_.refs_1_.refs_3_, ...), custom_call_target="tpu_custom_call" | custom-call | tf_op jit(solution)/shard_map/pallas_call | solution.py:113
  21.4 0.8 %shard_map.52 = (f32[12,40,128]{2,1,0:T(8,128)S(1)}, f32[12,40,128]{2,1,0:T(8,128)S(1)}, f32[56,128]{1,0:T(8,128)S(1)}, f32[56,128]{1,0:T(8,128)S(1)}) custom-call(f32[56,128]{1,0:T(8,128)S(1)} %collective-permute-done.4.refs_0_.refs_10_, f32[56,128]{1,0:T(8,128)S(1)} %collective-permute-done.5.refs_1_.refs_11_, ...), custom_call_target="tpu_custom_call" | custom-call | tf_op jit(solution)/shard_map/pallas_call | solution.py:113
  22.3 0.5 %collective-permute-start.7 = (f32[56,128]{1,0:T(8,128)S(1)}, f32[56,128]{1,0:T(8,128)S(1)}, u32[]{:S(2)}, u32[]{:S(2)}) collective-permute-start(f32[56,128]{1,0:T(8,128)S(1)} %get-tuple-element.62), channel_id=1, source_target_pairs={{0,8},{2,4},{4,2},{6,14},{8,0},{10,12},{12,10},{14,6},{16,24},{18,... | collective-permute-start | bytes 86024 | tf_op jit(solution)/shard_map/ppermute | solution.py:81
  22.7 1.8 %shard_map.53.refs_4_.refs_6_ = f32[3,16,64,128]{3,2,1,0:T(8,128)S(1)} custom-call(f32[3,16,64,128]{3,2,1,0:T(8,128)S(1)} %get-tuple-element.65.refs_0_, f32[3,16,64,128]{3,2,1,0:T(8,128)S(1)} %get-tuple-element.66.refs_1_, f32[3,64,128]{2,1,0:T(8,128)S(1)} %collective-permute-done.gz.refs_2_, f32[48,128]{1,0:T(8,128)S(1)} %collective-permute-done.1.gx.refs_3_, ...), custom_call_target="tpu_custom_call" | custom-call | tf_op jit(solution)/shard_map/pallas_call | solution.py:113
  24.5 1.6 %collective-permute-done.6.refs_0_.refs_12_ = f32[56,128]{1,0:T(8,128)S(1)} collective-permute-done((f32[56,128]{1,0:T(8,128)S(1)}, f32[56,128]{1,0:T(8,128)S(1)}, u32[]{:S(2)}, u32[]{:S(2)}) %collective-permute-start.6) | collective-permute-done | bytes 28704 | tf_op jit(solution)/shard_map/ppermute | solution.py:64
  26.1 0.1 collective-permute-done.7.refs_1_.refs_13_
  26.2 0.7 %shard_map.54 = (f32[12,40,128]{2,1,0:T(8,128)S(1)}, f32[12,40,128]{2,1,0:T(8,128)S(1)}, f32[32,1,128]{2,1,0:T(1,128)S(1)}) custom-call(f32[56,128]{1,0:T(8,128)S(1)} %collective-permute-done.6.refs_0_.refs_12_, f32[56,128]{1,0:T(8,128)S(1)} %collective-permute-done.7.refs_1_.refs_13_, f32[12,40,128]{2,1,0:T(8,128)S(1)} %get-tuple-element.63.refs_2_, ...), custom_call_target="tpu_custom_call" | custom-call | tf_op jit(solution)/shard_map/pallas_call | solution.py:113
  26.9 9.8 %all_to_all.5.refs_0_ = f32[32,1,128]{2,1,0:T(1,128)S(1)} all-to-all(f32[32,1,128]{2,1,0:T(1,128)S(1)} %get-tuple-element.69), channel_id=1, replica_groups=mesh['gx'=4,'gy'=4,'gz'=2] {'gx','gy','gz'}, dimensions={0} | all-to-all | bytes 32768 | tf_op jit(solution)/shard_map/all_to_all | solution.py:866
  36.6 2.1 %shard_map.55 = f32[3,16,64,128]{3,2,1,0:T(8,128)} custom-call(f32[32,1,128]{2,1,0:T(1,128)S(1)} %all_to_all.5.refs_0_, f32[12,40,128]{2,1,0:T(8,128)S(1)} %get-tuple-element.70.refs_1_, f32[12,40,128]{2,1,0:T(8,128)S(1)} %get-tuple-element.71.refs_2_, f32[16,64,128]{2,1,0:T(8,128)S(1)} %get-tuple-element.48.refs_5_.refs_1_.refs_3_, ...), custom_call_target="tpu_custom_call" | custom-call | tf_op jit(solution)/shard_map/pallas_call | solution.py:113
  (13 shorter events, 0.2 us)
Async XLA Ops:
  0.0 10.7 %copy-start = (f32[16,64,128]{2,1,0:T(8,128)S(1)}, f32[16,64,128]{2,1,0:T(8,128)}, u32[]{:S(2)}) copy-start(f32[16,64,128]{2,1,0:T(8,128)} %refs_2_.5) | copy-start | bytes 1572868
  0.0 10.8 %copy-start.1 = (f32[8,32,64]{2,1,0:T(8,128)S(1)}, f32[8,32,64]{2,1,0:T(8,128)}, u32[]{:S(2)}) copy-start(f32[8,32,64]{2,1,0:T(8,128)} %coarse.1) | copy-start | bytes 196612
  2.8 7.9 %collective-permute-start = (f32[3,64,128]{2,1,0:T(8,128)S(1)}, f32[3,64,128]{2,1,0:T(8,128)S(1)}, u32[]{:S(2)}, u32[]{:S(2)}) collective-permute-start(f32[3,64,128]{2,1,0:T(8,128)S(1)} %get-tuple-element.40), channel_id=1, source_target_pairs={{0,1},{1,0},{2,3},{3,2},{4,5},{5,4},{6,7},{7,6},{8,9},{9,8},{10,11... | collective-permute-start | bytes 294920 | tf_op jit(solution)/shard_map/ppermute | solution.py:59
  3.4 7.4 %collective-permute-start.2 = (f32[64,128]{1,0:T(8,128)S(1)}, f32[64,128]{1,0:T(8,128)S(1)}, u32[]{:S(2)}, u32[]{:S(2)}) collective-permute-start(f32[64,128]{1,0:T(8,128)S(1)} %get-tuple-element.42), channel_id=1, source_target_pairs={{0,2},{2,4},{4,6},{6,0},{1,3},{3,5},{5,7},{7,1},{8,10},{10,12},{12... | collective-permute-start | bytes 98312 | tf_op jit(solution)/shard_map/ppermute | solution.py:59
  6.0 4.7 %collective-permute-start.1 = (f32[48,128]{1,0:T(8,128)S(1)}, f32[48,128]{1,0:T(8,128)S(1)}, u32[]{:S(2)}, u32[]{:S(2)}) collective-permute-start(f32[48,128]{1,0:T(8,128)S(1)} %get-tuple-element.41), channel_id=1, source_target_pairs={{0,8},{8,16},{16,24},{24,0},{1,9},{9,17},{17,25},{25,1},{2,10},{10... | collective-permute-start | bytes 73736 | tf_op jit(solution)/shard_map/ppermute | solution.py:59
  11.3 1.5 %collective-permute-start.3 = (f32[424,128]{1,0:T(8,128)S(1)}, f32[424,128]{1,0:T(8,128)S(1)}, u32[]{:S(2)}, u32[]{:S(2)}) collective-permute-start(f32[424,128]{1,0:T(8,128)S(1)} %get-tuple-element.43), channel_id=1, source_target_pairs={{0,1},{1,0},{2,3},{3,2},{4,5},{5,4},{6,7},{7,6},{8,9},{9,8},{10,11... | collective-permute-start | bytes 651272 | tf_op jit(solution)/shard_map/ppermute | solution.py:64
  13.4 9.4 %collective-permute-start.8 = (f32[320,128]{1,0:T(8,128)S(1)}, f32[320,128]{1,0:T(8,128)S(1)}, u32[]{:S(2)}, u32[]{:S(2)}) collective-permute-start(f32[320,128]{1,0:T(8,128)S(1)} %get-tuple-element.67), channel_id=1, source_target_pairs={{0,1},{1,0},{2,3},{3,2},{4,5},{5,4},{6,7},{7,6},{8,9},{9,8},{10,11... | collective-permute-start | bytes 491528 | tf_op jit(solution)/shard_map/ppermute | solution.py:59
  13.6 7.8 %collective-permute-start.4 = (f32[56,128]{1,0:T(8,128)S(1)}, f32[56,128]{1,0:T(8,128)S(1)}, u32[]{:S(2)}, u32[]{:S(2)}) collective-permute-start(f32[56,128]{1,0:T(8,128)S(1)} %get-tuple-element.49), channel_id=1, source_target_pairs={{0,8},{8,0},{16,24},{24,16},{1,9},{9,1},{17,25},{25,17},{2,10},{10... | collective-permute-start | bytes 86024 | tf_op jit(solution)/shard_map/ppermute | solution.py:64
  14.5 7.0 %collective-permute-start.5 = (f32[56,128]{1,0:T(8,128)S(1)}, f32[56,128]{1,0:T(8,128)S(1)}, u32[]{:S(2)}, u32[]{:S(2)}) collective-permute-start(f32[56,128]{1,0:T(8,128)S(1)} %get-tuple-element.50), channel_id=1, source_target_pairs={{0,2},{2,0},{4,6},{6,4},{8,16},{10,18},{12,20},{14,22},{16,8},{18,... | collective-permute-start | bytes 86024 | tf_op jit(solution)/shard_map/ppermute | solution.py:81
  15.8 6.9 %collective-permute-start.9 = (f32[80,128]{1,0:T(8,128)S(1)}, f32[80,128]{1,0:T(8,128)S(1)}, u32[]{:S(2)}, u32[]{:S(2)}) collective-permute-start(f32[80,128]{1,0:T(8,128)S(1)} %shard_map.50.refs_9_), channel_id=1, source_target_pairs={{0,24},{8,0},{16,8},{24,16},{1,25},{9,1},{17,9},{25,17},{2,26},{10... | collective-permute-start | bytes 122888 | tf_op jit(solution)/shard_map/ppermute | solution.py:59
  18.2 4.5 %collective-permute-start.10 = (f32[64,128]{1,0:T(8,128)S(1)}, f32[64,128]{1,0:T(8,128)S(1)}, u32[]{:S(2)}, u32[]{:S(2)}) collective-permute-start(f32[64,128]{1,0:T(8,128)S(1)} %get-tuple-element.68), channel_id=1, source_target_pairs={{0,6},{2,0},{4,2},{6,4},{1,7},{3,1},{5,3},{7,5},{8,14},{10,8},{12,... | collective-permute-start | bytes 98312 | tf_op jit(solution)/shard_map/ppermute | solution.py:59
  22.2 3.9 %collective-permute-start.6 = (f32[56,128]{1,0:T(8,128)S(1)}, f32[56,128]{1,0:T(8,128)S(1)}, u32[]{:S(2)}, u32[]{:S(2)}) collective-permute-start(f32[56,128]{1,0:T(8,128)S(1)} %get-tuple-element.61), channel_id=1, source_target_pairs={{0,2},{2,0},{4,6},{6,4},{1,3},{3,1},{5,7},{7,5},{8,10},{10,8},{12,... | collective-permute-start | bytes 86024 | tf_op jit(solution)/shard_map/ppermute | solution.py:64
  22.3 3.9 %collective-permute-start.7 = (f32[56,128]{1,0:T(8,128)S(1)}, f32[56,128]{1,0:T(8,128)S(1)}, u32[]{:S(2)}, u32[]{:S(2)}) collective-permute-start(f32[56,128]{1,0:T(8,128)S(1)} %get-tuple-element.62), channel_id=1, source_target_pairs={{0,8},{2,4},{4,2},{6,14},{8,0},{10,12},{12,10},{14,6},{16,24},{18,... | collective-permute-start | bytes 86024 | tf_op jit(solution)/shard_map/ppermute | solution.py:81
